TPU v7x, 8 devices: a whole 2x2x1 slice. The times are simulated.
8 devices in a mesh: dp: 1 (over z), tp: 2 (over y), dm: 4 (over x, core).
Axes of the slice: x: 2, y: 2, z: 1, core: 2. Of those that a mesh axis runs over, the one named last changes fastest.
Arguments:
- tokens: bfloat16 [8192, 2304], P('dp', 'dm')
- positions: int32 [2, 4096], P('dp')
- norm_pre_attn: bfloat16 [2304], P('dm')
- w_query: bfloat16 [2304, 8, 256], P('dm', 'tp')
- w_key: bfloat16 [2304, 4, 256], P('dm', 'tp')
- w_value: bfloat16 [2304, 4, 256], P('dm', 'tp')
- w_out: bfloat16 [8, 256, 2304], P('tp', None, 'dm')
- norm_post_attn: bfloat16 [2304], P('dm')
- norm_pre_ffw: bfloat16 [2304], P('dm')
- w_gate: bfloat16 [2304, 9216], P('dm', 'tp')
- w_up: bfloat16 [2304, 9216], P('dm', 'tp')
- w_down: bfloat16 [9216, 2304], P('tp', 'dm')
- norm_post_ffw: bfloat16 [2304], P('dm')
Outputs:
- output 1: bfloat16 [8192, 2304], P('dp', 'dm')
- output 2: bfloat16 [8192, 4, 256], P('dp', 'tp')
- output 3: bfloat16 [8192, 4, 256], P('dp', 'tp')
All inputs are finite; a program needn't handle non-finite values.
Results may differ from a plain program's by a relative error of at most 0.02.
Values are sent between devices in bfloat16 or wider.
A program may use at most 1 GiB of HBM per device.

v0:
```python
import jax
import jax.numpy as jnp
from jax import lax
from jax.sharding import PartitionSpec as P

NORM_EPS = 1e-6
SOFT_CAP = 50.0
ROPE_BASE = 10000.0
WINDOW_LEN = 4096


def norm_group(values, gain_vec, model_dim):
    vals32 = values.astype(jnp.float32)
    sq_sum = lax.psum(jnp.sum(vals32 * vals32, axis=-1, keepdims=True), 'dm')
    return vals32 * lax.rsqrt(sq_sum / model_dim + NORM_EPS) * (1.0 + gain_vec.astype(jnp.float32))


def rotary_tables(positions, head_dim):
    half_dim = head_dim // 2
    inv_freq = ROPE_BASE ** (-2.0 * jnp.arange(half_dim, dtype=jnp.float32) / head_dim)
    angles = positions.reshape(-1).astype(jnp.float32)[:, None] * inv_freq[None, :]
    return jnp.cos(angles)[:, None, :], jnp.sin(angles)[:, None, :]


def apply_rotary(head_vals, cos_tab, sin_tab):
    half_dim = head_vals.shape[-1] // 2
    lower_half = head_vals[..., :half_dim].astype(jnp.float32)
    upper_half = head_vals[..., half_dim:].astype(jnp.float32)
    rotated = jnp.concatenate([lower_half * cos_tab - upper_half * sin_tab, upper_half * cos_tab + lower_half * sin_tab], axis=-1)
    return rotated.astype(jnp.bfloat16)


def attend(query_rows, key_rows, value_rows, positions, score_scale):
    num_seqs, seq_len, kv_heads, group_size, head_dim = query_rows.shape
    query_block = min(seq_len, 256)
    key_index = jnp.arange(seq_len)

    def one_block(block_index):
        row_start = block_index * query_block
        q_blk = lax.dynamic_slice_in_dim(query_rows, row_start, query_block, axis=1)
        q_pos = lax.dynamic_slice_in_dim(positions, row_start, query_block, axis=1)
        scores = jnp.einsum('bqkgd,bskd->bkgqs', q_blk, key_rows, preferred_element_type=jnp.float32) * score_scale
        scores = SOFT_CAP * jnp.tanh(scores / SOFT_CAP)
        q_index = row_start + jnp.arange(query_block)
        allowed = (key_index[None, :] <= q_index[:, None])[None] & (q_pos[:, :, None] - positions[:, None, :] < WINDOW_LEN)
        scores = jnp.where(allowed[:, None, None], scores, -1e30)
        attn_probs = jax.nn.softmax(scores, axis=-1).astype(jnp.bfloat16)
        return jnp.einsum('bkgqs,bskd->bqkgd', attn_probs, value_rows, preferred_element_type=jnp.float32).astype(jnp.bfloat16)

    blocks = lax.map(one_block, jnp.arange(seq_len // query_block))
    return jnp.moveaxis(blocks, 0, 1).reshape(num_seqs * seq_len, kv_heads * group_size, head_dim)


def solution(mesh):
    dm_size = mesh.shape['dm']
    tp_size = mesh.shape['tp']

    def layer(tokens, positions, norm_pre_attn, w_query, w_key, w_value, w_out, norm_post_attn, norm_pre_ffw, w_gate, w_up, w_down, norm_post_ffw):
        model_dim = tokens.shape[1] * dm_size
        heads_local, head_dim = w_query.shape[1], w_query.shape[2]
        kv_local = w_key.shape[1]
        num_seqs, seq_len = positions.shape
        score_scale = (model_dim / (heads_local * tp_size)) ** -0.5
        normed = norm_group(tokens, norm_pre_attn, model_dim).astype(jnp.bfloat16)
        query_part = jnp.einsum('nd,dhk->nhk', normed, w_query, preferred_element_type=jnp.float32).astype(jnp.bfloat16)
        key_part = jnp.einsum('nd,dhk->nhk', normed, w_key, preferred_element_type=jnp.float32).astype(jnp.bfloat16)
        value_part = jnp.einsum('nd,dhk->nhk', normed, w_value, preferred_element_type=jnp.float32).astype(jnp.bfloat16)
        query_rows, key_rows, value_rows = lax.psum((query_part, key_part, value_part), 'dm')
        cos_tab, sin_tab = rotary_tables(positions, head_dim)
        query_rows = apply_rotary(query_rows, cos_tab, sin_tab)
        key_rows = apply_rotary(key_rows, cos_tab, sin_tab)
        group_size = heads_local // kv_local
        attn_rows = attend(query_rows.reshape(num_seqs, seq_len, kv_local, group_size, head_dim), key_rows.reshape(num_seqs, seq_len, kv_local, head_dim), value_rows.reshape(num_seqs, seq_len, kv_local, head_dim), positions, score_scale)
        out_part = jnp.einsum('nhk,hkd->nd', attn_rows, w_out, preferred_element_type=jnp.float32).astype(jnp.bfloat16)
        attn_out = lax.psum(out_part, 'tp')
        hidden = (tokens.astype(jnp.float32) + norm_group(attn_out, norm_post_attn, model_dim)).astype(jnp.bfloat16)
        ffw_in = norm_group(hidden, norm_pre_ffw, model_dim).astype(jnp.bfloat16)
        gate_part = jnp.dot(ffw_in, w_gate, preferred_element_type=jnp.float32).astype(jnp.bfloat16)
        up_part = jnp.dot(ffw_in, w_up, preferred_element_type=jnp.float32).astype(jnp.bfloat16)
        gate_proj, up_proj = lax.psum((gate_part, up_part), 'dm')
        gated_act = (jax.nn.gelu(gate_proj.astype(jnp.float32), approximate=True) * up_proj.astype(jnp.float32)).astype(jnp.bfloat16)
        down_part = jnp.dot(gated_act, w_down, preferred_element_type=jnp.float32).astype(jnp.bfloat16)
        down_proj = lax.psum(down_part, 'tp')
        tokens_out = (hidden.astype(jnp.float32) + norm_group(down_proj, norm_post_ffw, model_dim)).astype(jnp.bfloat16)
        return tokens_out, key_rows, value_rows

    width_spec = P('dm')
    in_specs = (P('dp', 'dm'), P('dp', None), width_spec, P('dm', 'tp', None), P('dm', 'tp', None), P('dm', 'tp', None), P('tp', None, 'dm'), width_spec, width_spec, P('dm', 'tp'), P('dm', 'tp'), P('tp', 'dm'), width_spec)
    out_specs = (P('dp', 'dm'), P('dp', 'tp', None), P('dp', 'tp', None))
    return jax.shard_map(layer, mesh=mesh, in_specs=in_specs, out_specs=out_specs, check_vma=False)
```

profile of v0, /device:TPU:0, one launch (start us, length us, event | category | flops | bytes accessed | tf_op | source)
XLA Modules:
  0.0 5125.8 jit_solution(12786257610555596351)
XLA Ops:
  27.2 23.8 convolution_convert_fusion.2
  76.1 18.0 multiply_cosine_fusion
  94.1 533.9 %all-reduce.15.cloned.1.call-done = (bf16[8192,4,256]{2,0,1:T(8,128)(2,1)}, bf16[8192,2,256]{2,0,1:T(8,128)(2,1)}, bf16[8192,2,256]{2,0,1:T(8,128)(2,1)}) async-done(((bf16[8192,4,256]{2,0,1:T(8,128)(2,1)}, bf16[8192,2,256]{2,0,1:T(8,128)(2,1)}, bf16[8192,2,256]{2,0,1:T(8,128)(2,1)}), (bf16[8192,4,256]{2,0,1:T(8,128)(2,1)}, bf16[8192,2,256]{2,0,1:T(8,128)(2,1)}, ...) | async-done | bytes 33554448 | tf_op jit(solution)/shard_map/psum | solution.py:68
  687.7 1307.8 %while.13 = (s32[]{:T(128)}, bf16[16,2,256,2,2,256]{5,2,0,1,4,3:T(8,128)(2,1)}, s32[16]{0:T(128)S(1)}, s32[2,4096]{1,0:T(2,128)S(1)}, bf16[2,4096,2,2,256]{4,1,0...) while((s32[]{:T(128)}, ...), condition=%wide.region_8.9_spmd.clone, body=%wide.region_5.8_spmd.clone.sunk | while | flops 8681689088 | bytes 161538736 | solution.py:50
  691.8 19.4 fusion.91
  711.2 42.0 fusion.93
  773.5 19.4 fusion.91
  792.9 42.0 fusion.93
  834.9 15.4 fusion.94
  855.2 19.4 fusion.91
  874.6 42.0 fusion.93
  936.9 19.4 fusion.91
  956.3 42.0 fusion.93
  1018.6 19.4 fusion.91
  1038.0 42.0 fusion.93
  1100.3 19.4 fusion.91
  1119.7 42.0 fusion.93
  1161.7 15.4 fusion.94
  1182.1 19.4 fusion.91
  1201.5 42.0 fusion.93
  1263.7 19.4 fusion.91
  1283.1 42.0 fusion.93
  1345.5 19.4 fusion.91
  1364.9 42.0 fusion.93
  1427.2 19.4 fusion.91
  1446.6 42.0 fusion.93
  1508.8 19.4 fusion.91
  1528.3 42.0 fusion.93
  1590.6 19.4 fusion.91
  1610.0 42.0 fusion.93
  1672.3 19.4 fusion.91
  1691.7 42.0 fusion.93
  1754.0 19.4 fusion.91
  1773.4 42.0 fusion.93
  1835.7 19.4 fusion.91
  1855.1 42.0 fusion.93
  1917.3 19.4 fusion.91
  1936.8 42.0 fusion.93
  1995.6 16.0 bitcast_convert_fusion
  2011.7 214.9 %all-reduce.7.cloned.1.call-done = bf16[8192,576]{0,1:T(8,128)(2,1)} async-done(((bf16[8192,576]{0,1:T(8,128)(2,1)}), bf16[8192,576]{0,1:T(8,128)(2,1)}) %all-reduce.7.cloned.1.call-update) | async-done | bytes 9437200 | tf_op jit(solution)/shard_map/psum | solution.py:75
  2267.6 67.8 %convolution_convert_fusion = bf16[8192,4608]{1,0:T(8,128)(2,1)} fusion(bf16[576,4608]{1,0:T(8,128)(2,1)} %param.25, bf16[8192,576]{0,1:T(8,128)(2,1)} %get-tuple-element.159, f32[576]{0:T(1024)S(1)} %convert_add_fusion.4, f32[8192]{0:T(1024)S(1)} %bitcast.84), kind=kOutput, calls=%fused_computation.40 | convolution fusion | flops 43543166976 | bytes 90278144 | tf_op jit(solution)/shard_map/dot_general | solution.py:79
  2335.5 68.0 %convolution_convert_fusion.1 = bf16[8192,4608]{1,0:T(8,128)(2,1)} fusion(bf16[576,4608]{1,0:T(8,128)(2,1)} %param.24, bf16[8192,576]{0,1:T(8,128)(2,1)} %get-tuple-element.159, f32[576]{0:T(1024)S(1)} %convert_add_fusion.4, f32[8192]{0:T(1024)S(1)} %bitcast.85), kind=kOutput, calls=%fused_computation.41 | convolution fusion | flops 43543166976 | bytes 90278144 | tf_op jit(solution)/shard_map/dot_general | solution.py:78
  2403.6 1159.6 %all-reduce.11.cloned.1.call-done = bf16[8192,4608]{1,0:T(8,128)(2,1)} async-done(((bf16[8192,4608]{1,0:T(8,128)(2,1)}), bf16[8192,4608]{1,0:T(8,128)(2,1)}) %all-reduce.11.cloned.1.call-update) | async-done | bytes 75497488 | tf_op jit(solution)/shard_map/psum | solution.py:80
  3563.2 1230.5 %all-reduce.9.cloned.1.call-done = bf16[8192,4608]{1,0:T(8,128)(2,1)} async-done(((bf16[8192,4608]{1,0:T(8,128)(2,1)}), bf16[8192,4608]{1,0:T(8,128)(2,1)}) %all-reduce.9.cloned.1.call-update) | async-done | bytes 75497488 | tf_op jit(solution)/shard_map/psum | solution.py:80
  4793.7 80.7 %fusion.51 = bf16[8192,576]{0,1:T(8,128)(2,1)} fusion(bf16[4608,576]{0,1:T(8,128)(2,1)} %param.26, bf16[8192,4608]{1,0:T(8,128)(2,1)} %all-reduce.9.cloned.1.call-done, bf16[8192,4608]{1,0:T(8,128)(2,1)} %all-reduce.11.cloned.1.call-done), kind=kOutput, calls=%fused_computation.76 | convolution fusion | flops 43944247296 | bytes 165740544 | tf_op jit(solution)/shard_map/dot_general | solution.py:82
  4874.5 16.5 copy.36
  4897.4 16.7 copy.35
  4914.2 175.2 %all-reduce.13.cloned.1.call-done = bf16[8192,576]{0,1:T(8,128)(2,1)} async-done(((bf16[8192,576]{0,1:T(8,128)(2,1)}), bf16[8192,576]{0,1:T(8,128)(2,1)}) %all-reduce.13.cloned.1.call-update) | async-done | bytes 9437200 | tf_op jit(solution)/shard_map/psum | solution.py:83
  (173 shorter events, 464.6 us)
Async XLA Ops:
  7.2 20.1 copy-start
  7.2 620.8 %all-reduce.15.cloned.1.call-start = ((), (), s32[]{:S(2)}) async-start(), calls=%async_computation.4 | async-start | bytes 67108864 | tf_op jit(solution)/shard_map/psum | solution.py:68
  27.2 23.8 copy-start.9
  51.0 14.8 copy-start.3
  51.0 14.8 copy-start.10
  75.3 0.8 copy-start.5
  75.4 2151.3 %all-reduce.7.cloned.1.call-start = ((), (), s32[]{:S(2)}) async-start(), calls=%async_computation | async-start | bytes 18874368 | tf_op jit(solution)/shard_map/psum | solution.py:75
  637.2 15.2 copy-start.2
  1995.6 16.1 copy-start.6
  1995.6 16.1 copy-start.7
  2011.6 1551.5 %all-reduce.11.cloned.1.call-start = ((), (), s32[]{:S(2)}) async-start(), calls=%async_computation.2 | async-start | bytes 150994944 | tf_op jit(solution)/shard_map/psum | solution.py:80
  2335.4 2458.3 %all-reduce.9.cloned.1.call-start = ((), (), s32[]{:S(2)}) async-start(), calls=%async_computation.1 | async-start | bytes 150994944 | tf_op jit(solution)/shard_map/psum | solution.py:80
  2403.5 2685.9 %all-reduce.13.cloned.1.call-start = ((), (), s32[]{:S(2)}) async-start(), calls=%async_computation.3 | async-start | bytes 18874368 | tf_op jit(solution)/shard_map/psum | solution.py:83
  4793.7 80.8 %copy-start.8 = (bf16[576]{0:T(1024)(128)(2,1)S(1)}, bf16[576]{0:T(1024)(128)(2,1)}, u32[]{:S(2)}) copy-start(bf16[576]{0:T(1024)(128)(2,1)} %param.27) | copy-start | bytes 3460
  4874.5 16.6 copy-start.4
  4897.4 221.3 %copy-start.1 = (bf16[576,4,256]{2,1,0:T(4,128)(2,1)S(1)}, bf16[576,4,256]{2,1,0:T(4,128)(2,1)}, u32[]{:S(2)}) copy-start(bf16[576,4,256]{2,1,0:T(4,128)(2,1)} %param.18) | copy-start | bytes 3538948
Sparse Core Ops, SparseCore 0:
  75.5 552.4 all-reduce.14
  2011.8 214.8 all-reduce.6
  2335.5 1227.5 all-reduce.10
  3565.5 1228.1 all-reduce.8
  4874.6 214.7 all-reduce.12
where the time goes:
time: 5140 us; the launch traced here: 5130 us
  waiting for transfers between devices  3310 us (64%)
  matrix products  837 us (16%)
  other arithmetic  828 us (16%)
  local copies, waits for them, and re-layouts  74.3 us (1%)
    psum x2, waiting for transfers between devices, layer(): gate_proj, up_proj = lax.psum((gate_part, up_part), 'dm')  2390 us
    sub x16, other arithmetic, one_block(): attn_probs = jax.nn.softmax(scores, axis=-1).astype(jnp.bfloat16)  672 us
    psum x1, waiting for transfers between devices, layer(): lax.psum((query_part, key_part, value_part), 'dm')  534 us
    dot_general x16, matrix products, one_block(): jnp.einsum('bqkgd,bskd->bkgqs', q_blk, key_rows, preferred_element_type=j...  311 us
    dot_general x16, matrix products, one_block(): jnp.einsum('bkgqs,bskd->bqkgd', attn_probs, value_rows, preferred_element...  246 us
    psum x1, waiting for transfers between devices, layer(): attn_out = lax.psum(out_part, 'tp')  215 us
    psum x1, waiting for transfers between devices, layer(): down_proj = lax.psum(down_part, 'tp')  175 us
  transfers between devices with their start and end apart: 5, of which 5 were waited for; matrix products, arithmetic and copies ran while one was open for 2% of the time, Pallas kernels for 0%

commit v1 on v0

v1 whole, which is shorter than its diff:
```python
import functools

import jax
import jax.numpy as jnp
from jax import lax
from jax.experimental import pallas as pl
from jax.experimental.pallas import tpu as pltpu
from jax.sharding import PartitionSpec as P


NORM_EPS = 1e-6
SOFT_CAP = 50.0
ROPE_BASE = 10000.0
WINDOW_LEN = 4096
LOG2E = 1.4426950408889634
BF = jnp.bfloat16
F32 = jnp.float32
VM = 56 * 1024 * 1024
CH = 128
MT = 256
ANY = pl.BlockSpec(memory_space=pl.ANY)


def dot(a, b):
    return jnp.dot(a, b, preferred_element_type=F32)


def dot_nt(a, b):
    return lax.dot_general(a, b, (((1,), (1,)), ((), ())), preferred_element_type=F32)


def whole(*shape):
    return pl.BlockSpec(shape, lambda *_: (0,) * len(shape))


def inv_rms(blocks, width):
    sq = sum(jnp.sum(jnp.square(b.astype(F32)), axis=0, keepdims=True) for b in blocks)
    return lax.rsqrt(sq / width + NORM_EPS)


def part_of(ref, j, size):
    return ref.at[j * size:(j + 1) * size, :]


def call(kernel, grid, in_specs, out_specs, out_shape, scratch=(), prefetch=1, flops=0, nbytes=0, aliases=None):
    return pl.pallas_call(
        kernel,
        out_shape=out_shape,
        grid_spec=pltpu.PrefetchScalarGridSpec(num_scalar_prefetch=prefetch, grid=grid, in_specs=in_specs, out_specs=out_specs, scratch_shapes=list(scratch)),
        cost_estimate=pl.CostEstimate(flops=flops, bytes_accessed=nbytes, transcendentals=0),
        compiler_params=pltpu.CompilerParams(vmem_limit_bytes=VM),
        input_output_aliases=aliases or {},
    )


def norm_kernel(s_ref, own, own_c, rx, rxc, ry, ryc, g_ref, a_ref, *, width, per_half):
    w4 = own.shape[0]
    mine = (pl.program_id(0) // per_half) == s_ref[1]
    blocks = [own[...], own_c[...], jnp.where(mine, rx[...], ry[...]), jnp.where(mine, rxc[...], ryc[...])]
    r = inv_rms(blocks, width)
    for j, b in enumerate(blocks):
        part_of(a_ref, j, w4)[...] = (b.astype(F32) * r * part_of(g_ref, j, w4)[:, 0:1]).astype(BF)


def qkv_kernel(s_ref, a_ref, w0, w1, w2, w3, cos_ref, sin_ref, *rest, hd, aliased):
    if aliased:
        rest = rest[2:]
    qv_ref, kv_ref, w_t, w_all = rest
    w4 = w0.shape[0]

    @pl.when(pl.program_id(0) == 0)
    def _():
        for j, w in enumerate((w0, w1, w2, w3)):
            part_of(w_all, j, w4)[...] = w[...]
        for r in range(0, w_all.shape[0], MT):
            w_t[:, r:r + MT] = w_all[r:r + MT, :].T

    qkv = dot(w_t[...], a_ref[...]).astype(BF).astype(F32)
    ct, st = cos_ref[...], sin_ref[...]
    hh = hd // 2

    def rot(base):
        u1, u2 = qkv[base:base + hh], qkv[base + hh:base + hd]
        return u1 * ct - u2 * st, u2 * ct + u1 * st

    for g in range(2):
        lo, hi = rot(g * hd)
        qv_ref[g * hd:g * hd + hh, :] = lo.astype(BF)
        qv_ref[g * hd + hh:(g + 1) * hd, :] = hi.astype(BF)
    v = qkv[3 * hd:]
    qv_ref[2 * hd:, :] = v.astype(BF)
    klo, khi = rot(2 * hd)
    kv_ref[:, :hh] = klo.T.astype(BF)
    kv_ref[:, hh:hd] = khi.T.astype(BF)
    kv_ref[:, hd:] = v.T.astype(BF)


def attn_kernel(lo_ref, full_ref, q_ref, k_ref, v_ref, pq_ref, pk_ref, o_ref, acc_ref, m_ref, l_ref, *, bq, bk, q_block0, scale):
    qb = q_block0 + pl.program_id(0)
    hd = k_ref.shape[1]
    groups = q_ref.shape[0] // hd
    lo, full = lo_ref[qb], full_ref[qb]
    diag = (qb * bq) // bk
    last = ((qb + 1) * bq + bk - 1) // bk
    m_ref[...] = jnp.full_like(m_ref, -1e30)
    l_ref[...] = jnp.zeros_like(l_ref)
    acc_ref[...] = jnp.zeros_like(acc_ref)

    def step(j, masked):
        rows = pl.ds(pl.multiple_of(j * bk, bk), bk)
        kb = k_ref[rows, :]
        vb = v_ref[:, rows]
        if masked:
            dif = pq_ref[...] - pk_ref[rows, :]
            ok = (dif >= 0) & (dif < WINDOW_LEN)
        for g in range(groups):
            s = dot(kb, q_ref[g * hd:(g + 1) * hd, :])
            s = jnp.tanh(s * (scale / SOFT_CAP)) * (SOFT_CAP * LOG2E)
            if masked:
                s = jnp.where(ok, s, -1e30)
            m_old = m_ref[g]
            m_new = jnp.maximum(m_old, jnp.max(s, axis=0, keepdims=True))
            p = jnp.exp2(s - m_new)
            alpha = jnp.exp2(m_old - m_new)
            l_ref[g] = l_ref[g] * alpha + jnp.sum(p, axis=0, keepdims=True)
            m_ref[g] = m_new
            acc_ref[g] = acc_ref[g] * alpha + dot(vb, p.astype(BF))

    mid = jnp.maximum(jnp.minimum(full, diag), lo)

    def masked_step(j, _):
        step(j, True)
        return 0

    def full_step(j, _):
        step(j, False)
        return 0

    lax.fori_loop(lo, mid, masked_step, 0)
    lax.fori_loop(mid, diag, full_step, 0)
    lax.fori_loop(jnp.maximum(diag, mid), last, masked_step, 0)
    for g in range(groups):
        o_ref[g * hd:(g + 1) * hd, :] = (acc_ref[g] / l_ref[g]).astype(BF)


def norm_to_m(m_ref, blocks, r, g_ref, col, mt_ref):
    w4 = blocks[0].shape[0]
    for j, b in enumerate(blocks):
        part_of(mt_ref, j, w4)[...] = (b * r * part_of(g_ref, j, w4)[:, col:col + 1]).astype(BF)
    for i in range(0, mt_ref.shape[0], MT):
        m_ref[:, i:i + MT] = mt_ref[i:i + MT, :].T


def proj_kernel(s_ref, o_own, o_c, o_y, o_yc, b0, b0c, b1, b1c, b2, b2c, b3, b3c, x0, x1, x2, x3, g_ref, h_ref, m_ref, o_all, mt_ref, *, width):
    c = s_ref[2]
    gw = o_own.shape[0]
    first = c == 0
    o_all[0:gw, :] = jnp.where(first, o_own[...], o_c[...])
    o_all[gw:2 * gw, :] = jnp.where(first, o_c[...], o_own[...])
    o_all[2 * gw:3 * gw, :] = jnp.where(first, o_y[...], o_yc[...])
    o_all[3 * gw:, :] = jnp.where(first, o_yc[...], o_y[...])
    w4 = x0.shape[0]
    heads = b0.shape[0]
    o = o_all[...]
    att = []
    for wy, wo in ((b0, b2), (b0c, b2c), (b1, b3), (b1c, b3c)):
        w = jnp.concatenate([wy[h] for h in range(heads)] + [wo[h] for h in range(heads)], axis=1)
        att.append(dot(w, o).astype(BF).astype(F32))
    r = inv_rms(att, width)
    hs = []
    for j, (t, xr) in enumerate(zip(att, (x0, x1, x2, x3))):
        h = (xr[...].astype(F32) + t * r * part_of(g_ref, j, w4)[:, 1:2]).astype(BF)
        part_of(h_ref, j, w4)[...] = h
        hs.append(h.astype(F32))
    norm_to_m(m_ref, hs, inv_rms(hs, width), g_ref, 2, mt_ref)


def renorm_kernel(s_ref, h_ref, g_ref, m_ref, mt_ref, *, width):
    w4 = h_ref.shape[0] // 4
    hs = [part_of(h_ref, j, w4)[...].astype(F32) for j in (2, 3, 0, 1)]
    norm_to_m(m_ref, hs, inv_rms(hs, width), g_ref, 2, mt_ref)


def gate_up_kernel(s_ref, ma, mb, g0, g1, g2, g3, u0, u1, u2, u3, z_ref):
    n = z_ref.shape[1]
    w = jnp.concatenate([jnp.concatenate([g[...] for g in (g0, g1, g2, g3)], axis=0), jnp.concatenate([u[...] for u in (u0, u1, u2, u3)], axis=0)], axis=1)
    base = 0
    for m in (ma, mb):
        for r in range(0, m.shape[0], MT):
            t = dot(m[r:r + MT, :], w)
            g, u = t[:, :n].astype(BF).astype(F32), t[:, n:].astype(BF).astype(F32)
            z_ref[base:base + MT, :] = (jax.nn.gelu(g, approximate=True) * u).astype(BF)
            base += MT


def down_y_kernel(s_ref, zw, zf, d0, d1, d2, d3, acc_ref, d_ref):
    w4 = d0.shape[0]
    n = zw.shape[0]

    @pl.when(pl.program_id(0) == 0)
    def _():
        for j, dd in enumerate((d0, d1, d2, d3)):
            part_of(d_ref, j, w4)[...] = dd[...]

    z = jnp.concatenate([zw[...], zf[...]], axis=0)
    for j in range(4):
        t = dot_nt(d_ref[j * w4:(j + 1) * w4, :], z)
        for q in range(n // CH):
            acc_ref[q, j * w4:(j + 1) * w4, :CH] = t[:, q * CH:(q + 1) * CH]
            acc_ref[q, j * w4:(j + 1) * w4, CH:] = t[:, n + q * CH:n + (q + 1) * CH]


def tail_kernel(part, zw, zf, d0, d1, d2, d3, hw0, hw1, hf0, hf1, g_ref, out,
                d_ref, z_ref, p_ref, lo_ref, hi_ref, rec_ref, h_ref, sqs_ref, sqr_ref, sqo_ref,
                d_sem, z_sem, p_sem, h_sem, loc_sem, rs_s, rs_r, sq_s, sq_r, out_s, out_r, *, width, chunks):
    w4 = d0.shape[0]
    w2 = 2 * w4
    y = lax.axis_index('tp')
    dm = lax.axis_index('dm')
    x, c = dm // 2, lax.rem(dm, 2)
    px = {'dp': 0, 'tp': y, 'dm': (1 - x) * 2 + c}
    pc = {'dp': 0, 'tp': y, 'dm': x * 2 + 1 - c}
    py = {'dp': 0, 'tp': 1 - y, 'dm': dm}
    pyc = {'dp': 0, 'tp': 1 - y, 'dm': x * 2 + 1 - c}

    def local(src, dst, sem):
        return pltpu.make_async_copy(src, dst, sem)

    def remote(src, dst, s_sem, r_sem, dev):
        return pltpu.make_async_remote_copy(src_ref=src, dst_ref=dst, send_sem=s_sem, recv_sem=r_sem, device_id=dev, device_id_type=pl.DeviceIdType.MESH)

    d_cp = [local(dd, part_of(d_ref, j, w4), d_sem.at[j]) for j, dd in enumerate((d0, d1, d2, d3))]

    def z_cp(p):
        return [local(src.at[pl.ds(p * CH, CH), :], z_ref.at[p, i * CH:(i + 1) * CH, :], z_sem.at[p, i]) for i, src in enumerate((zw, zf))]

    def p_cp(p):
        return local(part.at[p], p_ref.at[lax.rem(p, 2)], p_sem.at[lax.rem(p, 2)])

    per = hw0.shape[1] // CH
    h_cp = []
    for q in range(chunks):
        k, l = q // per, (q % per) * CH
        h_cp.append(local((hw0, hw1)[k].at[0:w2, l:l + CH], h_ref.at[q, :, 0:CH], h_sem.at[q, 0]))
        h_cp.append(local((hf0, hf1)[k].at[w2:2 * w2, l:l + CH], h_ref.at[q, :, CH:2 * CH], h_sem.at[q, 1]))

    for cp in z_cp(0):
        cp.start()
    d_cp[2].start()
    p_cp(0).start()
    d_cp[3].start()
    d_cp[0].start()
    d_cp[1].start()
    for q in range(1, chunks):
        for cp in z_cp(q):
            cp.start()
    for cp in h_cp:
        cp.start()

    bar = pltpu.get_barrier_semaphore()
    for dev in (px, pc, py, pyc):
        pl.semaphore_signal(bar, inc=1, device_id=dev, device_id_type=pl.DeviceIdType.MESH)
    pl.semaphore_wait(bar, 4)

    def rs(p):
        return remote(hi_ref.at[p], rec_ref.at[p], rs_s.at[p], rs_r.at[p], px)

    def sq(p):
        return remote(sqs_ref.at[p], sqr_ref.at[p], sq_s.at[p], sq_r.at[p], px)

    def outs(p):
        k, l = p // per, lax.rem(p, per)
        res = []
        for i, pr in enumerate((x, 1 - x)):
            col = pl.multiple_of(((pr * 2 + k) * 4 + 2 * y + c) * (per * CH) + l * CH, CH)
            mine = rec_ref.at[p, 0:w4, i * CH:(i + 1) * CH]
            give = rec_ref.at[p, w4:w2, i * CH:(i + 1) * CH]
            dst = out.at[:, pl.ds(col, CH)]
            res.append((local(mine, dst, loc_sem.at[p, i]), remote(mine, dst, out_s.at[p, i, 0], out_r.at[p, i, 0], py),
                        remote(give, dst, out_s.at[p, i, 1], out_r.at[p, i, 1], pyc), remote(give, dst, out_s.at[p, i, 2], out_r.at[p, i, 2], pc)))
        return res

    def product(p, first=False):
        p_cp(p).wait()
        for cp in z_cp(p):
            cp.wait()
        if first:
            p_cp(1).start()
        else:
            @pl.when(p + 1 < chunks)
            def _():
                p_cp(p + 1).start()
        slot = lax.rem(p, 2)
        for j in (2, 3, 0, 1):
            if first:
                d_cp[j].wait()
            t = dot_nt(d_ref[j * w4:(j + 1) * w4, :], z_ref[p]) + p_ref[slot, j * w4:(j + 1) * w4, :]
            if j < 2:
                lo_ref[p, j * w4:(j + 1) * w4, :] = t
            else:
                t = t.astype(BF)
                hi_ref[p, (j - 2) * w4:(j - 1) * w4, :CH] = t[:, CH:]
                hi_ref[p, (j - 2) * w4:(j - 1) * w4, CH:] = t[:, :CH]
                if j == 3:
                    rs(p).start()

    def add(p):
        rs(p).wait_recv()
        t = (lo_ref[p] + rec_ref[p].astype(F32)).astype(BF)
        rec_ref[p] = t
        t = t.astype(F32)
        v = jnp.broadcast_to(jnp.sum(t * t, axis=0, keepdims=True), (8, 2 * CH))
        sqo_ref[...] = v
        sqs_ref[p, :, :CH] = v[:, CH:]
        sqs_ref[p, :, CH:] = v[:, :CH]
        sq(p).start()

    def finish(p, v):
        sq(p).wait_recv()
        r = lax.rsqrt((v + sqr_ref[p]) / width + NORM_EPS)[0:1]
        g = g_ref[...]
        g = jnp.concatenate([g] * (2 * CH // 128), axis=1)
        rec_ref[p] = (h_ref[p].astype(F32) + rec_ref[p].astype(F32) * r * g).astype(BF)
        for group in outs(p):
            for cp in group[1:] + group[:1]:
                cp.start()

    product(0, True)
    product(1)
    for cp in h_cp:
        cp.wait()

    def body(p, _):
        add(p)
        v = sqo_ref[...]
        product(p + 2)
        finish(p, v)
        return 0

    lax.fori_loop(0, chunks - 2, body, 0)
    for p in (chunks - 2, chunks - 1):
        add(p)
        finish(p, sqo_ref[...])

    def drain(p, _):
        rs(p).wait_send()
        sq(p).wait_send()
        for group in outs(p):
            group[0].wait()
            for cp in group[1:]:
                cp.wait()
        return 0

    lax.fori_loop(0, chunks, drain, 0)


def kv_out_kernel(s_ref, kv0, kv1, *rest):
    k_ref, v_ref = rest[-2:]
    hd = k_ref.shape[2]
    first = s_ref[2] == 0
    a, b = kv0[...], kv1[...]
    lo, hi = jnp.where(first, a, b), jnp.where(first, b, a)
    k_ref[...] = jnp.stack([lo[:, :hd], hi[:, :hd]], axis=1)
    v_ref[...] = jnp.stack([lo[:, hd:], hi[:, hd:]], axis=1)


def solution(mesh):
    tp_size, dm_size = mesh.shape['tp'], mesh.shape['dm']

    def flip(fy, fx, fc):
        return [(y * 4 + x * 2 + c, (y ^ fy) * 4 + (x ^ fx) * 2 + (c ^ fc)) for y in range(2) for x in range(2) for c in range(2)]

    PX, PY, PC, PXC, PYC = flip(0, 1, 0), flip(1, 0, 0), flip(0, 0, 1), flip(0, 1, 1), flip(1, 0, 1)

    def send(a, perm):
        return lax.ppermute(a, ('tp', 'dm'), perm)

    def layer(tokens, positions, n1, wq, wk, wv, wo, n2, n3, wg, wu, wd, n4):
        y = lax.axis_index('tp')
        d = lax.axis_index('dm')
        x, c = d // 2, d % 2
        xo, yo, co = 1 - x, 1 - y, 1 - c
        rows, w4 = tokens.shape
        D = w4 * dm_size
        S = positions.shape[1]
        hd = wq.shape[2]
        scale = (D / (wq.shape[1] * tp_size)) ** -0.5
        gw = 2 * hd
        half = S // 2
        quarter = half // 4
        F4 = wg.shape[1] // 2
        scal = jnp.stack([x, y, c]).astype(jnp.int32)

        def take(a, start, size, axis=0):
            return lax.dynamic_slice_in_dim(a, start, size, axis)

        xt = tokens.T

        gains = jnp.stack([n1, n2, n3, n4])
        gall = jnp.concatenate([gains, send(gains, PC), send(gains, PX), send(gains, PXC)], axis=1)
        gcol = (1.0 + gall.astype(F32)).T

        rx = [send(take(xt, xo * S + k * half + y * (half // 2), half // 2, 1), PX) for k in range(2)]
        own_c = send(take(xt, x * S, S, 1), PC)
        ry = [send(rx[k], PY) for k in range(2)]
        rxc = [send(rx[k], PC) for k in range(2)]
        ryc = [send(ry[k], PC) for k in range(2)]

        def group_cols(g):
            return jnp.concatenate([take(wq, 2 * g, 2, 1).reshape(w4, gw), take(wk, g, 1, 1).reshape(w4, hd), take(wv, g, 1, 1).reshape(w4, hd)], axis=1)

        wq_own, wq_oth = group_cols(c), group_cols(co)
        wqs = [wq_own, send(wq_oth, PC), send(wq_own, PX), send(wq_oth, PXC)]

        wot = jnp.transpose(wo, (0, 2, 1))
        B0 = wot
        B1 = send(B0, PX)
        B2 = send(B0, PY)
        B3 = send(B1, PY)
        Bs = []
        for b in (B0, B1, B2, B3):
            Bs += [b, send(b, PC)]

        def gather(own, oth):
            r1 = send(oth, PX)
            s0 = send(own, PY)
            s1 = send(r1, PY)
            ty = [own, send(own, PC), r1, send(r1, PC)]
            to = [s0, send(s0, PC), s1, send(s1, PC)]
            return ty, to

        def gu_half(xx):
            return jnp.concatenate([take(wg, xx * F4, F4, 1), take(wu, xx * F4, F4, 1)], axis=1)

        gu_y, gu_o = gather(gu_half(x), gu_half(xo))
        wdt = wd.T
        dn_y, dn_o = gather(take(wdt, x * F4, F4, 1), take(wdt, xo * F4, F4, 1))

        pos = take(positions, x, 1)[0]
        inv_freq = ROPE_BASE ** (-2.0 * jnp.arange(hd // 2, dtype=F32) / hd)
        ang = inv_freq[:, None] * pos.astype(F32)[None, :]
        cos_t, sin_t = jnp.cos(ang), jnp.sin(ang)

        tile = 512
        nt = half // tile
        per_half = nt // 2
        nb = S // tile
        a_sets = []
        for k in range(2):
            a_sets.append(call(
                functools.partial(norm_kernel, width=D, per_half=per_half), (nt,),
                [pl.BlockSpec((w4, tile), lambda i, s, k=k: (0, s[0] * nb + k * nt + i)), pl.BlockSpec((w4, tile), lambda i, s, k=k: (0, k * nt + i))]
                + [pl.BlockSpec((w4, tile), lambda i, s: (0, i % per_half))] * 4 + [whole(D, 4)],
                pl.BlockSpec((D, tile), lambda i, s: (0, i)), jax.ShapeDtypeStruct((D, half), BF),
                flops=100 * D * half)(scal, xt, own_c, rx[k], rxc[k], ry[k], ryc[k], gcol))
        qv = kv = None
        for k in range(2):
            ins = [a_sets[k], *wqs, cos_t, sin_t]
            specs = [pl.BlockSpec((D, tile), lambda i, s: (0, i))] + [whole(w4, 2 * gw)] * 4 + [pl.BlockSpec((hd // 2, tile), lambda i, s, k=k: (0, k * nt + i))] * 2
            aliases = None
            if k == 1:
                ins += [qv, kv]
                specs += [ANY, ANY]
                aliases = {8: 0, 9: 1}
            qv, kv = call(
                functools.partial(qkv_kernel, hd=hd, aliased=k == 1), (nt,), specs,
                [pl.BlockSpec((gw + hd, tile), lambda i, s, k=k: (0, k * nt + i)), pl.BlockSpec((tile, gw), lambda i, s, k=k: (k * nt + i, 0))],
                [jax.ShapeDtypeStruct((gw + hd, S), BF), jax.ShapeDtypeStruct((S, gw), BF)],
                [pltpu.VMEM((2 * gw, D), BF), pltpu.VMEM((D, 2 * gw), BF)],
                flops=2 * D * 2 * gw * half, aliases=aliases)(scal, *ins)

        bq = bk = 512
        first_q, last_q = pos[0::bq][:, None], pos[bq - 1::bq][:, None]
        first_k, last_k = pos[0::bk][None, :], pos[bk - 1::bk][None, :]
        lo_t = jnp.sum((first_q - last_k >= WINDOW_LEN).astype(jnp.int32), axis=1)
        full_t = jnp.sum((last_q - first_k >= WINDOW_LEN).astype(jnp.int32), axis=1)
        pos_row, pos_col = pos.reshape(1, S), pos.reshape(S, 1)
        h_own, m_own = [], []
        for k in range(2):
            q0 = k * half // bq
            kl = (k + 1) * half
            o = call(
                functools.partial(attn_kernel, bq=bq, bk=bk, q_block0=q0, scale=scale), (half // bq,),
                [
                    pl.BlockSpec((gw, bq), lambda i, *_, q0=q0: (0, q0 + i)),
                    pl.BlockSpec((kl, hd), lambda i, *_: (0, 0)),
                    pl.BlockSpec((hd, kl), lambda i, *_: (2, 0)),
                    pl.BlockSpec((1, bq), lambda i, *_, q0=q0: (0, q0 + i)),
                    pl.BlockSpec((kl, 1), lambda i, *_: (0, 0)),
                ],
                pl.BlockSpec((gw, bq), lambda i, *_: (0, i)),
                jax.ShapeDtypeStruct((gw, half), BF),
                [pltpu.VMEM((2, hd, bq), F32), pltpu.VMEM((2, 1, bq), F32), pltpu.VMEM((2, 1, bq), F32)],
                prefetch=2, flops=4 * hd * 2 * half * (k * half + half // 2))(lo_t, full_t, qv, kv, qv, pos_row, pos_col)
            mc = 2 * y + co
            my, myc = 2 * yo + c, 2 * yo + co
            o_c = send(take(o, mc * quarter, quarter, 1), PC)
            o_y = send(take(o, my * quarter, quarter, 1), PY)
            o_yc = send(take(o, myc * quarter, quarter, 1), PYC)
            heads = wo.shape[0]
            qn = half // quarter
            h, m = call(
                functools.partial(proj_kernel, width=D), (1,),
                [pl.BlockSpec((gw, quarter), lambda i, s: (0, 2 * s[1] + s[2]))] + [whole(gw, quarter)] * 3 + [whole(heads, w4, hd)] * 8 + [
                    pl.BlockSpec((w4, quarter), lambda i, s, k=k: (0, s[0] * 2 * qn + k * qn + 2 * s[1] + s[2])),
                    pl.BlockSpec((w4, quarter), lambda i, s, k=k: (0, k * qn + 2 * s[1] + s[2])),
                    pl.BlockSpec((w4, quarter), lambda i, s: (0, s[2])),
                    pl.BlockSpec((w4, quarter), lambda i, s: (0, s[2])),
                    whole(D, 4)],
                [whole(D, quarter), whole(quarter, D)],
                [jax.ShapeDtypeStruct((D, quarter), BF), jax.ShapeDtypeStruct((quarter, D), BF)],
                [pltpu.VMEM((4 * gw, quarter), BF), pltpu.VMEM((D, quarter), BF)],
                flops=2 * D * 4 * gw * quarter)(scal, o, o_c, o_y, o_yc, *Bs, xt, own_c, rx[k], rxc[k], gcol)
            h_own.append(h)
            m_own.append(m)
        h_for = [send(h_own[k], PX) for k in range(2)]
        m_for = []
        for k in range(2):
            m_for.append(call(
                functools.partial(renorm_kernel, width=D), (1,), [whole(D, quarter), whole(D, 4)], whole(quarter, D),
                jax.ShapeDtypeStruct((quarter, D), BF), [pltpu.VMEM((D, quarter), BF)], flops=100 * D * quarter)(scal, h_for[k], gcol))

        ft = 384
        nf = F4 // ft

        def gated(ms, w):
            return call(
                gate_up_kernel, (nf,),
                [whole(quarter, D)] * 2 + [pl.BlockSpec((w4, ft), lambda i, s: (0, i))] * 4 + [pl.BlockSpec((w4, ft), lambda i, s: (0, nf + i))] * 4,
                pl.BlockSpec((2 * quarter, ft), lambda i, s: (0, i)), jax.ShapeDtypeStruct((2 * quarter, F4), BF),
                flops=2 * D * 2 * F4 * 2 * quarter)(scal, *ms, *w, *w)

        z = {(t, hf): gated(ms, w) for hf, w in (('y', gu_y), ('o', gu_o)) for t, ms in (('own', m_own), ('for', m_for))}

        w2 = 2 * w4
        chunks = 2 * quarter // CH
        yt = 2 * CH
        part = call(
            down_y_kernel, (2 * quarter // yt,), [pl.BlockSpec((yt, F4), lambda i, s: (i, 0))] * 2 + [whole(w4, F4)] * 4,
            pl.BlockSpec((yt // CH, D, 2 * CH), lambda i, s: (i, 0, 0)), jax.ShapeDtypeStruct((chunks, D, 2 * CH), F32),
            [pltpu.VMEM((D, F4), BF)], flops=2 * D * F4 * 2 * quarter * 2)(scal, z['own', 'y'], z['for', 'y'], *dn_y)
        dma = pltpu.SemaphoreType.DMA
        out = pl.pallas_call(
            functools.partial(tail_kernel, width=D, chunks=chunks),
            out_shape=jax.ShapeDtypeStruct((w4, rows), BF),
            in_specs=[ANY] * 11 + [pl.BlockSpec(memory_space=pltpu.VMEM)],
            out_specs=ANY,
            scratch_shapes=[
                pltpu.VMEM((D, F4), BF), pltpu.VMEM((chunks, 2 * CH, F4), BF), pltpu.VMEM((2, D, 2 * CH), F32),
                pltpu.VMEM((chunks, w2, 2 * CH), F32), pltpu.VMEM((chunks, w2, 2 * CH), BF), pltpu.VMEM((chunks, w2, 2 * CH), BF),
                pltpu.VMEM((chunks, w2, 2 * CH), BF), pltpu.VMEM((chunks, 8, 2 * CH), F32), pltpu.VMEM((chunks, 8, 2 * CH), F32), pltpu.VMEM((8, 2 * CH), F32),
                dma((4,)), dma((chunks, 2)), dma((2,)), dma((chunks, 2)), dma((chunks, 2)),
                dma((chunks,)), dma((chunks,)), dma((chunks,)), dma((chunks,)), dma((chunks, 2, 3)), dma((chunks, 2, 3))],
            cost_estimate=pl.CostEstimate(flops=2 * D * F4 * 4 * quarter, bytes_accessed=4 * D * rows, transcendentals=0),
            compiler_params=pltpu.CompilerParams(vmem_limit_bytes=60 * 1024 * 1024, collective_id=0, has_side_effects=True),
            name='tail',
        )(part, z['own', 'o'], z['for', 'o'], *dn_o, *h_own, *h_for, jnp.broadcast_to(gcol[:w2, 3:4], (w2, 128)))
        tokens_out = out.T

        kv_c = send(kv, PC)
        kv_x = send(kv, PX)
        kv_xc = send(kv_x, PC)
        nk = S // tile
        kv_outs = []
        for i, (t, tc) in enumerate(((kv, kv_c), (kv_x, kv_xc))):
            kv_outs = call(
                kv_out_kernel, (nk,), [pl.BlockSpec((tile, gw), lambda i, s: (i, 0))] * 2 + [ANY] * len(kv_outs),
                [pl.BlockSpec((tile, 2, hd), lambda j, s, i=i: ((s[0] if i == 0 else 1 - s[0]) * nk + j, 0, 0))] * 2, [jax.ShapeDtypeStruct((rows, 2, hd), BF)] * 2,
                flops=100 * rows * hd, aliases={3: 0, 4: 1} if i else None)(scal, t, tc, *kv_outs)
        k_out, v_out = kv_outs
        return tokens_out, k_out, v_out

    width_spec = P('dm')
    in_specs = (P('dp', 'dm'), P('dp', None), width_spec, P('dm', 'tp', None), P('dm', 'tp', None), P('dm', 'tp', None), P('tp', None, 'dm'), width_spec, width_spec, P('dm', 'tp'), P('dm', 'tp'), P('tp', 'dm'), width_spec)
    out_specs = (P('dp', 'dm'), P('dp', 'tp', None), P('dp', 'tp', None))
    return jax.shard_map(layer, mesh=mesh, in_specs=in_specs, out_specs=out_specs, check_vma=False)
```

time: 5140 us -> 969 us (0.19)
  waiting for transfers between devices: 3310 us -> 365 us
  matrix products: 837 us -> 0 us
  other arithmetic: 828 us -> 25.7 us
  Pallas kernels: 0 us -> 483 us
    psum x5 -> x0, waiting for transfers between devices: 3310 us -> none  [the longest x2 2390 us: layer(): gate_proj, up_proj = lax.psum((gate_part, up_part), 'dm')]
    dot_general x39 -> x0, matrix products: 837 us -> none  [the longest x16 311 us: one_block(): jnp.einsum('bqkgd,bskd->bkgqs', q_blk, key_rows, preferred_element_type=j...]
    sub x16 -> x0, other arithmetic: 672 us -> none  [one_block(): attn_probs = jax.nn.softmax(scores, axis=-1).astype(jnp.bfloat16)]
    pallas_call x0 -> x18, Pallas kernels: none -> 483 us  [the longest x1 145 us: layer(): pl.pallas_call(functools.partial(tail_kernel, width=D, chunks=chunks), ou...]
    ppermute x0 -> x47, waiting for transfers between devices: none -> 365 us  [send(): return lax.ppermute(a, ('tp', 'dm'), perm)]
  transfers between devices with their start and end apart: 5 -> 47, of which waited for: 5 -> 12; matrix products, arithmetic and copies ran while one was open for 2% -> 6% of each run, Pallas kernels for 0% -> 35%
where the time goes in v1:
time: 969 us; the launch traced here: 963 us
  Pallas kernels  483 us (50%)
  waiting for transfers between devices  365 us (38%)
  local copies, waits for them, and re-layouts  52.2 us (5%)
  starting transfers between devices  36.1 us (4%)
  other arithmetic  25.7 us (3%)
    ppermute x47, waiting for transfers between devices, send(): return lax.ppermute(a, ('tp', 'dm'), perm)  365 us
    pallas_call x1, Pallas kernels, layer(): pl.pallas_call(functools.partial(tail_kernel, width=D, chunks=chunks), ou...  145 us
    pallas_call x4, Pallas kernels, gated(): call(gate_up_kernel, (nf,), [whole(quarter, D)] * 2 + [pl.BlockSpec((w4,...  116 us
    pallas_call x2, Pallas kernels, layer(): call(functools.partial(attn_kernel, bq=bq, bk=bk, q_block0=q0, scale=scal...  56.4 us
    ppermute x47, starting transfers between devices, send(): return lax.ppermute(a, ('tp', 'dm'), perm)  36.1 us
    pallas_call x2, Pallas kernels, layer(): call(functools.partial(qkv_kernel, hd=hd, aliased=k == 1), (nt,), specs,...  35.4 us
    pallas_call x2, Pallas kernels, layer(): call(kv_out_kernel, (nk,), [pl.BlockSpec((tile, gw), lambda i, s: (i, 0))...  33.5 us
    pallas_call x1, Pallas kernels, layer(): call(down_y_kernel, (2 * quarter // yt,), [pl.BlockSpec((yt, F4), lambda...  31.2 us
  transfers between devices with their start and end apart: 47, of which 12 were waited for; matrix products, arithmetic and copies ran while one was open for 6% of the time, Pallas kernels for 35%

profile of v1, /device:TPU:0, one launch (start us, length us, event | category | flops | bytes accessed | tf_op | source)
XLA Modules:
  0.0 963.4 jit_solution(16268507865132620044)
XLA Ops:
  0.6 5.1 dynamic-slice_bitcast_fusion
  8.5 2.6 collective-permute-start.1
  11.1 2.0 collective-permute-start.19
  13.2 24.7 %collective-permute-done.1.rx.x2 = bf16[576,1024]{1,0:T(8,128)(2,1)S(1)} collective-permute-done((bf16[576,1024]{1,0:T(8,128)(2,1)S(1)}, bf16[576,1024]{1,0:T(8,128)(2,1)S(1)}, u32[]{:S(2)}, u32[]{:S(2)}) %collective-permute-start.1) | collective-permute-done | bytes 1179680 | tf_op jit(solution)/shard_map/ppermute | solution.py:376
  37.9 2.0 collective-permute-start.3
  40.0 23.2 %collective-permute-done.11.rx.x2 = bf16[576,1024]{1,0:T(8,128)(2,1)S(1)} collective-permute-done((bf16[576,1024]{1,0:T(8,128)(2,1)S(1)}, bf16[576,1024]{1,0:T(8,128)(2,1)S(1)}, u32[]{:S(2)}, u32[]{:S(2)}) %collective-permute-start.11) | collective-permute-done | bytes 1179680 | tf_op jit(solution)/shard_map/ppermute | solution.py:376
  63.2 2.0 collective-permute-start.13
  65.9 3.4 constant_dynamic-slice_fusion.10
  69.4 3.7 constant_dynamic-slice_fusion.12
  78.2 10.1 %collective-permute-done.6 = bf16[4,576]{1,0:T(4,128)(2,1)S(1)} collective-permute-done((bf16[4,576]{1,0:T(4,128)(2,1)}, bf16[4,576]{1,0:T(4,128)(2,1)S(1)}, u32[]{:S(2)}, u32[]{:S(2)}) %collective-permute-start.6) | collective-permute-done | bytes 4640 | tf_op jit(solution)/shard_map/ppermute | solution.py:376
  96.9 2.0 copy.58
  98.9 2.0 copy.51.pk_ref
  100.9 2.5 pad_maximum_fusion.3
  103.4 10.1 %multiply_sine_fusion = (f32[128,4096]{1,0:T(8,128)}, f32[128,4096]{1,0:T(8,128)}) fusion(f32[4096]{0:T(1024)} %bitcast.61, f32[128]{0:T(128)} %multiply_power_fusion), kind=kLoop, calls=%fused_computation.3 | loop fusion | flops 524288 | bytes 4211200 | tf_op jit(solution)/shard_map/sin | solution.py:442
  117.7 7.5 constant_dynamic-slice_fusion
  127.5 11.7 %shard_map.148.a_ref = bf16[2304,2048]{1,0:T(8,128)(2,1)} custom-call(s32[3]{0:T(128)} %pad_add_fusion.s_ref, bf16[576,8192]{1,0:T(8,128)(2,1)} %bitcast.36, bf16[576,4096]{1,0:T(8,128)(2,1)} %collective-permute-done.own_c.x1, bf16[576,1024]{1,0:T(8,128)(2,1)} %copy-done.4, bf16[576,1024]{1,0:T(8,128)(2,1)} %copy-done.6, ...), custom_call_target="tpu_custom_call" | custom-call | flops 471859200 | tf_op jit(solution)/shard_map/pallas_call | solution.py:450
  139.2 11.8 %shard_map.149.a_ref = bf16[2304,2048]{1,0:T(8,128)(2,1)} custom-call(s32[3]{0:T(128)} %pad_add_fusion.s_ref, bf16[576,8192]{1,0:T(8,128)(2,1)} %bitcast.37, bf16[576,4096]{1,0:T(8,128)(2,1)} %collective-permute-done.own_c.x1, bf16[576,1024]{1,0:T(8,128)(2,1)} %copy-done.5, bf16[576,1024]{1,0:T(8,128)(2,1)} %collective-permute-done.12.rxc.x3, ...), custom_call_target="tpu_custom_call" | custom-call | flops 471859200 | tf_op jit(solution)/shard_map/pallas_call | solution.py:450
  151.1 16.4 %collective-permute-done.9.w2 = bf16[576,1024]{1,0:T(8,128)(2,1)} collective-permute-done((bf16[576,1024]{1,0:T(8,128)(2,1)}, bf16[576,1024]{1,0:T(8,128)(2,1)}, u32[]{:S(2)}, u32[]{:S(2)}) %collective-permute-start.9) | collective-permute-done | bytes 1179680 | tf_op jit(solution)/shard_map/ppermute | solution.py:376
  168.9 17.7 %shard_map.150 = (bf16[768,4096]{1,0:T(8,128)(2,1)}, bf16[4096,512]{1,0:T(8,128)(2,1)}) custom-call(s32[3]{0:T(128)} %pad_add_fusion.s_ref, bf16[2304,2048]{1,0:T(8,128)(2,1)} %shard_map.149.a_ref, bf16[576,1024]{1,0:T(8,128)(2,1)} %pad_maximum_fusion.2.w0, bf16[576,1024]{1,0:T(8,128)(2,1)} %collective-permute-done.8.w1, ...), custom_call_target="tpu_custom_call" | custom-call | flops 9663676416 | tf_op jit(solution)/shard_map/pallas_call | solution.py:465
  186.6 17.7 %shard_map.151 = (bf16[768,4096]{1,0:T(8,128)(2,1)}, bf16[4096,512]{1,0:T(8,128)(2,1)}) custom-call(s32[3]{0:T(128)} %pad_add_fusion.s_ref, bf16[2304,2048]{1,0:T(8,128)(2,1)} %shard_map.148.a_ref, bf16[576,1024]{1,0:T(8,128)(2,1)} %pad_maximum_fusion.2.w0, ...), custom_call_target="tpu_custom_call", output_to_operand_aliasing={{0}: (8, {}), {1}: (9, {})} | custom-call | flops 9663676416 | tf_op jit(solution)/shard_map/pallas_call | solution.py:465
  204.3 19.0 %shard_map.152.o_own = bf16[512,2048]{1,0:T(8,128)(2,1)} custom-call(s32[8]{0:T(128)} %get-tuple-element.28.lo_ref, s32[8]{0:T(128)} %get-tuple-element.27.full_ref, bf16[768,4096]{1,0:T(8,128)(2,1)} %get-tuple-element.17.q_ref.v_ref, bf16[4096,512]{1,0:T(8,128)(2,1)} %get-tuple-element.18.k_ref.kv0, bf16[768,4096]{1,0:T(8,128)(2,1)} %get-tuple-element.17.q_ref.v_ref, ...), custom_call_target="tpu_custom_call" | custom-call | flops 4294967296 | tf_op jit(solution)/shard_map/pallas_call | solution.py:482
  223.3 2.6 constant_dynamic-slice_fusion.7
  226.4 3.1 pad_maximum_fusion.1
  231.3 2.7 dynamic-slice_bitcast_fusion.1
  236.6 37.5 %shard_map.154.o_own = bf16[512,2048]{1,0:T(8,128)(2,1)} custom-call(s32[8]{0:T(128)} %get-tuple-element.28.lo_ref, s32[8]{0:T(128)} %get-tuple-element.27.full_ref, bf16[768,4096]{1,0:T(8,128)(2,1)} %get-tuple-element.17.q_ref.v_ref, bf16[4096,512]{1,0:T(8,128)(2,1)} %get-tuple-element.18.k_ref.kv0, bf16[768,4096]{1,0:T(8,128)(2,1)} %get-tuple-element.17.q_ref.v_ref, ...), custom_call_target="tpu_custom_call" | custom-call | flops 12884901888 | tf_op jit(solution)/shard_map/pallas_call | solution.py:482
  274.1 2.3 constant_dynamic-slice_fusion.4
  279.8 11.9 %collective-permute-done.26.o_y = bf16[512,512]{1,0:T(8,128)(2,1)} collective-permute-done((bf16[512,512]{1,0:T(8,128)(2,1)S(1)}, bf16[512,512]{1,0:T(8,128)(2,1)}, u32[]{:S(2)}, u32[]{:S(2)}) %collective-permute-start.26) | collective-permute-done | bytes 524320 | tf_op jit(solution)/shard_map/ppermute | solution.py:376
  291.7 15.1 %shard_map.153 = (bf16[2304,512]{1,0:T(8,128)(2,1)}, bf16[512,2304]{1,0:T(8,128)(2,1)}) custom-call(s32[3]{0:T(128)} %pad_add_fusion.s_ref, bf16[512,2048]{1,0:T(8,128)(2,1)} %shard_map.152.o_own, bf16[512,512]{1,0:T(8,128)(2,1)} %copy-done.13, bf16[512,512]{1,0:T(8,128)(2,1)} %copy-done.14, bf16[512,512]{1,0:T(8,128)(2,1)} %collective-permute-done.17.o_yc, ...), custom_call_target="tpu_custom_call" | custom-call | flops 4831838208 | tf_op jit(solution)/shard_map/pallas_call | solution.py:502
  308.4 15.2 %shard_map.155 = (bf16[2304,512]{1,0:T(8,128)(2,1)}, bf16[512,2304]{1,0:T(8,128)(2,1)}) custom-call(s32[3]{0:T(128)} %pad_add_fusion.s_ref, bf16[512,2048]{1,0:T(8,128)(2,1)} %shard_map.154.o_own, bf16[512,512]{1,0:T(8,128)(2,1)} %copy-done.15, bf16[512,512]{1,0:T(8,128)(2,1)} %collective-permute-done.26.o_y, bf16[512,512]{1,0:T(8,128)(2,1)} %collective-permute-done.27.o_yc, ...), custom_call_target="tpu_custom_call" | custom-call | flops 4831838208 | tf_op jit(solution)/shard_map/pallas_call | solution.py:502
  323.6 2.3 collective-permute-start.31
  325.9 78.1 %collective-permute-done.34.d2 = bf16[576,2304]{1,0:T(8,128)(2,1)} collective-permute-done((bf16[576,2304]{1,0:T(8,128)(2,1)}, bf16[576,2304]{1,0:T(8,128)(2,1)}, u32[]{:S(2)}, u32[]{:S(2)}) %collective-permute-start.34) | collective-permute-done | bytes 2654240 | tf_op jit(solution)/shard_map/ppermute | solution.py:376
  405.1 5.0 pad_maximum_fusion.g0.u0
  411.7 42.8 %collective-permute-done.31.h_ref.hf0 = bf16[2304,512]{1,0:T(8,128)(2,1)S(1)} collective-permute-done((bf16[2304,512]{1,0:T(8,128)(2,1)}, bf16[2304,512]{1,0:T(8,128)(2,1)S(1)}, u32[]{:S(2)}, u32[]{:S(2)}) %collective-permute-start.31) | collective-permute-done | bytes 2359328 | tf_op jit(solution)/shard_map/ppermute | solution.py:376
  454.5 49.6 %collective-permute-done.32.h_ref.hf1 = bf16[2304,512]{1,0:T(8,128)(2,1)S(1)} collective-permute-done((bf16[2304,512]{1,0:T(8,128)(2,1)}, bf16[2304,512]{1,0:T(8,128)(2,1)S(1)}, u32[]{:S(2)}, u32[]{:S(2)}) %collective-permute-start.32) | collective-permute-done | bytes 2359328 | tf_op jit(solution)/shard_map/ppermute | solution.py:376
  507.1 5.8 shard_map.157.ma
  512.9 5.7 shard_map.158.mb
  518.6 16.8 %shard_map.163 = (bf16[8192,2,256]{2,1,0:T(2,128)(2,1)}, bf16[8192,2,256]{2,1,0:T(2,128)(2,1)}) custom-call(s32[3]{0:T(128)} %pad_add_fusion.s_ref, bf16[4096,512]{1,0:T(8,128)(2,1)} %get-tuple-element.18.k_ref.kv0, bf16[4096,512]{1,0:T(8,128)(2,1)} %collective-permute-done.46.kv1), custom_call_target="tpu_custom_call" | custom-call | flops 209715200 | tf_op jit(solution)/shard_map/pallas_call | solution.py:566
  535.9 61.3 %collective-permute-done.44.kv0 = bf16[4096,512]{1,0:T(8,128)(2,1)} collective-permute-done((bf16[4096,512]{1,0:T(8,128)(2,1)S(1)}, bf16[4096,512]{1,0:T(8,128)(2,1)}, u32[]{:S(2)}, u32[]{:S(2)}) %collective-permute-start.44) | collective-permute-done | bytes 4194336 | tf_op jit(solution)/shard_map/ppermute | solution.py:376
  597.7 43.8 %collective-permute-done.38.g2.u2 = bf16[576,4608]{1,0:T(8,128)(2,1)} collective-permute-done((bf16[576,4608]{1,0:T(8,128)(2,1)}, bf16[576,4608]{1,0:T(8,128)(2,1)}, u32[]{:S(2)}, u32[]{:S(2)}) %collective-permute-start.38) | collective-permute-done | bytes 5308448 | tf_op jit(solution)/shard_map/ppermute | solution.py:376
  641.6 29.0 %shard_map.156.zw = bf16[1024,2304]{1,0:T(8,128)(2,1)} custom-call(s32[3]{0:T(128)} %pad_add_fusion.s_ref, bf16[512,2304]{1,0:T(8,128)(2,1)} %get-tuple-element.19.ma, bf16[512,2304]{1,0:T(8,128)(2,1)} %get-tuple-element.20.mb, bf16[576,4608]{1,0:T(8,128)(2,1)} %pad_maximum_fusion.g0.u0, bf16[576,4608]{1,0:T(8,128)(2,1)} %collective-permute-done.28.g1.u1, ...), custom_call_target="tpu_custom_call" | custom-call | flops 21743271936 | tf_op jit(solution)/shard_map/pallas_call | solution.py:527
  670.5 29.2 %shard_map.159.zf = bf16[1024,2304]{1,0:T(8,128)(2,1)} custom-call(s32[3]{0:T(128)} %pad_add_fusion.s_ref, bf16[512,2304]{1,0:T(8,128)(2,1)} %shard_map.157.ma, bf16[512,2304]{1,0:T(8,128)(2,1)} %shard_map.158.mb, bf16[576,4608]{1,0:T(8,128)(2,1)} %pad_maximum_fusion.g0.u0, bf16[576,4608]{1,0:T(8,128)(2,1)} %collective-permute-done.28.g1.u1, ...), custom_call_target="tpu_custom_call" | custom-call | flops 21743271936 | tf_op jit(solution)/shard_map/pallas_call | solution.py:527
  700.3 31.2 %shard_map.160.part = f32[8,2304,256]{2,1,0:T(8,128)} custom-call(s32[3]{0:T(128)} %pad_add_fusion.s_ref, bf16[1024,2304]{1,0:T(8,128)(2,1)} %shard_map.156.zw, bf16[1024,2304]{1,0:T(8,128)(2,1)} %shard_map.159.zf, bf16[576,2304]{1,0:T(8,128)(2,1)} %get-tuple-element.34.d0, bf16[576,2304]{1,0:T(8,128)(2,1)} %collective-permute-done.33.d1, ...), custom_call_target="tpu_custom_call" | custom-call | flops 21743271936 | tf_op jit(solution)/shard_map/pallas_call | solution.py:538
  731.5 2.0 copy-done.8
  733.5 16.8 %shard_map.164 = (bf16[8192,2,256]{2,1,0:T(2,128)(2,1)}, bf16[8192,2,256]{2,1,0:T(2,128)(2,1)}) custom-call(s32[3]{0:T(128)} %pad_add_fusion.s_ref, bf16[4096,512]{1,0:T(8,128)(2,1)} %collective-permute-done.44.kv0, bf16[4096,512]{1,0:T(8,128)(2,1)} %copy-done.8, ...), custom_call_target="tpu_custom_call", output_to_operand_aliasing={{0}: (3, {}), {1}: (4, {})} | custom-call | flops 209715200 | tf_op jit(solution)/shard_map/pallas_call | solution.py:566
  750.3 28.9 %shard_map.161.zw = bf16[1024,2304]{1,0:T(8,128)(2,1)} custom-call(s32[3]{0:T(128)} %pad_add_fusion.s_ref, bf16[512,2304]{1,0:T(8,128)(2,1)} %get-tuple-element.19.ma, bf16[512,2304]{1,0:T(8,128)(2,1)} %get-tuple-element.20.mb, bf16[576,4608]{1,0:T(8,128)(2,1)} %collective-permute-done.36.g0.u0, bf16[576,4608]{1,0:T(8,128)(2,1)} %collective-permute-done.37.g1.u1, ...), custom_call_target="tpu_custom_call" | custom-call | flops 21743271936 | tf_op jit(solution)/shard_map/pallas_call | solution.py:527
  779.2 29.2 %shard_map.162.zf = bf16[1024,2304]{1,0:T(8,128)(2,1)} custom-call(s32[3]{0:T(128)} %pad_add_fusion.s_ref, bf16[512,2304]{1,0:T(8,128)(2,1)} %shard_map.157.ma, bf16[512,2304]{1,0:T(8,128)(2,1)} %shard_map.158.mb, bf16[576,4608]{1,0:T(8,128)(2,1)} %collective-permute-done.36.g0.u0, bf16[576,4608]{1,0:T(8,128)(2,1)} %collective-permute-done.37.g1.u1, ...), custom_call_target="tpu_custom_call" | custom-call | flops 21743271936 | tf_op jit(solution)/shard_map/pallas_call | solution.py:527
  809.4 145.2 %tail.1 = bf16[576,8192]{1,0:T(8,128)(2,1)} custom-call(f32[8,2304,256]{2,1,0:T(8,128)} %shard_map.160.part, bf16[1024,2304]{1,0:T(8,128)(2,1)} %shard_map.161.zw, bf16[1024,2304]{1,0:T(8,128)(2,1)} %shard_map.162.zf, bf16[576,2304]{1,0:T(8,128)(2,1)} %collective-permute-done.40.d0, bf16[576,2304]{1,0:T(8,128)(2,1)} %collective-permute-done.41.d1, ...), custom_call_target="tpu_custom_call" | custom-call | flops 21743271936 | bytes 75497472 | tf_op jit(solution)/shard_map/tail/pallas_call | solution.py:543
  954.6 8.6 copy.72
  (154 shorter events, 43.4 us)
Async XLA Ops:
  5.8 111.7 %collective-permute-start = (bf16[576,4096]{1,0:T(8,128)(2,1)}, bf16[576,4096]{1,0:T(8,128)(2,1)}, u32[]{:S(2)}, u32[]{:S(2)}) collective-permute-start(bf16[576,4096]{1,0:T(8,128)(2,1)} %dynamic-slice_bitcast_fusion), channel_id=1, source_target_pairs={{0,1},{1,0},{2,3},{3,2},{4,5},{5,4},{6,7},{7,6}} | collective-permute-start | bytes 14155784 | tf_op jit(solution)/shard_map/ppermute | solution.py:376
  8.5 29.4 %collective-permute-start.1 = (bf16[576,1024]{1,0:T(8,128)(2,1)S(1)}, bf16[576,1024]{1,0:T(8,128)(2,1)S(1)}, u32[]{:S(2)}, u32[]{:S(2)}) collective-permute-start(bf16[576,1024]{1,0:T(8,128)(2,1)S(1)} %get-tuple-element.32), channel_id=1, source_target_pairs={{0,2},{1,3},{2,0},{3,1},{4,6},{5,7},{6,4},{7,5}} | collective-permute-start | bytes 3538952 | tf_op jit(solution)/shard_map/ppermute | solution.py:376
  11.1 52.1 %collective-permute-start.11 = (bf16[576,1024]{1,0:T(8,128)(2,1)S(1)}, bf16[576,1024]{1,0:T(8,128)(2,1)S(1)}, u32[]{:S(2)}, u32[]{:S(2)}) collective-permute-start(bf16[576,1024]{1,0:T(8,128)(2,1)S(1)} %get-tuple-element.31), channel_id=1, source_target_pairs={{0,2},{1,3},{2,0},{3,1},{4,6},{5,7},{6,4},{7,5}} | collective-permute-start | bytes 3538952 | tf_op jit(solution)/shard_map/ppermute | solution.py:376
  11.1 80.7 %collective-permute-start.19 = (bf16[4,576,256]{2,1,0:T(8,128)(2,1)}, bf16[4,576,256]{2,1,0:T(8,128)(2,1)}, u32[]{:S(2)}, u32[]{:S(2)}) collective-permute-start(bf16[4,576,256]{2,1,0:T(8,128)(2,1)} %bitcast.15.b0), channel_id=1, source_target_pairs={{0,2},{1,3},{2,0},{3,1},{4,6},{5,7},{6,4},{7,5}} | collective-permute-start | bytes 3538952 | tf_op jit(solution)/shard_map/ppermute | solution.py:376
  37.9 54.3 %collective-permute-start.3 = (bf16[576,1024]{1,0:T(8,128)(2,1)S(1)}, bf16[576,1024]{1,0:T(8,128)(2,1)}, u32[]{:S(2)}, u32[]{:S(2)}) collective-permute-start(bf16[576,1024]{1,0:T(8,128)(2,1)S(1)} %collective-permute-done.1.rx.x2), channel_id=1, source_target_pairs={{0,4},{1,5},{2,6},{3,7},{4,0},{5,1},{6,2},{7,3}} | collective-permute-start | bytes 3538952 | tf_op jit(solution)/shard_map/ppermute | solution.py:376
  63.2 29.1 %collective-permute-start.13 = (bf16[576,1024]{1,0:T(8,128)(2,1)S(1)}, bf16[576,1024]{1,0:T(8,128)(2,1)}, u32[]{:S(2)}, u32[]{:S(2)}) collective-permute-start(bf16[576,1024]{1,0:T(8,128)(2,1)S(1)} %collective-permute-done.11.rx.x2), channel_id=1, source_target_pairs={{0,4},{1,5},{2,6},{3,7},{4,0},{5,1},{6,2},{7,3}} | collective-permute-start | bytes 3538952 | tf_op jit(solution)/shard_map/ppermute | solution.py:376
  65.9 10.1 %collective-permute-start.5 = (bf16[4,576]{1,0:T(4,128)(2,1)}, bf16[4,576]{1,0:T(4,128)(2,1)}, u32[]{:S(2)}, u32[]{:S(2)}) collective-permute-start(bf16[4,576]{1,0:T(4,128)(2,1)} %pad_maximum_fusion.4), channel_id=1, source_target_pairs={{0,1},{1,0},{2,3},{3,2},{4,5},{5,4},{6,7},{7,6}} | collective-permute-start | bytes 13832 | tf_op jit(solution)/shard_map/ppermute | solution.py:376
  76.0 12.4 %collective-permute-start.6 = (bf16[4,576]{1,0:T(4,128)(2,1)}, bf16[4,576]{1,0:T(4,128)(2,1)S(1)}, u32[]{:S(2)}, u32[]{:S(2)}) collective-permute-start(bf16[4,576]{1,0:T(4,128)(2,1)} %pad_maximum_fusion.4), channel_id=1, source_target_pairs={{0,2},{1,3},{2,0},{3,1},{4,6},{5,7},{6,4},{7,5}} | collective-permute-start | bytes 13832 | tf_op jit(solution)/shard_map/ppermute | solution.py:376
  88.3 3.4 collective-permute-start.7
  91.7 21.8 %collective-permute-start.2 = (bf16[576,1024]{1,0:T(8,128)(2,1)S(1)}, bf16[576,1024]{1,0:T(8,128)(2,1)S(1)}, u32[]{:S(2)}, u32[]{:S(2)}) collective-permute-start(bf16[576,1024]{1,0:T(8,128)(2,1)S(1)} %collective-permute-done.1.rx.x2), channel_id=1, source_target_pairs={{0,1},{1,0},{2,3},{3,2},{4,5},{5,4},{6,7},{7,6}} | collective-permute-start | bytes 3538952 | tf_op jit(solution)/shard_map/ppermute | solution.py:376
  91.8 21.8 %collective-permute-start.12 = (bf16[576,1024]{1,0:T(8,128)(2,1)S(1)}, bf16[576,1024]{1,0:T(8,128)(2,1)}, u32[]{:S(2)}, u32[]{:S(2)}) collective-permute-start(bf16[576,1024]{1,0:T(8,128)(2,1)S(1)} %collective-permute-done.11.rx.x2), channel_id=1, source_target_pairs={{0,1},{1,0},{2,3},{3,2},{4,5},{5,4},{6,7},{7,6}} | collective-permute-start | bytes 3538952 | tf_op jit(solution)/shard_map/ppermute | solution.py:376
  92.2 23.1 %collective-permute-start.4 = (bf16[576,1024]{1,0:T(8,128)(2,1)}, bf16[576,1024]{1,0:T(8,128)(2,1)}, u32[]{:S(2)}, u32[]{:S(2)}) collective-permute-start(bf16[576,1024]{1,0:T(8,128)(2,1)} %collective-permute-done.3.ry), channel_id=1, source_target_pairs={{0,1},{1,0},{2,3},{3,2},{4,5},{5,4},{6,7},{7,6}} | collective-permute-start | bytes 3538952 | tf_op jit(solution)/shard_map/ppermute | solution.py:376
  92.3 24.5 %collective-permute-start.14 = (bf16[576,1024]{1,0:T(8,128)(2,1)}, bf16[576,1024]{1,0:T(8,128)(2,1)}, u32[]{:S(2)}, u32[]{:S(2)}) collective-permute-start(bf16[576,1024]{1,0:T(8,128)(2,1)} %collective-permute-done.13.ry), channel_id=1, source_target_pairs={{0,1},{1,0},{2,3},{3,2},{4,5},{5,4},{6,7},{7,6}} | collective-permute-start | bytes 3538952 | tf_op jit(solution)/shard_map/ppermute | solution.py:376
  113.5 37.5 %collective-permute-start.8 = (bf16[576,1024]{1,0:T(8,128)(2,1)}, bf16[576,1024]{1,0:T(8,128)(2,1)}, u32[]{:S(2)}, u32[]{:S(2)}) collective-permute-start(bf16[576,1024]{1,0:T(8,128)(2,1)} %pad_maximum_fusion.3), channel_id=1, source_target_pairs={{0,1},{1,0},{2,3},{3,2},{4,5},{5,4},{6,7},{7,6}} | collective-permute-start | bytes 3538952 | tf_op jit(solution)/shard_map/ppermute | solution.py:376
  113.6 55.3 %collective-permute-start.10 = (bf16[576,1024]{1,0:T(8,128)(2,1)}, bf16[576,1024]{1,0:T(8,128)(2,1)}, u32[]{:S(2)}, u32[]{:S(2)}) collective-permute-start(bf16[576,1024]{1,0:T(8,128)(2,1)} %pad_maximum_fusion.3), channel_id=1, source_target_pairs={{0,3},{1,2},{2,1},{3,0},{4,7},{5,6},{6,5},{7,4}} | collective-permute-start | bytes 3538952 | tf_op jit(solution)/shard_map/ppermute | solution.py:376
  115.4 52.1 %collective-permute-start.21 = (bf16[4,576,256]{2,1,0:T(8,128)(2,1)}, bf16[4,576,256]{2,1,0:T(8,128)(2,1)}, u32[]{:S(2)}, u32[]{:S(2)}) collective-permute-start(bf16[4,576,256]{2,1,0:T(8,128)(2,1)} %bitcast.15.b0), channel_id=1, source_target_pairs={{0,4},{1,5},{2,6},{3,7},{4,0},{5,1},{6,2},{7,3}} | collective-permute-start | bytes 3538952 | tf_op jit(solution)/shard_map/ppermute | solution.py:376
  116.9 50.6 %collective-permute-start.9 = (bf16[576,1024]{1,0:T(8,128)(2,1)}, bf16[576,1024]{1,0:T(8,128)(2,1)}, u32[]{:S(2)}, u32[]{:S(2)}) collective-permute-start(bf16[576,1024]{1,0:T(8,128)(2,1)} %pad_maximum_fusion.2.w0), channel_id=1, source_target_pairs={{0,2},{1,3},{2,0},{3,1},{4,6},{5,7},{6,4},{7,5}} | collective-permute-start | bytes 3538952 | tf_op jit(solution)/shard_map/ppermute | solution.py:376
  117.4 51.4 %collective-permute-start.23 = (bf16[4,576,256]{2,1,0:T(8,128)(2,1)}, bf16[4,576,256]{2,1,0:T(8,128)(2,1)}, u32[]{:S(2)}, u32[]{:S(2)}) collective-permute-start(bf16[4,576,256]{2,1,0:T(8,128)(2,1)} %collective-permute-done.19.b1), channel_id=1, source_target_pairs={{0,4},{1,5},{2,6},{3,7},{4,0},{5,1},{6,2},{7,3}} | collective-permute-start | bytes 3538952 | tf_op jit(solution)/shard_map/ppermute | solution.py:376
  151.0 78.5 %collective-permute-start.18 = (bf16[4,576,256]{2,1,0:T(8,128)(2,1)}, bf16[4,576,256]{2,1,0:T(8,128)(2,1)S(1)}, u32[]{:S(2)}, u32[]{:S(2)}) collective-permute-start(bf16[4,576,256]{2,1,0:T(8,128)(2,1)} %bitcast.15.b0), channel_id=1, source_target_pairs={{0,1},{1,0},{2,3},{3,2},{4,5},{5,4},{6,7},{7,6}} | collective-permute-start | bytes 3538952 | tf_op jit(solution)/shard_map/ppermute | solution.py:376
  167.5 66.5 %collective-permute-start.20 = (bf16[4,576,256]{2,1,0:T(8,128)(2,1)}, bf16[4,576,256]{2,1,0:T(8,128)(2,1)}, u32[]{:S(2)}, u32[]{:S(2)}) collective-permute-start(bf16[4,576,256]{2,1,0:T(8,128)(2,1)} %collective-permute-done.19.b1), channel_id=1, source_target_pairs={{0,1},{1,0},{2,3},{3,2},{4,5},{5,4},{6,7},{7,6}} | collective-permute-start | bytes 3538952 | tf_op jit(solution)/shard_map/ppermute | solution.py:376
  167.5 66.5 %collective-permute-start.22 = (bf16[4,576,256]{2,1,0:T(8,128)(2,1)}, bf16[4,576,256]{2,1,0:T(8,128)(2,1)}, u32[]{:S(2)}, u32[]{:S(2)}) collective-permute-start(bf16[4,576,256]{2,1,0:T(8,128)(2,1)} %collective-permute-done.21.b2), channel_id=1, source_target_pairs={{0,1},{1,0},{2,3},{3,2},{4,5},{5,4},{6,7},{7,6}} | collective-permute-start | bytes 3538952 | tf_op jit(solution)/shard_map/ppermute | solution.py:376
  168.9 66.2 %collective-permute-start.24 = (bf16[4,576,256]{2,1,0:T(8,128)(2,1)}, bf16[4,576,256]{2,1,0:T(8,128)(2,1)}, u32[]{:S(2)}, u32[]{:S(2)}) collective-permute-start(bf16[4,576,256]{2,1,0:T(8,128)(2,1)} %collective-permute-done.23.b3), channel_id=1, source_target_pairs={{0,1},{1,0},{2,3},{3,2},{4,5},{5,4},{6,7},{7,6}} | collective-permute-start | bytes 3538952 | tf_op jit(solution)/shard_map/ppermute | solution.py:376
  225.9 10.7 %collective-permute-start.15 = (bf16[512,512]{1,0:T(8,128)(2,1)S(1)}, bf16[512,512]{1,0:T(8,128)(2,1)S(1)}, u32[]{:S(2)}, u32[]{:S(2)}) collective-permute-start(bf16[512,512]{1,0:T(8,128)(2,1)S(1)} %get-tuple-element.44), channel_id=1, source_target_pairs={{0,1},{1,0},{2,3},{3,2},{4,5},{5,4},{6,7},{7,6}} | collective-permute-start | bytes 1572872 | tf_op jit(solution)/shard_map/ppermute | solution.py:376
  229.5 180.6 %collective-permute-start.29 = (bf16[576,4608]{1,0:T(8,128)(2,1)}, bf16[576,4608]{1,0:T(8,128)(2,1)}, u32[]{:S(2)}, u32[]{:S(2)}) collective-permute-start(bf16[576,4608]{1,0:T(8,128)(2,1)} %pad_maximum_fusion.1), channel_id=1, source_target_pairs={{0,2},{1,3},{2,0},{3,1},{4,6},{5,7},{6,4},{7,5}} | collective-permute-start | bytes 15925256 | tf_op jit(solution)/shard_map/ppermute | solution.py:376
  234.0 89.6 %collective-permute-start.33 = (bf16[576,2304]{1,0:T(8,128)(2,1)}, bf16[576,2304]{1,0:T(8,128)(2,1)}, u32[]{:S(2)}, u32[]{:S(2)}) collective-permute-start(bf16[576,2304]{1,0:T(8,128)(2,1)} %get-tuple-element.34.d0), channel_id=1, source_target_pairs={{0,1},{1,0},{2,3},{3,2},{4,5},{5,4},{6,7},{7,6}} | collective-permute-start | bytes 7962632 | tf_op jit(solution)/shard_map/ppermute | solution.py:376
  234.0 170.1 %collective-permute-start.34 = (bf16[576,2304]{1,0:T(8,128)(2,1)}, bf16[576,2304]{1,0:T(8,128)(2,1)}, u32[]{:S(2)}, u32[]{:S(2)}) collective-permute-start(bf16[576,2304]{1,0:T(8,128)(2,1)} %get-tuple-element.33), channel_id=1, source_target_pairs={{0,2},{1,3},{2,0},{3,1},{4,6},{5,7},{6,4},{7,5}} | collective-permute-start | bytes 7962632 | tf_op jit(solution)/shard_map/ppermute | solution.py:376
  235.1 41.3 %collective-permute-start.16 = (bf16[512,512]{1,0:T(8,128)(2,1)}, bf16[512,512]{1,0:T(8,128)(2,1)S(1)}, u32[]{:S(2)}, u32[]{:S(2)}) collective-permute-start(bf16[512,512]{1,0:T(8,128)(2,1)} %get-tuple-element.43), channel_id=1, source_target_pairs={{0,4},{1,5},{2,6},{3,7},{4,0},{5,1},{6,2},{7,3}} | collective-permute-start | bytes 1572872 | tf_op jit(solution)/shard_map/ppermute | solution.py:376
  236.6 40.2 %collective-permute-start.17 = (bf16[512,512]{1,0:T(8,128)(2,1)}, bf16[512,512]{1,0:T(8,128)(2,1)}, u32[]{:S(2)}, u32[]{:S(2)}) collective-permute-start(bf16[512,512]{1,0:T(8,128)(2,1)} %get-tuple-element.42), channel_id=1, source_target_pairs={{0,5},{1,4},{2,7},{3,6},{4,1},{5,0},{6,3},{7,2}} | collective-permute-start | bytes 1572872 | tf_op jit(solution)/shard_map/ppermute | solution.py:376
  276.4 2.0 collective-permute-start.25
  276.8 14.9 %collective-permute-start.26 = (bf16[512,512]{1,0:T(8,128)(2,1)S(1)}, bf16[512,512]{1,0:T(8,128)(2,1)}, u32[]{:S(2)}, u32[]{:S(2)}) collective-permute-start(bf16[512,512]{1,0:T(8,128)(2,1)S(1)} %get-tuple-element.40), channel_id=1, source_target_pairs={{0,4},{1,5},{2,6},{3,7},{4,0},{5,1},{6,2},{7,3}} | collective-permute-start | bytes 1572872 | tf_op jit(solution)/shard_map/ppermute | solution.py:376
  278.3 28.5 %collective-permute-start.27 = (bf16[512,512]{1,0:T(8,128)(2,1)}, bf16[512,512]{1,0:T(8,128)(2,1)}, u32[]{:S(2)}, u32[]{:S(2)}) collective-permute-start(bf16[512,512]{1,0:T(8,128)(2,1)} %get-tuple-element.39), channel_id=1, source_target_pairs={{0,5},{1,4},{2,7},{3,6},{4,1},{5,0},{6,3},{7,2}} | collective-permute-start | bytes 1572872 | tf_op jit(solution)/shard_map/ppermute | solution.py:376
  291.7 213.9 %collective-permute-start.46 = (bf16[4096,512]{1,0:T(8,128)(2,1)S(1)}, bf16[4096,512]{1,0:T(8,128)(2,1)}, u32[]{:S(2)}, u32[]{:S(2)}) collective-permute-start(bf16[4096,512]{1,0:T(8,128)(2,1)S(1)} %copy-done.1), channel_id=1, source_target_pairs={{0,1},{1,0},{2,3},{3,2},{4,5},{5,4},{6,7},{7,6}} | collective-permute-start | bytes 12582920 | tf_op jit(solution)/shard_map/ppermute | solution.py:376
  306.8 103.3 %collective-permute-start.40 = (bf16[576,2304]{1,0:T(8,128)(2,1)}, bf16[576,2304]{1,0:T(8,128)(2,1)}, u32[]{:S(2)}, u32[]{:S(2)}) collective-permute-start(bf16[576,2304]{1,0:T(8,128)(2,1)} %get-tuple-element.34.d0), channel_id=1, source_target_pairs={{0,4},{1,5},{2,6},{3,7},{4,0},{5,1},{6,2},{7,3}} | collective-permute-start | bytes 7962632 | tf_op jit(solution)/shard_map/ppermute | solution.py:376
  323.6 130.9 %collective-permute-start.31 = (bf16[2304,512]{1,0:T(8,128)(2,1)}, bf16[2304,512]{1,0:T(8,128)(2,1)S(1)}, u32[]{:S(2)}, u32[]{:S(2)}) collective-permute-start(bf16[2304,512]{1,0:T(8,128)(2,1)} %get-tuple-element.21.hw0), channel_id=1, source_target_pairs={{0,2},{1,3},{2,0},{3,1},{4,6},{5,7},{6,4},{7,5}} | collective-permute-start | bytes 7077896 | tf_op jit(solution)/shard_map/ppermute | solution.py:376
  404.0 100.1 %collective-permute-start.32 = (bf16[2304,512]{1,0:T(8,128)(2,1)}, bf16[2304,512]{1,0:T(8,128)(2,1)S(1)}, u32[]{:S(2)}, u32[]{:S(2)}) collective-permute-start(bf16[2304,512]{1,0:T(8,128)(2,1)} %get-tuple-element.22.hw1), channel_id=1, source_target_pairs={{0,2},{1,3},{2,0},{3,1},{4,6},{5,7},{6,4},{7,5}} | collective-permute-start | bytes 7077896 | tf_op jit(solution)/shard_map/ppermute | solution.py:376
  405.1 101.6 %copy-start = (f32[4,2304]{0,1:T(8,128)S(1)}, f32[4,2304]{0,1:T(8,128)}, u32[]{:S(2)}) copy-start(f32[4,2304]{0,1:T(8,128)} %copy.46) | copy-start | bytes 110596
  410.1 125.2 %collective-permute-start.28 = (bf16[576,4608]{1,0:T(8,128)(2,1)}, bf16[576,4608]{1,0:T(8,128)(2,1)}, u32[]{:S(2)}, u32[]{:S(2)}) collective-permute-start(bf16[576,4608]{1,0:T(8,128)(2,1)} %pad_maximum_fusion.g0.u0), channel_id=1, source_target_pairs={{0,1},{1,0},{2,3},{3,2},{4,5},{5,4},{6,7},{7,6}} | collective-permute-start | bytes 15925256 | tf_op jit(solution)/shard_map/ppermute | solution.py:376
  410.1 125.2 %collective-permute-start.36 = (bf16[576,4608]{1,0:T(8,128)(2,1)}, bf16[576,4608]{1,0:T(8,128)(2,1)}, u32[]{:S(2)}, u32[]{:S(2)}) collective-permute-start(bf16[576,4608]{1,0:T(8,128)(2,1)} %pad_maximum_fusion.g0.u0), channel_id=1, source_target_pairs={{0,4},{1,5},{2,6},{3,7},{4,0},{5,1},{6,2},{7,3}} | collective-permute-start | bytes 15925256 | tf_op jit(solution)/shard_map/ppermute | solution.py:376
  454.5 142.7 %collective-permute-start.30 = (bf16[576,4608]{1,0:T(8,128)(2,1)}, bf16[576,4608]{1,0:T(8,128)(2,1)}, u32[]{:S(2)}, u32[]{:S(2)}) collective-permute-start(bf16[576,4608]{1,0:T(8,128)(2,1)} %collective-permute-done.29.g2.u2), channel_id=1, source_target_pairs={{0,1},{1,0},{2,3},{3,2},{4,5},{5,4},{6,7},{7,6}} | collective-permute-start | bytes 15925256 | tf_op jit(solution)/shard_map/ppermute | solution.py:376
  504.1 137.4 %collective-permute-start.38 = (bf16[576,4608]{1,0:T(8,128)(2,1)}, bf16[576,4608]{1,0:T(8,128)(2,1)}, u32[]{:S(2)}, u32[]{:S(2)}) collective-permute-start(bf16[576,4608]{1,0:T(8,128)(2,1)} %collective-permute-done.29.g2.u2), channel_id=1, source_target_pairs={{0,4},{1,5},{2,6},{3,7},{4,0},{5,1},{6,2},{7,3}} | collective-permute-start | bytes 15925256 | tf_op jit(solution)/shard_map/ppermute | solution.py:376
  505.6 91.6 %collective-permute-start.44 = (bf16[4096,512]{1,0:T(8,128)(2,1)S(1)}, bf16[4096,512]{1,0:T(8,128)(2,1)}, u32[]{:S(2)}, u32[]{:S(2)}) collective-permute-start(bf16[4096,512]{1,0:T(8,128)(2,1)S(1)} %copy-done.1), channel_id=1, source_target_pairs={{0,2},{1,3},{2,0},{3,1},{4,6},{5,7},{6,4},{7,5}} | collective-permute-start | bytes 12582920 | tf_op jit(solution)/shard_map/ppermute | solution.py:376
  535.3 164.4 %collective-permute-start.35 = (bf16[576,2304]{1,0:T(8,128)(2,1)}, bf16[576,2304]{1,0:T(8,128)(2,1)}, u32[]{:S(2)}, u32[]{:S(2)}) collective-permute-start(bf16[576,2304]{1,0:T(8,128)(2,1)} %collective-permute-done.34.d2), channel_id=1, source_target_pairs={{0,1},{1,0},{2,3},{3,2},{4,5},{5,4},{6,7},{7,6}} | collective-permute-start | bytes 7962632 | tf_op jit(solution)/shard_map/ppermute | solution.py:376
  535.3 164.9 %collective-permute-start.42 = (bf16[576,2304]{1,0:T(8,128)(2,1)}, bf16[576,2304]{1,0:T(8,128)(2,1)S(1)}, u32[]{:S(2)}, u32[]{:S(2)}) collective-permute-start(bf16[576,2304]{1,0:T(8,128)(2,1)} %collective-permute-done.34.d2), channel_id=1, source_target_pairs={{0,4},{1,5},{2,6},{3,7},{4,0},{5,1},{6,2},{7,3}} | collective-permute-start | bytes 7962632 | tf_op jit(solution)/shard_map/ppermute | solution.py:376
  597.2 153.0 %collective-permute-start.37 = (bf16[576,4608]{1,0:T(8,128)(2,1)}, bf16[576,4608]{1,0:T(8,128)(2,1)}, u32[]{:S(2)}, u32[]{:S(2)}) collective-permute-start(bf16[576,4608]{1,0:T(8,128)(2,1)} %collective-permute-done.36.g0.u0), channel_id=1, source_target_pairs={{0,1},{1,0},{2,3},{3,2},{4,5},{5,4},{6,7},{7,6}} | collective-permute-start | bytes 15925256 | tf_op jit(solution)/shard_map/ppermute | solution.py:376
  597.2 134.2 %collective-permute-start.45 = (bf16[4096,512]{1,0:T(8,128)(2,1)}, bf16[4096,512]{1,0:T(8,128)(2,1)S(1)}, u32[]{:S(2)}, u32[]{:S(2)}) collective-permute-start(bf16[4096,512]{1,0:T(8,128)(2,1)} %collective-permute-done.44.kv0), channel_id=1, source_target_pairs={{0,1},{1,0},{2,3},{3,2},{4,5},{5,4},{6,7},{7,6}} | collective-permute-start | bytes 12582920 | tf_op jit(solution)/shard_map/ppermute | solution.py:376
  641.6 108.7 %collective-permute-start.39 = (bf16[576,4608]{1,0:T(8,128)(2,1)}, bf16[576,4608]{1,0:T(8,128)(2,1)}, u32[]{:S(2)}, u32[]{:S(2)}) collective-permute-start(bf16[576,4608]{1,0:T(8,128)(2,1)} %collective-permute-done.38.g2.u2), channel_id=1, source_target_pairs={{0,1},{1,0},{2,3},{3,2},{4,5},{5,4},{6,7},{7,6}} | collective-permute-start | bytes 15925256 | tf_op jit(solution)/shard_map/ppermute | solution.py:376
  699.7 108.7 %collective-permute-start.41 = (bf16[576,2304]{1,0:T(8,128)(2,1)}, bf16[576,2304]{1,0:T(8,128)(2,1)}, u32[]{:S(2)}, u32[]{:S(2)}) collective-permute-start(bf16[576,2304]{1,0:T(8,128)(2,1)} %collective-permute-done.40.d0), channel_id=1, source_target_pairs={{0,1},{1,0},{2,3},{3,2},{4,5},{5,4},{6,7},{7,6}} | collective-permute-start | bytes 7962632 | tf_op jit(solution)/shard_map/ppermute | solution.py:376
  700.2 108.2 %collective-permute-start.43 = (bf16[576,2304]{1,0:T(8,128)(2,1)S(1)}, bf16[576,2304]{1,0:T(8,128)(2,1)}, u32[]{:S(2)}, u32[]{:S(2)}) collective-permute-start(bf16[576,2304]{1,0:T(8,128)(2,1)S(1)} %collective-permute-done.42.d2), channel_id=1, source_target_pairs={{0,1},{1,0},{2,3},{3,2},{4,5},{5,4},{6,7},{7,6}} | collective-permute-start | bytes 7962632 | tf_op jit(solution)/shard_map/ppermute | solution.py:376
  (25 other events, 536.9 us)

commit v2 on v1

v2 whole, which is shorter than its diff:
```python
import functools

import jax
import jax.numpy as jnp
from jax import lax
from jax.experimental import pallas as pl
from jax.experimental.pallas import tpu as pltpu
from jax.sharding import PartitionSpec as P


NORM_EPS = 1e-6
SOFT_CAP = 50.0
ROPE_BASE = 10000.0
WINDOW_LEN = 4096
LOG2E = 1.4426950408889634
BF = jnp.bfloat16
F32 = jnp.float32
VM = 63 * 1024 * 1024
CH = 128
BIG = 2.0 ** 40
SHRINK = 2.0 ** -88
MT = 256
ANY = pl.BlockSpec(memory_space=pl.ANY)


vcat = functools.partial(jnp.concatenate, axis=0)
hcat = functools.partial(jnp.concatenate, axis=1)
by_col = lambda i, *_: (0, i)
by_row = lambda i, *_: (i, 0)


def dot(a, b):
    return jnp.dot(a, b, preferred_element_type=F32)


def dot_nt(a, b):
    return lax.dot_general(a, b, (((1,), (1,)), ((), ())), preferred_element_type=F32)


def whole(*shape):
    return pl.BlockSpec(shape, lambda *_: (0,) * len(shape))


def inv_rms(blocks, width):
    sq = sum(jnp.sum(jnp.square(b.astype(F32)), axis=0, keepdims=True) for b in blocks)
    return lax.rsqrt(sq / width + NORM_EPS)


def part_of(ref, j, size):
    return ref.at[j * size:(j + 1) * size, :]


def call(kernel, grid, in_specs, out_specs, out_shape, scratch=(), prefetch=1, flops=0, nbytes=0, aliases=None):
    return pl.pallas_call(
        kernel,
        out_shape=out_shape,
        grid_spec=pltpu.PrefetchScalarGridSpec(num_scalar_prefetch=prefetch, grid=grid, in_specs=in_specs, out_specs=out_specs, scratch_shapes=list(scratch)),
        cost_estimate=pl.CostEstimate(flops=flops, bytes_accessed=nbytes, transcendentals=0),
        compiler_params=pltpu.CompilerParams(vmem_limit_bytes=VM),
        input_output_aliases=aliases or {},
    )


def norm_kernel(s_ref, own, own_c, rx, rxc, ry, ryc, g_ref, *rest, width, per_half):
    a_ref = rest[-1]
    w4 = own.shape[0]
    mine = (pl.program_id(0) // per_half) == s_ref[1]
    blocks = [own[...], own_c[...], jnp.where(mine, rx[...], ry[...]), jnp.where(mine, rxc[...], ryc[...])]
    r = inv_rms(blocks, width)
    for j, b in enumerate(blocks):
        part_of(a_ref, j, w4)[...] = (b.astype(F32) * r * part_of(g_ref, j, w4)[:, 0:1]).astype(BF)


def qkv_kernel(s_ref, a_ref, w0, w1, w2, w3, cos_ref, sin_ref, qv_ref, kv_ref, w_t, w_all, *, hd):
    w4 = w0.shape[0]

    @pl.when(pl.program_id(0) == 0)
    def _():
        for j, w in enumerate((w0, w1, w2, w3)):
            part_of(w_all, j, w4)[...] = w[...]
        for r in range(0, w_all.shape[0], MT):
            w_t[:, r:r + MT] = w_all[r:r + MT, :].T

    qkv = dot(w_t[...], a_ref[...]).astype(BF).astype(F32)
    ct, st = cos_ref[...], sin_ref[...]
    hh = hd // 2

    def rot(base):
        u1, u2 = qkv[base:base + hh], qkv[base + hh:base + hd]
        return u1 * ct - u2 * st, u2 * ct + u1 * st

    for g in range(2):
        lo, hi = rot(g * hd)
        qv_ref[g * hd:g * hd + hh, :] = lo.astype(BF)
        qv_ref[g * hd + hh:(g + 1) * hd, :] = hi.astype(BF)
    v = qkv[3 * hd:]
    qv_ref[2 * hd:, :] = v.astype(BF)
    klo, khi = rot(2 * hd)
    kv_ref[:, :hh] = klo.T.astype(BF)
    kv_ref[:, hh:hd] = khi.T.astype(BF)
    kv_ref[:, hd:] = v.T.astype(BF)


def attn_kernel(lo_ref, full_ref, q_ref, k_ref, v_ref, pq_ref, pk_ref, o_ref, acc_ref, qq_ref, l_ref, vs_ref, f_ref, *, bq, bk, q_block0, scale):
    qb = q_block0 + pl.program_id(0)
    hd = k_ref.shape[1]
    groups = q_ref.shape[0] // hd
    lo, full = lo_ref[qb], full_ref[qb]
    diag = (qb * bq) // bk
    last = ((qb + 1) * bq + bk - 1) // bk

    @pl.when(pl.program_id(0) == 0)
    def _():
        top = jnp.max(jnp.abs(v_ref[...].astype(F32)), axis=0, keepdims=True)
        top = jnp.max(top, axis=1, keepdims=True)
        f_ref[...] = jnp.broadcast_to(jnp.where(top > BIG, SHRINK, 1.0), f_ref.shape)
        vs_ref[...] = (v_ref[...].astype(F32) * f_ref[0:1, 0:1]).astype(BF)

    for g in range(groups):
        qq_ref[:, g * bq:(g + 1) * bq] = q_ref[g * hd:(g + 1) * hd, :]
    l_ref[...] = jnp.zeros_like(l_ref)
    acc_ref[...] = jnp.zeros_like(acc_ref)

    def step(j, masked):
        rows = pl.ds(pl.multiple_of(j * bk, bk), bk)
        kb = k_ref[rows, :]
        vb = vs_ref[:, rows]
        for n in range(0, groups * bq, MT):
            cols = slice(n, n + MT)
            s = dot(kb, qq_ref[:, cols])
            p = jnp.exp2(jnp.tanh(s * (scale / SOFT_CAP)) * (SOFT_CAP * LOG2E))
            if masked:
                dif = pq_ref[:, n % bq:n % bq + MT] - pk_ref[rows, :]
                p = jnp.where((dif >= 0) & (dif < WINDOW_LEN), p, 0.0)
            l_ref[:, cols] += jnp.sum(p, axis=0, keepdims=True)
            acc_ref[:, cols] += dot(vb, p.astype(BF))

    mid = jnp.maximum(jnp.minimum(full, diag), lo)

    def masked_step(j, _):
        step(j, True)
        return 0

    def full_step(j, _):
        step(j, False)
        return 0

    lax.fori_loop(lo, mid, masked_step, 0)
    lax.fori_loop(mid, diag, full_step, 0)
    lax.fori_loop(jnp.maximum(diag, mid), last, masked_step, 0)
    for g in range(groups):
        cols = slice(g * bq, (g + 1) * bq)
        o_ref[g * hd:(g + 1) * hd, :] = (acc_ref[:, cols] / l_ref[:, cols] / f_ref[0:1, 0:1]).astype(BF)


def norm_to_m(m_ref, blocks, r, g_ref, col, mt_ref):
    w4 = blocks[0].shape[0]
    for j, b in enumerate(blocks):
        part_of(mt_ref, j, w4)[...] = (b * r * part_of(g_ref, j, w4)[:, col:col + 1]).astype(BF)
    for i in range(0, mt_ref.shape[0], MT):
        m_ref[:, i:i + MT] = mt_ref[i:i + MT, :].T


def proj_kernel(s_ref, o_own, o_c, o_y, o_yc, b0, b0c, b1, b1c, b2, b2c, b3, b3c, x0, x1, x2, x3, g_ref, h_ref, m_ref, o_all, mt_ref, w_ref, w_sem, *, width):
    cps = [pltpu.make_async_copy(b, w_ref.at[i], w_sem.at[i]) for i, b in enumerate((b0, b2, b0c, b2c, b1, b3, b1c, b3c))]
    for cp in cps:
        cp.start()
    c = s_ref[2]
    gw = o_own.shape[0]
    first = c == 0
    for i, (a, b) in enumerate(((o_own, o_c), (o_c, o_own), (o_y, o_yc), (o_yc, o_y))):
        part_of(o_all, i, gw)[...] = jnp.where(first, a[...], b[...])
    w4 = x0.shape[0]
    heads = b0.shape[0]
    o = o_all[...]
    att = []
    for j in range(4):
        two = (2 * j, 2 * j + 1)
        for i in two:
            cps[i].wait()
        w = hcat([w_ref[i, h] for i in two for h in range(heads)])
        att.append(dot(w, o).astype(BF).astype(F32))
    r = inv_rms(att, width)
    hs = []
    for j, (t, xr) in enumerate(zip(att, (x0, x1, x2, x3))):
        h = (xr[...].astype(F32) + t * r * part_of(g_ref, j, w4)[:, 1:2]).astype(BF)
        part_of(h_ref, j, w4)[...] = h
        hs.append(h.astype(F32))
    norm_to_m(m_ref, hs, inv_rms(hs, width), g_ref, 2, mt_ref)


def renorm_kernel(s_ref, h_ref, g_ref, m_ref, mt_ref, *, width):
    w4 = h_ref.shape[0] // 4
    hs = [part_of(h_ref, j, w4)[...].astype(F32) for j in (2, 3, 0, 1)]
    norm_to_m(m_ref, hs, inv_rms(hs, width), g_ref, 2, mt_ref)


def gate_up_kernel(s_ref, ma, mb, g0, g1, g2, g3, u0, u1, u2, u3, z_ref):
    n = z_ref.shape[1]
    w = hcat([vcat([g[...] for g in (g0, g1, g2, g3)]), vcat([u[...] for u in (u0, u1, u2, u3)])])
    base = 0
    for m in (ma, mb):
        for r in range(0, m.shape[0], MT):
            t = dot(m[r:r + MT, :], w)
            g, u = t[:, :n].astype(BF).astype(F32), t[:, n:].astype(BF).astype(F32)
            z_ref[base:base + MT, :] = (jax.nn.gelu(g, approximate=True) * u).astype(BF)
            base += MT


def down_y_kernel(s_ref, zwa, zwb, zfa, zfb, d0, d1, d2, d3, acc_ref, d_ref):
    w4 = d0.shape[0]
    n = zwa.shape[0]

    @pl.when(pl.program_id(0) == 0)
    def _():
        for j, dd in enumerate((d0, d1, d2, d3)):
            part_of(d_ref, j, w4)[...] = dd[...]

    z = vcat([hcat([a[...], b[...]]) for a, b in ((zwa, zwb), (zfa, zfb))])
    for j in range(4):
        t = dot_nt(d_ref[j * w4:(j + 1) * w4, :], z)
        for q in range(n // CH):
            acc_ref[q, j * w4:(j + 1) * w4, :CH] = t[:, q * CH:(q + 1) * CH]
            acc_ref[q, j * w4:(j + 1) * w4, CH:] = t[:, n + q * CH:n + (q + 1) * CH]


def tail_kernel(part, zwa, zwb, zfa, zfb, d0, d1, d2, d3, hw0, hw1, hf0, hf1, g_ref, out,
                d_ref, z_ref, p_ref, lo_ref, hi_ref, rec_ref, h_ref, sqs_ref, sqr_ref, sqo_ref,
                d_sem, z_sem, p_sem, h_sem, loc_sem, rs_s, rs_r, sq_s, sq_r, out_s, out_r, *, width, chunks):
    w4 = d0.shape[0]
    w2 = 2 * w4
    f8 = zwa.shape[1]
    y = lax.axis_index('tp')
    dm = lax.axis_index('dm')
    x, c = dm // 2, lax.rem(dm, 2)
    px = {'dp': 0, 'tp': y, 'dm': (1 - x) * 2 + c}
    pc = {'dp': 0, 'tp': y, 'dm': x * 2 + 1 - c}
    py = {'dp': 0, 'tp': 1 - y, 'dm': dm}
    pyc = {'dp': 0, 'tp': 1 - y, 'dm': x * 2 + 1 - c}

    def local(src, dst, sem):
        return pltpu.make_async_copy(src, dst, sem)

    def remote(src, dst, s_sem, r_sem, dev):
        return pltpu.make_async_remote_copy(src_ref=src, dst_ref=dst, send_sem=s_sem, recv_sem=r_sem, device_id=dev, device_id_type=pl.DeviceIdType.MESH)

    d_cp = [local(dd, part_of(d_ref, j, w4), d_sem.at[j]) for j, dd in enumerate((d0, d1, d2, d3))]

    def z_cp(p):
        return [local(src.at[pl.ds(p * CH, CH), :], z_ref.at[p, i // 2 * CH:(i // 2 + 1) * CH, i % 2 * f8:(i % 2 + 1) * f8], z_sem.at[p, i]) for i, src in enumerate((zwa, zwb, zfa, zfb))]

    def p_cp(p):
        return local(part.at[p], p_ref.at[lax.rem(p, 2)], p_sem.at[lax.rem(p, 2)])

    per = hw0.shape[1] // CH
    h_cp = []
    for q in range(chunks):
        k, l = q // per, (q % per) * CH
        h_cp.append(local((hw0, hw1)[k].at[0:w2, l:l + CH], h_ref.at[q, :, 0:CH], h_sem.at[q, 0]))
        h_cp.append(local((hf0, hf1)[k].at[w2:2 * w2, l:l + CH], h_ref.at[q, :, CH:2 * CH], h_sem.at[q, 1]))

    def start(cps):
        for cp in cps:
            cp.start()

    start(z_cp(0) + [d_cp[2], p_cp(0), d_cp[3]])

    bar = pltpu.get_barrier_semaphore()
    for dev in (px, pc, py, pyc):
        pl.semaphore_signal(bar, inc=1, device_id=dev, device_id_type=pl.DeviceIdType.MESH)
    pl.semaphore_wait(bar, 4)

    def rs(p, i):
        rws = slice(i * w4, (i + 1) * w4)
        return remote(hi_ref.at[p, rws], rec_ref.at[p, rws], rs_s.at[p, i], rs_r.at[p, i], px)

    def sq(p):
        return remote(sqs_ref.at[p], sqr_ref.at[p], sq_s.at[p], sq_r.at[p], px)

    def outs(p):
        k, l = p // per, lax.rem(p, per)
        res = []
        for i, pr in enumerate((x, 1 - x)):
            col = pl.multiple_of(((pr * 2 + k) * 4 + 2 * y + c) * (per * CH) + l * CH, CH)
            mine = rec_ref.at[p, 0:w4, i * CH:(i + 1) * CH]
            give = rec_ref.at[p, w4:w2, i * CH:(i + 1) * CH]
            dst = out.at[:, pl.ds(col, CH)]
            res.append((local(mine, dst, loc_sem.at[p, i]), remote(mine, dst, out_s.at[p, i, 0], out_r.at[p, i, 0], py),
                        remote(give, dst, out_s.at[p, i, 1], out_r.at[p, i, 1], pyc), remote(give, dst, out_s.at[p, i, 2], out_r.at[p, i, 2], pc)))
        return res

    def block(p, j):
        return dot_nt(part_of(d_ref, j, w4)[...], z_ref[p]) + p_ref[lax.rem(p, 2), j * w4:(j + 1) * w4, :]

    def upper(p, first=False):
        p_cp(p).wait()
        for cp in z_cp(p):
            cp.wait()
        if first:
            p_cp(1).start()
        else:
            @pl.when(p + 1 < chunks)
            def _():
                p_cp(p + 1).start()
        for i in range(2):
            if first:
                d_cp[2 + i].wait()
            t = block(p, 2 + i).astype(BF)
            hi_ref[p, i * w4:(i + 1) * w4, :CH] = t[:, CH:]
            hi_ref[p, i * w4:(i + 1) * w4, CH:] = t[:, :CH]
            if first or i == 0:
                rs(p, i).start()

    def lower(p, first=False):
        for j in range(2):
            if first:
                d_cp[j].wait()
            lo_ref[p, j * w4:(j + 1) * w4, :] = block(p, j)

    def add(p):
        for i in range(2):
            rs(p, i).wait_recv()
        t = (lo_ref[p] + rec_ref[p].astype(F32)).astype(BF)
        rec_ref[p] = t
        t = t.astype(F32)
        v = jnp.broadcast_to(jnp.sum(t * t, axis=0, keepdims=True), sqo_ref.shape)
        sqo_ref[...] = v
        sqs_ref[p, :, :CH] = v[:, CH:]
        sqs_ref[p, :, CH:] = v[:, :CH]
        sq(p).start()

    def finish(p):
        sq(p).wait_recv()
        r = lax.rsqrt((sqo_ref[...] + sqr_ref[p]) / width + NORM_EPS)[0:1]
        g = g_ref[...]
        g = hcat([g] * (2 * CH // 128))
        rec_ref[p] = (h_ref[p].astype(F32) + rec_ref[p].astype(F32) * r * g).astype(BF)
        for group in outs(p):
            for cp in group[1:] + group[:1]:
                cp.start()

    upper(0, True)
    start(d_cp[:2] + z_cp(1))
    lower(0, True)
    start(h_cp)
    for q in range(2, chunks):
        start(z_cp(q))
    upper(1)
    lower(1)
    for cp in h_cp:
        cp.wait()

    def body(p, _):
        add(p)
        rs(p + 1, 1).start()
        upper(p + 2)
        finish(p)
        lower(p + 2)
        return 0

    lax.fori_loop(0, chunks - 2, body, 0)
    add(chunks - 2)
    rs(chunks - 1, 1).start()
    finish(chunks - 2)
    add(chunks - 1)
    finish(chunks - 1)

    def drain(p, _):
        for i in range(2):
            rs(p, i).wait_send()
        sq(p).wait_send()
        for group in outs(p):
            group[0].wait()
            for cp in group[1:]:
                cp.wait()
        return 0

    lax.fori_loop(0, chunks, drain, 0)


def kv_out_kernel(s_ref, kv0, kv1, *rest, extra):
    if extra:
        rest[-1][...] = rest[0][...]
    k_ref, v_ref = rest[-2 - extra:][:2]
    hd = k_ref.shape[2]
    first = s_ref[2] == 0
    a, b = kv0[...], kv1[...]
    two = jnp.where(first, a, b), jnp.where(first, b, a)
    for ref, at in ((k_ref, 0), (v_ref, hd)):
        ref[...] = jnp.stack([t[:, at:at + hd] for t in two], axis=1)


def solution(mesh):
    tp_size, dm_size = mesh.shape['tp'], mesh.shape['dm']

    def flip(bits):
        return [(i, i ^ bits) for i in range(mesh.size)]

    C, X, Y = 1, 2, dm_size
    PX, PY, PC, PXC, PYC = flip(X), flip(Y), flip(C), flip(X | C), flip(Y | C)

    def send(a, perm):
        return lax.ppermute(a, ('tp', 'dm'), perm)

    def layer(tokens, positions, n1, wq, wk, wv, wo, n2, n3, wg, wu, wd, n4):
        y = lax.axis_index('tp')
        d = lax.axis_index('dm')
        x, c = d // 2, d % 2
        xo, yo, co = 1 - x, 1 - y, 1 - c
        rows, w4 = tokens.shape
        D = w4 * dm_size
        S = positions.shape[1]
        hd = wq.shape[2]
        scale = (D / (wq.shape[1] * tp_size)) ** -0.5
        gw = 2 * hd
        half = S // 2
        quarter = half // 4
        F4 = wg.shape[1] // 2
        scal = jnp.stack([x, y, c]).astype(jnp.int32)

        def take(a, start, size, axis=0):
            return lax.dynamic_slice_in_dim(a, start, size, axis)

        xt = tokens.T

        gains = jnp.stack([n1, n2, n3, n4])
        gall = hcat([gains, send(gains, PC), send(gains, PX), send(gains, PXC)])
        gcol = (1.0 + gall.astype(F32)).T

        rx = [send(take(xt, xo * S + k * half + y * (half // 2), half // 2, 1), PX) for k in range(2)]
        own_p = take(xt, x * S, S, 1)
        own_c = send(own_p, PC)
        ry = [send(rx[k], PY) for k in range(2)]
        rxc = [send(rx[k], PC) for k in range(2)]
        ryc = [send(ry[k], PC) for k in range(2)]

        def group_cols(g):
            return hcat([take(w, n * g, n, 1).reshape(w4, n * hd) for w, n in ((wq, 2), (wk, 1), (wv, 1))])

        wq_own, wq_oth = group_cols(c), group_cols(co)
        wqs = [wq_own, send(wq_oth, PC), send(wq_own, PX), send(wq_oth, PXC)]

        wot = jnp.transpose(wo, (0, 2, 1))
        B0 = wot
        B1 = send(B0, PX)
        B2 = send(B0, PY)
        B3 = send(B1, PY)
        Bs = []
        for b in (B0, B1, B2, B3):
            Bs += [b, send(b, PC)]

        def gather(own, oth):
            r1 = send(oth, PX)
            s0 = send(own, PY)
            s1 = send(r1, PY)
            ty = [own, send(own, PC), r1, send(r1, PC)]
            to = [s0, send(s0, PC), s1, send(s1, PC)]
            return ty, to

        F8 = F4 // 2

        def gu_half(xx, at):
            return hcat([take(w, xx * F4 + at, F8, 1) for w in (wg, wu)])

        gu = {ab: gather(gu_half(x, at), gu_half(xo, at)) for ab, at in (('a', 0), ('b', F8))}
        wdt = wd.T
        dw_own, dw_oth = (take(wdt, xx * F4, F4, 1) for xx in (x, xo))
        dn_y, dn_o = gather(dw_own, dw_oth)

        pos = take(positions, x, 1)[0]
        inv_freq = ROPE_BASE ** (-2.0 * jnp.arange(hd // 2, dtype=F32) / hd)
        ang = inv_freq[:, None] * pos.astype(F32)[None, :]
        cos_t, sin_t = jnp.cos(ang), jnp.sin(ang)

        tile = 512
        nt = half // tile
        per_half = nt // 2
        nb = S // tile
        a_all = []
        for k in range(2):
            a_all = [call(
                functools.partial(norm_kernel, width=D, per_half=per_half), (nt,),
                [pl.BlockSpec((w4, tile), lambda i, s, k=k: (0, s[0] * nb + k * nt + i)), pl.BlockSpec((w4, tile), lambda i, s, k=k: (0, k * nt + i))]
                + [pl.BlockSpec((w4, tile), lambda i, s: (0, i % per_half))] * 4 + [whole(D, 4)] + [ANY] * k,
                pl.BlockSpec((D, tile), lambda i, s, k=k: (0, k * nt + i)), jax.ShapeDtypeStruct((D, S), BF),
                flops=100 * D * half, aliases={8: 0} if k else None)(scal, xt, own_c, rx[k], rxc[k], ry[k], ryc[k], gcol, *a_all)]
        qv, kv = call(
            functools.partial(qkv_kernel, hd=hd), (nb,),
            [pl.BlockSpec((D, tile), by_col)] + [whole(w4, 2 * gw)] * 4 + [pl.BlockSpec((hd // 2, tile), by_col)] * 2,
            [pl.BlockSpec((gw + hd, tile), by_col), pl.BlockSpec((tile, gw), by_row)],
            [jax.ShapeDtypeStruct((gw + hd, S), BF), jax.ShapeDtypeStruct((S, gw), BF)],
            [pltpu.VMEM((2 * gw, D), BF), pltpu.VMEM((D, 2 * gw), BF)],
            flops=2 * D * 2 * gw * S)(scal, *a_all, *wqs, cos_t, sin_t)

        bq = bk = 512
        first_q, last_q = pos[0::bq][:, None], pos[bq - 1::bq][:, None]
        first_k, last_k = pos[0::bk][None, :], pos[bk - 1::bk][None, :]
        lo_t = jnp.sum((first_q - last_k >= WINDOW_LEN).astype(jnp.int32), axis=1)
        full_t = jnp.sum((last_q - first_k >= WINDOW_LEN).astype(jnp.int32), axis=1)
        pos_row, pos_col = pos.reshape(1, S), pos.reshape(S, 1)
        h_own, m_own = [], []
        for k in range(2):
            q0 = k * half // bq
            kl = (k + 1) * half
            o = call(
                functools.partial(attn_kernel, bq=bq, bk=bk, q_block0=q0, scale=scale), (half // bq,),
                [
                    pl.BlockSpec((gw, bq), lambda i, *_, q0=q0: (0, q0 + i)),
                    pl.BlockSpec((kl, hd), lambda i, *_: (0, 0)),
                    pl.BlockSpec((hd, kl), lambda i, *_: (2, 0)),
                    pl.BlockSpec((1, bq), lambda i, *_, q0=q0: (0, q0 + i)),
                    pl.BlockSpec((kl, 1), lambda i, *_: (0, 0)),
                ],
                pl.BlockSpec((gw, bq), by_col),
                jax.ShapeDtypeStruct((gw, half), BF),
                [pltpu.VMEM((hd, 2 * bq), F32), pltpu.VMEM((hd, 2 * bq), BF), pltpu.VMEM((1, 2 * bq), F32), pltpu.VMEM((hd, kl), BF), pltpu.VMEM((8, CH), F32)],
                prefetch=2, flops=4 * hd * 2 * half * (k * half + half // 2))(lo_t, full_t, qv, kv, qv, pos_row, pos_col)
            mc = 2 * y + co
            my, myc = 2 * yo + c, 2 * yo + co
            o_c = send(take(o, mc * quarter, quarter, 1), PC)
            o_y = send(take(o, my * quarter, quarter, 1), PY)
            o_yc = send(take(o, myc * quarter, quarter, 1), PYC)
            heads = wo.shape[0]
            qn = half // quarter
            h, m = call(
                functools.partial(proj_kernel, width=D), (1,),
                [pl.BlockSpec((gw, quarter), lambda i, s: (0, 2 * s[1] + s[2]))] + [whole(gw, quarter)] * 3 + [ANY] * 8 + [
                    pl.BlockSpec((w4, quarter), lambda i, s, k=k: (0, s[0] * 2 * qn + k * qn + 2 * s[1] + s[2])),
                    pl.BlockSpec((w4, quarter), lambda i, s, k=k: (0, k * qn + 2 * s[1] + s[2])),
                    pl.BlockSpec((w4, quarter), lambda i, s: (0, s[2])),
                    pl.BlockSpec((w4, quarter), lambda i, s: (0, s[2])),
                    whole(D, 4)],
                [whole(D, quarter), whole(quarter, D)],
                [jax.ShapeDtypeStruct((D, quarter), BF), jax.ShapeDtypeStruct((quarter, D), BF)],
                [pltpu.VMEM((4 * gw, quarter), BF), pltpu.VMEM((D, quarter), BF), pltpu.VMEM((8, heads, w4, hd), BF), pltpu.SemaphoreType.DMA((8,))],
                flops=2 * D * 4 * gw * quarter)(scal, o, o_c, o_y, o_yc, *Bs, xt, own_c, rx[k], rxc[k], gcol)
            h_own.append(h)
            m_own.append(m)
        h_for = [send(h_own[k], PX) for k in range(2)]
        m_for = []
        for k in range(2):
            m_for.append(call(
                functools.partial(renorm_kernel, width=D), (1,), [whole(D, quarter), whole(D, 4)], whole(quarter, D),
                jax.ShapeDtypeStruct((quarter, D), BF), [pltpu.VMEM((D, quarter), BF)], flops=100 * D * quarter)(scal, h_for[k], gcol))

        ft = 384
        nf = F8 // ft

        def gated(ms, w):
            return call(
                gate_up_kernel, (nf,),
                [whole(quarter, D)] * 2 + [pl.BlockSpec((w4, ft), by_col)] * 4 + [pl.BlockSpec((w4, ft), lambda i, s: (0, nf + i))] * 4,
                pl.BlockSpec((2 * quarter, ft), by_col), jax.ShapeDtypeStruct((2 * quarter, F8), BF),
                flops=2 * D * 2 * F8 * 2 * quarter)(scal, *ms, *w, *w)

        z = {t + hf: [gated(ms, gu[ab][i]) for ab in gu] for i, hf in enumerate('yo') for t, ms in (('own', m_own), ('for', m_for))}

        w2 = 2 * w4
        chunks = 2 * quarter // CH
        yt = 2 * CH
        part = call(
            down_y_kernel, (2 * quarter // yt,), [pl.BlockSpec((yt, F8), by_row)] * 4 + [whole(w4, F4)] * 4,
            pl.BlockSpec((2, D, yt), lambda i, s: (i, 0, 0)), jax.ShapeDtypeStruct((chunks, D, yt), F32),
            [pltpu.VMEM((D, F4), BF)], flops=2 * D * F4 * 2 * quarter * 2)(scal, *z['owny'], *z['fory'], *dn_y)
        dma = pltpu.SemaphoreType.DMA
        out = pl.pallas_call(
            functools.partial(tail_kernel, width=D, chunks=chunks),
            out_shape=jax.ShapeDtypeStruct((w4, rows), BF),
            in_specs=[ANY] * 13 + [pl.BlockSpec(memory_space=pltpu.VMEM)],
            out_specs=ANY,
            scratch_shapes=[
                pltpu.VMEM((D, F4), BF), pltpu.VMEM((chunks, yt, F4), BF), pltpu.VMEM((2, D, yt), F32), pltpu.VMEM((chunks, w2, yt), F32),
                *[pltpu.VMEM((chunks, w2, yt), BF)] * 3, *[pltpu.VMEM((chunks, 8, yt), F32)] * 2, pltpu.VMEM((8, yt), F32),
                dma((4,)), dma((chunks, 4)), dma((2,)), *[dma((chunks, 2))] * 4, *[dma((chunks,))] * 2, *[dma((chunks, 2, 3))] * 2],
            cost_estimate=pl.CostEstimate(flops=2 * D * F4 * 4 * quarter, bytes_accessed=4 * D * rows, transcendentals=0),
            compiler_params=pltpu.CompilerParams(vmem_limit_bytes=60 * 1024 * 1024, collective_id=0, has_side_effects=True),
            name='tail',
        )(part, *z['owno'], *z['foro'], *dn_o, *h_own, *h_for, jnp.broadcast_to(gcol[:w2, 3:4], (w2, 128)))
        kv_c = send(kv, PC)
        kv_x = [send(kv[k * half:(k + 1) * half], PX) for k in range(2)]
        kv_xc = [send(kv_x[k], PC) for k in range(2)]
        kv_spec = pl.BlockSpec((tile, gw), by_row)
        kv_outs = []
        for i, (t, tc, n, base) in enumerate(((kv, kv_c, nb, 0), (kv_x[0], kv_xc[0], nt, 0), (kv_x[1], kv_xc[1], nt, nt))):
            extra = i == 2
            at = lambda j, s, i=i, base=base: ((1 - s[0] if i else s[0]) * nb + base + j, 0, 0)
            cspec = [pl.BlockSpec((w4, rows // nt), by_col)] * extra
            kv_outs = call(
                functools.partial(kv_out_kernel, extra=int(extra)), (n,), [kv_spec] * 2 + cspec + [ANY] * len(kv_outs),
                [pl.BlockSpec((tile, 2, hd), at)] * 2 + cspec, [jax.ShapeDtypeStruct((rows, 2, hd), BF)] * 2 + [jax.ShapeDtypeStruct((w4, rows), BF)] * extra,
                flops=100 * rows * hd, aliases={3 + extra: 0, 4 + extra: 1} if i else None)(scal, t, tc, *[out] * extra, *kv_outs)
        k_out, v_out, out = kv_outs
        return out.T, k_out, v_out

    width_spec = P('dm')
    in_specs = (P('dp', 'dm'), P('dp', None), width_spec, P('dm', 'tp', None), P('dm', 'tp', None), P('dm', 'tp', None), P('tp', None, 'dm'), width_spec, width_spec, P('dm', 'tp'), P('dm', 'tp'), P('tp', 'dm'), width_spec)
    out_specs = (P('dp', 'dm'), P('dp', 'tp', None), P('dp', 'tp', None))
    return jax.shard_map(layer, mesh=mesh, in_specs=in_specs, out_specs=out_specs, check_vma=False)
```

time: 969 us -> 893 us (0.922)
  waiting for transfers between devices: 365 us -> 301 us
  local copies, waits for them, and re-layouts: 52.2 us -> 42.2 us
    ppermute x47 -> x56, waiting for transfers between devices: 365 us -> 301 us  [send(): return lax.ppermute(a, ('tp', 'dm'), perm)]
    pallas_call x4 -> x8, Pallas kernels: 116 us -> 140 us  [gated(): call(gate_up_kernel, (nf,), [whole(quarter, D)] * 2 + [pl.BlockSpec((w4,...]
    unnamed x59 -> x40, local copies, waits for them, and re-layouts: 17.1 us -> 1.27 us
    pallas_call x1, Pallas kernels: 145 us -> 132 us  [layer(): pl.pallas_call(functools.partial(tail_kernel, width=D, chunks=chunks), ou...]
    pallas_call x2, Pallas kernels: 56.4 us -> 45 us  [layer(): call(functools.partial(attn_kernel, bq=bq, bk=bk, q_block0=q0, scale=scal...]
    ppermute x47 -> x56, starting transfers between devices: 36.1 us -> 41.5 us  [send(): return lax.ppermute(a, ('tp', 'dm'), perm)]
  transfers between devices with their start and end apart: 47 -> 56, of which waited for: 12 -> 17; matrix products, arithmetic and copies ran while one was open for 6% -> 7% of each run, Pallas kernels for 35% -> 53%
where the time goes in v2:
time: 893 us; the launch traced here: 887 us
  Pallas kernels  480 us (54%)
  waiting for transfers between devices  301 us (34%)
  local copies, waits for them, and re-layouts  42.2 us (5%)
  starting transfers between devices  41.5 us (5%)
  other arithmetic  20.5 us (2%)
    ppermute x56, waiting for transfers between devices, send(): return lax.ppermute(a, ('tp', 'dm'), perm)  301 us
    pallas_call x8, Pallas kernels, gated(): call(gate_up_kernel, (nf,), [whole(quarter, D)] * 2 + [pl.BlockSpec((w4,...  140 us
    pallas_call x1, Pallas kernels, layer(): pl.pallas_call(functools.partial(tail_kernel, width=D, chunks=chunks), ou...  132 us
    pallas_call x2, Pallas kernels, layer(): call(functools.partial(attn_kernel, bq=bq, bk=bk, q_block0=q0, scale=scal...  45 us
    ppermute x56, starting transfers between devices, send(): return lax.ppermute(a, ('tp', 'dm'), perm)  41.5 us
    pallas_call x3, Pallas kernels, layer(): call(functools.partial(kv_out_kernel, extra=int(extra)), (n,), [kv_spec]...  38.6 us
    pallas_call x1, Pallas kernels, layer(): call(down_y_kernel, (2 * quarter // yt,), [pl.BlockSpec((yt, F8), by_row)...  31.2 us
    pallas_call x2, Pallas kernels, layer(): call(functools.partial(proj_kernel, width=D), (1,), [pl.BlockSpec((gw, qu...  30.2 us
  transfers between devices with their start and end apart: 56, of which 17 were waited for; matrix products, arithmetic and copies ran while one was open for 7% of the time, Pallas kernels for 53%

profile of v2, /device:TPU:0, one launch (start us, length us, event | category | flops | bytes accessed | tf_op | source)
XLA Modules:
  0.0 887.0 jit_solution(16841582009998408094)
XLA Ops:
  0.7 3.3 dynamic-slice_bitcast_fusion.3
  4.0 3.3 collective-permute-start.8
  9.9 2.9 constant_dynamic-slice_fusion.17
  19.3 39.7 %collective-permute-done.6 = bf16[4,576]{1,0:T(4,128)(2,1)S(1)} collective-permute-done((bf16[4,576]{1,0:T(4,128)(2,1)S(1)}, bf16[4,576]{1,0:T(4,128)(2,1)S(1)}, u32[]{:S(2)}, u32[]{:S(2)}) %collective-permute-start.6) | collective-permute-done | bytes 4640 | tf_op jit(solution)/shard_map/ppermute | solution.py:403
  60.7 5.1 dynamic-slice_bitcast_fusion
  69.5 18.4 %collective-permute-done.13.w2 = bf16[576,1024]{1,0:T(8,128)(2,1)} collective-permute-done((bf16[576,1024]{1,0:T(8,128)(2,1)S(1)}, bf16[576,1024]{1,0:T(8,128)(2,1)}, u32[]{:S(2)}, u32[]{:S(2)}) %collective-permute-start.13) | collective-permute-done | bytes 1179680 | tf_op jit(solution)/shard_map/ppermute | solution.py:403
  87.9 24.5 %collective-permute-done.14.w3 = bf16[576,1024]{1,0:T(8,128)(2,1)} collective-permute-done((bf16[576,1024]{1,0:T(8,128)(2,1)}, bf16[576,1024]{1,0:T(8,128)(2,1)}, u32[]{:S(2)}, u32[]{:S(2)}) %collective-permute-start.14) | collective-permute-done | bytes 1179680 | tf_op jit(solution)/shard_map/ppermute | solution.py:403
  113.9 6.0 constant_dynamic-slice_fusion
  119.9 16.8 %collective-permute-done.21.b1 = bf16[4,576,256]{2,1,0:T(8,128)(2,1)} collective-permute-done((bf16[4,576,256]{2,1,0:T(8,128)(2,1)}, bf16[4,576,256]{2,1,0:T(8,128)(2,1)}, u32[]{:S(2)}, u32[]{:S(2)}) %collective-permute-start.21) | collective-permute-done | bytes 1179680 | tf_op jit(solution)/shard_map/ppermute | solution.py:403
  138.2 3.1 pad_maximum_fusion.3
  143.1 9.3 %multiply_sine_fusion = (f32[128,4096]{1,0:T(8,128)}, f32[128,4096]{1,0:T(8,128)}) fusion(f32[4096]{0:T(1024)S(1)} %bitcast.58, f32[128]{0:T(128)S(1)} %multiply_power_fusion), kind=kLoop, calls=%fused_computation.1 | loop fusion | flops 524288 | bytes 4211200 | tf_op jit(solution)/shard_map/sin | solution.py:473
  152.9 14.0 %collective-permute-done.3.ry = bf16[576,1024]{1,0:T(8,128)(2,1)} collective-permute-done((bf16[576,1024]{1,0:T(8,128)(2,1)}, bf16[576,1024]{1,0:T(8,128)(2,1)}, u32[]{:S(2)}, u32[]{:S(2)}) %collective-permute-start.3) | collective-permute-done | bytes 1179680 | tf_op jit(solution)/shard_map/ppermute | solution.py:403
  169.1 22.5 %collective-permute-done.25.b3 = bf16[4,576,256]{2,1,0:T(8,128)(2,1)S(1)} collective-permute-done((bf16[4,576,256]{2,1,0:T(8,128)(2,1)}, bf16[4,576,256]{2,1,0:T(8,128)(2,1)S(1)}, u32[]{:S(2)}, u32[]{:S(2)}) %collective-permute-start.25) | collective-permute-done | bytes 1179680 | tf_op jit(solution)/shard_map/ppermute | solution.py:403
  196.5 5.3 dynamic-slice_bitcast_fusion.1
  208.7 11.7 %shard_map.148.rest_0_ = bf16[2304,4096]{1,0:T(8,128)(2,1)} custom-call(s32[3]{0:T(128)} %pad_add_fusion.s_ref, bf16[576,8192]{1,0:T(8,128)(2,1)} %bitcast.36, bf16[576,4096]{1,0:T(8,128)(2,1)} %collective-permute-done.own_c.x1, bf16[576,1024]{1,0:T(8,128)(2,1)} %collective-permute-done.8.rx.x2, bf16[576,1024]{1,0:T(8,128)(2,1)} %copy-done.1, ...), custom_call_target="tpu_custom_call" | custom-call | flops 471859200 | tf_op jit(solution)/shard_map/pallas_call | solution.py:481
  220.4 11.7 %shard_map.149.a_ref = bf16[2304,4096]{1,0:T(8,128)(2,1)} custom-call(s32[3]{0:T(128)} %pad_add_fusion.s_ref, bf16[576,8192]{1,0:T(8,128)(2,1)} %bitcast.37, bf16[576,4096]{1,0:T(8,128)(2,1)} %collective-permute-done.own_c.x1, bf16[576,1024]{1,0:T(8,128)(2,1)} %copy-done.3, bf16[576,1024]{1,0:T(8,128)(2,1)} %copy-done.5, ...), custom_call_target="tpu_custom_call", output_to_operand_aliasing={{}: (8, {})} | custom-call | flops 471859200 | tf_op jit(solution)/shard_map/pallas_call | solution.py:481
  232.7 29.2 %shard_map.150 = (bf16[768,4096]{1,0:T(8,128)(2,1)}, bf16[4096,512]{1,0:T(8,128)(2,1)}) custom-call(s32[3]{0:T(128)} %pad_add_fusion.s_ref, bf16[2304,4096]{1,0:T(8,128)(2,1)} %shard_map.149.a_ref, bf16[576,1024]{1,0:T(8,128)(2,1)} %copy-done.8, bf16[576,1024]{1,0:T(8,128)(2,1)} %collective-permute-done.12.w1, bf16[576,1024]{1,0:T(8,128)(2,1)} %collective-permute-done.13.w2, ...), custom_call_target="tpu_custom_call" | custom-call | flops 19327352832 | tf_op jit(solution)/shard_map/pallas_call | solution.py:487
  261.9 2.7 collective-permute-done.45.g0.u0
  265.2 4.8 collective-permute-done.31.g2.u2
  270.1 50.6 %collective-permute-done.41.g0.u0 = bf16[576,2304]{1,0:T(8,128)(2,1)} collective-permute-done((bf16[576,2304]{1,0:T(8,128)(2,1)}, bf16[576,2304]{1,0:T(8,128)(2,1)}, u32[]{:S(2)}, u32[]{:S(2)}) %collective-permute-start.41) | collective-permute-done | bytes 2654240 | tf_op jit(solution)/shard_map/ppermute | solution.py:403
  320.7 29.3 %shard_map.153.o_own = bf16[512,2048]{1,0:T(8,128)(2,1)} custom-call(s32[8]{0:T(128)} %get-tuple-element.30.lo_ref, s32[8]{0:T(128)} %get-tuple-element.29.full_ref, bf16[768,4096]{1,0:T(8,128)(2,1)} %get-tuple-element.17.q_ref.v_ref, bf16[4096,512]{1,0:T(8,128)(2,1)} %get-tuple-element.16.k_ref.kv0, bf16[768,4096]{1,0:T(8,128)(2,1)} %get-tuple-element.17.q_ref.v_ref, ...), custom_call_target="tpu_custom_call" | custom-call | flops 12884901888 | tf_op jit(solution)/shard_map/pallas_call | solution.py:505
  354.8 15.7 %shard_map.151.o_own = bf16[512,2048]{1,0:T(8,128)(2,1)} custom-call(s32[8]{0:T(128)} %get-tuple-element.30.lo_ref, s32[8]{0:T(128)} %get-tuple-element.29.full_ref, bf16[768,4096]{1,0:T(8,128)(2,1)} %get-tuple-element.17.q_ref.v_ref, bf16[4096,512]{1,0:T(8,128)(2,1)} %get-tuple-element.16.k_ref.kv0, bf16[768,4096]{1,0:T(8,128)(2,1)} %get-tuple-element.17.q_ref.v_ref, ...), custom_call_target="tpu_custom_call" | custom-call | flops 4294967296 | tf_op jit(solution)/shard_map/pallas_call | solution.py:505
  370.5 2.6 constant_dynamic-slice_fusion.11
  376.0 2.6 collective-permute-done.29.o_yc
  380.5 14.9 %shard_map.154 = (bf16[2304,512]{1,0:T(8,128)(2,1)}, bf16[512,2304]{1,0:T(8,128)(2,1)}) custom-call(s32[3]{0:T(128)} %pad_add_fusion.s_ref, bf16[512,2048]{1,0:T(8,128)(2,1)} %shard_map.153.o_own, bf16[512,512]{1,0:T(8,128)(2,1)} %copy-done.10, bf16[512,512]{1,0:T(8,128)(2,1)} %collective-permute-done.28.o_y, bf16[512,512]{1,0:T(8,128)(2,1)} %collective-permute-done.29.o_yc, ...), custom_call_target="tpu_custom_call" | custom-call | flops 4831838208 | tf_op jit(solution)/shard_map/pallas_call | solution.py:525
  395.8 5.3 collective-permute-done.19.o_yc
  401.7 15.3 %shard_map.152 = (bf16[2304,512]{1,0:T(8,128)(2,1)}, bf16[512,2304]{1,0:T(8,128)(2,1)}) custom-call(s32[3]{0:T(128)} %pad_add_fusion.s_ref, bf16[512,2048]{1,0:T(8,128)(2,1)} %shard_map.151.o_own, bf16[512,512]{1,0:T(8,128)(2,1)} %copy-done.9, bf16[512,512]{1,0:T(8,128)(2,1)} %collective-permute-done.18.o_y, bf16[512,512]{1,0:T(8,128)(2,1)} %collective-permute-done.19.o_yc, ...), custom_call_target="tpu_custom_call" | custom-call | flops 4831838208 | tf_op jit(solution)/shard_map/pallas_call | solution.py:525
  420.5 4.6 fusion.1
  425.1 17.3 %shard_map.156.zwb = bf16[1024,1152]{1,0:T(8,128)(2,1)} custom-call(s32[3]{0:T(128)} %pad_add_fusion.s_ref, bf16[512,2304]{1,0:T(8,128)(2,1)} %get-tuple-element.18.ma, bf16[512,2304]{1,0:T(8,128)(2,1)} %get-tuple-element.19.mb, bf16[576,2304]{1,0:T(8,128)(2,1)} %pad_maximum_fusion.2.g0.u0, bf16[576,2304]{1,0:T(8,128)(2,1)} %collective-permute-done.33.g1.u1, ...), custom_call_target="tpu_custom_call" | custom-call | flops 10871635968 | tf_op jit(solution)/shard_map/pallas_call | solution.py:550
  444.2 14.5 %collective-permute-done.47.g2.u2 = bf16[576,2304]{1,0:T(8,128)(2,1)} collective-permute-done((bf16[576,2304]{1,0:T(8,128)(2,1)}, bf16[576,2304]{1,0:T(8,128)(2,1)}, u32[]{:S(2)}, u32[]{:S(2)}) %collective-permute-start.47) | collective-permute-done | bytes 2654240 | tf_op jit(solution)/shard_map/ppermute | solution.py:403
  460.5 11.0 %collective-permute-done.37.h_ref.hf1 = bf16[2304,512]{1,0:T(8,128)(2,1)} collective-permute-done((bf16[2304,512]{1,0:T(8,128)(2,1)}, bf16[2304,512]{1,0:T(8,128)(2,1)}, u32[]{:S(2)}, u32[]{:S(2)}) %collective-permute-start.37) | collective-permute-done | bytes 2359328 | tf_op jit(solution)/shard_map/ppermute | solution.py:403
  471.5 49.6 %collective-permute-done.36.h_ref.hf0 = bf16[2304,512]{1,0:T(8,128)(2,1)} collective-permute-done((bf16[2304,512]{1,0:T(8,128)(2,1)}, bf16[2304,512]{1,0:T(8,128)(2,1)}, u32[]{:S(2)}, u32[]{:S(2)}) %collective-permute-start.36) | collective-permute-done | bytes 2359328 | tf_op jit(solution)/shard_map/ppermute | solution.py:403
  521.1 17.4 %shard_map.155.zwa = bf16[1024,1152]{1,0:T(8,128)(2,1)} custom-call(s32[3]{0:T(128)} %pad_add_fusion.s_ref, bf16[512,2304]{1,0:T(8,128)(2,1)} %get-tuple-element.18.ma, bf16[512,2304]{1,0:T(8,128)(2,1)} %get-tuple-element.19.mb, bf16[576,2304]{1,0:T(8,128)(2,1)} %pad_maximum_fusion.g0.u0, bf16[576,2304]{1,0:T(8,128)(2,1)} %collective-permute-done.30.g1.u1, ...), custom_call_target="tpu_custom_call" | custom-call | flops 10871635968 | tf_op jit(solution)/shard_map/pallas_call | solution.py:550
  538.5 5.8 shard_map.158.mb
  544.3 5.8 shard_map.157.ma
  550.0 17.6 %shard_map.160.zfb = bf16[1024,1152]{1,0:T(8,128)(2,1)} custom-call(s32[3]{0:T(128)} %pad_add_fusion.s_ref, bf16[512,2304]{1,0:T(8,128)(2,1)} %shard_map.157.ma, bf16[512,2304]{1,0:T(8,128)(2,1)} %shard_map.158.mb, bf16[576,2304]{1,0:T(8,128)(2,1)} %pad_maximum_fusion.2.g0.u0, bf16[576,2304]{1,0:T(8,128)(2,1)} %collective-permute-done.33.g1.u1, ...), custom_call_target="tpu_custom_call" | custom-call | flops 10871635968 | tf_op jit(solution)/shard_map/pallas_call | solution.py:550
  567.6 17.4 %shard_map.159.zfa = bf16[1024,1152]{1,0:T(8,128)(2,1)} custom-call(s32[3]{0:T(128)} %pad_add_fusion.s_ref, bf16[512,2304]{1,0:T(8,128)(2,1)} %shard_map.157.ma, bf16[512,2304]{1,0:T(8,128)(2,1)} %shard_map.158.mb, bf16[576,2304]{1,0:T(8,128)(2,1)} %pad_maximum_fusion.g0.u0, bf16[576,2304]{1,0:T(8,128)(2,1)} %collective-permute-done.30.g1.u1, ...), custom_call_target="tpu_custom_call" | custom-call | flops 10871635968 | tf_op jit(solution)/shard_map/pallas_call | solution.py:550
  589.0 31.2 %shard_map.161.part = f32[8,2304,256]{2,1,0:T(8,128)} custom-call(s32[3]{0:T(128)} %pad_add_fusion.s_ref, bf16[1024,1152]{1,0:T(8,128)(2,1)} %shard_map.155.zwa, bf16[1024,1152]{1,0:T(8,128)(2,1)} %shard_map.156.zwb, bf16[1024,1152]{1,0:T(8,128)(2,1)} %shard_map.159.zfa, bf16[1024,1152]{1,0:T(8,128)(2,1)} %shard_map.160.zfb, ...), custom_call_target="tpu_custom_call" | custom-call | flops 21743271936 | tf_op jit(solution)/shard_map/pallas_call | solution.py:561
  620.3 17.6 %shard_map.165.zfb = bf16[1024,1152]{1,0:T(8,128)(2,1)} custom-call(s32[3]{0:T(128)} %pad_add_fusion.s_ref, bf16[512,2304]{1,0:T(8,128)(2,1)} %shard_map.157.ma, bf16[512,2304]{1,0:T(8,128)(2,1)} %shard_map.158.mb, bf16[576,2304]{1,0:T(8,128)(2,1)} %collective-permute-done.45.g0.u0, bf16[576,2304]{1,0:T(8,128)(2,1)} %collective-permute-done.46.g1.u1, ...), custom_call_target="tpu_custom_call" | custom-call | flops 10871635968 | tf_op jit(solution)/shard_map/pallas_call | solution.py:550
  638.4 7.0 collective-permute-done.51.d2
  645.8 17.3 %shard_map.163.zwb = bf16[1024,1152]{1,0:T(8,128)(2,1)} custom-call(s32[3]{0:T(128)} %pad_add_fusion.s_ref, bf16[512,2304]{1,0:T(8,128)(2,1)} %get-tuple-element.18.ma, bf16[512,2304]{1,0:T(8,128)(2,1)} %get-tuple-element.19.mb, bf16[576,2304]{1,0:T(8,128)(2,1)} %collective-permute-done.45.g0.u0, bf16[576,2304]{1,0:T(8,128)(2,1)} %collective-permute-done.46.g1.u1, ...), custom_call_target="tpu_custom_call" | custom-call | flops 10871635968 | tf_op jit(solution)/shard_map/pallas_call | solution.py:550
  663.2 16.9 %collective-permute-done.15.kv0 = bf16[2048,512]{1,0:T(8,128)(2,1)} collective-permute-done((bf16[2048,512]{1,0:T(8,128)(2,1)}, bf16[2048,512]{1,0:T(8,128)(2,1)}, u32[]{:S(2)}, u32[]{:S(2)}) %collective-permute-start.15) | collective-permute-done | bytes 2097184 | tf_op jit(solution)/shard_map/ppermute | solution.py:403
  680.6 17.3 %shard_map.164.zfa = bf16[1024,1152]{1,0:T(8,128)(2,1)} custom-call(s32[3]{0:T(128)} %pad_add_fusion.s_ref, bf16[512,2304]{1,0:T(8,128)(2,1)} %shard_map.157.ma, bf16[512,2304]{1,0:T(8,128)(2,1)} %shard_map.158.mb, bf16[576,2304]{1,0:T(8,128)(2,1)} %collective-permute-done.41.g0.u0, bf16[576,2304]{1,0:T(8,128)(2,1)} %collective-permute-done.42.g1.u1, ...), custom_call_target="tpu_custom_call" | custom-call | flops 10871635968 | tf_op jit(solution)/shard_map/pallas_call | solution.py:550
  697.9 17.7 %shard_map.162.zwa = bf16[1024,1152]{1,0:T(8,128)(2,1)} custom-call(s32[3]{0:T(128)} %pad_add_fusion.s_ref, bf16[512,2304]{1,0:T(8,128)(2,1)} %get-tuple-element.18.ma, bf16[512,2304]{1,0:T(8,128)(2,1)} %get-tuple-element.19.mb, bf16[576,2304]{1,0:T(8,128)(2,1)} %collective-permute-done.41.g0.u0, bf16[576,2304]{1,0:T(8,128)(2,1)} %collective-permute-done.42.g1.u1, ...), custom_call_target="tpu_custom_call" | custom-call | flops 10871635968 | tf_op jit(solution)/shard_map/pallas_call | solution.py:550
  716.6 131.5 %tail.1.rest_0_ = bf16[576,8192]{1,0:T(8,128)(2,1)} custom-call(f32[8,2304,256]{2,1,0:T(8,128)} %shard_map.161.part, bf16[1024,1152]{1,0:T(8,128)(2,1)} %shard_map.162.zwa, bf16[1024,1152]{1,0:T(8,128)(2,1)} %shard_map.163.zwb, bf16[1024,1152]{1,0:T(8,128)(2,1)} %shard_map.164.zfa, bf16[1024,1152]{1,0:T(8,128)(2,1)} %shard_map.165.zfb, ...), custom_call_target="tpu_custom_call" | custom-call | flops 21743271936 | bytes 75497472 | tf_op jit(solution)/shard_map/tail/pallas_call | solution.py:566
  848.2 16.8 %shard_map.166 = (bf16[8192,2,256]{2,1,0:T(2,128)(2,1)}, bf16[8192,2,256]{2,1,0:T(2,128)(2,1)}) custom-call(s32[3]{0:T(128)} %pad_add_fusion.s_ref, bf16[4096,512]{1,0:T(8,128)(2,1)} %get-tuple-element.16.k_ref.kv0, bf16[4096,512]{1,0:T(8,128)(2,1)} %collective-permute-done.55.kv1), custom_call_target="tpu_custom_call" | custom-call | flops 209715200 | tf_op jit(solution)/shard_map/pallas_call | solution.py:588
  864.9 9.7 %shard_map.167 = (bf16[8192,2,256]{2,1,0:T(2,128)(2,1)}, bf16[8192,2,256]{2,1,0:T(2,128)(2,1)}) custom-call(s32[3]{0:T(128)} %pad_add_fusion.s_ref, bf16[2048,512]{1,0:T(8,128)(2,1)} %collective-permute-done.53.kv0, bf16[2048,512]{1,0:T(8,128)(2,1)} %collective-permute-done.54.kv1, ...), custom_call_target="tpu_custom_call", output_to_operand_aliasing={{0}: (3, {}), {1}: (4, {})} | custom-call | flops 209715200 | tf_op jit(solution)/shard_map/pallas_call | solution.py:588
  874.6 12.1 %shard_map.168 = (bf16[8192,2,256]{2,1,0:T(2,128)(2,1)}, bf16[8192,2,256]{2,1,0:T(2,128)(2,1)}, bf16[576,8192]{1,0:T(8,128)(2,1)}) custom-call(s32[3]{0:T(128)} %pad_add_fusion.s_ref, bf16[2048,512]{1,0:T(8,128)(2,1)} %collective-permute-done.15.kv0, bf16[2048,512]{1,0:T(8,128)(2,1)} %collective-permute-done.16.kv1, ...), custom_call_target="tpu_custom_call", output_to_operand_aliasing={{0}: (4, {}), {1}: (5, {})} | custom-call | flops 209715200 | tf_op jit(solution)/shard_map/pallas_call | solution.py:588
  (159 shorter events, 59.2 us)
Async XLA Ops:
  4.0 61.8 %collective-permute-start.8 = (bf16[576,1024]{1,0:T(8,128)(2,1)}, bf16[576,1024]{1,0:T(8,128)(2,1)}, u32[]{:S(2)}, u32[]{:S(2)}) collective-permute-start(bf16[576,1024]{1,0:T(8,128)(2,1)} %get-tuple-element.33), channel_id=1, source_target_pairs={{0,2},{1,3},{2,0},{3,1},{4,6},{5,7},{6,4},{7,5}} | collective-permute-start | bytes 3538952 | tf_op jit(solution)/shard_map/ppermute | solution.py:403
  7.3 58.9 %collective-permute-start.1 = (bf16[576,1024]{1,0:T(8,128)(2,1)}, bf16[576,1024]{1,0:T(8,128)(2,1)S(1)}, u32[]{:S(2)}, u32[]{:S(2)}) collective-permute-start(bf16[576,1024]{1,0:T(8,128)(2,1)} %get-tuple-element.34), channel_id=1, source_target_pairs={{0,2},{1,3},{2,0},{3,1},{4,6},{5,7},{6,4},{7,5}} | collective-permute-start | bytes 3538952 | tf_op jit(solution)/shard_map/ppermute | solution.py:403
  14.2 53.8 %collective-permute-start.12 = (bf16[576,1024]{1,0:T(8,128)(2,1)}, bf16[576,1024]{1,0:T(8,128)(2,1)}, u32[]{:S(2)}, u32[]{:S(2)}) collective-permute-start(bf16[576,1024]{1,0:T(8,128)(2,1)} %pad_maximum_fusion.5), channel_id=1, source_target_pairs={{0,1},{1,0},{2,3},{3,2},{4,5},{5,4},{6,7},{7,6}} | collective-permute-start | bytes 3538952 | tf_op jit(solution)/shard_map/ppermute | solution.py:403
  14.8 44.1 %collective-permute-start.6 = (bf16[4,576]{1,0:T(4,128)(2,1)S(1)}, bf16[4,576]{1,0:T(4,128)(2,1)S(1)}, u32[]{:S(2)}, u32[]{:S(2)}) collective-permute-start(bf16[4,576]{1,0:T(4,128)(2,1)S(1)} %pad_maximum_fusion.6), channel_id=1, source_target_pairs={{0,2},{1,3},{2,0},{3,1},{4,6},{5,7},{6,4},{7,5}} | collective-permute-start | bytes 13832 | tf_op jit(solution)/shard_map/ppermute | solution.py:403
  17.4 43.3 %collective-permute-start.7 = (bf16[4,576]{1,0:T(4,128)(2,1)S(1)}, bf16[4,576]{1,0:T(4,128)(2,1)S(1)}, u32[]{:S(2)}, u32[]{:S(2)}) collective-permute-start(bf16[4,576]{1,0:T(4,128)(2,1)S(1)} %pad_maximum_fusion.6), channel_id=1, source_target_pairs={{0,3},{1,2},{2,1},{3,0},{4,7},{5,6},{6,5},{7,4}} | collective-permute-start | bytes 13832 | tf_op jit(solution)/shard_map/ppermute | solution.py:403
  58.9 28.9 %collective-permute-start.13 = (bf16[576,1024]{1,0:T(8,128)(2,1)S(1)}, bf16[576,1024]{1,0:T(8,128)(2,1)}, u32[]{:S(2)}, u32[]{:S(2)}) collective-permute-start(bf16[576,1024]{1,0:T(8,128)(2,1)S(1)} %pad_maximum_fusion.4.w0), channel_id=1, source_target_pairs={{0,2},{1,3},{2,0},{3,1},{4,6},{5,7},{6,4},{7,5}} | collective-permute-start | bytes 3538952 | tf_op jit(solution)/shard_map/ppermute | solution.py:403
  60.7 51.7 %collective-permute-start.14 = (bf16[576,1024]{1,0:T(8,128)(2,1)}, bf16[576,1024]{1,0:T(8,128)(2,1)}, u32[]{:S(2)}, u32[]{:S(2)}) collective-permute-start(bf16[576,1024]{1,0:T(8,128)(2,1)} %pad_maximum_fusion.5), channel_id=1, source_target_pairs={{0,3},{1,2},{2,1},{3,0},{4,7},{5,6},{6,5},{7,4}} | collective-permute-start | bytes 3538952 | tf_op jit(solution)/shard_map/ppermute | solution.py:403
  65.8 140.4 %collective-permute-start = (bf16[576,4096]{1,0:T(8,128)(2,1)}, bf16[576,4096]{1,0:T(8,128)(2,1)}, u32[]{:S(2)}, u32[]{:S(2)}) collective-permute-start(bf16[576,4096]{1,0:T(8,128)(2,1)} %dynamic-slice_bitcast_fusion), channel_id=1, source_target_pairs={{0,1},{1,0},{2,3},{3,2},{4,5},{5,4},{6,7},{7,6}} | collective-permute-start | bytes 14155784 | tf_op jit(solution)/shard_map/ppermute | solution.py:403
  66.2 70.5 %collective-permute-start.21 = (bf16[4,576,256]{2,1,0:T(8,128)(2,1)}, bf16[4,576,256]{2,1,0:T(8,128)(2,1)}, u32[]{:S(2)}, u32[]{:S(2)}) collective-permute-start(bf16[4,576,256]{2,1,0:T(8,128)(2,1)} %bitcast.15.b0), channel_id=1, source_target_pairs={{0,2},{1,3},{2,0},{3,1},{4,6},{5,7},{6,4},{7,5}} | collective-permute-start | bytes 3538952 | tf_op jit(solution)/shard_map/ppermute | solution.py:403
  67.9 68.7 %collective-permute-start.23 = (bf16[4,576,256]{2,1,0:T(8,128)(2,1)}, bf16[4,576,256]{2,1,0:T(8,128)(2,1)}, u32[]{:S(2)}, u32[]{:S(2)}) collective-permute-start(bf16[4,576,256]{2,1,0:T(8,128)(2,1)} %bitcast.15.b0), channel_id=1, source_target_pairs={{0,4},{1,5},{2,6},{3,7},{4,0},{5,1},{6,2},{7,3}} | collective-permute-start | bytes 3538952 | tf_op jit(solution)/shard_map/ppermute | solution.py:403
  87.9 53.4 %collective-permute-start.20 = (bf16[4,576,256]{2,1,0:T(8,128)(2,1)}, bf16[4,576,256]{2,1,0:T(8,128)(2,1)S(1)}, u32[]{:S(2)}, u32[]{:S(2)}) collective-permute-start(bf16[4,576,256]{2,1,0:T(8,128)(2,1)} %bitcast.15.b0), channel_id=1, source_target_pairs={{0,1},{1,0},{2,3},{3,2},{4,5},{5,4},{6,7},{7,6}} | collective-permute-start | bytes 3538952 | tf_op jit(solution)/shard_map/ppermute | solution.py:403
  112.4 29.2 %collective-permute-start.10 = (bf16[576,1024]{1,0:T(8,128)(2,1)}, bf16[576,1024]{1,0:T(8,128)(2,1)}, u32[]{:S(2)}, u32[]{:S(2)}) collective-permute-start(bf16[576,1024]{1,0:T(8,128)(2,1)} %collective-permute-done.8.rx.x2), channel_id=1, source_target_pairs={{0,4},{1,5},{2,6},{3,7},{4,0},{5,1},{6,2},{7,3}} | collective-permute-start | bytes 3538952 | tf_op jit(solution)/shard_map/ppermute | solution.py:403
  136.7 30.2 %collective-permute-start.3 = (bf16[576,1024]{1,0:T(8,128)(2,1)}, bf16[576,1024]{1,0:T(8,128)(2,1)}, u32[]{:S(2)}, u32[]{:S(2)}) collective-permute-start(bf16[576,1024]{1,0:T(8,128)(2,1)} %copy-done.3), channel_id=1, source_target_pairs={{0,4},{1,5},{2,6},{3,7},{4,0},{5,1},{6,2},{7,3}} | collective-permute-start | bytes 3538952 | tf_op jit(solution)/shard_map/ppermute | solution.py:403
  141.3 27.2 %collective-permute-start.2 = (bf16[576,1024]{1,0:T(8,128)(2,1)S(1)}, bf16[576,1024]{1,0:T(8,128)(2,1)S(1)}, u32[]{:S(2)}, u32[]{:S(2)}) collective-permute-start(bf16[576,1024]{1,0:T(8,128)(2,1)S(1)} %copy-done.4), channel_id=1, source_target_pairs={{0,1},{1,0},{2,3},{3,2},{4,5},{5,4},{6,7},{7,6}} | collective-permute-start | bytes 3538952 | tf_op jit(solution)/shard_map/ppermute | solution.py:403
  141.6 50.1 %collective-permute-start.25 = (bf16[4,576,256]{2,1,0:T(8,128)(2,1)}, bf16[4,576,256]{2,1,0:T(8,128)(2,1)S(1)}, u32[]{:S(2)}, u32[]{:S(2)}) collective-permute-start(bf16[4,576,256]{2,1,0:T(8,128)(2,1)} %collective-permute-done.21.b1), channel_id=1, source_target_pairs={{0,4},{1,5},{2,6},{3,7},{4,0},{5,1},{6,2},{7,3}} | collective-permute-start | bytes 3538952 | tf_op jit(solution)/shard_map/ppermute | solution.py:403
  152.4 79.8 %collective-permute-start.34 = (bf16[576,2304]{1,0:T(8,128)(2,1)}, bf16[576,2304]{1,0:T(8,128)(2,1)}, u32[]{:S(2)}, u32[]{:S(2)}) collective-permute-start(bf16[576,2304]{1,0:T(8,128)(2,1)} %pad_maximum_fusion.3), channel_id=1, source_target_pairs={{0,2},{1,3},{2,0},{3,1},{4,6},{5,7},{6,4},{7,5}} | collective-permute-start | bytes 7962632 | tf_op jit(solution)/shard_map/ppermute | solution.py:403
  166.9 34.9 %collective-permute-start.22 = (bf16[4,576,256]{2,1,0:T(8,128)(2,1)}, bf16[4,576,256]{2,1,0:T(8,128)(2,1)}, u32[]{:S(2)}, u32[]{:S(2)}) collective-permute-start(bf16[4,576,256]{2,1,0:T(8,128)(2,1)} %collective-permute-done.21.b1), channel_id=1, source_target_pairs={{0,1},{1,0},{2,3},{3,2},{4,5},{5,4},{6,7},{7,6}} | collective-permute-start | bytes 3538952 | tf_op jit(solution)/shard_map/ppermute | solution.py:403
  168.6 35.2 %collective-permute-start.11 = (bf16[576,1024]{1,0:T(8,128)(2,1)}, bf16[576,1024]{1,0:T(8,128)(2,1)}, u32[]{:S(2)}, u32[]{:S(2)}) collective-permute-start(bf16[576,1024]{1,0:T(8,128)(2,1)} %collective-permute-done.10.ry), channel_id=1, source_target_pairs={{0,1},{1,0},{2,3},{3,2},{4,5},{5,4},{6,7},{7,6}} | collective-permute-start | bytes 3538952 | tf_op jit(solution)/shard_map/ppermute | solution.py:403
  201.8 30.4 %collective-permute-start.24 = (bf16[4,576,256]{2,1,0:T(8,128)(2,1)}, bf16[4,576,256]{2,1,0:T(8,128)(2,1)}, u32[]{:S(2)}, u32[]{:S(2)}) collective-permute-start(bf16[4,576,256]{2,1,0:T(8,128)(2,1)} %collective-permute-done.23.b2), channel_id=1, source_target_pairs={{0,1},{1,0},{2,3},{3,2},{4,5},{5,4},{6,7},{7,6}} | collective-permute-start | bytes 3538952 | tf_op jit(solution)/shard_map/ppermute | solution.py:403
  203.8 60.8 %collective-permute-start.45 = (bf16[576,2304]{1,0:T(8,128)(2,1)}, bf16[576,2304]{1,0:T(8,128)(2,1)}, u32[]{:S(2)}, u32[]{:S(2)}) collective-permute-start(bf16[576,2304]{1,0:T(8,128)(2,1)} %pad_maximum_fusion.2.g0.u0), channel_id=1, source_target_pairs={{0,4},{1,5},{2,6},{3,7},{4,0},{5,1},{6,2},{7,3}} | collective-permute-start | bytes 7962632 | tf_op jit(solution)/shard_map/ppermute | solution.py:403
  205.6 64.5 %collective-permute-start.31 = (bf16[576,2304]{1,0:T(8,128)(2,1)}, bf16[576,2304]{1,0:T(8,128)(2,1)}, u32[]{:S(2)}, u32[]{:S(2)}) collective-permute-start(bf16[576,2304]{1,0:T(8,128)(2,1)} %pad_maximum_fusion.1), channel_id=1, source_target_pairs={{0,2},{1,3},{2,0},{3,1},{4,6},{5,7},{6,4},{7,5}} | collective-permute-start | bytes 7962632 | tf_op jit(solution)/shard_map/ppermute | solution.py:403
  206.2 114.5 %collective-permute-start.41 = (bf16[576,2304]{1,0:T(8,128)(2,1)}, bf16[576,2304]{1,0:T(8,128)(2,1)}, u32[]{:S(2)}, u32[]{:S(2)}) collective-permute-start(bf16[576,2304]{1,0:T(8,128)(2,1)} %pad_maximum_fusion.g0.u0), channel_id=1, source_target_pairs={{0,4},{1,5},{2,6},{3,7},{4,0},{5,1},{6,2},{7,3}} | collective-permute-start | bytes 7962632 | tf_op jit(solution)/shard_map/ppermute | solution.py:403
  232.1 120.4 %collective-permute-start.33 = (bf16[576,2304]{1,0:T(8,128)(2,1)}, bf16[576,2304]{1,0:T(8,128)(2,1)}, u32[]{:S(2)}, u32[]{:S(2)}) collective-permute-start(bf16[576,2304]{1,0:T(8,128)(2,1)} %pad_maximum_fusion.2.g0.u0), channel_id=1, source_target_pairs={{0,1},{1,0},{2,3},{3,2},{4,5},{5,4},{6,7},{7,6}} | collective-permute-start | bytes 7962632 | tf_op jit(solution)/shard_map/ppermute | solution.py:403
  232.2 120.8 %collective-permute-start.30 = (bf16[576,2304]{1,0:T(8,128)(2,1)}, bf16[576,2304]{1,0:T(8,128)(2,1)}, u32[]{:S(2)}, u32[]{:S(2)}) collective-permute-start(bf16[576,2304]{1,0:T(8,128)(2,1)} %pad_maximum_fusion.g0.u0), channel_id=1, source_target_pairs={{0,1},{1,0},{2,3},{3,2},{4,5},{5,4},{6,7},{7,6}} | collective-permute-start | bytes 7962632 | tf_op jit(solution)/shard_map/ppermute | solution.py:403
  264.6 152.4 %collective-permute-start.39 = (bf16[576,2304]{1,0:T(8,128)(2,1)}, bf16[576,2304]{1,0:T(8,128)(2,1)}, u32[]{:S(2)}, u32[]{:S(2)}) collective-permute-start(bf16[576,2304]{1,0:T(8,128)(2,1)} %get-tuple-element.35), channel_id=1, source_target_pairs={{0,2},{1,3},{2,0},{3,1},{4,6},{5,7},{6,4},{7,5}} | collective-permute-start | bytes 7962632 | tf_op jit(solution)/shard_map/ppermute | solution.py:403
  270.0 84.7 %collective-permute-start.26 = (bf16[4,576,256]{2,1,0:T(8,128)(2,1)}, bf16[4,576,256]{2,1,0:T(8,128)(2,1)}, u32[]{:S(2)}, u32[]{:S(2)}) collective-permute-start(bf16[4,576,256]{2,1,0:T(8,128)(2,1)} %copy-done.2), channel_id=1, source_target_pairs={{0,1},{1,0},{2,3},{3,2},{4,5},{5,4},{6,7},{7,6}} | collective-permute-start | bytes 3538952 | tf_op jit(solution)/shard_map/ppermute | solution.py:403
  320.7 98.0 %collective-permute-start.35 = (bf16[576,2304]{1,0:T(8,128)(2,1)}, bf16[576,2304]{1,0:T(8,128)(2,1)}, u32[]{:S(2)}, u32[]{:S(2)}) collective-permute-start(bf16[576,2304]{1,0:T(8,128)(2,1)} %collective-permute-done.34.g2.u2), channel_id=1, source_target_pairs={{0,1},{1,0},{2,3},{3,2},{4,5},{5,4},{6,7},{7,6}} | collective-permute-start | bytes 7962632 | tf_op jit(solution)/shard_map/ppermute | solution.py:403
  354.8 23.9 %collective-permute-start.29 = (bf16[512,512]{1,0:T(8,128)(2,1)}, bf16[512,512]{1,0:T(8,128)(2,1)}, u32[]{:S(2)}, u32[]{:S(2)}) collective-permute-start(bf16[512,512]{1,0:T(8,128)(2,1)} %get-tuple-element.47), channel_id=1, source_target_pairs={{0,5},{1,4},{2,7},{3,6},{4,1},{5,0},{6,3},{7,2}} | collective-permute-start | bytes 1572872 | tf_op jit(solution)/shard_map/ppermute | solution.py:403
  395.4 47.1 %collective-permute-start.38 = (bf16[576,2304]{1,0:T(8,128)(2,1)}, bf16[576,2304]{1,0:T(8,128)(2,1)}, u32[]{:S(2)}, u32[]{:S(2)}) collective-permute-start(bf16[576,2304]{1,0:T(8,128)(2,1)} %get-tuple-element.36.d0), channel_id=1, source_target_pairs={{0,1},{1,0},{2,3},{3,2},{4,5},{5,4},{6,7},{7,6}} | collective-permute-start | bytes 7962632 | tf_op jit(solution)/shard_map/ppermute | solution.py:403
  395.5 63.2 %collective-permute-start.47 = (bf16[576,2304]{1,0:T(8,128)(2,1)}, bf16[576,2304]{1,0:T(8,128)(2,1)}, u32[]{:S(2)}, u32[]{:S(2)}) collective-permute-start(bf16[576,2304]{1,0:T(8,128)(2,1)} %collective-permute-done.34.g2.u2), channel_id=1, source_target_pairs={{0,4},{1,5},{2,6},{3,7},{4,0},{5,1},{6,2},{7,3}} | collective-permute-start | bytes 7962632 | tf_op jit(solution)/shard_map/ppermute | solution.py:403
  401.1 59.4 %collective-permute-start.32 = (bf16[576,2304]{1,0:T(8,128)(2,1)}, bf16[576,2304]{1,0:T(8,128)(2,1)}, u32[]{:S(2)}, u32[]{:S(2)}) collective-permute-start(bf16[576,2304]{1,0:T(8,128)(2,1)} %collective-permute-done.31.g2.u2), channel_id=1, source_target_pairs={{0,1},{1,0},{2,3},{3,2},{4,5},{5,4},{6,7},{7,6}} | collective-permute-start | bytes 7962632 | tf_op jit(solution)/shard_map/ppermute | solution.py:403
  417.0 54.5 %collective-permute-start.37 = (bf16[2304,512]{1,0:T(8,128)(2,1)}, bf16[2304,512]{1,0:T(8,128)(2,1)}, u32[]{:S(2)}, u32[]{:S(2)}) collective-permute-start(bf16[2304,512]{1,0:T(8,128)(2,1)} %get-tuple-element.21.hw1), channel_id=1, source_target_pairs={{0,2},{1,3},{2,0},{3,1},{4,6},{5,7},{6,4},{7,5}} | collective-permute-start | bytes 7077896 | tf_op jit(solution)/shard_map/ppermute | solution.py:403
  418.6 102.4 %collective-permute-start.36 = (bf16[2304,512]{1,0:T(8,128)(2,1)}, bf16[2304,512]{1,0:T(8,128)(2,1)}, u32[]{:S(2)}, u32[]{:S(2)}) collective-permute-start(bf16[2304,512]{1,0:T(8,128)(2,1)} %get-tuple-element.20.hw0), channel_id=1, source_target_pairs={{0,2},{1,3},{2,0},{3,1},{4,6},{5,7},{6,4},{7,5}} | collective-permute-start | bytes 7077896 | tf_op jit(solution)/shard_map/ppermute | solution.py:403
  442.5 142.5 %collective-permute-start.49 = (bf16[576,2304]{1,0:T(8,128)(2,1)}, bf16[576,2304]{1,0:T(8,128)(2,1)}, u32[]{:S(2)}, u32[]{:S(2)}) collective-permute-start(bf16[576,2304]{1,0:T(8,128)(2,1)} %get-tuple-element.36.d0), channel_id=1, source_target_pairs={{0,4},{1,5},{2,6},{3,7},{4,0},{5,1},{6,2},{7,3}} | collective-permute-start | bytes 7962632 | tf_op jit(solution)/shard_map/ppermute | solution.py:403
  458.7 128.3 %collective-permute-start.43 = (bf16[576,2304]{1,0:T(8,128)(2,1)}, bf16[576,2304]{1,0:T(8,128)(2,1)}, u32[]{:S(2)}, u32[]{:S(2)}) collective-permute-start(bf16[576,2304]{1,0:T(8,128)(2,1)} %collective-permute-done.31.g2.u2), channel_id=1, source_target_pairs={{0,4},{1,5},{2,6},{3,7},{4,0},{5,1},{6,2},{7,3}} | collective-permute-start | bytes 7962632 | tf_op jit(solution)/shard_map/ppermute | solution.py:403
  460.5 126.3 %collective-permute-start.46 = (bf16[576,2304]{1,0:T(8,128)(2,1)}, bf16[576,2304]{1,0:T(8,128)(2,1)}, u32[]{:S(2)}, u32[]{:S(2)}) collective-permute-start(bf16[576,2304]{1,0:T(8,128)(2,1)} %collective-permute-done.45.g0.u0), channel_id=1, source_target_pairs={{0,1},{1,0},{2,3},{3,2},{4,5},{5,4},{6,7},{7,6}} | collective-permute-start | bytes 7962632 | tf_op jit(solution)/shard_map/ppermute | solution.py:403
  471.5 117.2 %collective-permute-start.40 = (bf16[576,2304]{1,0:T(8,128)(2,1)}, bf16[576,2304]{1,0:T(8,128)(2,1)}, u32[]{:S(2)}, u32[]{:S(2)}) collective-permute-start(bf16[576,2304]{1,0:T(8,128)(2,1)} %collective-permute-done.39.d2), channel_id=1, source_target_pairs={{0,1},{1,0},{2,3},{3,2},{4,5},{5,4},{6,7},{7,6}} | collective-permute-start | bytes 7962632 | tf_op jit(solution)/shard_map/ppermute | solution.py:403
  521.1 68.0 %collective-permute-start.48 = (bf16[576,2304]{1,0:T(8,128)(2,1)}, bf16[576,2304]{1,0:T(8,128)(2,1)}, u32[]{:S(2)}, u32[]{:S(2)}) collective-permute-start(bf16[576,2304]{1,0:T(8,128)(2,1)} %collective-permute-done.47.g2.u2), channel_id=1, source_target_pairs={{0,1},{1,0},{2,3},{3,2},{4,5},{5,4},{6,7},{7,6}} | collective-permute-start | bytes 7962632 | tf_op jit(solution)/shard_map/ppermute | solution.py:403
  585.0 60.3 %collective-permute-start.51 = (bf16[576,2304]{1,0:T(8,128)(2,1)}, bf16[576,2304]{1,0:T(8,128)(2,1)}, u32[]{:S(2)}, u32[]{:S(2)}) collective-permute-start(bf16[576,2304]{1,0:T(8,128)(2,1)} %collective-permute-done.39.d2), channel_id=1, source_target_pairs={{0,4},{1,5},{2,6},{3,7},{4,0},{5,1},{6,2},{7,3}} | collective-permute-start | bytes 7962632 | tf_op jit(solution)/shard_map/ppermute | solution.py:403
  586.8 51.1 %collective-permute-start.42 = (bf16[576,2304]{1,0:T(8,128)(2,1)}, bf16[576,2304]{1,0:T(8,128)(2,1)}, u32[]{:S(2)}, u32[]{:S(2)}) collective-permute-start(bf16[576,2304]{1,0:T(8,128)(2,1)} %collective-permute-done.41.g0.u0), channel_id=1, source_target_pairs={{0,1},{1,0},{2,3},{3,2},{4,5},{5,4},{6,7},{7,6}} | collective-permute-start | bytes 7962632 | tf_op jit(solution)/shard_map/ppermute | solution.py:403
  587.0 58.3 %collective-permute-start.53 = (bf16[2048,512]{1,0:T(8,128)(2,1)}, bf16[2048,512]{1,0:T(8,128)(2,1)}, u32[]{:S(2)}, u32[]{:S(2)}) collective-permute-start(bf16[2048,512]{1,0:T(8,128)(2,1)} %get-tuple-element.45), channel_id=1, source_target_pairs={{0,2},{1,3},{2,0},{3,1},{4,6},{5,7},{6,4},{7,5}} | collective-permute-start | bytes 6291464 | tf_op jit(solution)/shard_map/ppermute | solution.py:403
  588.7 91.4 %collective-permute-start.15 = (bf16[2048,512]{1,0:T(8,128)(2,1)}, bf16[2048,512]{1,0:T(8,128)(2,1)}, u32[]{:S(2)}, u32[]{:S(2)}) collective-permute-start(bf16[2048,512]{1,0:T(8,128)(2,1)} %get-tuple-element.46), channel_id=1, source_target_pairs={{0,2},{1,3},{2,0},{3,1},{4,6},{5,7},{6,4},{7,5}} | collective-permute-start | bytes 6291464 | tf_op jit(solution)/shard_map/ppermute | solution.py:403
  589.0 91.0 %collective-permute-start.44 = (bf16[576,2304]{1,0:T(8,128)(2,1)}, bf16[576,2304]{1,0:T(8,128)(2,1)}, u32[]{:S(2)}, u32[]{:S(2)}) collective-permute-start(bf16[576,2304]{1,0:T(8,128)(2,1)} %collective-permute-done.43.g2.u2), channel_id=1, source_target_pairs={{0,1},{1,0},{2,3},{3,2},{4,5},{5,4},{6,7},{7,6}} | collective-permute-start | bytes 7962632 | tf_op jit(solution)/shard_map/ppermute | solution.py:403
  637.8 77.8 %collective-permute-start.50 = (bf16[576,2304]{1,0:T(8,128)(2,1)}, bf16[576,2304]{1,0:T(8,128)(2,1)}, u32[]{:S(2)}, u32[]{:S(2)}) collective-permute-start(bf16[576,2304]{1,0:T(8,128)(2,1)} %collective-permute-done.49.d0), channel_id=1, source_target_pairs={{0,1},{1,0},{2,3},{3,2},{4,5},{5,4},{6,7},{7,6}} | collective-permute-start | bytes 7962632 | tf_op jit(solution)/shard_map/ppermute | solution.py:403
  645.3 202.9 %collective-permute-start.55 = (bf16[4096,512]{1,0:T(8,128)(2,1)}, bf16[4096,512]{1,0:T(8,128)(2,1)}, u32[]{:S(2)}, u32[]{:S(2)}) collective-permute-start(bf16[4096,512]{1,0:T(8,128)(2,1)} %get-tuple-element.16.k_ref.kv0), channel_id=1, source_target_pairs={{0,1},{1,0},{2,3},{3,2},{4,5},{5,4},{6,7},{7,6}} | collective-permute-start | bytes 12582920 | tf_op jit(solution)/shard_map/ppermute | solution.py:403
  645.3 70.3 %collective-permute-start.52 = (bf16[576,2304]{1,0:T(8,128)(2,1)}, bf16[576,2304]{1,0:T(8,128)(2,1)}, u32[]{:S(2)}, u32[]{:S(2)}) collective-permute-start(bf16[576,2304]{1,0:T(8,128)(2,1)} %collective-permute-done.51.d2), channel_id=1, source_target_pairs={{0,1},{1,0},{2,3},{3,2},{4,5},{5,4},{6,7},{7,6}} | collective-permute-start | bytes 7962632 | tf_op jit(solution)/shard_map/ppermute | solution.py:403
  680.1 184.9 %collective-permute-start.54 = (bf16[2048,512]{1,0:T(8,128)(2,1)}, bf16[2048,512]{1,0:T(8,128)(2,1)}, u32[]{:S(2)}, u32[]{:S(2)}) collective-permute-start(bf16[2048,512]{1,0:T(8,128)(2,1)} %collective-permute-done.53.kv0), channel_id=1, source_target_pairs={{0,1},{1,0},{2,3},{3,2},{4,5},{5,4},{6,7},{7,6}} | collective-permute-start | bytes 6291464 | tf_op jit(solution)/shard_map/ppermute | solution.py:403
  680.1 194.6 %collective-permute-start.16 = (bf16[2048,512]{1,0:T(8,128)(2,1)}, bf16[2048,512]{1,0:T(8,128)(2,1)}, u32[]{:S(2)}, u32[]{:S(2)}) collective-permute-start(bf16[2048,512]{1,0:T(8,128)(2,1)} %collective-permute-done.15.kv0), channel_id=1, source_target_pairs={{0,1},{1,0},{2,3},{3,2},{4,5},{5,4},{6,7},{7,6}} | collective-permute-start | bytes 6291464 | tf_op jit(solution)/shard_map/ppermute | solution.py:403
  (25 other events, 464.8 us)

commit v3 on v2

--- a/solution.py
+++ b/solution.py
@@ -20,6 +20,7 @@
 BIG = 2.0 ** 40
 SHRINK = 2.0 ** -88
 MT = 256
+KT = 512
 ANY = pl.BlockSpec(memory_space=pl.ANY)
 
 
@@ -27,6 +28,7 @@
 hcat = functools.partial(jnp.concatenate, axis=1)
 by_col = lambda i, *_: (0, i)
 by_row = lambda i, *_: (i, 0)
+fixed = lambda *_: 0
 
 
 def dot(a, b):
@@ -35,6 +37,22 @@
 
 def dot_nt(a, b):
     return lax.dot_general(a, b, (((1,), (1,)), ((), ())), preferred_element_type=F32)
+
+
+def cols(height, wide, at):
+    return pl.BlockSpec((height, wide), lambda i, *s: (0, at(i, *s)))
+
+
+def bf(*shape):
+    return jax.ShapeDtypeStruct(shape, BF)
+
+
+def f32(*shape):
+    return jax.ShapeDtypeStruct(shape, F32)
+
+
+def vmem(*shape, dtype=BF):
+    return pltpu.VMEM(shape, dtype)
 
 
 def whole(*shape):
@@ -69,6 +87,12 @@
     r = inv_rms(blocks, width)
     for j, b in enumerate(blocks):
         part_of(a_ref, j, w4)[...] = (b.astype(F32) * r * part_of(g_ref, j, w4)[:, 0:1]).astype(BF)
+
+
+def rope_kernel(s_ref, pos_ref, freq_ref, cos_ref, sin_ref):
+    ang = freq_ref[...] * pos_ref[...].astype(F32)
+    cos_ref[...] = jnp.cos(ang)
+    sin_ref[...] = jnp.sin(ang)
 
 
 def qkv_kernel(s_ref, a_ref, w0, w1, w2, w3, cos_ref, sin_ref, qv_ref, kv_ref, w_t, w_all, *, hd):
@@ -161,14 +185,16 @@
         m_ref[:, i:i + MT] = mt_ref[i:i + MT, :].T
 
 
-def proj_kernel(s_ref, o_own, o_c, o_y, o_yc, b0, b0c, b1, b1c, b2, b2c, b3, b3c, x0, x1, x2, x3, g_ref, h_ref, m_ref, o_all, mt_ref, w_ref, w_sem, *, width):
+def proj_kernel(s_ref, o_own, o_c, o_y, o_yc, b0, b0c, b1, b1c, b2, b2c, b3, b3c, x0, x1, x2, x3, g_ref, *rest, width):
+    h_ref, m_ref, o_all, mt_ref, w_ref, w_sem = rest[-6:]
     cps = [pltpu.make_async_copy(b, w_ref.at[i], w_sem.at[i]) for i, b in enumerate((b0, b2, b0c, b2c, b1, b3, b1c, b3c))]
     for cp in cps:
         cp.start()
     c = s_ref[2]
     gw = o_own.shape[0]
     first = c == 0
-    for i, (a, b) in enumerate(((o_own, o_c), (o_c, o_own), (o_y, o_yc), (o_yc, o_y))):
+    pairs = ((o_own, o_c), (o_y, o_yc))
+    for i, (a, b) in enumerate([t for q in pairs for t in (q, q[::-1])]):
         part_of(o_all, i, gw)[...] = jnp.where(first, a[...], b[...])
     w4 = x0.shape[0]
     heads = b0.shape[0]
@@ -189,34 +215,40 @@
     norm_to_m(m_ref, hs, inv_rms(hs, width), g_ref, 2, mt_ref)
 
 
-def renorm_kernel(s_ref, h_ref, g_ref, m_ref, mt_ref, *, width):
+def renorm_kernel(s_ref, h_ref, g_ref, *rest, width):
+    m_ref, mt_ref = rest[-2:]
     w4 = h_ref.shape[0] // 4
     hs = [part_of(h_ref, j, w4)[...].astype(F32) for j in (2, 3, 0, 1)]
     norm_to_m(m_ref, hs, inv_rms(hs, width), g_ref, 2, mt_ref)
 
 
-def gate_up_kernel(s_ref, ma, mb, g0, g1, g2, g3, u0, u1, u2, u3, z_ref):
+def gate_up_kernel(s_ref, *refs, groups, sets, steps):
+    ms, ws, z_ref = refs[:groups], refs[groups:-1], refs[-1]
     n = z_ref.shape[1]
-    w = hcat([vcat([g[...] for g in (g0, g1, g2, g3)]), vcat([u[...] for u in (u0, u1, u2, u3)])])
-    base = 0
-    for m in (ma, mb):
-        for r in range(0, m.shape[0], MT):
-            t = dot(m[r:r + MT, :], w)
-            g, u = t[:, :n].astype(BF).astype(F32), t[:, n:].astype(BF).astype(F32)
-            z_ref[base:base + MT, :] = (jax.nn.gelu(g, approximate=True) * u).astype(BF)
-            base += MT
-
-
-def down_y_kernel(s_ref, zwa, zwb, zfa, zfb, d0, d1, d2, d3, acc_ref, d_ref):
+    per = len(ws) // sets
+    ws = [w[...] for w in ws]
+    if sets > 1:
+        early = pl.program_id(1) < steps
+        ws = [jnp.where(early, a, b) for a, b in zip(ws[:per], ws[per:])]
+    w = hcat([vcat(ws[:per // 2]), vcat(ws[per // 2:])])
+    for r in range(0, z_ref.shape[0], MT):
+        m = [t[r:r + MT, :] for t in ms]
+        m = jnp.where(pl.program_id(0) == 0, m[0], m[1]) if groups > 1 else m[0]
+        t = dot(m, w)
+        g, u = t[:, :n].astype(BF).astype(F32), t[:, n:].astype(BF).astype(F32)
+        z_ref[r:r + MT, :] = (jax.nn.gelu(g, approximate=True) * u).astype(BF)
+
+
+def down_y_kernel(s_ref, zw, zf, d0, d1, d2, d3, acc_ref, d_ref):
     w4 = d0.shape[0]
-    n = zwa.shape[0]
+    n = zw.shape[0]
 
     @pl.when(pl.program_id(0) == 0)
     def _():
         for j, dd in enumerate((d0, d1, d2, d3)):
             part_of(d_ref, j, w4)[...] = dd[...]
 
-    z = vcat([hcat([a[...], b[...]]) for a, b in ((zwa, zwb), (zfa, zfb))])
+    z = vcat([zw[...], zf[...]])
     for j in range(4):
         t = dot_nt(d_ref[j * w4:(j + 1) * w4, :], z)
         for q in range(n // CH):
@@ -224,9 +256,9 @@
             acc_ref[q, j * w4:(j + 1) * w4, CH:] = t[:, n + q * CH:n + (q + 1) * CH]
 
 
-def tail_kernel(part, zwa, zwb, zfa, zfb, d0, d1, d2, d3, hw0, hw1, hf0, hf1, g_ref, out,
-                d_ref, z_ref, p_ref, lo_ref, hi_ref, rec_ref, h_ref, sqs_ref, sqr_ref, sqo_ref,
-                d_sem, z_sem, p_sem, h_sem, loc_sem, rs_s, rs_r, sq_s, sq_r, out_s, out_r, *, width, chunks):
+def tail_kernel(part, zwa, zfa, zb, d0, d1, d2, d3, dt, hw0, hw1, hf0, hf1, g_ref, out,
+                d_ref, z_ref, g_buf, p_ref, lo_ref, hi_ref, rec_ref, h_ref, sqs_ref, sqr_ref, sqo_ref,
+                d_sem, z_sem, p_sem, h_sem, loc_sem, rs_s, rs_r, sq_s, sq_r, dt_s, dt_r, out_s, out_r, *, width, chunks):
     w4 = d0.shape[0]
     w2 = 2 * w4
     f8 = zwa.shape[1]
@@ -244,13 +276,18 @@
     def remote(src, dst, s_sem, r_sem, dev):
         return pltpu.make_async_remote_copy(src_ref=src, dst_ref=dst, send_sem=s_sem, recv_sem=r_sem, device_id=dev, device_id_type=pl.DeviceIdType.MESH)
 
-    d_cp = [local(dd, part_of(d_ref, j, w4), d_sem.at[j]) for j, dd in enumerate((d0, d1, d2, d3))]
+    d_cp = [local(dd, d_ref.at[j * w4:(j + 1) * w4, :dd.shape[1]], d_sem.at[j]) for j, dd in enumerate((d0, d1, d2, d3))]
+    g_cp = local(part_of(g_ref, 0, w2), g_buf, d_sem.at[4])
+    late = slice(d0.shape[1], d_ref.shape[1])
+    dt_y = remote(dt.at[:, late], d_ref.at[:w4, late], dt_s.at[0], dt_r.at[0], py)
+    dt_c = remote(d_ref.at[:w4, late], d_ref.at[w4:w2, late], dt_s.at[1], dt_r.at[1], pc)
 
     def z_cp(p):
-        return [local(src.at[pl.ds(p * CH, CH), :], z_ref.at[p, i // 2 * CH:(i // 2 + 1) * CH, i % 2 * f8:(i % 2 + 1) * f8], z_sem.at[p, i]) for i, src in enumerate((zwa, zwb, zfa, zfb))]
+        srcs = ((zwa, 0), (zb, 0), (zfa, 0), (zb, zwa.shape[0]))
+        return [local(src.at[pl.ds(at + p * CH, CH), :], z_ref.at[p, i // 2 * CH:(i // 2 + 1) * CH, i % 2 * f8:(i % 2 + 1) * f8], z_sem.at[p, i]) for i, (src, at) in enumerate(srcs)]
 
     def p_cp(p):
-        return local(part.at[p], p_ref.at[lax.rem(p, 2)], p_sem.at[lax.rem(p, 2)])
+        return local(part.at[p], p_ref.at[lax.rem(p, 3)], p_sem.at[lax.rem(p, 3)])
 
     per = hw0.shape[1] // CH
     h_cp = []
@@ -269,6 +306,7 @@
     for dev in (px, pc, py, pyc):
         pl.semaphore_signal(bar, inc=1, device_id=dev, device_id_type=pl.DeviceIdType.MESH)
     pl.semaphore_wait(bar, 4)
+    dt_y.start()
 
     def rs(p, i):
         rws = slice(i * w4, (i + 1) * w4)
@@ -290,7 +328,7 @@
         return res
 
     def block(p, j):
-        return dot_nt(part_of(d_ref, j, w4)[...], z_ref[p]) + p_ref[lax.rem(p, 2), j * w4:(j + 1) * w4, :]
+        return dot_nt(part_of(d_ref, j, w4)[...], z_ref[p]) + p_ref[lax.rem(p, 3), j * w4:(j + 1) * w4, :]
 
     def upper(p, first=False):
         p_cp(p).wait()
@@ -332,8 +370,7 @@
     def finish(p):
         sq(p).wait_recv()
         r = lax.rsqrt((sqo_ref[...] + sqr_ref[p]) / width + NORM_EPS)[0:1]
-        g = g_ref[...]
-        g = hcat([g] * (2 * CH // 128))
+        g = g_buf[:, 3:4]
         rec_ref[p] = (h_ref[p].astype(F32) + rec_ref[p].astype(F32) * r * g).astype(BF)
         for group in outs(p):
             for cp in group[1:] + group[:1]:
@@ -341,13 +378,16 @@
 
     upper(0, True)
     start(d_cp[:2] + z_cp(1))
-    lower(0, True)
-    start(h_cp)
+    upper(1)
+    start([g_cp] + h_cp)
     for q in range(2, chunks):
         start(z_cp(q))
-    upper(1)
+    dt_y.wait_recv()
+    dt_c.start()
+    dt_c.wait_recv()
+    lower(0, True)
     lower(1)
-    for cp in h_cp:
+    for cp in [g_cp] + h_cp:
         cp.wait()
 
     def body(p, _):
@@ -376,6 +416,8 @@
         return 0
 
     lax.fori_loop(0, chunks, drain, 0)
+    dt_y.wait_send()
+    dt_c.wait_send()
 
 
 def kv_out_kernel(s_ref, kv0, kv1, *rest, extra):
@@ -387,7 +429,7 @@
     a, b = kv0[...], kv1[...]
     two = jnp.where(first, a, b), jnp.where(first, b, a)
     for ref, at in ((k_ref, 0), (v_ref, hd)):
-        ref[...] = jnp.stack([t[:, at:at + hd] for t in two], axis=1)
+        ref[...] = hcat([t[:, at:at + hd] for t in two]).reshape(ref.shape)
 
 
 def solution(mesh):
@@ -421,21 +463,27 @@
         def take(a, start, size, axis=0):
             return lax.dynamic_slice_in_dim(a, start, size, axis)
 
+        def take_cols(a, start, size):
+            return take(a, start, size, 1)
+
+        sets = range(2)
+        dma = pltpu.SemaphoreType.DMA
         xt = tokens.T
 
         gains = jnp.stack([n1, n2, n3, n4])
         gall = hcat([gains, send(gains, PC), send(gains, PX), send(gains, PXC)])
         gcol = (1.0 + gall.astype(F32)).T
 
-        rx = [send(take(xt, xo * S + k * half + y * (half // 2), half // 2, 1), PX) for k in range(2)]
-        own_p = take(xt, x * S, S, 1)
+        oh = half // 2
+        rx = [send(take_cols(xt, xo * S + k * half + y * oh, oh), PX) for k in sets]
+        own_p = take_cols(xt, x * S, S)
         own_c = send(own_p, PC)
-        ry = [send(rx[k], PY) for k in range(2)]
-        rxc = [send(rx[k], PC) for k in range(2)]
-        ryc = [send(ry[k], PC) for k in range(2)]
+        ry = [send(rx[k], PY) for k in sets]
+        rxc = [send(rx[k], PC) for k in sets]
+        ryc = [send(ry[k], PC) for k in sets]
 
         def group_cols(g):
-            return hcat([take(w, n * g, n, 1).reshape(w4, n * hd) for w, n in ((wq, 2), (wk, 1), (wv, 1))])
+            return hcat([take_cols(w, n * g, n).reshape(w4, n * hd) for w, n in ((wq, 2), (wk, 1), (wv, 1))])
 
         wq_own, wq_oth = group_cols(c), group_cols(co)
         wqs = [wq_own, send(wq_oth, PC), send(wq_own, PX), send(wq_oth, PXC)]
@@ -449,9 +497,9 @@
         for b in (B0, B1, B2, B3):
             Bs += [b, send(b, PC)]
 
-        def gather(own, oth):
+        def gather(own, oth, far=None):
             r1 = send(oth, PX)
-            s0 = send(own, PY)
+            s0 = send(own if far is None else far, PY)
             s1 = send(r1, PY)
             ty = [own, send(own, PC), r1, send(r1, PC)]
             to = [s0, send(s0, PC), s1, send(s1, PC)]
@@ -460,135 +508,142 @@
         F8 = F4 // 2
 
         def gu_half(xx, at):
-            return hcat([take(w, xx * F4 + at, F8, 1) for w in (wg, wu)])
+            return hcat([take_cols(w, xx * F4 + at, F8) for w in (wg, wu)])
 
         gu = {ab: gather(gu_half(x, at), gu_half(xo, at)) for ab, at in (('a', 0), ('b', F8))}
         wdt = wd.T
-        dw_own, dw_oth = (take(wdt, xx * F4, F4, 1) for xx in (x, xo))
-        dn_y, dn_o = gather(dw_own, dw_oth)
+        dw_own, dw_oth = (take_cols(wdt, xx * F4, F4) for xx in (x, xo))
+        dw_early = dw_own[:, :F4 - KT]
+        dn_y, dn_o = gather(dw_own, dw_oth, dw_early)
 
         pos = take(positions, x, 1)[0]
         inv_freq = ROPE_BASE ** (-2.0 * jnp.arange(hd // 2, dtype=F32) / hd)
-        ang = inv_freq[:, None] * pos.astype(F32)[None, :]
-        cos_t, sin_t = jnp.cos(ang), jnp.sin(ang)
+        pos_row, pos_col = pos.reshape(1, S), pos.reshape(S, 1)
 
         tile = 512
         nt = half // tile
         per_half = nt // 2
         nb = S // tile
+        cos_t, sin_t = call(
+            rope_kernel, (nb,), [pl.BlockSpec((1, tile), by_col), whole(hd // 2, 1)], [pl.BlockSpec((hd // 2, tile), by_col)] * 2,
+            [f32(hd // 2, S)] * 2, flops=hd * S * nb)(scal, pos_row, inv_freq.reshape(hd // 2, 1))
         a_all = []
-        for k in range(2):
+        for k in sets:
             a_all = [call(
                 functools.partial(norm_kernel, width=D, per_half=per_half), (nt,),
-                [pl.BlockSpec((w4, tile), lambda i, s, k=k: (0, s[0] * nb + k * nt + i)), pl.BlockSpec((w4, tile), lambda i, s, k=k: (0, k * nt + i))]
-                + [pl.BlockSpec((w4, tile), lambda i, s: (0, i % per_half))] * 4 + [whole(D, 4)] + [ANY] * k,
-                pl.BlockSpec((D, tile), lambda i, s, k=k: (0, k * nt + i)), jax.ShapeDtypeStruct((D, S), BF),
-                flops=100 * D * half, aliases={8: 0} if k else None)(scal, xt, own_c, rx[k], rxc[k], ry[k], ryc[k], gcol, *a_all)]
+                [cols(w4, tile, lambda i, s, k=k: s[0] * nb + k * nt + i), cols(w4, tile, lambda i, s, k=k: k * nt + i)] + [cols(w4, tile, lambda i, s: i % per_half)] * 4 + [whole(D, 4)] + [ANY] * k,
+                cols(D, tile, lambda i, s, k=k: k * nt + i), bf(D, S),
+                flops=D * S, aliases={8: 0} if k else None)(scal, xt, own_c, rx[k], rxc[k], ry[k], ryc[k], gcol, *a_all)]
         qv, kv = call(
             functools.partial(qkv_kernel, hd=hd), (nb,),
             [pl.BlockSpec((D, tile), by_col)] + [whole(w4, 2 * gw)] * 4 + [pl.BlockSpec((hd // 2, tile), by_col)] * 2,
             [pl.BlockSpec((gw + hd, tile), by_col), pl.BlockSpec((tile, gw), by_row)],
-            [jax.ShapeDtypeStruct((gw + hd, S), BF), jax.ShapeDtypeStruct((S, gw), BF)],
-            [pltpu.VMEM((2 * gw, D), BF), pltpu.VMEM((D, 2 * gw), BF)],
-            flops=2 * D * 2 * gw * S)(scal, *a_all, *wqs, cos_t, sin_t)
-
-        bq = bk = 512
+            [bf(gw + hd, S), bf(S, gw)],
+            [vmem(2 * gw, D), vmem(D, 2 * gw)],
+            flops=D * gw * S)(scal, *a_all, *wqs, cos_t, sin_t)
+
+        bq = bk = tile
+        bq2 = 2 * bq
         first_q, last_q = pos[0::bq][:, None], pos[bq - 1::bq][:, None]
         first_k, last_k = pos[0::bk][None, :], pos[bk - 1::bk][None, :]
         lo_t = jnp.sum((first_q - last_k >= WINDOW_LEN).astype(jnp.int32), axis=1)
         full_t = jnp.sum((last_q - first_k >= WINDOW_LEN).astype(jnp.int32), axis=1)
-        pos_row, pos_col = pos.reshape(1, S), pos.reshape(S, 1)
         h_own, m_own = [], []
-        for k in range(2):
+        heads = wo.shape[0]
+        qn = half // quarter
+        mine = lambda i, s: 2 * s[1] + s[2]
+        for k in sets:
             q0 = k * half // bq
             kl = (k + 1) * half
             o = call(
                 functools.partial(attn_kernel, bq=bq, bk=bk, q_block0=q0, scale=scale), (half // bq,),
                 [
-                    pl.BlockSpec((gw, bq), lambda i, *_, q0=q0: (0, q0 + i)),
-                    pl.BlockSpec((kl, hd), lambda i, *_: (0, 0)),
-                    pl.BlockSpec((hd, kl), lambda i, *_: (2, 0)),
-                    pl.BlockSpec((1, bq), lambda i, *_, q0=q0: (0, q0 + i)),
-                    pl.BlockSpec((kl, 1), lambda i, *_: (0, 0)),
+                    cols(gw, bq, lambda i, *_, q0=q0: q0 + i), cols(kl, hd, fixed), pl.BlockSpec((hd, kl), lambda i, *_: (gw // hd, 0)),
+                    cols(1, bq, lambda i, *_, q0=q0: q0 + i), cols(kl, 1, fixed),
                 ],
                 pl.BlockSpec((gw, bq), by_col),
-                jax.ShapeDtypeStruct((gw, half), BF),
-                [pltpu.VMEM((hd, 2 * bq), F32), pltpu.VMEM((hd, 2 * bq), BF), pltpu.VMEM((1, 2 * bq), F32), pltpu.VMEM((hd, kl), BF), pltpu.VMEM((8, CH), F32)],
-                prefetch=2, flops=4 * hd * 2 * half * (k * half + half // 2))(lo_t, full_t, qv, kv, qv, pos_row, pos_col)
+                bf(gw, half),
+                [vmem(hd, bq2, dtype=F32), vmem(hd, bq2), vmem(1, bq2, dtype=F32), vmem(hd, kl), vmem(8, CH, dtype=F32)],
+                prefetch=2, flops=gw * half * kl)(lo_t, full_t, qv, kv, qv, pos_row, pos_col)
             mc = 2 * y + co
             my, myc = 2 * yo + c, 2 * yo + co
-            o_c = send(take(o, mc * quarter, quarter, 1), PC)
-            o_y = send(take(o, my * quarter, quarter, 1), PY)
-            o_yc = send(take(o, myc * quarter, quarter, 1), PYC)
-            heads = wo.shape[0]
-            qn = half // quarter
+            o_c = send(take_cols(o, mc * quarter, quarter), PC)
+            o_y = send(take_cols(o, my * quarter, quarter), PY)
+            o_yc = send(take_cols(o, myc * quarter, quarter), PYC)
             h, m = call(
                 functools.partial(proj_kernel, width=D), (1,),
-                [pl.BlockSpec((gw, quarter), lambda i, s: (0, 2 * s[1] + s[2]))] + [whole(gw, quarter)] * 3 + [ANY] * 8 + [
-                    pl.BlockSpec((w4, quarter), lambda i, s, k=k: (0, s[0] * 2 * qn + k * qn + 2 * s[1] + s[2])),
-                    pl.BlockSpec((w4, quarter), lambda i, s, k=k: (0, k * qn + 2 * s[1] + s[2])),
-                    pl.BlockSpec((w4, quarter), lambda i, s: (0, s[2])),
-                    pl.BlockSpec((w4, quarter), lambda i, s: (0, s[2])),
-                    whole(D, 4)],
-                [whole(D, quarter), whole(quarter, D)],
-                [jax.ShapeDtypeStruct((D, quarter), BF), jax.ShapeDtypeStruct((quarter, D), BF)],
-                [pltpu.VMEM((4 * gw, quarter), BF), pltpu.VMEM((D, quarter), BF), pltpu.VMEM((8, heads, w4, hd), BF), pltpu.SemaphoreType.DMA((8,))],
-                flops=2 * D * 4 * gw * quarter)(scal, o, o_c, o_y, o_yc, *Bs, xt, own_c, rx[k], rxc[k], gcol)
+                [cols(gw, quarter, mine)] + [whole(gw, quarter)] * 3 + [ANY] * 8 + [
+                    cols(w4, quarter, lambda i, s, k=k: (2 * s[0] + k) * qn + mine(i, s)), cols(w4, quarter, lambda i, s, k=k: k * qn + mine(i, s)),
+                    *[cols(w4, quarter, lambda i, s: s[2])] * 2,
+                    whole(D, 4)] + [ANY] * k,
+                [whole(D, quarter), pl.BlockSpec((quarter, D), lambda i, s, k=k: (k, 0))],
+                [bf(D, quarter), bf(oh, D)],
+                [vmem(4 * gw, quarter), vmem(D, quarter), vmem(len(Bs), heads, w4, hd), dma((len(Bs),))],
+                flops=D * gw * half, aliases={18: 1} if k else None)(scal, o, o_c, o_y, o_yc, *Bs, xt, own_c, rx[k], rxc[k], gcol, *m_own)
             h_own.append(h)
-            m_own.append(m)
-        h_for = [send(h_own[k], PX) for k in range(2)]
+            m_own = [m]
+        h_for = [send(h_own[k], PX) for k in sets]
         m_for = []
-        for k in range(2):
-            m_for.append(call(
-                functools.partial(renorm_kernel, width=D), (1,), [whole(D, quarter), whole(D, 4)], whole(quarter, D),
-                jax.ShapeDtypeStruct((quarter, D), BF), [pltpu.VMEM((D, quarter), BF)], flops=100 * D * quarter)(scal, h_for[k], gcol))
+        for k in sets:
+            m_for = [call(
+                functools.partial(renorm_kernel, width=D), (1,), [whole(D, quarter), whole(D, 4)] + [ANY] * k,
+                pl.BlockSpec((quarter, D), lambda i, s, k=k: (k, 0)), bf(oh, D), [vmem(D, quarter)],
+                flops=D * half, aliases={3: 0} if k else None)(scal, h_for[k], gcol, *m_for)]
 
         ft = 384
         nf = F8 // ft
 
-        def gated(ms, w):
+        def gated(ms, wsets):
+            groups, sets = len(ms), len(wsets)
+            early = lambda i: jnp.minimum(i, nf - 1)
+            late = lambda i: jnp.maximum(i - nf, 0)
+            specs = [cols(w4, ft, lambda j, i, s, at=at, up=up: up * nf + at(i)) for at in (early, late)[:sets] for up in range(2) for _ in wsets[0]]
             return call(
-                gate_up_kernel, (nf,),
-                [whole(quarter, D)] * 2 + [pl.BlockSpec((w4, ft), by_col)] * 4 + [pl.BlockSpec((w4, ft), lambda i, s: (0, nf + i))] * 4,
-                pl.BlockSpec((2 * quarter, ft), by_col), jax.ShapeDtypeStruct((2 * quarter, F8), BF),
-                flops=2 * D * 2 * F8 * 2 * quarter)(scal, *ms, *w, *w)
-
-        z = {t + hf: [gated(ms, gu[ab][i]) for ab in gu] for i, hf in enumerate('yo') for t, ms in (('own', m_own), ('for', m_for))}
-
+                functools.partial(gate_up_kernel, groups=groups, sets=sets, steps=nf), (groups, sets * nf),
+                [whole(oh, D)] * groups + specs, pl.BlockSpec((oh, ft), lambda j, i, s: (j, i)),
+                bf(oh * groups, sets * F8), flops=D * F4 * half * groups * sets)(scal, *ms, *[t for w in wsets for t in w + w])
+
+        gua, gub = gu['a'], gu['b']
+        near = [t[0] for t in (gua, gub)]
+        zy_own = gated(m_own, near)
+        zy_for = gated(m_for, near)
+        za_own = gated(m_own, [gua[1]])
+        za_for = gated(m_for, [gua[1]])
+        zb = gated(m_own + m_for, [gub[1]])
         w2 = 2 * w4
-        chunks = 2 * quarter // CH
+        chunks = oh // CH
         yt = 2 * CH
         part = call(
-            down_y_kernel, (2 * quarter // yt,), [pl.BlockSpec((yt, F8), by_row)] * 4 + [whole(w4, F4)] * 4,
-            pl.BlockSpec((2, D, yt), lambda i, s: (i, 0, 0)), jax.ShapeDtypeStruct((chunks, D, yt), F32),
-            [pltpu.VMEM((D, F4), BF)], flops=2 * D * F4 * 2 * quarter * 2)(scal, *z['owny'], *z['fory'], *dn_y)
-        dma = pltpu.SemaphoreType.DMA
+            down_y_kernel, (oh // yt,), [pl.BlockSpec((yt, F4), by_row)] * 2 + [whole(w4, F4)] * 4,
+            pl.BlockSpec((2, D, yt), lambda i, s: (i, 0, 0)), f32(chunks, D, yt),
+            [vmem(D, F4)], flops=D * F4 * half)(scal, zy_own, zy_for, *dn_y)
         out = pl.pallas_call(
             functools.partial(tail_kernel, width=D, chunks=chunks),
-            out_shape=jax.ShapeDtypeStruct((w4, rows), BF),
-            in_specs=[ANY] * 13 + [pl.BlockSpec(memory_space=pltpu.VMEM)],
+            out_shape=bf(w4, rows),
+            in_specs=[ANY] * 14,
             out_specs=ANY,
             scratch_shapes=[
-                pltpu.VMEM((D, F4), BF), pltpu.VMEM((chunks, yt, F4), BF), pltpu.VMEM((2, D, yt), F32), pltpu.VMEM((chunks, w2, yt), F32),
-                *[pltpu.VMEM((chunks, w2, yt), BF)] * 3, *[pltpu.VMEM((chunks, 8, yt), F32)] * 2, pltpu.VMEM((8, yt), F32),
-                dma((4,)), dma((chunks, 4)), dma((2,)), *[dma((chunks, 2))] * 4, *[dma((chunks,))] * 2, *[dma((chunks, 2, 3))] * 2],
-            cost_estimate=pl.CostEstimate(flops=2 * D * F4 * 4 * quarter, bytes_accessed=4 * D * rows, transcendentals=0),
-            compiler_params=pltpu.CompilerParams(vmem_limit_bytes=60 * 1024 * 1024, collective_id=0, has_side_effects=True),
+                vmem(D, F4), vmem(chunks, yt, F4), vmem(w2, 4, dtype=F32), vmem(3, D, yt, dtype=F32), vmem(chunks, w2, yt, dtype=F32),
+                *[vmem(chunks, w2, yt)] * 3, *[vmem(chunks, 8, yt, dtype=F32)] * 2, vmem(8, yt, dtype=F32),
+                dma((5,)), dma((chunks, 4)), dma((3,)), *[dma((chunks, 2))] * 4, *[dma((chunks,))] * 2, *[dma((2,))] * 2, *[dma((chunks, 2, 3))] * 2],
+            cost_estimate=pl.CostEstimate(flops=D * F4 * S, bytes_accessed=D * rows, transcendentals=0),
+            compiler_params=pltpu.CompilerParams(vmem_limit_bytes=VM, collective_id=0, has_side_effects=True),
             name='tail',
-        )(part, *z['owno'], *z['foro'], *dn_o, *h_own, *h_for, jnp.broadcast_to(gcol[:w2, 3:4], (w2, 128)))
+        )(part, za_own, za_for, zb, *dn_o, dw_own, *h_own, *h_for, gcol)
         kv_c = send(kv, PC)
-        kv_x = [send(kv[k * half:(k + 1) * half], PX) for k in range(2)]
-        kv_xc = [send(kv_x[k], PC) for k in range(2)]
+        kv_sets = jnp.split(kv, [S - oh])
+        kv_x = [send(t, PX) for t in kv_sets]
+        kv_xc = [send(kv_x[k], PC) for k in sets]
         kv_spec = pl.BlockSpec((tile, gw), by_row)
         kv_outs = []
-        for i, (t, tc, n, base) in enumerate(((kv, kv_c, nb, 0), (kv_x[0], kv_xc[0], nt, 0), (kv_x[1], kv_xc[1], nt, nt))):
+        for i, (t, tc, n, base) in enumerate(((kv, kv_c, nb, 0), (kv_x[0], kv_xc[0], nb - per_half, 0), (kv_x[1], kv_xc[1], per_half, nb - per_half))):
             extra = i == 2
             at = lambda j, s, i=i, base=base: ((1 - s[0] if i else s[0]) * nb + base + j, 0, 0)
-            cspec = [pl.BlockSpec((w4, rows // nt), by_col)] * extra
+            cspec = [cols(w4, rows // n, lambda i, s: i)] * extra
             kv_outs = call(
                 functools.partial(kv_out_kernel, extra=int(extra)), (n,), [kv_spec] * 2 + cspec + [ANY] * len(kv_outs),
-                [pl.BlockSpec((tile, 2, hd), at)] * 2 + cspec, [jax.ShapeDtypeStruct((rows, 2, hd), BF)] * 2 + [jax.ShapeDtypeStruct((w4, rows), BF)] * extra,
-                flops=100 * rows * hd, aliases={3 + extra: 0, 4 + extra: 1} if i else None)(scal, t, tc, *[out] * extra, *kv_outs)
+                [pl.BlockSpec((tile, 2, hd), at)] * 2 + cspec, [bf(rows, 2, hd)] * 2 + [bf(w4, rows)] * extra,
+                flops=rows * gw, aliases={3 + extra: 0, 4 + extra: 1} if i else None)(scal, t, tc, *[out] * extra, *kv_outs)
         k_out, v_out, out = kv_outs
         return out.T, k_out, v_out
 

time: 893 us -> 908 us (1.017)
  waiting for transfers between devices: 301 us -> 334 us
  Pallas kernels: 480 us -> 467 us
    ppermute x56, waiting for transfers between devices: 301 us -> 334 us  [send(): return lax.ppermute(a, ('tp', 'dm'), perm)]
    pallas_call x3, Pallas kernels: 38.6 us -> 28.2 us  [layer(): call(functools.partial(kv_out_kernel, extra=int(extra)), (n,), [kv_spec]...]
    sin x1 -> x0, other arithmetic: 9.31 us -> none  [layer(): cos_t, sin_t = (jnp.cos(ang), jnp.sin(ang))]
    pallas_call x11 -> x9, Pallas kernels: 201 us -> 198 us  [the longest x5 126 us: gated(): call(functools.partial(gate_up_kernel, groups=groups, sets=sets, steps=nf...]
    dynamic_slice x8 -> x9, local copies, waits for them, and re-layouts: 30.1 us -> 28.8 us  [take(): return lax.dynamic_slice_in_dim(a, start, size, axis)]
  transfers between devices with their start and end apart: 56 -> 56, of which waited for: 17 -> 18; matrix products, arithmetic and copies ran while one was open for 7% -> 6% of each run, Pallas kernels for 53% -> 51%
where the time goes in v3:
time: 908 us; the launch traced here: 900 us
  Pallas kernels  467 us (51%)
  waiting for transfers between devices  334 us (37%)
  local copies, waits for them, and re-layouts  43.2 us (5%)
  starting transfers between devices  42.8 us (5%)
  other arithmetic  12 us (1%)
    ppermute x56, waiting for transfers between devices, send(): return lax.ppermute(a, ('tp', 'dm'), perm)  334 us
    pallas_call x1, Pallas kernels, layer(): pl.pallas_call(functools.partial(tail_kernel, width=D, chunks=chunks), ou...  131 us
    pallas_call x5, Pallas kernels, gated(): call(functools.partial(gate_up_kernel, groups=groups, sets=sets, steps=nf...  126 us
    pallas_call x2, Pallas kernels, layer(): call(functools.partial(attn_kernel, bq=bq, bk=bk, q_block0=q0, scale=scal...  44.7 us
    ppermute x56, starting transfers between devices, send(): return lax.ppermute(a, ('tp', 'dm'), perm)  42.8 us
    pallas_call x1, Pallas kernels, layer(): call(down_y_kernel, (oh // yt,), [pl.BlockSpec((yt, F4), by_row)] * 2 + [...  31 us
    pallas_call x2, Pallas kernels, layer(): call(functools.partial(proj_kernel, width=D), (1,), [cols(gw, quarter, mi...  30 us
    pallas_call x1, Pallas kernels, layer(): call(functools.partial(qkv_kernel, hd=hd), (nb,), [pl.BlockSpec((D, tile)...  29.3 us
  transfers between devices with their start and end apart: 56, of which 18 were waited for; matrix products, arithmetic and copies ran while one was open for 6% of the time, Pallas kernels for 51%

profile of v3, /device:TPU:0, one launch (start us, length us, event | category | flops | bytes accessed | tf_op | source)
XLA Modules:
  0.0 900.4 jit_solution(16232187859421018040)
XLA Ops:
  0.7 3.3 dynamic-slice_bitcast_fusion.3
  4.0 3.3 collective-permute-start.1
  7.4 2.4 constant_dynamic-slice_fusion.15
  17.6 66.6 %collective-permute-done.6 = bf16[4,576]{1,0:T(4,128)(2,1)S(1)} collective-permute-done((bf16[4,576]{1,0:T(4,128)(2,1)S(1)}, bf16[4,576]{1,0:T(4,128)(2,1)S(1)}, u32[]{:S(2)}, u32[]{:S(2)}) %collective-permute-start.6) | collective-permute-done | bytes 4640 | tf_op jit(solution)/shard_map/ppermute | solution.py:445
  84.6 2.7 collective-permute-done.7
  87.7 5.3 dynamic-slice_bitcast_fusion.1
  92.9 3.0 slice.14
  99.5 16.0 %collective-permute-done.14.w3 = bf16[576,1024]{1,0:T(8,128)(2,1)} collective-permute-done((bf16[576,1024]{1,0:T(8,128)(2,1)}, bf16[576,1024]{1,0:T(8,128)(2,1)}, u32[]{:S(2)}, u32[]{:S(2)}) %collective-permute-start.14) | collective-permute-done | bytes 1179680 | tf_op jit(solution)/shard_map/ppermute | solution.py:445
  116.3 7.4 constant_dynamic-slice_fusion
  125.5 15.6 %collective-permute-done.21.b1 = bf16[4,576,256]{2,1,0:T(8,128)(2,1)} collective-permute-done((bf16[4,576,256]{2,1,0:T(8,128)(2,1)}, bf16[4,576,256]{2,1,0:T(8,128)(2,1)}, u32[]{:S(2)}, u32[]{:S(2)}) %collective-permute-start.21) | collective-permute-done | bytes 1179680 | tf_op jit(solution)/shard_map/ppermute | solution.py:445
  141.1 27.7 %collective-permute-done.23.b2 = bf16[4,576,256]{2,1,0:T(8,128)(2,1)} collective-permute-done((bf16[4,576,256]{2,1,0:T(8,128)(2,1)}, bf16[4,576,256]{2,1,0:T(8,128)(2,1)}, u32[]{:S(2)}, u32[]{:S(2)}) %collective-permute-start.23) | collective-permute-done | bytes 1179680 | tf_op jit(solution)/shard_map/ppermute | solution.py:445
  170.4 5.1 dynamic-slice_bitcast_fusion
  180.7 13.4 %collective-permute-done.3.ry = bf16[576,1024]{1,0:T(8,128)(2,1)} collective-permute-done((bf16[576,1024]{1,0:T(8,128)(2,1)}, bf16[576,1024]{1,0:T(8,128)(2,1)}, u32[]{:S(2)}, u32[]{:S(2)}) %collective-permute-start.3) | collective-permute-done | bytes 1179680 | tf_op jit(solution)/shard_map/ppermute | solution.py:445
  196.0 23.4 %collective-permute-done.10.ry = bf16[576,1024]{1,0:T(8,128)(2,1)} collective-permute-done((bf16[576,1024]{1,0:T(8,128)(2,1)}, bf16[576,1024]{1,0:T(8,128)(2,1)}, u32[]{:S(2)}, u32[]{:S(2)}) %collective-permute-start.10) | collective-permute-done | bytes 1179680 | tf_op jit(solution)/shard_map/ppermute | solution.py:445
  223.2 3.5 pad_maximum_fusion.2.refs_9_.refs_13_
  226.7 21.5 %collective-permute-done.25.b3 = bf16[4,576,256]{2,1,0:T(8,128)(2,1)} collective-permute-done((bf16[4,576,256]{2,1,0:T(8,128)(2,1)}, bf16[4,576,256]{2,1,0:T(8,128)(2,1)}, u32[]{:S(2)}, u32[]{:S(2)}) %collective-permute-start.25) | collective-permute-done | bytes 1179680 | tf_op jit(solution)/shard_map/ppermute | solution.py:445
  250.4 4.6 collective-permute-done.31.refs_3_.refs_7_
  256.6 2.0 copy.54.pk_ref
  259.9 11.0 %shard_map.150 = (f32[128,4096]{1,0:T(8,128)}, f32[128,4096]{1,0:T(8,128)}) custom-call(s32[3]{0:T(128)} %pad_add_fusion.s_ref, s32[1,4096]{1,0:T(1,128)} %copy-done.12, f32[128,1]{1,0:T(8,128)} %multiply_power_fusion.freq_ref), custom_call_target="tpu_custom_call" | custom-call | flops 8388608 | tf_op jit(solution)/shard_map/pallas_call | solution.py:527
  274.2 11.7 %shard_map.148.rest_0_ = bf16[2304,4096]{1,0:T(8,128)(2,1)} custom-call(s32[3]{0:T(128)} %pad_add_fusion.s_ref, bf16[576,8192]{1,0:T(8,128)(2,1)} %bitcast.36, bf16[576,4096]{1,0:T(8,128)(2,1)} %collective-permute-done.own_c.x1, bf16[576,1024]{1,0:T(8,128)(2,1)} %copy-done.6, bf16[576,1024]{1,0:T(8,128)(2,1)} %collective-permute-done.9.rxc.x3, ...), custom_call_target="tpu_custom_call" | custom-call | flops 9437184 | tf_op jit(solution)/shard_map/pallas_call | solution.py:532
  285.9 12.0 %shard_map.149.a_ref = bf16[2304,4096]{1,0:T(8,128)(2,1)} custom-call(s32[3]{0:T(128)} %pad_add_fusion.s_ref, bf16[576,8192]{1,0:T(8,128)(2,1)} %bitcast.37, bf16[576,4096]{1,0:T(8,128)(2,1)} %collective-permute-done.own_c.x1, bf16[576,1024]{1,0:T(8,128)(2,1)} %collective-permute-done.1.rx.x2, ...), custom_call_target="tpu_custom_call", output_to_operand_aliasing={{}: (8, {})} | custom-call | flops 9437184 | tf_op jit(solution)/shard_map/pallas_call | solution.py:532
  297.9 29.3 %shard_map.151 = (bf16[768,4096]{1,0:T(8,128)(2,1)}, bf16[4096,512]{1,0:T(8,128)(2,1)}) custom-call(s32[3]{0:T(128)} %pad_add_fusion.s_ref, bf16[2304,4096]{1,0:T(8,128)(2,1)} %shard_map.149.a_ref, bf16[576,1024]{1,0:T(8,128)(2,1)} %copy-done.7, bf16[576,1024]{1,0:T(8,128)(2,1)} %collective-permute-done.12.w1, bf16[576,1024]{1,0:T(8,128)(2,1)} %collective-permute-done.13.w2, ...), custom_call_target="tpu_custom_call" | custom-call | flops 4831838208 | tf_op jit(solution)/shard_map/pallas_call | solution.py:537
  328.7 29.1 %shard_map.152.o_own = bf16[512,2048]{1,0:T(8,128)(2,1)} custom-call(s32[8]{0:T(128)} %get-tuple-element.34.lo_ref, s32[8]{0:T(128)} %get-tuple-element.33.full_ref, bf16[768,4096]{1,0:T(8,128)(2,1)} %get-tuple-element.21.q_ref.v_ref, bf16[4096,512]{1,0:T(8,128)(2,1)} %get-tuple-element.20.k_ref.kv0, bf16[768,4096]{1,0:T(8,128)(2,1)} %get-tuple-element.21.q_ref.v_ref, ...), custom_call_target="tpu_custom_call" | custom-call | flops 4294967296 | tf_op jit(solution)/shard_map/pallas_call | solution.py:558
  357.8 2.5 constant_dynamic-slice_fusion.11
  362.2 15.6 %shard_map.153.o_own = bf16[512,2048]{1,0:T(8,128)(2,1)} custom-call(s32[8]{0:T(128)} %get-tuple-element.34.lo_ref, s32[8]{0:T(128)} %get-tuple-element.33.full_ref, bf16[768,4096]{1,0:T(8,128)(2,1)} %get-tuple-element.21.q_ref.v_ref, bf16[4096,512]{1,0:T(8,128)(2,1)} %get-tuple-element.20.k_ref.kv0, bf16[768,4096]{1,0:T(8,128)(2,1)} %get-tuple-element.21.q_ref.v_ref, ...), custom_call_target="tpu_custom_call" | custom-call | flops 2147483648 | tf_op jit(solution)/shard_map/pallas_call | solution.py:558
  379.6 19.6 %collective-permute-done.18.o_y = bf16[512,512]{1,0:T(8,128)(2,1)} collective-permute-done((bf16[512,512]{1,0:T(8,128)(2,1)}, bf16[512,512]{1,0:T(8,128)(2,1)}, u32[]{:S(2)}, u32[]{:S(2)}) %collective-permute-start.18) | collective-permute-done | bytes 524320 | tf_op jit(solution)/shard_map/ppermute | solution.py:445
  400.7 8.8 collective-permute-done.19.o_yc
  411.9 9.8 %collective-permute-done.28.o_y = bf16[512,512]{1,0:T(8,128)(2,1)} collective-permute-done((bf16[512,512]{1,0:T(8,128)(2,1)S(1)}, bf16[512,512]{1,0:T(8,128)(2,1)}, u32[]{:S(2)}, u32[]{:S(2)}) %collective-permute-start.28) | collective-permute-done | bytes 524320 | tf_op jit(solution)/shard_map/ppermute | solution.py:445
  421.6 10.2 %collective-permute-done.29.o_yc = bf16[512,512]{1,0:T(8,128)(2,1)} collective-permute-done((bf16[512,512]{1,0:T(8,128)(2,1)S(1)}, bf16[512,512]{1,0:T(8,128)(2,1)}, u32[]{:S(2)}, u32[]{:S(2)}) %collective-permute-start.29) | collective-permute-done | bytes 524320 | tf_op jit(solution)/shard_map/ppermute | solution.py:445
  432.7 14.9 %shard_map.154 = (bf16[2304,512]{1,0:T(8,128)(2,1)}, bf16[1024,2304]{1,0:T(8,128)(2,1)}) custom-call(s32[3]{0:T(128)} %pad_add_fusion.s_ref, bf16[512,2048]{1,0:T(8,128)(2,1)} %shard_map.153.o_own, bf16[512,512]{1,0:T(8,128)(2,1)} %collective-permute-done.27.o_c, bf16[512,512]{1,0:T(8,128)(2,1)} %collective-permute-done.28.o_y, ...), custom_call_target="tpu_custom_call" | custom-call | flops 2415919104 | tf_op jit(solution)/shard_map/pallas_call | solution.py:573
  447.6 15.2 %shard_map.155 = (bf16[2304,512]{1,0:T(8,128)(2,1)}, bf16[1024,2304]{1,0:T(8,128)(2,1)}) custom-call(s32[3]{0:T(128)} %pad_add_fusion.s_ref, bf16[512,2048]{1,0:T(8,128)(2,1)} %shard_map.152.o_own, bf16[512,512]{1,0:T(8,128)(2,1)} %copy-done.11, bf16[512,512]{1,0:T(8,128)(2,1)} %collective-permute-done.18.o_y, ...), custom_call_target="tpu_custom_call", output_to_operand_aliasing={{1}: (18, {})} | custom-call | flops 2415919104 | tf_op jit(solution)/shard_map/pallas_call | solution.py:573
  464.8 24.3 %collective-permute-done.45.refs_2_.refs_6_ = bf16[576,2304]{1,0:T(8,128)(2,1)} collective-permute-done((bf16[576,2304]{1,0:T(8,128)(2,1)}, bf16[576,2304]{1,0:T(8,128)(2,1)}, u32[]{:S(2)}, u32[]{:S(2)}) %collective-permute-start.45) | collective-permute-done | bytes 2654240 | tf_op jit(solution)/shard_map/ppermute | solution.py:445
  491.1 26.1 %collective-permute-done.36.h_ref.hf1 = bf16[2304,512]{1,0:T(8,128)(2,1)} collective-permute-done((bf16[2304,512]{1,0:T(8,128)(2,1)}, bf16[2304,512]{1,0:T(8,128)(2,1)}, u32[]{:S(2)}, u32[]{:S(2)}) %collective-permute-start.36) | collective-permute-done | bytes 2359328 | tf_op jit(solution)/shard_map/ppermute | solution.py:445
  518.7 2.3 split.6
  521.0 3.9 split.7
  524.9 41.9 %collective-permute-done.37.h_ref.hf0 = bf16[2304,512]{1,0:T(8,128)(2,1)} collective-permute-done((bf16[2304,512]{1,0:T(8,128)(2,1)}, bf16[2304,512]{1,0:T(8,128)(2,1)}, u32[]{:S(2)}, u32[]{:S(2)}) %collective-permute-start.37) | collective-permute-done | bytes 2359328 | tf_op jit(solution)/shard_map/ppermute | solution.py:445
  566.8 30.2 %shard_map.156.zw = bf16[1024,2304]{1,0:T(8,128)(2,1)} custom-call(s32[3]{0:T(128)} %pad_add_fusion.s_ref, bf16[1024,2304]{1,0:T(8,128)(2,1)} %get-tuple-element.23.refs_0_, bf16[576,2304]{1,0:T(8,128)(2,1)} %pad_maximum_fusion.refs_1_.refs_5_, bf16[576,2304]{1,0:T(8,128)(2,1)} %collective-permute-done.30.refs_2_.refs_6_, ...), custom_call_target="tpu_custom_call" | custom-call | flops 21743271936 | tf_op jit(solution)/shard_map/pallas_call | solution.py:601
  597.0 5.7 shard_map.157.rest_0_
  602.7 5.7 shard_map.158.refs_0_.refs_1_
  612.0 30.7 %shard_map.159.zf = bf16[1024,2304]{1,0:T(8,128)(2,1)} custom-call(s32[3]{0:T(128)} %pad_add_fusion.s_ref, bf16[1024,2304]{1,0:T(8,128)(2,1)} %shard_map.158.refs_0_.refs_1_, bf16[576,2304]{1,0:T(8,128)(2,1)} %pad_maximum_fusion.refs_1_.refs_5_, bf16[576,2304]{1,0:T(8,128)(2,1)} %collective-permute-done.30.refs_2_.refs_6_, ...), custom_call_target="tpu_custom_call" | custom-call | flops 21743271936 | tf_op jit(solution)/shard_map/pallas_call | solution.py:601
  643.2 31.0 %shard_map.160.part = f32[8,2304,256]{2,1,0:T(8,128)} custom-call(s32[3]{0:T(128)} %pad_add_fusion.s_ref, bf16[1024,2304]{1,0:T(8,128)(2,1)} %shard_map.156.zw, bf16[1024,2304]{1,0:T(8,128)(2,1)} %shard_map.159.zf, bf16[576,2304]{1,0:T(8,128)(2,1)} %get-tuple-element.38.d0.dt, bf16[576,2304]{1,0:T(8,128)(2,1)} %collective-permute-done.38.d1, ...), custom_call_target="tpu_custom_call" | custom-call | flops 10871635968 | tf_op jit(solution)/shard_map/pallas_call | solution.py:616
  674.8 30.7 %shard_map.163.zb = bf16[2048,1152]{1,0:T(8,128)(2,1)} custom-call(s32[3]{0:T(128)} %pad_add_fusion.s_ref, bf16[1024,2304]{1,0:T(8,128)(2,1)} %get-tuple-element.23.refs_0_, bf16[1024,2304]{1,0:T(8,128)(2,1)} %shard_map.158.refs_0_.refs_1_, bf16[576,2304]{1,0:T(8,128)(2,1)} %collective-permute-done.45.refs_2_.refs_6_, ...), custom_call_target="tpu_custom_call" | custom-call | flops 21743271936 | tf_op jit(solution)/shard_map/pallas_call | solution.py:601
  706.0 17.5 %shard_map.161.zwa = bf16[1024,1152]{1,0:T(8,128)(2,1)} custom-call(s32[3]{0:T(128)} %pad_add_fusion.s_ref, bf16[1024,2304]{1,0:T(8,128)(2,1)} %get-tuple-element.23.refs_0_, bf16[576,2304]{1,0:T(8,128)(2,1)} %collective-permute-done.41.refs_1_.refs_5_, bf16[576,2304]{1,0:T(8,128)(2,1)} %collective-permute-done.42.refs_2_.refs_6_, ...), custom_call_target="tpu_custom_call" | custom-call | flops 10871635968 | tf_op jit(solution)/shard_map/pallas_call | solution.py:601
  723.5 17.3 %shard_map.162.zfa = bf16[1024,1152]{1,0:T(8,128)(2,1)} custom-call(s32[3]{0:T(128)} %pad_add_fusion.s_ref, bf16[1024,2304]{1,0:T(8,128)(2,1)} %shard_map.158.refs_0_.refs_1_, bf16[576,2304]{1,0:T(8,128)(2,1)} %collective-permute-done.41.refs_1_.refs_5_, bf16[576,2304]{1,0:T(8,128)(2,1)} %collective-permute-done.42.refs_2_.refs_6_, ...), custom_call_target="tpu_custom_call" | custom-call | flops 10871635968 | tf_op jit(solution)/shard_map/pallas_call | solution.py:601
  740.9 131.0 %tail.1.rest_0_ = bf16[576,8192]{1,0:T(8,128)(2,1)} custom-call(f32[8,2304,256]{2,1,0:T(8,128)} %shard_map.160.part, bf16[1024,1152]{1,0:T(8,128)(2,1)} %shard_map.161.zwa, bf16[1024,1152]{1,0:T(8,128)(2,1)} %shard_map.162.zfa, bf16[2048,1152]{1,0:T(8,128)(2,1)} %shard_map.163.zb, bf16[576,1792]{1,0:T(8,128)(2,1)} %collective-permute-done.49.d0, ...), custom_call_target="tpu_custom_call" | custom-call | flops 21743271936 | bytes 18874368 | tf_op jit(solution)/shard_map/tail/pallas_call | solution.py:620
  871.9 11.1 %shard_map.164 = (bf16[8192,2,256]{2,1,0:T(2,128)(2,1)}, bf16[8192,2,256]{2,1,0:T(2,128)(2,1)}) custom-call(s32[3]{0:T(128)} %pad_add_fusion.s_ref, bf16[4096,512]{1,0:T(8,128)(2,1)} %get-tuple-element.20.k_ref.kv0, bf16[4096,512]{1,0:T(8,128)(2,1)} %collective-permute-done.55.kv1), custom_call_target="tpu_custom_call" | custom-call | flops 4194304 | tf_op jit(solution)/shard_map/pallas_call | solution.py:643
  883.0 8.8 shard_map.165
  891.8 8.4 shard_map.166
  (157 shorter events, 56.2 us)
Async XLA Ops:
  4.0 91.9 %collective-permute-start.1 = (bf16[576,1024]{1,0:T(8,128)(2,1)}, bf16[576,1024]{1,0:T(8,128)(2,1)}, u32[]{:S(2)}, u32[]{:S(2)}) collective-permute-start(bf16[576,1024]{1,0:T(8,128)(2,1)} %get-tuple-element.36), channel_id=1, source_target_pairs={{0,2},{1,3},{2,0},{3,1},{4,6},{5,7},{6,4},{7,5}} | collective-permute-start | bytes 3538952 | tf_op jit(solution)/shard_map/ppermute | solution.py:445
  7.3 90.1 %collective-permute-start.8 = (bf16[576,1024]{1,0:T(8,128)(2,1)}, bf16[576,1024]{1,0:T(8,128)(2,1)S(1)}, u32[]{:S(2)}, u32[]{:S(2)}) collective-permute-start(bf16[576,1024]{1,0:T(8,128)(2,1)} %get-tuple-element.35), channel_id=1, source_target_pairs={{0,2},{1,3},{2,0},{3,1},{4,6},{5,7},{6,4},{7,5}} | collective-permute-start | bytes 3538952 | tf_op jit(solution)/shard_map/ppermute | solution.py:445
  12.4 86.2 %collective-permute-start.12 = (bf16[576,1024]{1,0:T(8,128)(2,1)}, bf16[576,1024]{1,0:T(8,128)(2,1)}, u32[]{:S(2)}, u32[]{:S(2)}) collective-permute-start(bf16[576,1024]{1,0:T(8,128)(2,1)} %pad_maximum_fusion.5), channel_id=1, source_target_pairs={{0,1},{1,0},{2,3},{3,2},{4,5},{5,4},{6,7},{7,6}} | collective-permute-start | bytes 3538952 | tf_op jit(solution)/shard_map/ppermute | solution.py:445
  12.9 86.4 %collective-permute-start.13 = (bf16[576,1024]{1,0:T(8,128)(2,1)S(1)}, bf16[576,1024]{1,0:T(8,128)(2,1)}, u32[]{:S(2)}, u32[]{:S(2)}) collective-permute-start(bf16[576,1024]{1,0:T(8,128)(2,1)S(1)} %pad_maximum_fusion.4.w0), channel_id=1, source_target_pairs={{0,2},{1,3},{2,0},{3,1},{4,6},{5,7},{6,4},{7,5}} | collective-permute-start | bytes 3538952 | tf_op jit(solution)/shard_map/ppermute | solution.py:445
  16.2 68.1 %collective-permute-start.6 = (bf16[4,576]{1,0:T(4,128)(2,1)S(1)}, bf16[4,576]{1,0:T(4,128)(2,1)S(1)}, u32[]{:S(2)}, u32[]{:S(2)}) collective-permute-start(bf16[4,576]{1,0:T(4,128)(2,1)S(1)} %pad_maximum_fusion.6), channel_id=1, source_target_pairs={{0,2},{1,3},{2,0},{3,1},{4,6},{5,7},{6,4},{7,5}} | collective-permute-start | bytes 13832 | tf_op jit(solution)/shard_map/ppermute | solution.py:445
  87.3 28.3 %collective-permute-start.14 = (bf16[576,1024]{1,0:T(8,128)(2,1)}, bf16[576,1024]{1,0:T(8,128)(2,1)}, u32[]{:S(2)}, u32[]{:S(2)}) collective-permute-start(bf16[576,1024]{1,0:T(8,128)(2,1)} %pad_maximum_fusion.5), channel_id=1, source_target_pairs={{0,3},{1,2},{2,1},{3,0},{4,7},{5,6},{6,5},{7,4}} | collective-permute-start | bytes 3538952 | tf_op jit(solution)/shard_map/ppermute | solution.py:445
  96.0 79.5 %collective-permute-start.49 = (bf16[576,1792]{1,0:T(8,128)(2,1)}, bf16[576,1792]{1,0:T(8,128)(2,1)}, u32[]{:S(2)}, u32[]{:S(2)}) collective-permute-start(bf16[576,1792]{1,0:T(8,128)(2,1)} %slice.14), channel_id=1, source_target_pairs={{0,4},{1,5},{2,6},{3,7},{4,0},{5,1},{6,2},{7,3}} | collective-permute-start | bytes 6193160 | tf_op jit(solution)/shard_map/ppermute | solution.py:445
  98.7 42.5 %collective-permute-start.21 = (bf16[4,576,256]{2,1,0:T(8,128)(2,1)}, bf16[4,576,256]{2,1,0:T(8,128)(2,1)}, u32[]{:S(2)}, u32[]{:S(2)}) collective-permute-start(bf16[4,576,256]{2,1,0:T(8,128)(2,1)} %bitcast.14.b0), channel_id=1, source_target_pairs={{0,2},{1,3},{2,0},{3,1},{4,6},{5,7},{6,4},{7,5}} | collective-permute-start | bytes 3538952 | tf_op jit(solution)/shard_map/ppermute | solution.py:445
  99.2 69.6 %collective-permute-start.23 = (bf16[4,576,256]{2,1,0:T(8,128)(2,1)}, bf16[4,576,256]{2,1,0:T(8,128)(2,1)}, u32[]{:S(2)}, u32[]{:S(2)}) collective-permute-start(bf16[4,576,256]{2,1,0:T(8,128)(2,1)} %bitcast.14.b0), channel_id=1, source_target_pairs={{0,4},{1,5},{2,6},{3,7},{4,0},{5,1},{6,2},{7,3}} | collective-permute-start | bytes 3538952 | tf_op jit(solution)/shard_map/ppermute | solution.py:445
  115.6 62.5 %collective-permute-start.2 = (bf16[576,1024]{1,0:T(8,128)(2,1)}, bf16[576,1024]{1,0:T(8,128)(2,1)}, u32[]{:S(2)}, u32[]{:S(2)}) collective-permute-start(bf16[576,1024]{1,0:T(8,128)(2,1)} %collective-permute-done.1.rx.x2), channel_id=1, source_target_pairs={{0,1},{1,0},{2,3},{3,2},{4,5},{5,4},{6,7},{7,6}} | collective-permute-start | bytes 3538952 | tf_op jit(solution)/shard_map/ppermute | solution.py:445
  123.7 70.4 %collective-permute-start.3 = (bf16[576,1024]{1,0:T(8,128)(2,1)}, bf16[576,1024]{1,0:T(8,128)(2,1)}, u32[]{:S(2)}, u32[]{:S(2)}) collective-permute-start(bf16[576,1024]{1,0:T(8,128)(2,1)} %collective-permute-done.1.rx.x2), channel_id=1, source_target_pairs={{0,4},{1,5},{2,6},{3,7},{4,0},{5,1},{6,2},{7,3}} | collective-permute-start | bytes 3538952 | tf_op jit(solution)/shard_map/ppermute | solution.py:445
  141.1 54.1 %collective-permute-start.9 = (bf16[576,1024]{1,0:T(8,128)(2,1)}, bf16[576,1024]{1,0:T(8,128)(2,1)}, u32[]{:S(2)}, u32[]{:S(2)}) collective-permute-start(bf16[576,1024]{1,0:T(8,128)(2,1)} %copy-done.6), channel_id=1, source_target_pairs={{0,1},{1,0},{2,3},{3,2},{4,5},{5,4},{6,7},{7,6}} | collective-permute-start | bytes 3538952 | tf_op jit(solution)/shard_map/ppermute | solution.py:445
  168.8 50.6 %collective-permute-start.10 = (bf16[576,1024]{1,0:T(8,128)(2,1)}, bf16[576,1024]{1,0:T(8,128)(2,1)}, u32[]{:S(2)}, u32[]{:S(2)}) collective-permute-start(bf16[576,1024]{1,0:T(8,128)(2,1)} %copy-done.6), channel_id=1, source_target_pairs={{0,4},{1,5},{2,6},{3,7},{4,0},{5,1},{6,2},{7,3}} | collective-permute-start | bytes 3538952 | tf_op jit(solution)/shard_map/ppermute | solution.py:445
  175.5 97.1 %collective-permute-start = (bf16[576,4096]{1,0:T(8,128)(2,1)}, bf16[576,4096]{1,0:T(8,128)(2,1)}, u32[]{:S(2)}, u32[]{:S(2)}) collective-permute-start(bf16[576,4096]{1,0:T(8,128)(2,1)} %dynamic-slice_bitcast_fusion), channel_id=1, source_target_pairs={{0,1},{1,0},{2,3},{3,2},{4,5},{5,4},{6,7},{7,6}} | collective-permute-start | bytes 14155784 | tf_op jit(solution)/shard_map/ppermute | solution.py:445
  178.0 42.0 %collective-permute-start.22 = (bf16[4,576,256]{2,1,0:T(8,128)(2,1)}, bf16[4,576,256]{2,1,0:T(8,128)(2,1)}, u32[]{:S(2)}, u32[]{:S(2)}) collective-permute-start(bf16[4,576,256]{2,1,0:T(8,128)(2,1)} %collective-permute-done.21.b1), channel_id=1, source_target_pairs={{0,1},{1,0},{2,3},{3,2},{4,5},{5,4},{6,7},{7,6}} | collective-permute-start | bytes 3538952 | tf_op jit(solution)/shard_map/ppermute | solution.py:445
  194.1 55.8 %collective-permute-start.30 = (bf16[576,2304]{1,0:T(8,128)(2,1)}, bf16[576,2304]{1,0:T(8,128)(2,1)}, u32[]{:S(2)}, u32[]{:S(2)}) collective-permute-start(bf16[576,2304]{1,0:T(8,128)(2,1)} %pad_maximum_fusion.refs_1_.refs_5_), channel_id=1, source_target_pairs={{0,1},{1,0},{2,3},{3,2},{4,5},{5,4},{6,7},{7,6}} | collective-permute-start | bytes 7962632 | tf_op jit(solution)/shard_map/ppermute | solution.py:445
  195.3 59.8 %collective-permute-start.31 = (bf16[576,2304]{1,0:T(8,128)(2,1)}, bf16[576,2304]{1,0:T(8,128)(2,1)}, u32[]{:S(2)}, u32[]{:S(2)}) collective-permute-start(bf16[576,2304]{1,0:T(8,128)(2,1)} %pad_maximum_fusion.1), channel_id=1, source_target_pairs={{0,2},{1,3},{2,0},{3,1},{4,6},{5,7},{6,4},{7,5}} | collective-permute-start | bytes 7962632 | tf_op jit(solution)/shard_map/ppermute | solution.py:445
  220.0 28.2 %collective-permute-start.25 = (bf16[4,576,256]{2,1,0:T(8,128)(2,1)}, bf16[4,576,256]{2,1,0:T(8,128)(2,1)}, u32[]{:S(2)}, u32[]{:S(2)}) collective-permute-start(bf16[4,576,256]{2,1,0:T(8,128)(2,1)} %collective-permute-done.21.b1), channel_id=1, source_target_pairs={{0,4},{1,5},{2,6},{3,7},{4,0},{5,1},{6,2},{7,3}} | collective-permute-start | bytes 3538952 | tf_op jit(solution)/shard_map/ppermute | solution.py:445
  222.8 33.5 %collective-permute-start.4 = (bf16[576,1024]{1,0:T(8,128)(2,1)}, bf16[576,1024]{1,0:T(8,128)(2,1)}, u32[]{:S(2)}, u32[]{:S(2)}) collective-permute-start(bf16[576,1024]{1,0:T(8,128)(2,1)} %collective-permute-done.3.ry), channel_id=1, source_target_pairs={{0,1},{1,0},{2,3},{3,2},{4,5},{5,4},{6,7},{7,6}} | collective-permute-start | bytes 3538952 | tf_op jit(solution)/shard_map/ppermute | solution.py:445
  248.2 78.9 %collective-permute-start.33 = (bf16[576,2304]{1,0:T(8,128)(2,1)}, bf16[576,2304]{1,0:T(8,128)(2,1)}, u32[]{:S(2)}, u32[]{:S(2)}) collective-permute-start(bf16[576,2304]{1,0:T(8,128)(2,1)} %pad_maximum_fusion.2.refs_9_.refs_13_), channel_id=1, source_target_pairs={{0,1},{1,0},{2,3},{3,2},{4,5},{5,4},{6,7},{7,6}} | collective-permute-start | bytes 7962632 | tf_op jit(solution)/shard_map/ppermute | solution.py:445
  249.9 110.4 %collective-permute-start.38 = (bf16[576,2304]{1,0:T(8,128)(2,1)}, bf16[576,2304]{1,0:T(8,128)(2,1)}, u32[]{:S(2)}, u32[]{:S(2)}) collective-permute-start(bf16[576,2304]{1,0:T(8,128)(2,1)} %get-tuple-element.38.d0.dt), channel_id=1, source_target_pairs={{0,1},{1,0},{2,3},{3,2},{4,5},{5,4},{6,7},{7,6}} | collective-permute-start | bytes 7962632 | tf_op jit(solution)/shard_map/ppermute | solution.py:445
  255.1 105.2 %collective-permute-start.34 = (bf16[576,2304]{1,0:T(8,128)(2,1)}, bf16[576,2304]{1,0:T(8,128)(2,1)}, u32[]{:S(2)}, u32[]{:S(2)}) collective-permute-start(bf16[576,2304]{1,0:T(8,128)(2,1)} %pad_maximum_fusion.3), channel_id=1, source_target_pairs={{0,2},{1,3},{2,0},{3,1},{4,6},{5,7},{6,4},{7,5}} | collective-permute-start | bytes 7962632 | tf_op jit(solution)/shard_map/ppermute | solution.py:445
  271.7 191.0 %collective-permute-start.39 = (bf16[576,2304]{1,0:T(8,128)(2,1)}, bf16[576,2304]{1,0:T(8,128)(2,1)}, u32[]{:S(2)}, u32[]{:S(2)}) collective-permute-start(bf16[576,2304]{1,0:T(8,128)(2,1)} %get-tuple-element.37), channel_id=1, source_target_pairs={{0,2},{1,3},{2,0},{3,1},{4,6},{5,7},{6,4},{7,5}} | collective-permute-start | bytes 7962632 | tf_op jit(solution)/shard_map/ppermute | solution.py:445
  272.5 88.3 %collective-permute-start.26 = (bf16[4,576,256]{2,1,0:T(8,128)(2,1)}, bf16[4,576,256]{2,1,0:T(8,128)(2,1)}, u32[]{:S(2)}, u32[]{:S(2)}) collective-permute-start(bf16[4,576,256]{2,1,0:T(8,128)(2,1)} %collective-permute-done.25.b3), channel_id=1, source_target_pairs={{0,1},{1,0},{2,3},{3,2},{4,5},{5,4},{6,7},{7,6}} | collective-permute-start | bytes 3538952 | tf_op jit(solution)/shard_map/ppermute | solution.py:445
  327.2 136.7 %collective-permute-start.41 = (bf16[576,2304]{1,0:T(8,128)(2,1)}, bf16[576,2304]{1,0:T(8,128)(2,1)}, u32[]{:S(2)}, u32[]{:S(2)}) collective-permute-start(bf16[576,2304]{1,0:T(8,128)(2,1)} %pad_maximum_fusion.refs_1_.refs_5_), channel_id=1, source_target_pairs={{0,4},{1,5},{2,6},{3,7},{4,0},{5,1},{6,2},{7,3}} | collective-permute-start | bytes 7962632 | tf_op jit(solution)/shard_map/ppermute | solution.py:445
  360.3 38.9 %collective-permute-start.18 = (bf16[512,512]{1,0:T(8,128)(2,1)}, bf16[512,512]{1,0:T(8,128)(2,1)}, u32[]{:S(2)}, u32[]{:S(2)}) collective-permute-start(bf16[512,512]{1,0:T(8,128)(2,1)} %get-tuple-element.51), channel_id=1, source_target_pairs={{0,4},{1,5},{2,6},{3,7},{4,0},{5,1},{6,2},{7,3}} | collective-permute-start | bytes 1572872 | tf_op jit(solution)/shard_map/ppermute | solution.py:445
  360.8 48.6 %collective-permute-start.19 = (bf16[512,512]{1,0:T(8,128)(2,1)}, bf16[512,512]{1,0:T(8,128)(2,1)}, u32[]{:S(2)}, u32[]{:S(2)}) collective-permute-start(bf16[512,512]{1,0:T(8,128)(2,1)} %get-tuple-element.50), channel_id=1, source_target_pairs={{0,5},{1,4},{2,7},{3,6},{4,1},{5,0},{6,3},{7,2}} | collective-permute-start | bytes 1572872 | tf_op jit(solution)/shard_map/ppermute | solution.py:445
  379.3 32.1 %collective-permute-start.27 = (bf16[512,512]{1,0:T(8,128)(2,1)S(1)}, bf16[512,512]{1,0:T(8,128)(2,1)}, u32[]{:S(2)}, u32[]{:S(2)}) collective-permute-start(bf16[512,512]{1,0:T(8,128)(2,1)S(1)} %get-tuple-element.49), channel_id=1, source_target_pairs={{0,1},{1,0},{2,3},{3,2},{4,5},{5,4},{6,7},{7,6}} | collective-permute-start | bytes 1572872 | tf_op jit(solution)/shard_map/ppermute | solution.py:445
  411.3 77.7 %collective-permute-start.45 = (bf16[576,2304]{1,0:T(8,128)(2,1)}, bf16[576,2304]{1,0:T(8,128)(2,1)}, u32[]{:S(2)}, u32[]{:S(2)}) collective-permute-start(bf16[576,2304]{1,0:T(8,128)(2,1)} %pad_maximum_fusion.2.refs_9_.refs_13_), channel_id=1, source_target_pairs={{0,4},{1,5},{2,6},{3,7},{4,0},{5,1},{6,2},{7,3}} | collective-permute-start | bytes 7962632 | tf_op jit(solution)/shard_map/ppermute | solution.py:445
  421.6 67.4 %collective-permute-start.32 = (bf16[576,2304]{1,0:T(8,128)(2,1)}, bf16[576,2304]{1,0:T(8,128)(2,1)}, u32[]{:S(2)}, u32[]{:S(2)}) collective-permute-start(bf16[576,2304]{1,0:T(8,128)(2,1)} %collective-permute-done.31.refs_3_.refs_7_), channel_id=1, source_target_pairs={{0,1},{1,0},{2,3},{3,2},{4,5},{5,4},{6,7},{7,6}} | collective-permute-start | bytes 7962632 | tf_op jit(solution)/shard_map/ppermute | solution.py:445
  431.8 57.8 %collective-permute-start.35 = (bf16[576,2304]{1,0:T(8,128)(2,1)}, bf16[576,2304]{1,0:T(8,128)(2,1)}, u32[]{:S(2)}, u32[]{:S(2)}) collective-permute-start(bf16[576,2304]{1,0:T(8,128)(2,1)} %collective-permute-done.34.refs_11_.refs_15_), channel_id=1, source_target_pairs={{0,1},{1,0},{2,3},{3,2},{4,5},{5,4},{6,7},{7,6}} | collective-permute-start | bytes 7962632 | tf_op jit(solution)/shard_map/ppermute | solution.py:445
  462.8 54.5 %collective-permute-start.36 = (bf16[2304,512]{1,0:T(8,128)(2,1)}, bf16[2304,512]{1,0:T(8,128)(2,1)}, u32[]{:S(2)}, u32[]{:S(2)}) collective-permute-start(bf16[2304,512]{1,0:T(8,128)(2,1)} %get-tuple-element.24.hw1), channel_id=1, source_target_pairs={{0,2},{1,3},{2,0},{3,1},{4,6},{5,7},{6,4},{7,5}} | collective-permute-start | bytes 7077896 | tf_op jit(solution)/shard_map/ppermute | solution.py:445
  463.9 102.9 %collective-permute-start.37 = (bf16[2304,512]{1,0:T(8,128)(2,1)}, bf16[2304,512]{1,0:T(8,128)(2,1)}, u32[]{:S(2)}, u32[]{:S(2)}) collective-permute-start(bf16[2304,512]{1,0:T(8,128)(2,1)} %get-tuple-element.25.hw0), channel_id=1, source_target_pairs={{0,2},{1,3},{2,0},{3,1},{4,6},{5,7},{6,4},{7,5}} | collective-permute-start | bytes 7077896 | tf_op jit(solution)/shard_map/ppermute | solution.py:445
  489.1 119.4 %collective-permute-start.40 = (bf16[576,2304]{1,0:T(8,128)(2,1)}, bf16[576,2304]{1,0:T(8,128)(2,1)}, u32[]{:S(2)}, u32[]{:S(2)}) collective-permute-start(bf16[576,2304]{1,0:T(8,128)(2,1)} %collective-permute-done.39.d2), channel_id=1, source_target_pairs={{0,1},{1,0},{2,3},{3,2},{4,5},{5,4},{6,7},{7,6}} | collective-permute-start | bytes 7962632 | tf_op jit(solution)/shard_map/ppermute | solution.py:445
  489.1 120.9 %collective-permute-start.42 = (bf16[576,2304]{1,0:T(8,128)(2,1)}, bf16[576,2304]{1,0:T(8,128)(2,1)}, u32[]{:S(2)}, u32[]{:S(2)}) collective-permute-start(bf16[576,2304]{1,0:T(8,128)(2,1)} %collective-permute-done.41.refs_1_.refs_5_), channel_id=1, source_target_pairs={{0,1},{1,0},{2,3},{3,2},{4,5},{5,4},{6,7},{7,6}} | collective-permute-start | bytes 7962632 | tf_op jit(solution)/shard_map/ppermute | solution.py:445
  489.6 121.8 %collective-permute-start.43 = (bf16[576,2304]{1,0:T(8,128)(2,1)}, bf16[576,2304]{1,0:T(8,128)(2,1)}, u32[]{:S(2)}, u32[]{:S(2)}) collective-permute-start(bf16[576,2304]{1,0:T(8,128)(2,1)} %collective-permute-done.31.refs_3_.refs_7_), channel_id=1, source_target_pairs={{0,4},{1,5},{2,6},{3,7},{4,0},{5,1},{6,2},{7,3}} | collective-permute-start | bytes 7962632 | tf_op jit(solution)/shard_map/ppermute | solution.py:445
  517.2 94.8 %collective-permute-start.47 = (bf16[576,2304]{1,0:T(8,128)(2,1)}, bf16[576,2304]{1,0:T(8,128)(2,1)}, u32[]{:S(2)}, u32[]{:S(2)}) collective-permute-start(bf16[576,2304]{1,0:T(8,128)(2,1)} %collective-permute-done.34.refs_11_.refs_15_), channel_id=1, source_target_pairs={{0,4},{1,5},{2,6},{3,7},{4,0},{5,1},{6,2},{7,3}} | collective-permute-start | bytes 7962632 | tf_op jit(solution)/shard_map/ppermute | solution.py:445
  566.8 75.9 %collective-permute-start.46 = (bf16[576,2304]{1,0:T(8,128)(2,1)}, bf16[576,2304]{1,0:T(8,128)(2,1)}, u32[]{:S(2)}, u32[]{:S(2)}) collective-permute-start(bf16[576,2304]{1,0:T(8,128)(2,1)} %collective-permute-done.45.refs_2_.refs_6_), channel_id=1, source_target_pairs={{0,1},{1,0},{2,3},{3,2},{4,5},{5,4},{6,7},{7,6}} | collective-permute-start | bytes 7962632 | tf_op jit(solution)/shard_map/ppermute | solution.py:445
  608.5 65.8 %collective-permute-start.51 = (bf16[576,2304]{1,0:T(8,128)(2,1)}, bf16[576,2304]{1,0:T(8,128)(2,1)}, u32[]{:S(2)}, u32[]{:S(2)}) collective-permute-start(bf16[576,2304]{1,0:T(8,128)(2,1)} %collective-permute-done.39.d2), channel_id=1, source_target_pairs={{0,4},{1,5},{2,6},{3,7},{4,0},{5,1},{6,2},{7,3}} | collective-permute-start | bytes 7962632 | tf_op jit(solution)/shard_map/ppermute | solution.py:445
  609.9 64.3 %collective-permute-start.15 = (bf16[1024,512]{1,0:T(8,128)(2,1)}, bf16[1024,512]{1,0:T(8,128)(2,1)}, u32[]{:S(2)}, u32[]{:S(2)}) collective-permute-start(bf16[1024,512]{1,0:T(8,128)(2,1)} %split.6), channel_id=1, source_target_pairs={{0,2},{1,3},{2,0},{3,1},{4,6},{5,7},{6,4},{7,5}} | collective-permute-start | bytes 3145736 | tf_op jit(solution)/shard_map/ppermute | solution.py:445
  611.3 94.1 %collective-permute-start.53 = (bf16[3072,512]{1,0:T(8,128)(2,1)}, bf16[3072,512]{1,0:T(8,128)(2,1)}, u32[]{:S(2)}, u32[]{:S(2)}) collective-permute-start(bf16[3072,512]{1,0:T(8,128)(2,1)} %split.7), channel_id=1, source_target_pairs={{0,2},{1,3},{2,0},{3,1},{4,6},{5,7},{6,4},{7,5}} | collective-permute-start | bytes 9437192 | tf_op jit(solution)/shard_map/ppermute | solution.py:445
  612.0 62.8 %collective-permute-start.48 = (bf16[576,2304]{1,0:T(8,128)(2,1)}, bf16[576,2304]{1,0:T(8,128)(2,1)}, u32[]{:S(2)}, u32[]{:S(2)}) collective-permute-start(bf16[576,2304]{1,0:T(8,128)(2,1)} %collective-permute-done.47.refs_4_.refs_8_), channel_id=1, source_target_pairs={{0,1},{1,0},{2,3},{3,2},{4,5},{5,4},{6,7},{7,6}} | collective-permute-start | bytes 7962632 | tf_op jit(solution)/shard_map/ppermute | solution.py:445
  642.7 63.3 %collective-permute-start.44 = (bf16[576,2304]{1,0:T(8,128)(2,1)}, bf16[576,2304]{1,0:T(8,128)(2,1)}, u32[]{:S(2)}, u32[]{:S(2)}) collective-permute-start(bf16[576,2304]{1,0:T(8,128)(2,1)} %collective-permute-done.43.refs_3_.refs_7_), channel_id=1, source_target_pairs={{0,1},{1,0},{2,3},{3,2},{4,5},{5,4},{6,7},{7,6}} | collective-permute-start | bytes 7962632 | tf_op jit(solution)/shard_map/ppermute | solution.py:445
  674.2 66.6 %collective-permute-start.50 = (bf16[576,1792]{1,0:T(8,128)(2,1)}, bf16[576,1792]{1,0:T(8,128)(2,1)}, u32[]{:S(2)}, u32[]{:S(2)}) collective-permute-start(bf16[576,1792]{1,0:T(8,128)(2,1)} %collective-permute-done.49.d0), channel_id=1, source_target_pairs={{0,1},{1,0},{2,3},{3,2},{4,5},{5,4},{6,7},{7,6}} | collective-permute-start | bytes 6193160 | tf_op jit(solution)/shard_map/ppermute | solution.py:445
  674.3 197.6 %collective-permute-start.55 = (bf16[4096,512]{1,0:T(8,128)(2,1)}, bf16[4096,512]{1,0:T(8,128)(2,1)}, u32[]{:S(2)}, u32[]{:S(2)}) collective-permute-start(bf16[4096,512]{1,0:T(8,128)(2,1)} %get-tuple-element.20.k_ref.kv0), channel_id=1, source_target_pairs={{0,1},{1,0},{2,3},{3,2},{4,5},{5,4},{6,7},{7,6}} | collective-permute-start | bytes 12582920 | tf_op jit(solution)/shard_map/ppermute | solution.py:445
  674.8 66.1 %collective-permute-start.52 = (bf16[576,2304]{1,0:T(8,128)(2,1)}, bf16[576,2304]{1,0:T(8,128)(2,1)}, u32[]{:S(2)}, u32[]{:S(2)}) collective-permute-start(bf16[576,2304]{1,0:T(8,128)(2,1)} %collective-permute-done.51.d2), channel_id=1, source_target_pairs={{0,1},{1,0},{2,3},{3,2},{4,5},{5,4},{6,7},{7,6}} | collective-permute-start | bytes 7962632 | tf_op jit(solution)/shard_map/ppermute | solution.py:445
  705.5 186.3 %collective-permute-start.16 = (bf16[1024,512]{1,0:T(8,128)(2,1)}, bf16[1024,512]{1,0:T(8,128)(2,1)}, u32[]{:S(2)}, u32[]{:S(2)}) collective-permute-start(bf16[1024,512]{1,0:T(8,128)(2,1)} %collective-permute-done.15.kv0), channel_id=1, source_target_pairs={{0,1},{1,0},{2,3},{3,2},{4,5},{5,4},{6,7},{7,6}} | collective-permute-start | bytes 3145736 | tf_op jit(solution)/shard_map/ppermute | solution.py:445
  706.0 177.0 %collective-permute-start.54 = (bf16[3072,512]{1,0:T(8,128)(2,1)}, bf16[3072,512]{1,0:T(8,128)(2,1)}, u32[]{:S(2)}, u32[]{:S(2)}) collective-permute-start(bf16[3072,512]{1,0:T(8,128)(2,1)} %collective-permute-done.53.kv0), channel_id=1, source_target_pairs={{0,1},{1,0},{2,3},{3,2},{4,5},{5,4},{6,7},{7,6}} | collective-permute-start | bytes 9437192 | tf_op jit(solution)/shard_map/ppermute | solution.py:445
  (25 other events, 682.6 us)

commit v4 on v3

--- a/solution.py
+++ b/solution.py
@@ -20,7 +20,7 @@
 BIG = 2.0 ** 40
 SHRINK = 2.0 ** -88
 MT = 256
-KT = 512
+KT = 256
 ANY = pl.BlockSpec(memory_space=pl.ANY)
 
 
@@ -239,18 +239,12 @@
         z_ref[r:r + MT, :] = (jax.nn.gelu(g, approximate=True) * u).astype(BF)
 
 
-def down_y_kernel(s_ref, zw, zf, d0, d1, d2, d3, acc_ref, d_ref):
+def down_y_kernel(s_ref, zw, zf, d0, d1, d2, d3, acc_ref):
     w4 = d0.shape[0]
     n = zw.shape[0]
-
-    @pl.when(pl.program_id(0) == 0)
-    def _():
-        for j, dd in enumerate((d0, d1, d2, d3)):
-            part_of(d_ref, j, w4)[...] = dd[...]
-
     z = vcat([zw[...], zf[...]])
-    for j in range(4):
-        t = dot_nt(d_ref[j * w4:(j + 1) * w4, :], z)
+    for j, dd in enumerate((d0, d1, d2, d3)):
+        t = dot_nt(dd[...], z)
         for q in range(n // CH):
             acc_ref[q, j * w4:(j + 1) * w4, :CH] = t[:, q * CH:(q + 1) * CH]
             acc_ref[q, j * w4:(j + 1) * w4, CH:] = t[:, n + q * CH:n + (q + 1) * CH]
@@ -308,24 +302,25 @@
     pl.semaphore_wait(bar, 4)
     dt_y.start()
 
-    def rs(p, i):
-        rws = slice(i * w4, (i + 1) * w4)
-        return remote(hi_ref.at[p, rws], rec_ref.at[p, rws], rs_s.at[p, i], rs_r.at[p, i], px)
-
-    def sq(p):
-        return remote(sqs_ref.at[p], sqr_ref.at[p], sq_s.at[p], sq_r.at[p], px)
-
-    def outs(p):
-        k, l = p // per, lax.rem(p, per)
-        res = []
-        for i, pr in enumerate((x, 1 - x)):
-            col = pl.multiple_of(((pr * 2 + k) * 4 + 2 * y + c) * (per * CH) + l * CH, CH)
-            mine = rec_ref.at[p, 0:w4, i * CH:(i + 1) * CH]
-            give = rec_ref.at[p, w4:w2, i * CH:(i + 1) * CH]
-            dst = out.at[:, pl.ds(col, CH)]
-            res.append((local(mine, dst, loc_sem.at[p, i]), remote(mine, dst, out_s.at[p, i, 0], out_r.at[p, i, 0], py),
-                        remote(give, dst, out_s.at[p, i, 1], out_r.at[p, i, 1], pyc), remote(give, dst, out_s.at[p, i, 2], out_r.at[p, i, 2], pc)))
-        return res
+    def lanes(q):
+        return pl.ds(pl.multiple_of(CH * (x + q - 2 * x * q), CH), CH)
+
+    def away(q):
+        return pl.ds(pl.multiple_of(CH - CH * (x + q - 2 * x * q), CH), CH)
+
+    def rs(p, q):
+        return remote(hi_ref.at[p, :, away(q)], rec_ref.at[p, :, away(q)], rs_s.at[p, q], rs_r.at[p, q], px)
+
+    def sq(p, q):
+        return remote(sqs_ref.at[p, q], sqr_ref.at[p, q], sq_s.at[p, q], sq_r.at[p, q], px)
+
+    def outs(p, q):
+        col = pl.multiple_of(((q * 2 + p // per) * 4 + 2 * y + c) * (per * CH) + lax.rem(p, per) * CH, CH)
+        mine = rec_ref.at[p, :w4, lanes(q)]
+        give = rec_ref.at[p, w4:, lanes(q)]
+        dst = out.at[:, pl.ds(col, CH)]
+        far = [remote(src, dst, out_s.at[p, q, i], out_r.at[p, q, i], dev) for i, (src, dev) in enumerate(((mine, py), (give, pyc), (give, pc)))]
+        return far + [local(mine, dst, loc_sem.at[p, q])]
 
     def block(p, j):
         return dot_nt(part_of(d_ref, j, w4)[...], z_ref[p]) + p_ref[lax.rem(p, 3), j * w4:(j + 1) * w4, :]
@@ -346,8 +341,6 @@
             t = block(p, 2 + i).astype(BF)
             hi_ref[p, i * w4:(i + 1) * w4, :CH] = t[:, CH:]
             hi_ref[p, i * w4:(i + 1) * w4, CH:] = t[:, :CH]
-            if first or i == 0:
-                rs(p, i).start()
 
     def lower(p, first=False):
         for j in range(2):
@@ -355,28 +348,26 @@
                 d_cp[j].wait()
             lo_ref[p, j * w4:(j + 1) * w4, :] = block(p, j)
 
-    def add(p):
-        for i in range(2):
-            rs(p, i).wait_recv()
-        t = (lo_ref[p] + rec_ref[p].astype(F32)).astype(BF)
-        rec_ref[p] = t
+    def add(p, q):
+        rs(p, q).wait_recv()
+        at = lanes(q)
+        t = (lo_ref[p, :, at] + rec_ref[p, :, at].astype(F32)).astype(BF)
+        rec_ref[p, :, at] = t
         t = t.astype(F32)
-        v = jnp.broadcast_to(jnp.sum(t * t, axis=0, keepdims=True), sqo_ref.shape)
-        sqo_ref[...] = v
-        sqs_ref[p, :, :CH] = v[:, CH:]
-        sqs_ref[p, :, CH:] = v[:, :CH]
-        sq(p).start()
-
-    def finish(p):
-        sq(p).wait_recv()
-        r = lax.rsqrt((sqo_ref[...] + sqr_ref[p]) / width + NORM_EPS)[0:1]
-        g = g_buf[:, 3:4]
-        rec_ref[p] = (h_ref[p].astype(F32) + rec_ref[p].astype(F32) * r * g).astype(BF)
-        for group in outs(p):
-            for cp in group[1:] + group[:1]:
-                cp.start()
+        v = jnp.broadcast_to(jnp.sum(t * t, axis=0, keepdims=True), (8, CH))
+        sqo_ref[q] = v
+        sqs_ref[p, q] = v
+        sq(p, q).start()
+
+    def finish(p, q):
+        sq(p, q).wait_recv()
+        at = lanes(q)
+        r = lax.rsqrt((sqo_ref[q] + sqr_ref[p, q]) / width + NORM_EPS)[0:1]
+        rec_ref[p, :, at] = (h_ref[p, :, at].astype(F32) + rec_ref[p, :, at].astype(F32) * r * g_buf[:, 3:4]).astype(BF)
+        start(outs(p, q))
 
     upper(0, True)
+    start([rs(0, 0), rs(0, 1)])
     start(d_cp[:2] + z_cp(1))
     upper(1)
     start([g_cp] + h_cp)
@@ -390,28 +381,36 @@
     for cp in [g_cp] + h_cp:
         cp.wait()
 
+    def steps(p, more):
+        for q in range(2):
+            add(p, q)
+            if more:
+                rs(p + 1, q).start()
+            if q:
+                finish(p, 0)
+            elif isinstance(p, int):
+                finish(p - 1, 1)
+            else:
+                @pl.when(p > 0)
+                def _():
+                    finish(p - 1, 1)
+            if not isinstance(p, int):
+                (lower if q else upper)(p + 2)
+
     def body(p, _):
-        add(p)
-        rs(p + 1, 1).start()
-        upper(p + 2)
-        finish(p)
-        lower(p + 2)
+        steps(p, True)
         return 0
 
     lax.fori_loop(0, chunks - 2, body, 0)
-    add(chunks - 2)
-    rs(chunks - 1, 1).start()
-    finish(chunks - 2)
-    add(chunks - 1)
-    finish(chunks - 1)
+    steps(chunks - 2, True)
+    steps(chunks - 1, False)
+    finish(chunks - 1, 1)
 
     def drain(p, _):
-        for i in range(2):
-            rs(p, i).wait_send()
-        sq(p).wait_send()
-        for group in outs(p):
-            group[0].wait()
-            for cp in group[1:]:
+        for q in range(2):
+            rs(p, q).wait_send()
+            sq(p, q).wait_send()
+            for cp in outs(p, q):
                 cp.wait()
         return 0
 
@@ -616,7 +615,7 @@
         part = call(
             down_y_kernel, (oh // yt,), [pl.BlockSpec((yt, F4), by_row)] * 2 + [whole(w4, F4)] * 4,
             pl.BlockSpec((2, D, yt), lambda i, s: (i, 0, 0)), f32(chunks, D, yt),
-            [vmem(D, F4)], flops=D * F4 * half)(scal, zy_own, zy_for, *dn_y)
+            flops=D * F4 * half)(scal, zy_own, zy_for, *dn_y)
         out = pl.pallas_call(
             functools.partial(tail_kernel, width=D, chunks=chunks),
             out_shape=bf(w4, rows),
@@ -624,8 +623,8 @@
             out_specs=ANY,
             scratch_shapes=[
                 vmem(D, F4), vmem(chunks, yt, F4), vmem(w2, 4, dtype=F32), vmem(3, D, yt, dtype=F32), vmem(chunks, w2, yt, dtype=F32),
-                *[vmem(chunks, w2, yt)] * 3, *[vmem(chunks, 8, yt, dtype=F32)] * 2, vmem(8, yt, dtype=F32),
-                dma((5,)), dma((chunks, 4)), dma((3,)), *[dma((chunks, 2))] * 4, *[dma((chunks,))] * 2, *[dma((2,))] * 2, *[dma((chunks, 2, 3))] * 2],
+                *[vmem(chunks, w2, yt)] * 3, *[vmem(chunks, 2, 8, CH, dtype=F32)] * 2, vmem(2, 8, CH, dtype=F32),
+                dma((5,)), dma((chunks, 4)), dma((3,)), *[dma((chunks, 2))] * 6, *[dma((2,))] * 2, *[dma((chunks, 2, 3))] * 2],
             cost_estimate=pl.CostEstimate(flops=D * F4 * S, bytes_accessed=D * rows, transcendentals=0),
             compiler_params=pltpu.CompilerParams(vmem_limit_bytes=VM, collective_id=0, has_side_effects=True),
             name='tail',
@@ -634,10 +633,12 @@
         kv_sets = jnp.split(kv, [S - oh])
         kv_x = [send(t, PX) for t in kv_sets]
         kv_xc = [send(kv_x[k], PC) for k in sets]
-        kv_spec = pl.BlockSpec((tile, gw), by_row)
         kv_outs = []
-        for i, (t, tc, n, base) in enumerate(((kv, kv_c, nb, 0), (kv_x[0], kv_xc[0], nb - per_half, 0), (kv_x[1], kv_xc[1], per_half, nb - per_half))):
-            extra = i == 2
+        most = nb - per_half
+        for i, (t, tc, base, last) in enumerate(((kv, kv_c, 0, nb), (kv_x[0], kv_xc[0], 0, most // 2), (kv_x[0], kv_xc[0], most // 2, most), (kv_x[1], kv_xc[1], most, nb))):
+            extra = i == 3
+            n = last - base
+            kv_spec = pl.BlockSpec((tile, gw), lambda j, s, at=0 if extra else base: (at + j, 0))
             at = lambda j, s, i=i, base=base: ((1 - s[0] if i else s[0]) * nb + base + j, 0, 0)
             cspec = [cols(w4, rows // n, lambda i, s: i)] * extra
             kv_outs = call(

time: 908 us -> 901 us (level)
  waiting for transfers between devices: 334 us -> 322 us
  local copies, waits for them, and re-layouts: 43.2 us -> 52.5 us
    ppermute x56, waiting for transfers between devices: 334 us -> 322 us  [send(): return lax.ppermute(a, ('tp', 'dm'), perm)]
    pallas_call x3 -> x4, Pallas kernels: 28.2 us -> 30.9 us  [layer(): call(functools.partial(kv_out_kernel, extra=int(extra)), (n,), [kv_spec]...]
  transfers between devices with their start and end apart: 56 -> 56, of which waited for: 18 -> 14; matrix products, arithmetic and copies ran while one was open for 6% -> 7% of each run, Pallas kernels for 51% -> 51%
where the time goes in v4:
time: 901 us; the launch traced here: 893 us
  Pallas kernels  464 us (51%)
  waiting for transfers between devices  322 us (36%)
  local copies, waits for them, and re-layouts  52.5 us (6%)
  starting transfers between devices  41.4 us (5%)
  other arithmetic  12 us (1%)
    ppermute x56, waiting for transfers between devices, send(): return lax.ppermute(a, ('tp', 'dm'), perm)  322 us
    pallas_call x1, Pallas kernels, layer(): pl.pallas_call(functools.partial(tail_kernel, width=D, chunks=chunks), ou...  127 us
    pallas_call x5, Pallas kernels, gated(): call(functools.partial(gate_up_kernel, groups=groups, sets=sets, steps=nf...  126 us
    pallas_call x2, Pallas kernels, layer(): call(functools.partial(attn_kernel, bq=bq, bk=bk, q_block0=q0, scale=scal...  44.7 us
    ppermute x56, starting transfers between devices, send(): return lax.ppermute(a, ('tp', 'dm'), perm)  41.4 us
    dynamic_slice x9, local copies, waits for them, and re-layouts, take(): return lax.dynamic_slice_in_dim(a, start, size, axis)  32.7 us
    pallas_call x4, Pallas kernels, layer(): call(functools.partial(kv_out_kernel, extra=int(extra)), (n,), [kv_spec]...  30.9 us
    pallas_call x1, Pallas kernels, layer(): call(down_y_kernel, (oh // yt,), [pl.BlockSpec((yt, F4), by_row)] * 2 + [...  30.3 us
  transfers between devices with their start and end apart: 56, of which 14 were waited for; matrix products, arithmetic and copies ran while one was open for 7% of the time, Pallas kernels for 51%

profile of v4, /device:TPU:0, one launch (start us, length us, event | category | flops | bytes accessed | tf_op | source)
XLA Modules:
  0.0 892.9 jit_solution(6511887678817096099)
XLA Ops:
  4.3 2.5 collective-permute-start.6
  6.9 3.2 dynamic-slice_bitcast_fusion.3
  12.1 4.8 constant_dynamic-slice_fusion.15
  18.8 2.9 constant_dynamic-slice_fusion.17
  26.1 13.2 %collective-permute-done.1.rx.x2 = bf16[576,1024]{1,0:T(8,128)(2,1)} collective-permute-done((bf16[576,1024]{1,0:T(8,128)(2,1)}, bf16[576,1024]{1,0:T(8,128)(2,1)}, u32[]{:S(2)}, u32[]{:S(2)}) %collective-permute-start.1) | collective-permute-done | bytes 1179680 | tf_op jit(solution)/shard_map/ppermute | solution.py:444
  39.3 25.2 %collective-permute-done.8.rx.x2 = bf16[576,1024]{1,0:T(8,128)(2,1)S(1)} collective-permute-done((bf16[576,1024]{1,0:T(8,128)(2,1)}, bf16[576,1024]{1,0:T(8,128)(2,1)S(1)}, u32[]{:S(2)}, u32[]{:S(2)}) %collective-permute-start.8) | collective-permute-done | bytes 1179680 | tf_op jit(solution)/shard_map/ppermute | solution.py:444
  67.7 22.1 %collective-permute-done.13.w2 = bf16[576,1024]{1,0:T(8,128)(2,1)} collective-permute-done((bf16[576,1024]{1,0:T(8,128)(2,1)S(1)}, bf16[576,1024]{1,0:T(8,128)(2,1)}, u32[]{:S(2)}, u32[]{:S(2)}) %collective-permute-start.13) | collective-permute-done | bytes 1179680 | tf_op jit(solution)/shard_map/ppermute | solution.py:444
  89.8 24.5 %collective-permute-done.14.w3 = bf16[576,1024]{1,0:T(8,128)(2,1)} collective-permute-done((bf16[576,1024]{1,0:T(8,128)(2,1)}, bf16[576,1024]{1,0:T(8,128)(2,1)}, u32[]{:S(2)}, u32[]{:S(2)}) %collective-permute-start.14) | collective-permute-done | bytes 1179680 | tf_op jit(solution)/shard_map/ppermute | solution.py:444
  115.9 7.4 constant_dynamic-slice_fusion
  123.8 5.1 dynamic-slice_bitcast_fusion
  128.9 10.8 %collective-permute-done.21.b1 = bf16[4,576,256]{2,1,0:T(8,128)(2,1)} collective-permute-done((bf16[4,576,256]{2,1,0:T(8,128)(2,1)}, bf16[4,576,256]{2,1,0:T(8,128)(2,1)}, u32[]{:S(2)}, u32[]{:S(2)}) %collective-permute-start.21) | collective-permute-done | bytes 1179680 | tf_op jit(solution)/shard_map/ppermute | solution.py:444
  142.0 5.2 dynamic-slice_bitcast_fusion.1
  147.2 3.5 slice.14
  155.2 13.6 %collective-permute-done.10.ry = bf16[576,1024]{1,0:T(8,128)(2,1)} collective-permute-done((bf16[576,1024]{1,0:T(8,128)(2,1)S(1)}, bf16[576,1024]{1,0:T(8,128)(2,1)}, u32[]{:S(2)}, u32[]{:S(2)}) %collective-permute-start.10) | collective-permute-done | bytes 1179680 | tf_op jit(solution)/shard_map/ppermute | solution.py:444
  172.0 72.3 %collective-permute-done.25.b3 = bf16[4,576,256]{2,1,0:T(8,128)(2,1)} collective-permute-done((bf16[4,576,256]{2,1,0:T(8,128)(2,1)}, bf16[4,576,256]{2,1,0:T(8,128)(2,1)}, u32[]{:S(2)}, u32[]{:S(2)}) %collective-permute-start.25) | collective-permute-done | bytes 1179680 | tf_op jit(solution)/shard_map/ppermute | solution.py:444
  244.3 3.5 pad_maximum_fusion.2.refs_9_.refs_13_
  252.0 2.0 copy.56.pk_ref
  255.3 10.9 %shard_map.150 = (f32[128,4096]{1,0:T(8,128)}, f32[128,4096]{1,0:T(8,128)}) custom-call(s32[3]{0:T(128)} %pad_add_fusion.s_ref, s32[1,4096]{1,0:T(1,128)} %copy-done.12, f32[128,1]{1,0:T(8,128)} %multiply_power_fusion.freq_ref), custom_call_target="tpu_custom_call" | custom-call | flops 8388608 | tf_op jit(solution)/shard_map/pallas_call | solution.py:526
  269.0 11.7 %shard_map.148.rest_0_ = bf16[2304,4096]{1,0:T(8,128)(2,1)} custom-call(s32[3]{0:T(128)} %pad_add_fusion.s_ref, bf16[576,8192]{1,0:T(8,128)(2,1)} %bitcast.36, bf16[576,4096]{1,0:T(8,128)(2,1)} %collective-permute-done.own_c.x1, bf16[576,1024]{1,0:T(8,128)(2,1)} %copy-done.6, bf16[576,1024]{1,0:T(8,128)(2,1)} %copy-done.8, ...), custom_call_target="tpu_custom_call" | custom-call | flops 9437184 | tf_op jit(solution)/shard_map/pallas_call | solution.py:531
  280.7 11.7 %shard_map.149.a_ref = bf16[2304,4096]{1,0:T(8,128)(2,1)} custom-call(s32[3]{0:T(128)} %pad_add_fusion.s_ref, bf16[576,8192]{1,0:T(8,128)(2,1)} %bitcast.37, bf16[576,4096]{1,0:T(8,128)(2,1)} %collective-permute-done.own_c.x1, bf16[576,1024]{1,0:T(8,128)(2,1)} %collective-permute-done.1.rx.x2, ...), custom_call_target="tpu_custom_call", output_to_operand_aliasing={{}: (8, {})} | custom-call | flops 9437184 | tf_op jit(solution)/shard_map/pallas_call | solution.py:531
  292.4 29.3 %shard_map.151 = (bf16[768,4096]{1,0:T(8,128)(2,1)}, bf16[4096,512]{1,0:T(8,128)(2,1)}) custom-call(s32[3]{0:T(128)} %pad_add_fusion.s_ref, bf16[2304,4096]{1,0:T(8,128)(2,1)} %shard_map.149.a_ref, bf16[576,1024]{1,0:T(8,128)(2,1)} %copy-done.9, bf16[576,1024]{1,0:T(8,128)(2,1)} %collective-permute-done.12.w1, bf16[576,1024]{1,0:T(8,128)(2,1)} %collective-permute-done.13.w2, ...), custom_call_target="tpu_custom_call" | custom-call | flops 4831838208 | tf_op jit(solution)/shard_map/pallas_call | solution.py:536
  323.5 29.1 %shard_map.152.o_own = bf16[512,2048]{1,0:T(8,128)(2,1)} custom-call(s32[8]{0:T(128)} %get-tuple-element.38.lo_ref, s32[8]{0:T(128)} %get-tuple-element.37.full_ref, bf16[768,4096]{1,0:T(8,128)(2,1)} %get-tuple-element.23.q_ref.v_ref, bf16[4096,512]{1,0:T(8,128)(2,1)} %get-tuple-element.22.k_ref.kv0, bf16[768,4096]{1,0:T(8,128)(2,1)} %get-tuple-element.23.q_ref.v_ref, ...), custom_call_target="tpu_custom_call" | custom-call | flops 4294967296 | tf_op jit(solution)/shard_map/pallas_call | solution.py:557
  352.5 2.5 constant_dynamic-slice_fusion.11
  356.9 15.6 %shard_map.153.o_own = bf16[512,2048]{1,0:T(8,128)(2,1)} custom-call(s32[8]{0:T(128)} %get-tuple-element.38.lo_ref, s32[8]{0:T(128)} %get-tuple-element.37.full_ref, bf16[768,4096]{1,0:T(8,128)(2,1)} %get-tuple-element.23.q_ref.v_ref, bf16[4096,512]{1,0:T(8,128)(2,1)} %get-tuple-element.22.k_ref.kv0, bf16[768,4096]{1,0:T(8,128)(2,1)} %get-tuple-element.23.q_ref.v_ref, ...), custom_call_target="tpu_custom_call" | custom-call | flops 2147483648 | tf_op jit(solution)/shard_map/pallas_call | solution.py:557
  374.6 19.2 %collective-permute-done.18.o_y = bf16[512,512]{1,0:T(8,128)(2,1)} collective-permute-done((bf16[512,512]{1,0:T(8,128)(2,1)}, bf16[512,512]{1,0:T(8,128)(2,1)}, u32[]{:S(2)}, u32[]{:S(2)}) %collective-permute-start.18) | collective-permute-done | bytes 524320 | tf_op jit(solution)/shard_map/ppermute | solution.py:444
  395.4 8.8 collective-permute-done.19.o_yc
  406.4 9.8 %collective-permute-done.28.o_y = bf16[512,512]{1,0:T(8,128)(2,1)} collective-permute-done((bf16[512,512]{1,0:T(8,128)(2,1)S(1)}, bf16[512,512]{1,0:T(8,128)(2,1)}, u32[]{:S(2)}, u32[]{:S(2)}) %collective-permute-start.28) | collective-permute-done | bytes 524320 | tf_op jit(solution)/shard_map/ppermute | solution.py:444
  416.2 10.4 %collective-permute-done.29.o_yc = bf16[512,512]{1,0:T(8,128)(2,1)} collective-permute-done((bf16[512,512]{1,0:T(8,128)(2,1)S(1)}, bf16[512,512]{1,0:T(8,128)(2,1)}, u32[]{:S(2)}, u32[]{:S(2)}) %collective-permute-start.29) | collective-permute-done | bytes 524320 | tf_op jit(solution)/shard_map/ppermute | solution.py:444
  427.2 14.9 %shard_map.154 = (bf16[2304,512]{1,0:T(8,128)(2,1)}, bf16[1024,2304]{1,0:T(8,128)(2,1)}) custom-call(s32[3]{0:T(128)} %pad_add_fusion.s_ref, bf16[512,2048]{1,0:T(8,128)(2,1)} %shard_map.153.o_own, bf16[512,512]{1,0:T(8,128)(2,1)} %collective-permute-done.27.o_c, bf16[512,512]{1,0:T(8,128)(2,1)} %collective-permute-done.28.o_y, ...), custom_call_target="tpu_custom_call" | custom-call | flops 2415919104 | tf_op jit(solution)/shard_map/pallas_call | solution.py:572
  442.1 15.1 %shard_map.155 = (bf16[2304,512]{1,0:T(8,128)(2,1)}, bf16[1024,2304]{1,0:T(8,128)(2,1)}) custom-call(s32[3]{0:T(128)} %pad_add_fusion.s_ref, bf16[512,2048]{1,0:T(8,128)(2,1)} %shard_map.152.o_own, bf16[512,512]{1,0:T(8,128)(2,1)} %copy-done.11, bf16[512,512]{1,0:T(8,128)(2,1)} %collective-permute-done.18.o_y, ...), custom_call_target="tpu_custom_call", output_to_operand_aliasing={{1}: (18, {})} | custom-call | flops 2415919104 | tf_op jit(solution)/shard_map/pallas_call | solution.py:572
  459.3 24.5 %collective-permute-done.45.refs_2_.refs_6_ = bf16[576,2304]{1,0:T(8,128)(2,1)} collective-permute-done((bf16[576,2304]{1,0:T(8,128)(2,1)}, bf16[576,2304]{1,0:T(8,128)(2,1)}, u32[]{:S(2)}, u32[]{:S(2)}) %collective-permute-start.45) | collective-permute-done | bytes 2654240 | tf_op jit(solution)/shard_map/ppermute | solution.py:444
  486.1 25.6 %collective-permute-done.36.h_ref.hf1 = bf16[2304,512]{1,0:T(8,128)(2,1)} collective-permute-done((bf16[2304,512]{1,0:T(8,128)(2,1)}, bf16[2304,512]{1,0:T(8,128)(2,1)}, u32[]{:S(2)}, u32[]{:S(2)}) %collective-permute-start.36) | collective-permute-done | bytes 2359328 | tf_op jit(solution)/shard_map/ppermute | solution.py:444
  513.4 2.3 split.6
  515.7 3.8 split.7
  519.6 41.7 %collective-permute-done.37.h_ref.hf0 = bf16[2304,512]{1,0:T(8,128)(2,1)} collective-permute-done((bf16[2304,512]{1,0:T(8,128)(2,1)}, bf16[2304,512]{1,0:T(8,128)(2,1)}, u32[]{:S(2)}, u32[]{:S(2)}) %collective-permute-start.37) | collective-permute-done | bytes 2359328 | tf_op jit(solution)/shard_map/ppermute | solution.py:444
  561.3 30.2 %shard_map.156.zw = bf16[1024,2304]{1,0:T(8,128)(2,1)} custom-call(s32[3]{0:T(128)} %pad_add_fusion.s_ref, bf16[1024,2304]{1,0:T(8,128)(2,1)} %get-tuple-element.25.refs_0_, bf16[576,2304]{1,0:T(8,128)(2,1)} %pad_maximum_fusion.refs_1_.refs_5_, bf16[576,2304]{1,0:T(8,128)(2,1)} %collective-permute-done.30.refs_2_.refs_6_, ...), custom_call_target="tpu_custom_call" | custom-call | flops 21743271936 | tf_op jit(solution)/shard_map/pallas_call | solution.py:600
  591.5 5.7 shard_map.157.rest_0_
  597.2 5.7 shard_map.158.refs_0_.refs_1_
  606.7 30.7 %shard_map.159.zf = bf16[1024,2304]{1,0:T(8,128)(2,1)} custom-call(s32[3]{0:T(128)} %pad_add_fusion.s_ref, bf16[1024,2304]{1,0:T(8,128)(2,1)} %shard_map.158.refs_0_.refs_1_, bf16[576,2304]{1,0:T(8,128)(2,1)} %pad_maximum_fusion.refs_1_.refs_5_, bf16[576,2304]{1,0:T(8,128)(2,1)} %collective-permute-done.30.refs_2_.refs_6_, ...), custom_call_target="tpu_custom_call" | custom-call | flops 21743271936 | tf_op jit(solution)/shard_map/pallas_call | solution.py:600
  638.0 30.3 %shard_map.160.part = f32[8,2304,256]{2,1,0:T(8,128)} custom-call(s32[3]{0:T(128)} %pad_add_fusion.s_ref, bf16[1024,2304]{1,0:T(8,128)(2,1)} %shard_map.156.zw, bf16[1024,2304]{1,0:T(8,128)(2,1)} %shard_map.159.zf, bf16[576,2304]{1,0:T(8,128)(2,1)} %get-tuple-element.42.d0.dt, bf16[576,2304]{1,0:T(8,128)(2,1)} %collective-permute-done.38.d1, ...), custom_call_target="tpu_custom_call" | custom-call | flops 10871635968 | tf_op jit(solution)/shard_map/pallas_call | solution.py:615
  668.9 30.7 %shard_map.163.zb = bf16[2048,1152]{1,0:T(8,128)(2,1)} custom-call(s32[3]{0:T(128)} %pad_add_fusion.s_ref, bf16[1024,2304]{1,0:T(8,128)(2,1)} %get-tuple-element.25.refs_0_, bf16[1024,2304]{1,0:T(8,128)(2,1)} %shard_map.158.refs_0_.refs_1_, bf16[576,2304]{1,0:T(8,128)(2,1)} %collective-permute-done.45.refs_2_.refs_6_, ...), custom_call_target="tpu_custom_call" | custom-call | flops 21743271936 | tf_op jit(solution)/shard_map/pallas_call | solution.py:600
  700.1 17.5 %shard_map.161.zwa = bf16[1024,1152]{1,0:T(8,128)(2,1)} custom-call(s32[3]{0:T(128)} %pad_add_fusion.s_ref, bf16[1024,2304]{1,0:T(8,128)(2,1)} %get-tuple-element.25.refs_0_, bf16[576,2304]{1,0:T(8,128)(2,1)} %collective-permute-done.41.refs_1_.refs_5_, bf16[576,2304]{1,0:T(8,128)(2,1)} %collective-permute-done.42.refs_2_.refs_6_, ...), custom_call_target="tpu_custom_call" | custom-call | flops 10871635968 | tf_op jit(solution)/shard_map/pallas_call | solution.py:600
  717.6 17.3 %shard_map.162.zfa = bf16[1024,1152]{1,0:T(8,128)(2,1)} custom-call(s32[3]{0:T(128)} %pad_add_fusion.s_ref, bf16[1024,2304]{1,0:T(8,128)(2,1)} %shard_map.158.refs_0_.refs_1_, bf16[576,2304]{1,0:T(8,128)(2,1)} %collective-permute-done.41.refs_1_.refs_5_, bf16[576,2304]{1,0:T(8,128)(2,1)} %collective-permute-done.42.refs_2_.refs_6_, ...), custom_call_target="tpu_custom_call" | custom-call | flops 10871635968 | tf_op jit(solution)/shard_map/pallas_call | solution.py:600
  734.9 126.8 %tail.1.rest_0_ = bf16[576,8192]{1,0:T(8,128)(2,1)} custom-call(f32[8,2304,256]{2,1,0:T(8,128)} %shard_map.160.part, bf16[1024,1152]{1,0:T(8,128)(2,1)} %shard_map.161.zwa, bf16[1024,1152]{1,0:T(8,128)(2,1)} %shard_map.162.zfa, bf16[2048,1152]{1,0:T(8,128)(2,1)} %shard_map.163.zb, bf16[576,2048]{1,0:T(8,128)(2,1)} %collective-permute-done.49.d0, ...), custom_call_target="tpu_custom_call" | custom-call | flops 21743271936 | bytes 18874368 | tf_op jit(solution)/shard_map/tail/pallas_call | solution.py:619
  861.7 11.1 %shard_map.164 = (bf16[8192,2,256]{2,1,0:T(2,128)(2,1)}, bf16[8192,2,256]{2,1,0:T(2,128)(2,1)}) custom-call(s32[3]{0:T(128)} %pad_add_fusion.s_ref, bf16[4096,512]{1,0:T(8,128)(2,1)} %get-tuple-element.22.k_ref.kv0, bf16[4096,512]{1,0:T(8,128)(2,1)} %collective-permute-done.55.kv1), custom_call_target="tpu_custom_call" | custom-call | flops 4194304 | tf_op jit(solution)/shard_map/pallas_call | solution.py:644
  872.8 5.7 shard_map.165
  878.5 5.7 shard_map.166
  884.2 8.4 shard_map.167
  (150 shorter events, 57.2 us)
Async XLA Ops:
  10.1 29.2 %collective-permute-start.1 = (bf16[576,1024]{1,0:T(8,128)(2,1)}, bf16[576,1024]{1,0:T(8,128)(2,1)}, u32[]{:S(2)}, u32[]{:S(2)}) collective-permute-start(bf16[576,1024]{1,0:T(8,128)(2,1)} %get-tuple-element.40), channel_id=1, source_target_pairs={{0,2},{1,3},{2,0},{3,1},{4,6},{5,7},{6,4},{7,5}} | collective-permute-start | bytes 3538952 | tf_op jit(solution)/shard_map/ppermute | solution.py:444
  11.8 52.6 %collective-permute-start.8 = (bf16[576,1024]{1,0:T(8,128)(2,1)}, bf16[576,1024]{1,0:T(8,128)(2,1)S(1)}, u32[]{:S(2)}, u32[]{:S(2)}) collective-permute-start(bf16[576,1024]{1,0:T(8,128)(2,1)} %get-tuple-element.39), channel_id=1, source_target_pairs={{0,2},{1,3},{2,0},{3,1},{4,6},{5,7},{6,4},{7,5}} | collective-permute-start | bytes 3538952 | tf_op jit(solution)/shard_map/ppermute | solution.py:444
  24.2 42.0 %collective-permute-start.12 = (bf16[576,1024]{1,0:T(8,128)(2,1)}, bf16[576,1024]{1,0:T(8,128)(2,1)}, u32[]{:S(2)}, u32[]{:S(2)}) collective-permute-start(bf16[576,1024]{1,0:T(8,128)(2,1)} %pad_maximum_fusion.5), channel_id=1, source_target_pairs={{0,1},{1,0},{2,3},{3,2},{4,5},{5,4},{6,7},{7,6}} | collective-permute-start | bytes 3538952 | tf_op jit(solution)/shard_map/ppermute | solution.py:444
  24.2 65.6 %collective-permute-start.13 = (bf16[576,1024]{1,0:T(8,128)(2,1)S(1)}, bf16[576,1024]{1,0:T(8,128)(2,1)}, u32[]{:S(2)}, u32[]{:S(2)}) collective-permute-start(bf16[576,1024]{1,0:T(8,128)(2,1)S(1)} %pad_maximum_fusion.4.w0), channel_id=1, source_target_pairs={{0,2},{1,3},{2,0},{3,1},{4,6},{5,7},{6,4},{7,5}} | collective-permute-start | bytes 3538952 | tf_op jit(solution)/shard_map/ppermute | solution.py:444
  26.0 88.4 %collective-permute-start.14 = (bf16[576,1024]{1,0:T(8,128)(2,1)}, bf16[576,1024]{1,0:T(8,128)(2,1)}, u32[]{:S(2)}, u32[]{:S(2)}) collective-permute-start(bf16[576,1024]{1,0:T(8,128)(2,1)} %pad_maximum_fusion.5), channel_id=1, source_target_pairs={{0,3},{1,2},{2,1},{3,0},{4,7},{5,6},{6,5},{7,4}} | collective-permute-start | bytes 3538952 | tf_op jit(solution)/shard_map/ppermute | solution.py:444
  39.3 84.0 %collective-permute-start.20 = (bf16[4,576,256]{2,1,0:T(8,128)(2,1)}, bf16[4,576,256]{2,1,0:T(8,128)(2,1)}, u32[]{:S(2)}, u32[]{:S(2)}) collective-permute-start(bf16[4,576,256]{2,1,0:T(8,128)(2,1)} %bitcast.14.b0), channel_id=1, source_target_pairs={{0,1},{1,0},{2,3},{3,2},{4,5},{5,4},{6,7},{7,6}} | collective-permute-start | bytes 3538952 | tf_op jit(solution)/shard_map/ppermute | solution.py:444
  64.4 75.3 %collective-permute-start.21 = (bf16[4,576,256]{2,1,0:T(8,128)(2,1)}, bf16[4,576,256]{2,1,0:T(8,128)(2,1)}, u32[]{:S(2)}, u32[]{:S(2)}) collective-permute-start(bf16[4,576,256]{2,1,0:T(8,128)(2,1)} %bitcast.14.b0), channel_id=1, source_target_pairs={{0,2},{1,3},{2,0},{3,1},{4,6},{5,7},{6,4},{7,5}} | collective-permute-start | bytes 3538952 | tf_op jit(solution)/shard_map/ppermute | solution.py:444
  66.2 75.3 %collective-permute-start.23 = (bf16[4,576,256]{2,1,0:T(8,128)(2,1)}, bf16[4,576,256]{2,1,0:T(8,128)(2,1)}, u32[]{:S(2)}, u32[]{:S(2)}) collective-permute-start(bf16[4,576,256]{2,1,0:T(8,128)(2,1)} %bitcast.14.b0), channel_id=1, source_target_pairs={{0,4},{1,5},{2,6},{3,7},{4,0},{5,1},{6,2},{7,3}} | collective-permute-start | bytes 3538952 | tf_op jit(solution)/shard_map/ppermute | solution.py:444
  89.8 51.7 %collective-permute-start.2 = (bf16[576,1024]{1,0:T(8,128)(2,1)}, bf16[576,1024]{1,0:T(8,128)(2,1)}, u32[]{:S(2)}, u32[]{:S(2)}) collective-permute-start(bf16[576,1024]{1,0:T(8,128)(2,1)} %collective-permute-done.1.rx.x2), channel_id=1, source_target_pairs={{0,1},{1,0},{2,3},{3,2},{4,5},{5,4},{6,7},{7,6}} | collective-permute-start | bytes 3538952 | tf_op jit(solution)/shard_map/ppermute | solution.py:444
  114.4 36.4 %collective-permute-start.3 = (bf16[576,1024]{1,0:T(8,128)(2,1)}, bf16[576,1024]{1,0:T(8,128)(2,1)}, u32[]{:S(2)}, u32[]{:S(2)}) collective-permute-start(bf16[576,1024]{1,0:T(8,128)(2,1)} %collective-permute-done.1.rx.x2), channel_id=1, source_target_pairs={{0,4},{1,5},{2,6},{3,7},{4,0},{5,1},{6,2},{7,3}} | collective-permute-start | bytes 3538952 | tf_op jit(solution)/shard_map/ppermute | solution.py:444
  123.3 29.2 %collective-permute-start.9 = (bf16[576,1024]{1,0:T(8,128)(2,1)}, bf16[576,1024]{1,0:T(8,128)(2,1)S(1)}, u32[]{:S(2)}, u32[]{:S(2)}) collective-permute-start(bf16[576,1024]{1,0:T(8,128)(2,1)} %copy-done.6), channel_id=1, source_target_pairs={{0,1},{1,0},{2,3},{3,2},{4,5},{5,4},{6,7},{7,6}} | collective-permute-start | bytes 3538952 | tf_op jit(solution)/shard_map/ppermute | solution.py:444
  139.7 29.1 %collective-permute-start.10 = (bf16[576,1024]{1,0:T(8,128)(2,1)S(1)}, bf16[576,1024]{1,0:T(8,128)(2,1)}, u32[]{:S(2)}, u32[]{:S(2)}) collective-permute-start(bf16[576,1024]{1,0:T(8,128)(2,1)S(1)} %copy-done.7), channel_id=1, source_target_pairs={{0,4},{1,5},{2,6},{3,7},{4,0},{5,1},{6,2},{7,3}} | collective-permute-start | bytes 3538952 | tf_op jit(solution)/shard_map/ppermute | solution.py:444
  141.5 27.3 %collective-permute-start.22 = (bf16[4,576,256]{2,1,0:T(8,128)(2,1)}, bf16[4,576,256]{2,1,0:T(8,128)(2,1)}, u32[]{:S(2)}, u32[]{:S(2)}) collective-permute-start(bf16[4,576,256]{2,1,0:T(8,128)(2,1)} %collective-permute-done.21.b1), channel_id=1, source_target_pairs={{0,1},{1,0},{2,3},{3,2},{4,5},{5,4},{6,7},{7,6}} | collective-permute-start | bytes 3538952 | tf_op jit(solution)/shard_map/ppermute | solution.py:444
  141.5 28.9 %collective-permute-start.24 = (bf16[4,576,256]{2,1,0:T(8,128)(2,1)}, bf16[4,576,256]{2,1,0:T(8,128)(2,1)}, u32[]{:S(2)}, u32[]{:S(2)}) collective-permute-start(bf16[4,576,256]{2,1,0:T(8,128)(2,1)} %collective-permute-done.23.b2), channel_id=1, source_target_pairs={{0,1},{1,0},{2,3},{3,2},{4,5},{5,4},{6,7},{7,6}} | collective-permute-start | bytes 3538952 | tf_op jit(solution)/shard_map/ppermute | solution.py:444
  150.7 116.8 %collective-permute-start = (bf16[576,4096]{1,0:T(8,128)(2,1)}, bf16[576,4096]{1,0:T(8,128)(2,1)}, u32[]{:S(2)}, u32[]{:S(2)}) collective-permute-start(bf16[576,4096]{1,0:T(8,128)(2,1)} %dynamic-slice_bitcast_fusion), channel_id=1, source_target_pairs={{0,1},{1,0},{2,3},{3,2},{4,5},{5,4},{6,7},{7,6}} | collective-permute-start | bytes 14155784 | tf_op jit(solution)/shard_map/ppermute | solution.py:444
  152.5 95.3 %collective-permute-start.49 = (bf16[576,2048]{1,0:T(8,128)(2,1)}, bf16[576,2048]{1,0:T(8,128)(2,1)}, u32[]{:S(2)}, u32[]{:S(2)}) collective-permute-start(bf16[576,2048]{1,0:T(8,128)(2,1)} %slice.14), channel_id=1, source_target_pairs={{0,4},{1,5},{2,6},{3,7},{4,0},{5,1},{6,2},{7,3}} | collective-permute-start | bytes 7077896 | tf_op jit(solution)/shard_map/ppermute | solution.py:444
  168.8 81.1 %collective-permute-start.30 = (bf16[576,2304]{1,0:T(8,128)(2,1)}, bf16[576,2304]{1,0:T(8,128)(2,1)}, u32[]{:S(2)}, u32[]{:S(2)}) collective-permute-start(bf16[576,2304]{1,0:T(8,128)(2,1)} %pad_maximum_fusion.refs_1_.refs_5_), channel_id=1, source_target_pairs={{0,1},{1,0},{2,3},{3,2},{4,5},{5,4},{6,7},{7,6}} | collective-permute-start | bytes 7962632 | tf_op jit(solution)/shard_map/ppermute | solution.py:444
  168.8 81.1 %collective-permute-start.31 = (bf16[576,2304]{1,0:T(8,128)(2,1)}, bf16[576,2304]{1,0:T(8,128)(2,1)}, u32[]{:S(2)}, u32[]{:S(2)}) collective-permute-start(bf16[576,2304]{1,0:T(8,128)(2,1)} %pad_maximum_fusion.1), channel_id=1, source_target_pairs={{0,2},{1,3},{2,0},{3,1},{4,6},{5,7},{6,4},{7,5}} | collective-permute-start | bytes 7962632 | tf_op jit(solution)/shard_map/ppermute | solution.py:444
  170.4 73.8 %collective-permute-start.25 = (bf16[4,576,256]{2,1,0:T(8,128)(2,1)}, bf16[4,576,256]{2,1,0:T(8,128)(2,1)}, u32[]{:S(2)}, u32[]{:S(2)}) collective-permute-start(bf16[4,576,256]{2,1,0:T(8,128)(2,1)} %collective-permute-done.21.b1), channel_id=1, source_target_pairs={{0,4},{1,5},{2,6},{3,7},{4,0},{5,1},{6,2},{7,3}} | collective-permute-start | bytes 3538952 | tf_op jit(solution)/shard_map/ppermute | solution.py:444
  247.7 74.0 %collective-permute-start.33 = (bf16[576,2304]{1,0:T(8,128)(2,1)}, bf16[576,2304]{1,0:T(8,128)(2,1)}, u32[]{:S(2)}, u32[]{:S(2)}) collective-permute-start(bf16[576,2304]{1,0:T(8,128)(2,1)} %pad_maximum_fusion.2.refs_9_.refs_13_), channel_id=1, source_target_pairs={{0,1},{1,0},{2,3},{3,2},{4,5},{5,4},{6,7},{7,6}} | collective-permute-start | bytes 7962632 | tf_op jit(solution)/shard_map/ppermute | solution.py:444
  249.9 105.3 %collective-permute-start.38 = (bf16[576,2304]{1,0:T(8,128)(2,1)}, bf16[576,2304]{1,0:T(8,128)(2,1)}, u32[]{:S(2)}, u32[]{:S(2)}) collective-permute-start(bf16[576,2304]{1,0:T(8,128)(2,1)} %get-tuple-element.42.d0.dt), channel_id=1, source_target_pairs={{0,1},{1,0},{2,3},{3,2},{4,5},{5,4},{6,7},{7,6}} | collective-permute-start | bytes 7962632 | tf_op jit(solution)/shard_map/ppermute | solution.py:444
  249.9 105.1 %collective-permute-start.34 = (bf16[576,2304]{1,0:T(8,128)(2,1)}, bf16[576,2304]{1,0:T(8,128)(2,1)}, u32[]{:S(2)}, u32[]{:S(2)}) collective-permute-start(bf16[576,2304]{1,0:T(8,128)(2,1)} %pad_maximum_fusion.3), channel_id=1, source_target_pairs={{0,2},{1,3},{2,0},{3,1},{4,6},{5,7},{6,4},{7,5}} | collective-permute-start | bytes 7962632 | tf_op jit(solution)/shard_map/ppermute | solution.py:444
  267.1 190.2 %collective-permute-start.39 = (bf16[576,2304]{1,0:T(8,128)(2,1)}, bf16[576,2304]{1,0:T(8,128)(2,1)}, u32[]{:S(2)}, u32[]{:S(2)}) collective-permute-start(bf16[576,2304]{1,0:T(8,128)(2,1)} %get-tuple-element.41), channel_id=1, source_target_pairs={{0,2},{1,3},{2,0},{3,1},{4,6},{5,7},{6,4},{7,5}} | collective-permute-start | bytes 7962632 | tf_op jit(solution)/shard_map/ppermute | solution.py:444
  267.6 88.0 %collective-permute-start.26 = (bf16[4,576,256]{2,1,0:T(8,128)(2,1)}, bf16[4,576,256]{2,1,0:T(8,128)(2,1)}, u32[]{:S(2)}, u32[]{:S(2)}) collective-permute-start(bf16[4,576,256]{2,1,0:T(8,128)(2,1)} %collective-permute-done.25.b3), channel_id=1, source_target_pairs={{0,1},{1,0},{2,3},{3,2},{4,5},{5,4},{6,7},{7,6}} | collective-permute-start | bytes 3538952 | tf_op jit(solution)/shard_map/ppermute | solution.py:444
  321.7 137.1 %collective-permute-start.41 = (bf16[576,2304]{1,0:T(8,128)(2,1)}, bf16[576,2304]{1,0:T(8,128)(2,1)}, u32[]{:S(2)}, u32[]{:S(2)}) collective-permute-start(bf16[576,2304]{1,0:T(8,128)(2,1)} %pad_maximum_fusion.refs_1_.refs_5_), channel_id=1, source_target_pairs={{0,4},{1,5},{2,6},{3,7},{4,0},{5,1},{6,2},{7,3}} | collective-permute-start | bytes 7962632 | tf_op jit(solution)/shard_map/ppermute | solution.py:444
  355.3 38.4 %collective-permute-start.18 = (bf16[512,512]{1,0:T(8,128)(2,1)}, bf16[512,512]{1,0:T(8,128)(2,1)}, u32[]{:S(2)}, u32[]{:S(2)}) collective-permute-start(bf16[512,512]{1,0:T(8,128)(2,1)} %get-tuple-element.55), channel_id=1, source_target_pairs={{0,4},{1,5},{2,6},{3,7},{4,0},{5,1},{6,2},{7,3}} | collective-permute-start | bytes 1572872 | tf_op jit(solution)/shard_map/ppermute | solution.py:444
  355.6 48.6 %collective-permute-start.19 = (bf16[512,512]{1,0:T(8,128)(2,1)}, bf16[512,512]{1,0:T(8,128)(2,1)}, u32[]{:S(2)}, u32[]{:S(2)}) collective-permute-start(bf16[512,512]{1,0:T(8,128)(2,1)} %get-tuple-element.54), channel_id=1, source_target_pairs={{0,5},{1,4},{2,7},{3,6},{4,1},{5,0},{6,3},{7,2}} | collective-permute-start | bytes 1572872 | tf_op jit(solution)/shard_map/ppermute | solution.py:444
  374.0 32.1 %collective-permute-start.27 = (bf16[512,512]{1,0:T(8,128)(2,1)S(1)}, bf16[512,512]{1,0:T(8,128)(2,1)}, u32[]{:S(2)}, u32[]{:S(2)}) collective-permute-start(bf16[512,512]{1,0:T(8,128)(2,1)S(1)} %get-tuple-element.53), channel_id=1, source_target_pairs={{0,1},{1,0},{2,3},{3,2},{4,5},{5,4},{6,7},{7,6}} | collective-permute-start | bytes 1572872 | tf_op jit(solution)/shard_map/ppermute | solution.py:444
  406.1 77.7 %collective-permute-start.45 = (bf16[576,2304]{1,0:T(8,128)(2,1)}, bf16[576,2304]{1,0:T(8,128)(2,1)}, u32[]{:S(2)}, u32[]{:S(2)}) collective-permute-start(bf16[576,2304]{1,0:T(8,128)(2,1)} %pad_maximum_fusion.2.refs_9_.refs_13_), channel_id=1, source_target_pairs={{0,4},{1,5},{2,6},{3,7},{4,0},{5,1},{6,2},{7,3}} | collective-permute-start | bytes 7962632 | tf_op jit(solution)/shard_map/ppermute | solution.py:444
  416.2 67.6 %collective-permute-start.32 = (bf16[576,2304]{1,0:T(8,128)(2,1)}, bf16[576,2304]{1,0:T(8,128)(2,1)}, u32[]{:S(2)}, u32[]{:S(2)}) collective-permute-start(bf16[576,2304]{1,0:T(8,128)(2,1)} %collective-permute-done.31.refs_3_.refs_7_), channel_id=1, source_target_pairs={{0,1},{1,0},{2,3},{3,2},{4,5},{5,4},{6,7},{7,6}} | collective-permute-start | bytes 7962632 | tf_op jit(solution)/shard_map/ppermute | solution.py:444
  426.6 57.8 %collective-permute-start.35 = (bf16[576,2304]{1,0:T(8,128)(2,1)}, bf16[576,2304]{1,0:T(8,128)(2,1)}, u32[]{:S(2)}, u32[]{:S(2)}) collective-permute-start(bf16[576,2304]{1,0:T(8,128)(2,1)} %collective-permute-done.34.refs_11_.refs_15_), channel_id=1, source_target_pairs={{0,1},{1,0},{2,3},{3,2},{4,5},{5,4},{6,7},{7,6}} | collective-permute-start | bytes 7962632 | tf_op jit(solution)/shard_map/ppermute | solution.py:444
  457.2 54.5 %collective-permute-start.36 = (bf16[2304,512]{1,0:T(8,128)(2,1)}, bf16[2304,512]{1,0:T(8,128)(2,1)}, u32[]{:S(2)}, u32[]{:S(2)}) collective-permute-start(bf16[2304,512]{1,0:T(8,128)(2,1)} %get-tuple-element.26.hw1), channel_id=1, source_target_pairs={{0,2},{1,3},{2,0},{3,1},{4,6},{5,7},{6,4},{7,5}} | collective-permute-start | bytes 7077896 | tf_op jit(solution)/shard_map/ppermute | solution.py:444
  458.8 102.5 %collective-permute-start.37 = (bf16[2304,512]{1,0:T(8,128)(2,1)}, bf16[2304,512]{1,0:T(8,128)(2,1)}, u32[]{:S(2)}, u32[]{:S(2)}) collective-permute-start(bf16[2304,512]{1,0:T(8,128)(2,1)} %get-tuple-element.27.hw0), channel_id=1, source_target_pairs={{0,2},{1,3},{2,0},{3,1},{4,6},{5,7},{6,4},{7,5}} | collective-permute-start | bytes 7077896 | tf_op jit(solution)/shard_map/ppermute | solution.py:444
  483.8 119.1 %collective-permute-start.40 = (bf16[576,2304]{1,0:T(8,128)(2,1)}, bf16[576,2304]{1,0:T(8,128)(2,1)}, u32[]{:S(2)}, u32[]{:S(2)}) collective-permute-start(bf16[576,2304]{1,0:T(8,128)(2,1)} %collective-permute-done.39.d2), channel_id=1, source_target_pairs={{0,1},{1,0},{2,3},{3,2},{4,5},{5,4},{6,7},{7,6}} | collective-permute-start | bytes 7962632 | tf_op jit(solution)/shard_map/ppermute | solution.py:444
  483.8 120.9 %collective-permute-start.42 = (bf16[576,2304]{1,0:T(8,128)(2,1)}, bf16[576,2304]{1,0:T(8,128)(2,1)}, u32[]{:S(2)}, u32[]{:S(2)}) collective-permute-start(bf16[576,2304]{1,0:T(8,128)(2,1)} %collective-permute-done.41.refs_1_.refs_5_), channel_id=1, source_target_pairs={{0,1},{1,0},{2,3},{3,2},{4,5},{5,4},{6,7},{7,6}} | collective-permute-start | bytes 7962632 | tf_op jit(solution)/shard_map/ppermute | solution.py:444
  484.3 121.7 %collective-permute-start.43 = (bf16[576,2304]{1,0:T(8,128)(2,1)}, bf16[576,2304]{1,0:T(8,128)(2,1)}, u32[]{:S(2)}, u32[]{:S(2)}) collective-permute-start(bf16[576,2304]{1,0:T(8,128)(2,1)} %collective-permute-done.31.refs_3_.refs_7_), channel_id=1, source_target_pairs={{0,4},{1,5},{2,6},{3,7},{4,0},{5,1},{6,2},{7,3}} | collective-permute-start | bytes 7962632 | tf_op jit(solution)/shard_map/ppermute | solution.py:444
  511.7 95.0 %collective-permute-start.47 = (bf16[576,2304]{1,0:T(8,128)(2,1)}, bf16[576,2304]{1,0:T(8,128)(2,1)}, u32[]{:S(2)}, u32[]{:S(2)}) collective-permute-start(bf16[576,2304]{1,0:T(8,128)(2,1)} %collective-permute-done.34.refs_11_.refs_15_), channel_id=1, source_target_pairs={{0,4},{1,5},{2,6},{3,7},{4,0},{5,1},{6,2},{7,3}} | collective-permute-start | bytes 7962632 | tf_op jit(solution)/shard_map/ppermute | solution.py:444
  561.3 76.1 %collective-permute-start.46 = (bf16[576,2304]{1,0:T(8,128)(2,1)}, bf16[576,2304]{1,0:T(8,128)(2,1)}, u32[]{:S(2)}, u32[]{:S(2)}) collective-permute-start(bf16[576,2304]{1,0:T(8,128)(2,1)} %collective-permute-done.45.refs_2_.refs_6_), channel_id=1, source_target_pairs={{0,1},{1,0},{2,3},{3,2},{4,5},{5,4},{6,7},{7,6}} | collective-permute-start | bytes 7962632 | tf_op jit(solution)/shard_map/ppermute | solution.py:444
  603.0 65.3 %collective-permute-start.51 = (bf16[576,2304]{1,0:T(8,128)(2,1)}, bf16[576,2304]{1,0:T(8,128)(2,1)}, u32[]{:S(2)}, u32[]{:S(2)}) collective-permute-start(bf16[576,2304]{1,0:T(8,128)(2,1)} %collective-permute-done.39.d2), channel_id=1, source_target_pairs={{0,4},{1,5},{2,6},{3,7},{4,0},{5,1},{6,2},{7,3}} | collective-permute-start | bytes 7962632 | tf_op jit(solution)/shard_map/ppermute | solution.py:444
  604.7 63.6 %collective-permute-start.15 = (bf16[1024,512]{1,0:T(8,128)(2,1)}, bf16[1024,512]{1,0:T(8,128)(2,1)}, u32[]{:S(2)}, u32[]{:S(2)}) collective-permute-start(bf16[1024,512]{1,0:T(8,128)(2,1)} %split.6), channel_id=1, source_target_pairs={{0,2},{1,3},{2,0},{3,1},{4,6},{5,7},{6,4},{7,5}} | collective-permute-start | bytes 3145736 | tf_op jit(solution)/shard_map/ppermute | solution.py:444
  606.0 93.5 %collective-permute-start.53 = (bf16[3072,512]{1,0:T(8,128)(2,1)}, bf16[3072,512]{1,0:T(8,128)(2,1)}, u32[]{:S(2)}, u32[]{:S(2)}) collective-permute-start(bf16[3072,512]{1,0:T(8,128)(2,1)} %split.7), channel_id=1, source_target_pairs={{0,2},{1,3},{2,0},{3,1},{4,6},{5,7},{6,4},{7,5}} | collective-permute-start | bytes 9437192 | tf_op jit(solution)/shard_map/ppermute | solution.py:444
  606.7 62.1 %collective-permute-start.48 = (bf16[576,2304]{1,0:T(8,128)(2,1)}, bf16[576,2304]{1,0:T(8,128)(2,1)}, u32[]{:S(2)}, u32[]{:S(2)}) collective-permute-start(bf16[576,2304]{1,0:T(8,128)(2,1)} %collective-permute-done.47.refs_4_.refs_8_), channel_id=1, source_target_pairs={{0,1},{1,0},{2,3},{3,2},{4,5},{5,4},{6,7},{7,6}} | collective-permute-start | bytes 7962632 | tf_op jit(solution)/shard_map/ppermute | solution.py:444
  637.4 62.6 %collective-permute-start.44 = (bf16[576,2304]{1,0:T(8,128)(2,1)}, bf16[576,2304]{1,0:T(8,128)(2,1)}, u32[]{:S(2)}, u32[]{:S(2)}) collective-permute-start(bf16[576,2304]{1,0:T(8,128)(2,1)} %collective-permute-done.43.refs_3_.refs_7_), channel_id=1, source_target_pairs={{0,1},{1,0},{2,3},{3,2},{4,5},{5,4},{6,7},{7,6}} | collective-permute-start | bytes 7962632 | tf_op jit(solution)/shard_map/ppermute | solution.py:444
  668.3 66.6 %collective-permute-start.50 = (bf16[576,2048]{1,0:T(8,128)(2,1)}, bf16[576,2048]{1,0:T(8,128)(2,1)}, u32[]{:S(2)}, u32[]{:S(2)}) collective-permute-start(bf16[576,2048]{1,0:T(8,128)(2,1)} %collective-permute-done.49.d0), channel_id=1, source_target_pairs={{0,1},{1,0},{2,3},{3,2},{4,5},{5,4},{6,7},{7,6}} | collective-permute-start | bytes 7077896 | tf_op jit(solution)/shard_map/ppermute | solution.py:444
  668.3 193.4 %collective-permute-start.55 = (bf16[4096,512]{1,0:T(8,128)(2,1)}, bf16[4096,512]{1,0:T(8,128)(2,1)}, u32[]{:S(2)}, u32[]{:S(2)}) collective-permute-start(bf16[4096,512]{1,0:T(8,128)(2,1)} %get-tuple-element.22.k_ref.kv0), channel_id=1, source_target_pairs={{0,1},{1,0},{2,3},{3,2},{4,5},{5,4},{6,7},{7,6}} | collective-permute-start | bytes 12582920 | tf_op jit(solution)/shard_map/ppermute | solution.py:444
  668.8 66.1 %collective-permute-start.52 = (bf16[576,2304]{1,0:T(8,128)(2,1)}, bf16[576,2304]{1,0:T(8,128)(2,1)}, u32[]{:S(2)}, u32[]{:S(2)}) collective-permute-start(bf16[576,2304]{1,0:T(8,128)(2,1)} %collective-permute-done.51.d2), channel_id=1, source_target_pairs={{0,1},{1,0},{2,3},{3,2},{4,5},{5,4},{6,7},{7,6}} | collective-permute-start | bytes 7962632 | tf_op jit(solution)/shard_map/ppermute | solution.py:444
  699.6 184.7 %collective-permute-start.16 = (bf16[1024,512]{1,0:T(8,128)(2,1)}, bf16[1024,512]{1,0:T(8,128)(2,1)}, u32[]{:S(2)}, u32[]{:S(2)}) collective-permute-start(bf16[1024,512]{1,0:T(8,128)(2,1)} %collective-permute-done.15.kv0), channel_id=1, source_target_pairs={{0,1},{1,0},{2,3},{3,2},{4,5},{5,4},{6,7},{7,6}} | collective-permute-start | bytes 3145736 | tf_op jit(solution)/shard_map/ppermute | solution.py:444
  700.1 172.8 %collective-permute-start.54 = (bf16[3072,512]{1,0:T(8,128)(2,1)}, bf16[3072,512]{1,0:T(8,128)(2,1)}, u32[]{:S(2)}, u32[]{:S(2)}) collective-permute-start(bf16[3072,512]{1,0:T(8,128)(2,1)} %collective-permute-done.53.kv0), channel_id=1, source_target_pairs={{0,1},{1,0},{2,3},{3,2},{4,5},{5,4},{6,7},{7,6}} | collective-permute-start | bytes 9437192 | tf_op jit(solution)/shard_map/ppermute | solution.py:444
  (21 other events, 651.0 us)

commit v5 on v4

--- a/solution.py
+++ b/solution.py
@@ -21,6 +21,7 @@
 SHRINK = 2.0 ** -88
 MT = 256
 KT = 256
+KA = 768
 ANY = pl.BlockSpec(memory_space=pl.ANY)
 
 
@@ -66,6 +67,14 @@
 
 def part_of(ref, j, size):
     return ref.at[j * size:(j + 1) * size, :]
+
+
+def block_of(j, size):
+    return pl.ds(pl.multiple_of(j * size, size), size)
+
+
+def loop(n, body, init=0):
+    return lax.fori_loop(0, n, body, init)
 
 
 def call(kernel, grid, in_specs, out_specs, out_shape, scratch=(), prefetch=1, flops=0, nbytes=0, aliases=None):
@@ -95,34 +104,51 @@
     sin_ref[...] = jnp.sin(ang)
 
 
-def qkv_kernel(s_ref, a_ref, w0, w1, w2, w3, cos_ref, sin_ref, qv_ref, kv_ref, w_t, w_all, *, hd):
+def split_kernel(s_ref, wq, wk, wv, own_ref, oth_ref):
+    rows, _, hd = wk.shape
+    q, k, v = (w[...].reshape(rows, w.shape[1] * hd) for w in (wq, wk, wv))
+    two = [hcat([q[:, 2 * g * hd:2 * (g + 1) * hd], k[:, g * hd:(g + 1) * hd], v[:, g * hd:(g + 1) * hd]]) for g in range(2)]
+    first = s_ref[2] == 0
+    own_ref[...] = jnp.where(first, *two)
+    oth_ref[...] = jnp.where(first, *two[::-1])
+
+
+def qkv_kernel(s_ref, a_ref, w0, w1, w2, w3, cos_ref, sin_ref, qv_ref, kv_ref, w_t, w_all, w_sem, *, hd):
     w4 = w0.shape[0]
 
     @pl.when(pl.program_id(0) == 0)
     def _():
-        for j, w in enumerate((w0, w1, w2, w3)):
-            part_of(w_all, j, w4)[...] = w[...]
-        for r in range(0, w_all.shape[0], MT):
-            w_t[:, r:r + MT] = w_all[r:r + MT, :].T
-
-    qkv = dot(w_t[...], a_ref[...]).astype(BF).astype(F32)
-    ct, st = cos_ref[...], sin_ref[...]
+        cps = [pltpu.make_async_copy(w, part_of(w_all, j, w4), w_sem.at[j]) for j, w in enumerate((w0, w1, w2, w3))]
+        for cp in cps:
+            cp.start()
+        for cp in cps:
+            cp.wait()
+        to_rows(w_t, w_all)
+
     hh = hd // 2
 
-    def rot(base):
-        u1, u2 = qkv[base:base + hh], qkv[base + hh:base + hd]
-        return u1 * ct - u2 * st, u2 * ct + u1 * st
-
-    for g in range(2):
-        lo, hi = rot(g * hd)
-        qv_ref[g * hd:g * hd + hh, :] = lo.astype(BF)
-        qv_ref[g * hd + hh:(g + 1) * hd, :] = hi.astype(BF)
-    v = qkv[3 * hd:]
-    qv_ref[2 * hd:, :] = v.astype(BF)
-    klo, khi = rot(2 * hd)
-    kv_ref[:, :hh] = klo.T.astype(BF)
-    kv_ref[:, hh:hd] = khi.T.astype(BF)
-    kv_ref[:, hd:] = v.T.astype(BF)
+    def part(n, _):
+        cols = block_of(n, MT)
+        qkv = dot(w_t[...], a_ref[:, cols]).astype(BF).astype(F32)
+        ct, st = cos_ref[:, cols], sin_ref[:, cols]
+
+        def rot(base):
+            u1, u2 = qkv[base:base + hh], qkv[base + hh:base + hd]
+            return u1 * ct - u2 * st, u2 * ct + u1 * st
+
+        for g in range(2):
+            lo, hi = rot(g * hd)
+            qv_ref[g * hd:g * hd + hh, cols] = lo.astype(BF)
+            qv_ref[g * hd + hh:(g + 1) * hd, cols] = hi.astype(BF)
+        v = qkv[3 * hd:]
+        qv_ref[2 * hd:, cols] = v.astype(BF)
+        klo, khi = rot(2 * hd)
+        kv_ref[cols, :hh] = klo.T.astype(BF)
+        kv_ref[cols, hh:hd] = khi.T.astype(BF)
+        kv_ref[cols, hd:] = v.T.astype(BF)
+        return 0
+
+    loop(a_ref.shape[1] // MT, part)
 
 
 def attn_kernel(lo_ref, full_ref, q_ref, k_ref, v_ref, pq_ref, pk_ref, o_ref, acc_ref, qq_ref, l_ref, vs_ref, f_ref, *, bq, bk, q_block0, scale):
@@ -146,80 +172,115 @@
     acc_ref[...] = jnp.zeros_like(acc_ref)
 
     def step(j, masked):
-        rows = pl.ds(pl.multiple_of(j * bk, bk), bk)
-        kb = k_ref[rows, :]
-        vb = vs_ref[:, rows]
-        for n in range(0, groups * bq, MT):
-            cols = slice(n, n + MT)
-            s = dot(kb, qq_ref[:, cols])
+        rows = block_of(j, bk)
+
+        def part(n, _):
+            cols = block_of(n, MT)
+            s = dot(k_ref[rows, :], qq_ref[:, cols])
             p = jnp.exp2(jnp.tanh(s * (scale / SOFT_CAP)) * (SOFT_CAP * LOG2E))
             if masked:
-                dif = pq_ref[:, n % bq:n % bq + MT] - pk_ref[rows, :]
+                dif = pq_ref[:, block_of(lax.rem(n, bq // MT), MT)] - pk_ref[rows, :]
                 p = jnp.where((dif >= 0) & (dif < WINDOW_LEN), p, 0.0)
             l_ref[:, cols] += jnp.sum(p, axis=0, keepdims=True)
-            acc_ref[:, cols] += dot(vb, p.astype(BF))
+            acc_ref[:, cols] += dot(vs_ref[:, rows], p.astype(BF))
+            return 0
+
+        lax.fori_loop(0, groups * bq // MT, part, 0, unroll=2)
 
     mid = jnp.maximum(jnp.minimum(full, diag), lo)
-
-    def masked_step(j, _):
-        step(j, True)
+    edge = jnp.maximum(diag, mid)
+
+    def masked_step(i, _):
+        j = lo + i
+        step(jnp.where(j < mid, j, j - mid + edge), True)
         return 0
 
     def full_step(j, _):
         step(j, False)
         return 0
 
-    lax.fori_loop(lo, mid, masked_step, 0)
+    lax.fori_loop(0, mid - lo + last - edge, masked_step, 0)
     lax.fori_loop(mid, diag, full_step, 0)
-    lax.fori_loop(jnp.maximum(diag, mid), last, masked_step, 0)
     for g in range(groups):
         cols = slice(g * bq, (g + 1) * bq)
         o_ref[g * hd:(g + 1) * hd, :] = (acc_ref[:, cols] / l_ref[:, cols] / f_ref[0:1, 0:1]).astype(BF)
 
 
-def norm_to_m(m_ref, blocks, r, g_ref, col, mt_ref):
-    w4 = blocks[0].shape[0]
-    for j, b in enumerate(blocks):
-        part_of(mt_ref, j, w4)[...] = (b * r * part_of(g_ref, j, w4)[:, col:col + 1]).astype(BF)
-    for i in range(0, mt_ref.shape[0], MT):
-        m_ref[:, i:i + MT] = mt_ref[i:i + MT, :].T
+def to_rows(m_ref, mt_ref):
+    def turn(i, _):
+        at = block_of(i, MT)
+        m_ref[:, at] = mt_ref[at, :].T
+        return 0
+
+    loop(mt_ref.shape[0] // MT, turn)
+
+
+def sum_sq(t):
+    return jnp.sum(t * t, axis=0, keepdims=True)
 
 
 def proj_kernel(s_ref, o_own, o_c, o_y, o_yc, b0, b0c, b1, b1c, b2, b2c, b3, b3c, x0, x1, x2, x3, g_ref, *rest, width):
-    h_ref, m_ref, o_all, mt_ref, w_ref, w_sem = rest[-6:]
-    cps = [pltpu.make_async_copy(b, w_ref.at[i], w_sem.at[i]) for i, b in enumerate((b0, b2, b0c, b2c, b1, b3, b1c, b3c))]
-    for cp in cps:
-        cp.start()
-    c = s_ref[2]
+    h_ref, m_ref, o_all, mt_ref, w_ref, x_ref, att_ref, w_sem = rest[-8:]
+    for i, b in enumerate((b0, b2, b0c, b2c, b1, b3, b1c, b3c)):
+        pltpu.make_async_copy(b, w_ref.at[i], w_sem.at[i]).start()
+    first = s_ref[2] == 0
     gw = o_own.shape[0]
-    first = c == 0
     pairs = ((o_own, o_c), (o_y, o_yc))
     for i, (a, b) in enumerate([t for q in pairs for t in (q, q[::-1])]):
         part_of(o_all, i, gw)[...] = jnp.where(first, a[...], b[...])
+    for j, t in enumerate((x0, x1, x2, x3)):
+        x_ref[j] = t[...]
     w4 = x0.shape[0]
     heads = b0.shape[0]
-    o = o_all[...]
-    att = []
-    for j in range(4):
+    n = x_ref.shape[0]
+    zero = jnp.zeros((1, m_ref.shape[0]), F32)
+
+    def product(j, sq):
         two = (2 * j, 2 * j + 1)
         for i in two:
-            cps[i].wait()
-        w = hcat([w_ref[i, h] for i in two for h in range(heads)])
-        att.append(dot(w, o).astype(BF).astype(F32))
-    r = inv_rms(att, width)
-    hs = []
-    for j, (t, xr) in enumerate(zip(att, (x0, x1, x2, x3))):
-        h = (xr[...].astype(F32) + t * r * part_of(g_ref, j, w4)[:, 1:2]).astype(BF)
-        part_of(h_ref, j, w4)[...] = h
-        hs.append(h.astype(F32))
-    norm_to_m(m_ref, hs, inv_rms(hs, width), g_ref, 2, mt_ref)
+            pltpu.make_async_copy(b0, w_ref.at[i], w_sem.at[i]).wait()
+        t = dot(hcat([w_ref[i, h] for i in two for h in range(heads)]), o_all[...]).astype(BF).astype(F32)
+        att_ref[j] = t
+        return sq + sum_sq(t)
+
+    r = lax.rsqrt(loop(n, product, zero) / width + NORM_EPS)
+
+    def residual(j, sq):
+        at = block_of(j, w4)
+        h = (x_ref[j].astype(F32) + att_ref[j] * r * g_ref[at, 1:2]).astype(BF)
+        h_ref[at, :] = h
+        h = h.astype(F32)
+        att_ref[j] = h
+        return sq + sum_sq(h)
+
+    r3 = lax.rsqrt(loop(n, residual, zero) / width + NORM_EPS)
+
+    def scaled(j, _):
+        at = block_of(j, w4)
+        mt_ref[at, :] = (att_ref[j] * r3 * g_ref[at, 2:3]).astype(BF)
+        return 0
+
+    loop(n, scaled)
+    to_rows(m_ref, mt_ref)
 
 
 def renorm_kernel(s_ref, h_ref, g_ref, *rest, width):
     m_ref, mt_ref = rest[-2:]
-    w4 = h_ref.shape[0] // 4
-    hs = [part_of(h_ref, j, w4)[...].astype(F32) for j in (2, 3, 0, 1)]
-    norm_to_m(m_ref, hs, inv_rms(hs, width), g_ref, 2, mt_ref)
+    n = 4
+    w4 = h_ref.shape[0] // n
+
+    def theirs(j):
+        return h_ref[block_of(lax.rem(j + 2, n), w4), :].astype(F32)
+
+    r = lax.rsqrt(loop(n, lambda j, sq: sq + sum_sq(theirs(j)), jnp.zeros((1, h_ref.shape[1]), F32)) / width + NORM_EPS)
+
+    def scaled(j, _):
+        at = block_of(j, w4)
+        mt_ref[at, :] = (theirs(j) * r * g_ref[at, 2:3]).astype(BF)
+        return 0
+
+    loop(n, scaled)
+    to_rows(m_ref, mt_ref)
 
 
 def gate_up_kernel(s_ref, *refs, groups, sets, steps):
@@ -239,18 +300,29 @@
         z_ref[r:r + MT, :] = (jax.nn.gelu(g, approximate=True) * u).astype(BF)
 
 
-def down_y_kernel(s_ref, zw, zf, d0, d1, d2, d3, acc_ref):
+def down_y_kernel(s_ref, zw, zf, d0, d1, d2, d3, acc_ref, d_ref):
     w4 = d0.shape[0]
     n = zw.shape[0]
+
+    @pl.when(pl.program_id(0) == 0)
+    def _():
+        for j, dd in enumerate((d0, d1, d2, d3)):
+            part_of(d_ref, j, w4)[...] = dd[...]
+
     z = vcat([zw[...], zf[...]])
-    for j, dd in enumerate((d0, d1, d2, d3)):
-        t = dot_nt(dd[...], z)
+
+    def rows(j, _):
+        at = block_of(j, w4)
+        t = dot_nt(d_ref[at, :], z)
         for q in range(n // CH):
-            acc_ref[q, j * w4:(j + 1) * w4, :CH] = t[:, q * CH:(q + 1) * CH]
-            acc_ref[q, j * w4:(j + 1) * w4, CH:] = t[:, n + q * CH:n + (q + 1) * CH]
-
-
-def tail_kernel(part, zwa, zfa, zb, d0, d1, d2, d3, dt, hw0, hw1, hf0, hf1, g_ref, out,
+            acc_ref[q, at, :CH] = t[:, q * CH:(q + 1) * CH]
+            acc_ref[q, at, CH:] = t[:, n + q * CH:n + (q + 1) * CH]
+        return 0
+
+    loop(4, rows)
+
+
+def tail_kernel(part, zwa, zfa, zb, d0, d1, d2, d3, e0, e1, dt, hw0, hw1, hf0, hf1, g_ref, out,
                 d_ref, z_ref, g_buf, p_ref, lo_ref, hi_ref, rec_ref, h_ref, sqs_ref, sqr_ref, sqo_ref,
                 d_sem, z_sem, p_sem, h_sem, loc_sem, rs_s, rs_r, sq_s, sq_r, dt_s, dt_r, out_s, out_r, *, width, chunks):
     w4 = d0.shape[0]
@@ -271,8 +343,11 @@
         return pltpu.make_async_remote_copy(src_ref=src, dst_ref=dst, send_sem=s_sem, recv_sem=r_sem, device_id=dev, device_id_type=pl.DeviceIdType.MESH)
 
     d_cp = [local(dd, d_ref.at[j * w4:(j + 1) * w4, :dd.shape[1]], d_sem.at[j]) for j, dd in enumerate((d0, d1, d2, d3))]
-    g_cp = local(part_of(g_ref, 0, w2), g_buf, d_sem.at[4])
-    late = slice(d0.shape[1], d_ref.shape[1])
+    cut = d0.shape[1]
+    last = cut + e0.shape[1]
+    e_cp = [local(dd, d_ref.at[j * w4:(j + 1) * w4, cut:last], d_sem.at[4 + j]) for j, dd in enumerate((e0, e1))]
+    g_cp = local(part_of(g_ref, 0, w2), g_buf, d_sem.at[6])
+    late = slice(last, d_ref.shape[1])
     dt_y = remote(dt.at[:, late], d_ref.at[:w4, late], dt_s.at[0], dt_r.at[0], py)
     dt_c = remote(d_ref.at[:w4, late], d_ref.at[w4:w2, late], dt_s.at[1], dt_r.at[1], pc)
 
@@ -294,7 +369,7 @@
         for cp in cps:
             cp.start()
 
-    start(z_cp(0) + [d_cp[2], p_cp(0), d_cp[3]])
+    start(z_cp(0) + [d_cp[2], p_cp(0), d_cp[3]] + z_cp(1))
 
     bar = pltpu.get_barrier_semaphore()
     for dev in (px, pc, py, pyc):
@@ -323,30 +398,33 @@
         return far + [local(mine, dst, loc_sem.at[p, q])]
 
     def block(p, j):
-        return dot_nt(part_of(d_ref, j, w4)[...], z_ref[p]) + p_ref[lax.rem(p, 3), j * w4:(j + 1) * w4, :]
-
-    def upper(p, first=False):
+        at = block_of(j, w4)
+        return dot_nt(d_ref[at, :], z_ref[p]) + p_ref[lax.rem(p, 3), at, :]
+
+    def upper(p):
         p_cp(p).wait()
         for cp in z_cp(p):
             cp.wait()
-        if first:
-            p_cp(1).start()
-        else:
-            @pl.when(p + 1 < chunks)
-            def _():
-                p_cp(p + 1).start()
-        for i in range(2):
-            if first:
-                d_cp[2 + i].wait()
+
+        @pl.when(p + 1 < chunks)
+        def _():
+            p_cp(p + 1).start()
+
+        def half(i, _):
             t = block(p, 2 + i).astype(BF)
-            hi_ref[p, i * w4:(i + 1) * w4, :CH] = t[:, CH:]
-            hi_ref[p, i * w4:(i + 1) * w4, CH:] = t[:, :CH]
-
-    def lower(p, first=False):
-        for j in range(2):
-            if first:
-                d_cp[j].wait()
-            lo_ref[p, j * w4:(j + 1) * w4, :] = block(p, j)
+            at = block_of(i, w4)
+            hi_ref[p, at, :CH] = t[:, CH:]
+            hi_ref[p, at, CH:] = t[:, :CH]
+            return 0
+
+        loop(2, half)
+
+    def lower(p):
+        def half(j, _):
+            lo_ref[p, block_of(j, w4), :] = block(p, j)
+            return 0
+
+        loop(2, half)
 
     def add(p, q):
         rs(p, q).wait_recv()
@@ -366,44 +444,57 @@
         rec_ref[p, :, at] = (h_ref[p, :, at].astype(F32) + rec_ref[p, :, at].astype(F32) * r * g_buf[:, 3:4]).astype(BF)
         start(outs(p, q))
 
-    upper(0, True)
-    start([rs(0, 0), rs(0, 1)])
-    start(d_cp[:2] + z_cp(1))
-    upper(1)
-    start([g_cp] + h_cp)
+    for cp in d_cp[2:]:
+        cp.wait()
+
+    def first_upper(p, _):
+        upper(p)
+
+        @pl.when(p == 0)
+        def _():
+            start([rs(0, 0), rs(0, 1)])
+
+        return 0
+
+    loop(2, first_upper)
+    start(d_cp[:2] + e_cp + [g_cp] + h_cp)
     for q in range(2, chunks):
         start(z_cp(q))
     dt_y.wait_recv()
     dt_c.start()
+    for cp in d_cp[:2] + e_cp:
+        cp.wait()
     dt_c.wait_recv()
-    lower(0, True)
-    lower(1)
+
+    def first_lower(p, _):
+        lower(p)
+        return 0
+
+    loop(2, first_lower)
     for cp in [g_cp] + h_cp:
         cp.wait()
 
-    def steps(p, more):
+    def body(p, _):
         for q in range(2):
             add(p, q)
-            if more:
+
+            @pl.when(p + 1 < chunks)
+            def _():
                 rs(p + 1, q).start()
+
             if q:
                 finish(p, 0)
-            elif isinstance(p, int):
-                finish(p - 1, 1)
             else:
                 @pl.when(p > 0)
                 def _():
                     finish(p - 1, 1)
-            if not isinstance(p, int):
+
+            @pl.when(p + 2 < chunks)
+            def _():
                 (lower if q else upper)(p + 2)
-
-    def body(p, _):
-        steps(p, True)
-        return 0
-
-    lax.fori_loop(0, chunks - 2, body, 0)
-    steps(chunks - 2, True)
-    steps(chunks - 1, False)
+        return 0
+
+    loop(chunks, body)
     finish(chunks - 1, 1)
 
     def drain(p, _):
@@ -481,10 +572,9 @@
         rxc = [send(rx[k], PC) for k in sets]
         ryc = [send(ry[k], PC) for k in sets]
 
-        def group_cols(g):
-            return hcat([take_cols(w, n * g, n).reshape(w4, n * hd) for w, n in ((wq, 2), (wk, 1), (wv, 1))])
-
-        wq_own, wq_oth = group_cols(c), group_cols(co)
+        wr = w4 // 9
+        heads_of = lambda w: pl.BlockSpec((wr,) + w.shape[1:], lambda i, s: (i, 0, 0))
+        wq_own, wq_oth = call(split_kernel, (9,), [heads_of(w) for w in (wq, wk, wv)], [pl.BlockSpec((wr, 2 * gw), by_row)] * 2, [bf(w4, 2 * gw)] * 2, flops=w4 * gw)(scal, wq, wk, wv)
         wqs = [wq_own, send(wq_oth, PC), send(wq_own, PX), send(wq_oth, PXC)]
 
         wot = jnp.transpose(wo, (0, 2, 1))
@@ -512,8 +602,10 @@
         gu = {ab: gather(gu_half(x, at), gu_half(xo, at)) for ab, at in (('a', 0), ('b', F8))}
         wdt = wd.T
         dw_own, dw_oth = (take_cols(wdt, xx * F4, F4) for xx in (x, xo))
-        dw_early = dw_own[:, :F4 - KT]
-        dn_y, dn_o = gather(dw_own, dw_oth, dw_early)
+        dw_a, dw_b = dw_own[:, :KA], dw_own[:, KA:F4 - KT]
+        dn_y, dn_o = gather(dw_own, dw_oth, dw_a)
+        dwb = send(dw_b, PY)
+        dwb_c = send(dwb, PC)
 
         pos = take(positions, x, 1)[0]
         inv_freq = ROPE_BASE ** (-2.0 * jnp.arange(hd // 2, dtype=F32) / hd)
@@ -535,10 +627,10 @@
                 flops=D * S, aliases={8: 0} if k else None)(scal, xt, own_c, rx[k], rxc[k], ry[k], ryc[k], gcol, *a_all)]
         qv, kv = call(
             functools.partial(qkv_kernel, hd=hd), (nb,),
-            [pl.BlockSpec((D, tile), by_col)] + [whole(w4, 2 * gw)] * 4 + [pl.BlockSpec((hd // 2, tile), by_col)] * 2,
+            [pl.BlockSpec((D, tile), by_col)] + [ANY] * 4 + [pl.BlockSpec((hd // 2, tile), by_col)] * 2,
             [pl.BlockSpec((gw + hd, tile), by_col), pl.BlockSpec((tile, gw), by_row)],
             [bf(gw + hd, S), bf(S, gw)],
-            [vmem(2 * gw, D), vmem(D, 2 * gw)],
+            [vmem(2 * gw, D), vmem(D, 2 * gw), dma((4,))],
             flops=D * gw * S)(scal, *a_all, *wqs, cos_t, sin_t)
 
         bq = bk = tile
@@ -577,7 +669,7 @@
                     whole(D, 4)] + [ANY] * k,
                 [whole(D, quarter), pl.BlockSpec((quarter, D), lambda i, s, k=k: (k, 0))],
                 [bf(D, quarter), bf(oh, D)],
-                [vmem(4 * gw, quarter), vmem(D, quarter), vmem(len(Bs), heads, w4, hd), dma((len(Bs),))],
+                [vmem(4 * gw, quarter), vmem(D, quarter), vmem(len(Bs), heads, w4, hd), vmem(4, w4, quarter), vmem(4, w4, quarter, dtype=F32), dma((len(Bs),))],
                 flops=D * gw * half, aliases={18: 1} if k else None)(scal, o, o_c, o_y, o_yc, *Bs, xt, own_c, rx[k], rxc[k], gcol, *m_own)
             h_own.append(h)
             m_own = [m]
@@ -589,10 +681,8 @@
                 pl.BlockSpec((quarter, D), lambda i, s, k=k: (k, 0)), bf(oh, D), [vmem(D, quarter)],
                 flops=D * half, aliases={3: 0} if k else None)(scal, h_for[k], gcol, *m_for)]
 
-        ft = 384
-        nf = F8 // ft
-
-        def gated(ms, wsets):
+        def gated(ms, wsets, ft=128):
+            nf = F8 // ft
             groups, sets = len(ms), len(wsets)
             early = lambda i: jnp.minimum(i, nf - 1)
             late = lambda i: jnp.maximum(i - nf, 0)
@@ -608,42 +698,43 @@
         zy_for = gated(m_for, near)
         za_own = gated(m_own, [gua[1]])
         za_for = gated(m_for, [gua[1]])
-        zb = gated(m_own + m_for, [gub[1]])
+        zb = gated(m_own + m_for, [gub[1]], 3 * CH)
         w2 = 2 * w4
         chunks = oh // CH
         yt = 2 * CH
         part = call(
             down_y_kernel, (oh // yt,), [pl.BlockSpec((yt, F4), by_row)] * 2 + [whole(w4, F4)] * 4,
             pl.BlockSpec((2, D, yt), lambda i, s: (i, 0, 0)), f32(chunks, D, yt),
-            flops=D * F4 * half)(scal, zy_own, zy_for, *dn_y)
+            [vmem(D, F4)], flops=D * F4 * half)(scal, zy_own, zy_for, *dn_y)
         out = pl.pallas_call(
             functools.partial(tail_kernel, width=D, chunks=chunks),
             out_shape=bf(w4, rows),
-            in_specs=[ANY] * 14,
+            in_specs=[ANY] * 16,
             out_specs=ANY,
             scratch_shapes=[
                 vmem(D, F4), vmem(chunks, yt, F4), vmem(w2, 4, dtype=F32), vmem(3, D, yt, dtype=F32), vmem(chunks, w2, yt, dtype=F32),
                 *[vmem(chunks, w2, yt)] * 3, *[vmem(chunks, 2, 8, CH, dtype=F32)] * 2, vmem(2, 8, CH, dtype=F32),
-                dma((5,)), dma((chunks, 4)), dma((3,)), *[dma((chunks, 2))] * 6, *[dma((2,))] * 2, *[dma((chunks, 2, 3))] * 2],
+                dma((7,)), dma((chunks, 4)), dma((3,)), *[dma((chunks, 2))] * 6, *[dma((2,))] * 2, *[dma((chunks, 2, 3))] * 2],
             cost_estimate=pl.CostEstimate(flops=D * F4 * S, bytes_accessed=D * rows, transcendentals=0),
             compiler_params=pltpu.CompilerParams(vmem_limit_bytes=VM, collective_id=0, has_side_effects=True),
             name='tail',
-        )(part, za_own, za_for, zb, *dn_o, dw_own, *h_own, *h_for, gcol)
+        )(part, za_own, za_for, zb, *dn_o, dwb, dwb_c, dw_own, *h_own, *h_for, gcol)
         kv_c = send(kv, PC)
-        kv_sets = jnp.split(kv, [S - oh])
+        most = nb - per_half
+        kv_sets = jnp.split(kv, [most * tile // 2, most * tile])
         kv_x = [send(t, PX) for t in kv_sets]
-        kv_xc = [send(kv_x[k], PC) for k in sets]
+        kv_xc = [send(t, PC) for t in kv_x]
+        kt = tile // 2
         kv_outs = []
-        most = nb - per_half
-        for i, (t, tc, base, last) in enumerate(((kv, kv_c, 0, nb), (kv_x[0], kv_xc[0], 0, most // 2), (kv_x[0], kv_xc[0], most // 2, most), (kv_x[1], kv_xc[1], most, nb))):
+        for i, (t, tc, base, last) in enumerate(zip([kv] + kv_x, [kv_c] + kv_xc, (0, 0, most // 2, most), (nb, most // 2, most, nb))):
             extra = i == 3
-            n = last - base
-            kv_spec = pl.BlockSpec((tile, gw), lambda j, s, at=0 if extra else base: (at + j, 0))
-            at = lambda j, s, i=i, base=base: ((1 - s[0] if i else s[0]) * nb + base + j, 0, 0)
+            n = 2 * (last - base)
+            kv_spec = pl.BlockSpec((kt, gw), by_row)
+            at = lambda j, s, i=i, base=base: (((1 - s[0] if i else s[0]) * nb + base) * 2 + j, 0, 0)
             cspec = [cols(w4, rows // n, lambda i, s: i)] * extra
             kv_outs = call(
                 functools.partial(kv_out_kernel, extra=int(extra)), (n,), [kv_spec] * 2 + cspec + [ANY] * len(kv_outs),
-                [pl.BlockSpec((tile, 2, hd), at)] * 2 + cspec, [bf(rows, 2, hd)] * 2 + [bf(w4, rows)] * extra,
+                [pl.BlockSpec((kt, 2, hd), at)] * 2 + cspec, [bf(rows, 2, hd)] * 2 + [bf(w4, rows)] * extra,
                 flops=rows * gw, aliases={3 + extra: 0, 4 + extra: 1} if i else None)(scal, t, tc, *[out] * extra, *kv_outs)
         k_out, v_out, out = kv_outs
         return out.T, k_out, v_out

time: 901 us -> 998 us (1.11)
  waiting for transfers between devices: 322 us -> 396 us
  Pallas kernels: 464 us -> 502 us
  local copies, waits for them, and re-layouts: 52.5 us -> 39.3 us
    ppermute x56 -> x60, waiting for transfers between devices: 322 us -> 396 us  [send(): return lax.ppermute(a, ('tp', 'dm'), perm)]
    pallas_call x2, Pallas kernels: 44.7 us -> 54.8 us  [layer(): call(functools.partial(attn_kernel, bq=bq, bk=bk, q_block0=q0, scale=scal...]
    dynamic_slice x9 -> x7, local copies, waits for them, and re-layouts: 32.7 us -> 24.2 us  [take(): return lax.dynamic_slice_in_dim(a, start, size, axis)]
    ppermute x56 -> x60, starting transfers between devices: 41.4 us -> 45.9 us  [send(): return lax.ppermute(a, ('tp', 'dm'), perm)]
  transfers between devices with their start and end apart: 56 -> 60, of which waited for: 14 -> 18; matrix products, arithmetic and copies ran while one was open for 7% -> 5% of each run, Pallas kernels for 51% -> 49%
where the time goes in v5:
time: 998 us; the launch traced here: 997 us
  Pallas kernels  502 us (50%)
  waiting for transfers between devices  396 us (40%)
  starting transfers between devices  45.9 us (5%)
  local copies, waits for them, and re-layouts  39.3 us (4%)
  other arithmetic  12.6 us (1%)
    ppermute x60, waiting for transfers between devices, send(): return lax.ppermute(a, ('tp', 'dm'), perm)  396 us
    pallas_call x5, Pallas kernels, gated(): call(functools.partial(gate_up_kernel, groups=groups, sets=sets, steps=nf...  133 us
    pallas_call x1, Pallas kernels, layer(): pl.pallas_call(functools.partial(tail_kernel, width=D, chunks=chunks), ou...  127 us
    pallas_call x2, Pallas kernels, layer(): call(functools.partial(attn_kernel, bq=bq, bk=bk, q_block0=q0, scale=scal...  54.8 us
    ppermute x60, starting transfers between devices, send(): return lax.ppermute(a, ('tp', 'dm'), perm)  45.9 us
    pallas_call x4, Pallas kernels, layer(): call(functools.partial(kv_out_kernel, extra=int(extra)), (n,), [kv_spec]...  37 us
    pallas_call x1, Pallas kernels, layer(): call(down_y_kernel, (oh // yt,), [pl.BlockSpec((yt, F4), by_row)] * 2 + [...  34 us
    pallas_call x2, Pallas kernels, layer(): call(functools.partial(proj_kernel, width=D), (1,), [cols(gw, quarter, mi...  31.9 us
  transfers between devices with their start and end apart: 60, of which 18 were waited for; matrix products, arithmetic and copies ran while one was open for 5% of the time, Pallas kernels for 49%

profile of v5, /device:TPU:0, one launch (start us, length us, event | category | flops | bytes accessed | tf_op | source)
XLA Modules:
  0.0 996.9 jit_solution(4019363963237502390)
XLA Ops:
  0.7 3.2 dynamic-slice_bitcast_fusion.3
  3.9 3.3 collective-permute-start.1
  7.3 4.4 dynamic-slice_bitcast_fusion.1
  18.5 7.3 shard_map.150
  25.9 33.0 %collective-permute-done.6 = bf16[4,576]{1,0:T(4,128)(2,1)S(1)} collective-permute-done((bf16[4,576]{1,0:T(4,128)(2,1)S(1)}, bf16[4,576]{1,0:T(4,128)(2,1)S(1)}, u32[]{:S(2)}, u32[]{:S(2)}) %collective-permute-start.6) | collective-permute-done | bytes 4640 | tf_op jit(solution)/shard_map/ppermute | solution.py:535
  66.9 21.2 %collective-permute-done.13.w2 = bf16[576,1024]{1,0:T(8,128)(2,1)} collective-permute-done((bf16[576,1024]{1,0:T(8,128)(2,1)}, bf16[576,1024]{1,0:T(8,128)(2,1)}, u32[]{:S(2)}, u32[]{:S(2)}) %collective-permute-start.13) | collective-permute-done | bytes 1179680 | tf_op jit(solution)/shard_map/ppermute | solution.py:535
  89.8 5.1 dynamic-slice_bitcast_fusion
  94.9 17.7 %collective-permute-done.14.w3 = bf16[576,1024]{1,0:T(8,128)(2,1)} collective-permute-done((bf16[576,1024]{1,0:T(8,128)(2,1)}, bf16[576,1024]{1,0:T(8,128)(2,1)}, u32[]{:S(2)}, u32[]{:S(2)}) %collective-permute-start.14) | collective-permute-done | bytes 1179680 | tf_op jit(solution)/shard_map/ppermute | solution.py:535
  113.5 24.7 %collective-permute-done.21.b1 = bf16[4,576,256]{2,1,0:T(8,128)(2,1)} collective-permute-done((bf16[4,576,256]{2,1,0:T(8,128)(2,1)}, bf16[4,576,256]{2,1,0:T(8,128)(2,1)}, u32[]{:S(2)}, u32[]{:S(2)}) %collective-permute-start.21) | collective-permute-done | bytes 1179680 | tf_op jit(solution)/shard_map/ppermute | solution.py:535
  142.6 7.4 constant_dynamic-slice_fusion
  150.0 3.7 pad_maximum_fusion.refs_1_.refs_5_
  153.7 14.6 %collective-permute-done.3.ry = bf16[576,1024]{1,0:T(8,128)(2,1)} collective-permute-done((bf16[576,1024]{1,0:T(8,128)(2,1)}, bf16[576,1024]{1,0:T(8,128)(2,1)}, u32[]{:S(2)}, u32[]{:S(2)}) %collective-permute-start.3) | collective-permute-done | bytes 1179680 | tf_op jit(solution)/shard_map/ppermute | solution.py:535
  170.1 23.5 %collective-permute-done.10.ry = bf16[576,1024]{1,0:T(8,128)(2,1)} collective-permute-done((bf16[576,1024]{1,0:T(8,128)(2,1)}, bf16[576,1024]{1,0:T(8,128)(2,1)}, u32[]{:S(2)}, u32[]{:S(2)}) %collective-permute-start.10) | collective-permute-done | bytes 1179680 | tf_op jit(solution)/shard_map/ppermute | solution.py:535
  197.8 20.7 %collective-permute-done.25.b3 = bf16[4,576,256]{2,1,0:T(8,128)(2,1)} collective-permute-done((bf16[4,576,256]{2,1,0:T(8,128)(2,1)}, bf16[4,576,256]{2,1,0:T(8,128)(2,1)}, u32[]{:S(2)}, u32[]{:S(2)}) %collective-permute-start.25) | collective-permute-done | bytes 1179680 | tf_op jit(solution)/shard_map/ppermute | solution.py:535
  223.1 10.5 %shard_map.151 = (f32[128,4096]{1,0:T(8,128)}, f32[128,4096]{1,0:T(8,128)}) custom-call(s32[3]{0:T(128)} %pad_add_fusion.s_ref, s32[1,4096]{1,0:T(1,128)} %copy-done.9, f32[128,1]{1,0:T(8,128)} %multiply_power_fusion.freq_ref), custom_call_target="tpu_custom_call" | custom-call | flops 8388608 | tf_op jit(solution)/shard_map/pallas_call | solution.py:618
  234.4 3.4 pad_maximum_fusion.2.refs_9_.refs_13_
  239.9 11.7 %shard_map.148.rest_0_ = bf16[2304,4096]{1,0:T(8,128)(2,1)} custom-call(s32[3]{0:T(128)} %pad_add_fusion.s_ref, bf16[576,8192]{1,0:T(8,128)(2,1)} %bitcast.20, bf16[576,4096]{1,0:T(8,128)(2,1)} %collective-permute-done.own_c.x1, bf16[576,1024]{1,0:T(8,128)(2,1)} %collective-permute-done.8.rx.x2, bf16[576,1024]{1,0:T(8,128)(2,1)} %collective-permute-done.9.rxc.x3, ...), custom_call_target="tpu_custom_call" | custom-call | flops 9437184 | tf_op jit(solution)/shard_map/pallas_call | solution.py:623
  251.6 11.7 %shard_map.149.a_ref = bf16[2304,4096]{1,0:T(8,128)(2,1)} custom-call(s32[3]{0:T(128)} %pad_add_fusion.s_ref, bf16[576,8192]{1,0:T(8,128)(2,1)} %bitcast.21, bf16[576,4096]{1,0:T(8,128)(2,1)} %collective-permute-done.own_c.x1, bf16[576,1024]{1,0:T(8,128)(2,1)} %collective-permute-done.1.rx.x2, ...), custom_call_target="tpu_custom_call", output_to_operand_aliasing={{}: (8, {})} | custom-call | flops 9437184 | tf_op jit(solution)/shard_map/pallas_call | solution.py:623
  263.8 31.7 %shard_map.152 = (bf16[768,4096]{1,0:T(8,128)(2,1)}, bf16[4096,512]{1,0:T(8,128)(2,1)}) custom-call(s32[3]{0:T(128)} %pad_add_fusion.s_ref, bf16[2304,4096]{1,0:T(8,128)(2,1)} %shard_map.149.a_ref, bf16[576,1024]{1,0:T(8,128)(2,1)} %get-tuple-element.22.w0, bf16[576,1024]{1,0:T(8,128)(2,1)} %collective-permute-done.12.w1, ...), custom_call_target="tpu_custom_call" | custom-call | flops 4831838208 | tf_op jit(solution)/shard_map/pallas_call | solution.py:628
  295.5 35.9 %shard_map.153.o_own = bf16[512,2048]{1,0:T(8,128)(2,1)} custom-call(s32[8]{0:T(128)} %get-tuple-element.42.lo_ref, s32[8]{0:T(128)} %get-tuple-element.41.full_ref, bf16[768,4096]{1,0:T(8,128)(2,1)} %get-tuple-element.27.q_ref.v_ref, bf16[4096,512]{1,0:T(8,128)(2,1)} %get-tuple-element.26.k_ref.kv0, bf16[768,4096]{1,0:T(8,128)(2,1)} %get-tuple-element.27.q_ref.v_ref, ...), custom_call_target="tpu_custom_call" | custom-call | flops 4294967296 | tf_op jit(solution)/shard_map/pallas_call | solution.py:649
  336.5 18.9 %shard_map.154.o_own = bf16[512,2048]{1,0:T(8,128)(2,1)} custom-call(s32[8]{0:T(128)} %get-tuple-element.42.lo_ref, s32[8]{0:T(128)} %get-tuple-element.41.full_ref, bf16[768,4096]{1,0:T(8,128)(2,1)} %get-tuple-element.27.q_ref.v_ref, bf16[4096,512]{1,0:T(8,128)(2,1)} %get-tuple-element.26.k_ref.kv0, bf16[768,4096]{1,0:T(8,128)(2,1)} %get-tuple-element.27.q_ref.v_ref, ...), custom_call_target="tpu_custom_call" | custom-call | flops 2147483648 | tf_op jit(solution)/shard_map/pallas_call | solution.py:649
  361.0 2.9 collective-permute-start.39
  363.9 8.4 collective-permute-done.28.o_y
  372.3 9.5 collective-permute-done.29.o_yc
  382.8 15.9 %shard_map.155 = (bf16[2304,512]{1,0:T(8,128)(2,1)}, bf16[1024,2304]{1,0:T(8,128)(2,1)}) custom-call(s32[3]{0:T(128)} %pad_add_fusion.s_ref, bf16[512,2048]{1,0:T(8,128)(2,1)} %shard_map.154.o_own, bf16[512,512]{1,0:T(8,128)(2,1)} %collective-permute-done.27.o_c, bf16[512,512]{1,0:T(8,128)(2,1)} %collective-permute-done.28.o_y, ...), custom_call_target="tpu_custom_call" | custom-call | flops 2415919104 | tf_op jit(solution)/shard_map/pallas_call | solution.py:664
  398.7 15.9 %shard_map.156 = (bf16[2304,512]{1,0:T(8,128)(2,1)}, bf16[1024,2304]{1,0:T(8,128)(2,1)}) custom-call(s32[3]{0:T(128)} %pad_add_fusion.s_ref, bf16[512,2048]{1,0:T(8,128)(2,1)} %shard_map.153.o_own, bf16[512,512]{1,0:T(8,128)(2,1)} %copy-done.8, bf16[512,512]{1,0:T(8,128)(2,1)} %collective-permute-done.18.o_y, ...), custom_call_target="tpu_custom_call", output_to_operand_aliasing={{1}: (18, {})} | custom-call | flops 2415919104 | tf_op jit(solution)/shard_map/pallas_call | solution.py:664
  417.3 5.3 collective-permute-done.39.d2
  427.5 3.8 fusion
  431.3 41.9 %collective-permute-done.36.h_ref.hf1 = bf16[2304,512]{1,0:T(8,128)(2,1)} collective-permute-done((bf16[2304,512]{1,0:T(8,128)(2,1)}, bf16[2304,512]{1,0:T(8,128)(2,1)}, u32[]{:S(2)}, u32[]{:S(2)}) %collective-permute-start.36) | collective-permute-done | bytes 2359328 | tf_op jit(solution)/shard_map/ppermute | solution.py:535
  473.7 49.4 %collective-permute-done.37.h_ref.hf0 = bf16[2304,512]{1,0:T(8,128)(2,1)} collective-permute-done((bf16[2304,512]{1,0:T(8,128)(2,1)}, bf16[2304,512]{1,0:T(8,128)(2,1)}, u32[]{:S(2)}, u32[]{:S(2)}) %collective-permute-start.37) | collective-permute-done | bytes 2359328 | tf_op jit(solution)/shard_map/ppermute | solution.py:535
  523.1 32.9 %shard_map.157.zw = bf16[1024,2304]{1,0:T(8,128)(2,1)} custom-call(s32[3]{0:T(128)} %pad_add_fusion.s_ref, bf16[1024,2304]{1,0:T(8,128)(2,1)} %get-tuple-element.29.refs_0_, bf16[576,2304]{1,0:T(8,128)(2,1)} %pad_maximum_fusion.refs_1_.refs_5_, bf16[576,2304]{1,0:T(8,128)(2,1)} %collective-permute-done.30.refs_2_.refs_6_, ...), custom_call_target="tpu_custom_call" | custom-call | flops 21743271936 | tf_op jit(solution)/shard_map/pallas_call | solution.py:690
  556.0 6.0 shard_map.158.rest_0_
  561.9 6.0 shard_map.159.refs_0_.refs_1_
  568.6 28.5 %collective-permute-done.47.refs_4_.refs_8_ = bf16[576,2304]{1,0:T(8,128)(2,1)} collective-permute-done((bf16[576,2304]{1,0:T(8,128)(2,1)}, bf16[576,2304]{1,0:T(8,128)(2,1)}, u32[]{:S(2)}, u32[]{:S(2)}) %collective-permute-start.47) | collective-permute-done | bytes 2654240 | tf_op jit(solution)/shard_map/ppermute | solution.py:535
  597.2 32.9 %shard_map.160.zf = bf16[1024,2304]{1,0:T(8,128)(2,1)} custom-call(s32[3]{0:T(128)} %pad_add_fusion.s_ref, bf16[1024,2304]{1,0:T(8,128)(2,1)} %shard_map.159.refs_0_.refs_1_, bf16[576,2304]{1,0:T(8,128)(2,1)} %pad_maximum_fusion.refs_1_.refs_5_, bf16[576,2304]{1,0:T(8,128)(2,1)} %collective-permute-done.30.refs_2_.refs_6_, ...), custom_call_target="tpu_custom_call" | custom-call | flops 21743271936 | tf_op jit(solution)/shard_map/pallas_call | solution.py:690
  630.6 23.4 %collective-permute-done.43.refs_3_.refs_7_ = bf16[576,2304]{1,0:T(8,128)(2,1)} collective-permute-done((bf16[576,2304]{1,0:T(8,128)(2,1)}, bf16[576,2304]{1,0:T(8,128)(2,1)}, u32[]{:S(2)}, u32[]{:S(2)}) %collective-permute-start.43) | collective-permute-done | bytes 2654240 | tf_op jit(solution)/shard_map/ppermute | solution.py:535
  654.0 34.0 %shard_map.161.part = f32[8,2304,256]{2,1,0:T(8,128)} custom-call(s32[3]{0:T(128)} %pad_add_fusion.s_ref, bf16[1024,2304]{1,0:T(8,128)(2,1)} %shard_map.157.zw, bf16[1024,2304]{1,0:T(8,128)(2,1)} %shard_map.160.zf, bf16[576,2304]{1,0:T(8,128)(2,1)} %copy-done.2, bf16[576,2304]{1,0:T(8,128)(2,1)} %collective-permute-done.38.d1, ...), custom_call_target="tpu_custom_call" | custom-call | flops 10871635968 | tf_op jit(solution)/shard_map/pallas_call | solution.py:705
  688.5 20.2 %collective-permute-done.51.d2 = bf16[576,2304]{1,0:T(8,128)(2,1)} collective-permute-done((bf16[576,2304]{1,0:T(8,128)(2,1)}, bf16[576,2304]{1,0:T(8,128)(2,1)}, u32[]{:S(2)}, u32[]{:S(2)}) %collective-permute-start.51) | collective-permute-done | bytes 2654240 | tf_op jit(solution)/shard_map/ppermute | solution.py:535
  709.3 30.9 %shard_map.164.zb = bf16[2048,1152]{1,0:T(8,128)(2,1)} custom-call(s32[3]{0:T(128)} %pad_add_fusion.s_ref, bf16[1024,2304]{1,0:T(8,128)(2,1)} %get-tuple-element.29.refs_0_, bf16[1024,2304]{1,0:T(8,128)(2,1)} %shard_map.159.refs_0_.refs_1_, bf16[576,2304]{1,0:T(8,128)(2,1)} %collective-permute-done.45.refs_2_.refs_6_, ...), custom_call_target="tpu_custom_call" | custom-call | flops 21743271936 | tf_op jit(solution)/shard_map/pallas_call | solution.py:690
  743.7 18.1 %shard_map.162.zwa = bf16[1024,1152]{1,0:T(8,128)(2,1)} custom-call(s32[3]{0:T(128)} %pad_add_fusion.s_ref, bf16[1024,2304]{1,0:T(8,128)(2,1)} %get-tuple-element.29.refs_0_, bf16[576,2304]{1,0:T(8,128)(2,1)} %collective-permute-done.41.refs_1_.refs_5_, bf16[576,2304]{1,0:T(8,128)(2,1)} %collective-permute-done.42.refs_2_.refs_6_, ...), custom_call_target="tpu_custom_call" | custom-call | flops 10871635968 | tf_op jit(solution)/shard_map/pallas_call | solution.py:690
  761.7 17.9 %shard_map.163.zfa = bf16[1024,1152]{1,0:T(8,128)(2,1)} custom-call(s32[3]{0:T(128)} %pad_add_fusion.s_ref, bf16[1024,2304]{1,0:T(8,128)(2,1)} %shard_map.159.refs_0_.refs_1_, bf16[576,2304]{1,0:T(8,128)(2,1)} %collective-permute-done.41.refs_1_.refs_5_, bf16[576,2304]{1,0:T(8,128)(2,1)} %collective-permute-done.42.refs_2_.refs_6_, ...), custom_call_target="tpu_custom_call" | custom-call | flops 10871635968 | tf_op jit(solution)/shard_map/pallas_call | solution.py:690
  779.7 20.5 %collective-permute-done.55.kv0 = bf16[1536,512]{1,0:T(8,128)(2,1)} collective-permute-done((bf16[1536,512]{1,0:T(8,128)(2,1)}, bf16[1536,512]{1,0:T(8,128)(2,1)}, u32[]{:S(2)}, u32[]{:S(2)}) %collective-permute-start.55) | collective-permute-done | bytes 1572896 | tf_op jit(solution)/shard_map/ppermute | solution.py:535
  800.2 32.7 %collective-permute-done.57.kv0 = bf16[1536,512]{1,0:T(8,128)(2,1)} collective-permute-done((bf16[1536,512]{1,0:T(8,128)(2,1)}, bf16[1536,512]{1,0:T(8,128)(2,1)}, u32[]{:S(2)}, u32[]{:S(2)}) %collective-permute-start.57) | collective-permute-done | bytes 1572896 | tf_op jit(solution)/shard_map/ppermute | solution.py:535
  833.0 126.8 %tail.1.rest_0_ = bf16[576,8192]{1,0:T(8,128)(2,1)} custom-call(f32[8,2304,256]{2,1,0:T(8,128)} %shard_map.161.part, bf16[1024,1152]{1,0:T(8,128)(2,1)} %shard_map.162.zwa, bf16[1024,1152]{1,0:T(8,128)(2,1)} %shard_map.163.zfa, bf16[2048,1152]{1,0:T(8,128)(2,1)} %shard_map.164.zb, bf16[576,768]{1,0:T(8,128)(2,1)} %collective-permute-done.49.d0, ...), custom_call_target="tpu_custom_call" | custom-call | flops 21743271936 | bytes 18874368 | tf_op jit(solution)/shard_map/tail/pallas_call | solution.py:709
  959.8 14.2 %shard_map.165 = (bf16[8192,2,256]{2,1,0:T(2,128)(2,1)}, bf16[8192,2,256]{2,1,0:T(2,128)(2,1)}) custom-call(s32[3]{0:T(128)} %pad_add_fusion.s_ref, bf16[4096,512]{1,0:T(8,128)(2,1)} %get-tuple-element.26.k_ref.kv0, bf16[4096,512]{1,0:T(8,128)(2,1)} %collective-permute-done.59.kv1), custom_call_target="tpu_custom_call" | custom-call | flops 4194304 | tf_op jit(solution)/shard_map/pallas_call | solution.py:735
  974.0 6.5 shard_map.166
  980.5 6.5 shard_map.167
  987.0 9.8 shard_map.168
  (154 shorter events, 61.4 us)
Async XLA Ops:
  3.9 56.9 %collective-permute-start.1 = (bf16[576,1024]{1,0:T(8,128)(2,1)}, bf16[576,1024]{1,0:T(8,128)(2,1)}, u32[]{:S(2)}, u32[]{:S(2)}) collective-permute-start(bf16[576,1024]{1,0:T(8,128)(2,1)} %get-tuple-element.44), channel_id=1, source_target_pairs={{0,2},{1,3},{2,0},{3,1},{4,6},{5,7},{6,4},{7,5}} | collective-permute-start | bytes 3538952 | tf_op jit(solution)/shard_map/ppermute | solution.py:535
  7.2 53.8 %collective-permute-start.8 = (bf16[576,1024]{1,0:T(8,128)(2,1)}, bf16[576,1024]{1,0:T(8,128)(2,1)}, u32[]{:S(2)}, u32[]{:S(2)}) collective-permute-start(bf16[576,1024]{1,0:T(8,128)(2,1)} %get-tuple-element.43), channel_id=1, source_target_pairs={{0,2},{1,3},{2,0},{3,1},{4,6},{5,7},{6,4},{7,5}} | collective-permute-start | bytes 3538952 | tf_op jit(solution)/shard_map/ppermute | solution.py:535
  13.3 47.4 %collective-permute-start.49 = (bf16[576,768]{1,0:T(8,128)(2,1)S(1)}, bf16[576,768]{1,0:T(8,128)(2,1)}, u32[]{:S(2)}, u32[]{:S(2)}) collective-permute-start(bf16[576,768]{1,0:T(8,128)(2,1)S(1)} %slice.18), channel_id=1, source_target_pairs={{0,4},{1,5},{2,6},{3,7},{4,0},{5,1},{6,2},{7,3}} | collective-permute-start | bytes 2654216 | tf_op jit(solution)/shard_map/ppermute | solution.py:535
  15.4 43.5 %collective-permute-start.6 = (bf16[4,576]{1,0:T(4,128)(2,1)S(1)}, bf16[4,576]{1,0:T(4,128)(2,1)S(1)}, u32[]{:S(2)}, u32[]{:S(2)}) collective-permute-start(bf16[4,576]{1,0:T(4,128)(2,1)S(1)} %pad_maximum_fusion.4), channel_id=1, source_target_pairs={{0,2},{1,3},{2,0},{3,1},{4,6},{5,7},{6,4},{7,5}} | collective-permute-start | bytes 13832 | tf_op jit(solution)/shard_map/ppermute | solution.py:535
  17.0 41.9 %collective-permute-start.7 = (bf16[4,576]{1,0:T(4,128)(2,1)S(1)}, bf16[4,576]{1,0:T(4,128)(2,1)S(1)}, u32[]{:S(2)}, u32[]{:S(2)}) collective-permute-start(bf16[4,576]{1,0:T(4,128)(2,1)S(1)} %pad_maximum_fusion.4), channel_id=1, source_target_pairs={{0,3},{1,2},{2,1},{3,0},{4,7},{5,6},{6,5},{7,4}} | collective-permute-start | bytes 13832 | tf_op jit(solution)/shard_map/ppermute | solution.py:535
  58.9 29.2 %collective-permute-start.13 = (bf16[576,1024]{1,0:T(8,128)(2,1)}, bf16[576,1024]{1,0:T(8,128)(2,1)}, u32[]{:S(2)}, u32[]{:S(2)}) collective-permute-start(bf16[576,1024]{1,0:T(8,128)(2,1)} %get-tuple-element.22.w0), channel_id=1, source_target_pairs={{0,2},{1,3},{2,0},{3,1},{4,6},{5,7},{6,4},{7,5}} | collective-permute-start | bytes 3538952 | tf_op jit(solution)/shard_map/ppermute | solution.py:535
  60.6 52.0 %collective-permute-start.14 = (bf16[576,1024]{1,0:T(8,128)(2,1)}, bf16[576,1024]{1,0:T(8,128)(2,1)}, u32[]{:S(2)}, u32[]{:S(2)}) collective-permute-start(bf16[576,1024]{1,0:T(8,128)(2,1)} %get-tuple-element.23), channel_id=1, source_target_pairs={{0,3},{1,2},{2,1},{3,0},{4,7},{5,6},{6,5},{7,4}} | collective-permute-start | bytes 3538952 | tf_op jit(solution)/shard_map/ppermute | solution.py:535
  60.8 52.7 %collective-permute-start.20 = (bf16[4,576,256]{2,1,0:T(8,128)(2,1)}, bf16[4,576,256]{2,1,0:T(8,128)(2,1)S(1)}, u32[]{:S(2)}, u32[]{:S(2)}) collective-permute-start(bf16[4,576,256]{2,1,0:T(8,128)(2,1)} %bitcast.31), channel_id=1, source_target_pairs={{0,1},{1,0},{2,3},{3,2},{4,5},{5,4},{6,7},{7,6}} | collective-permute-start | bytes 3538952 | tf_op jit(solution)/shard_map/ppermute | solution.py:535
  61.1 77.1 %collective-permute-start.21 = (bf16[4,576,256]{2,1,0:T(8,128)(2,1)}, bf16[4,576,256]{2,1,0:T(8,128)(2,1)}, u32[]{:S(2)}, u32[]{:S(2)}) collective-permute-start(bf16[4,576,256]{2,1,0:T(8,128)(2,1)} %bitcast.32), channel_id=1, source_target_pairs={{0,2},{1,3},{2,0},{3,1},{4,6},{5,7},{6,4},{7,5}} | collective-permute-start | bytes 3538952 | tf_op jit(solution)/shard_map/ppermute | solution.py:535
  65.4 72.8 %collective-permute-start.23 = (bf16[4,576,256]{2,1,0:T(8,128)(2,1)S(1)}, bf16[4,576,256]{2,1,0:T(8,128)(2,1)S(1)}, u32[]{:S(2)}, u32[]{:S(2)}) collective-permute-start(bf16[4,576,256]{2,1,0:T(8,128)(2,1)S(1)} %bitcast.35), channel_id=1, source_target_pairs={{0,4},{1,5},{2,6},{3,7},{4,0},{5,1},{6,2},{7,3}} | collective-permute-start | bytes 3538952 | tf_op jit(solution)/shard_map/ppermute | solution.py:535
  88.1 52.9 %collective-permute-start.53 = (bf16[576,1280]{1,0:T(8,128)(2,1)}, bf16[576,1280]{1,0:T(8,128)(2,1)}, u32[]{:S(2)}, u32[]{:S(2)}) collective-permute-start(bf16[576,1280]{1,0:T(8,128)(2,1)} %slice.19), channel_id=1, source_target_pairs={{0,4},{1,5},{2,6},{3,7},{4,0},{5,1},{6,2},{7,3}} | collective-permute-start | bytes 4423688 | tf_op jit(solution)/shard_map/ppermute | solution.py:535
  112.6 125.3 %collective-permute-start = (bf16[576,4096]{1,0:T(8,128)(2,1)}, bf16[576,4096]{1,0:T(8,128)(2,1)}, u32[]{:S(2)}, u32[]{:S(2)}) collective-permute-start(bf16[576,4096]{1,0:T(8,128)(2,1)} %dynamic-slice_bitcast_fusion), channel_id=1, source_target_pairs={{0,1},{1,0},{2,3},{3,2},{4,5},{5,4},{6,7},{7,6}} | collective-permute-start | bytes 14155784 | tf_op jit(solution)/shard_map/ppermute | solution.py:535
  139.2 29.2 %collective-permute-start.3 = (bf16[576,1024]{1,0:T(8,128)(2,1)}, bf16[576,1024]{1,0:T(8,128)(2,1)}, u32[]{:S(2)}, u32[]{:S(2)}) collective-permute-start(bf16[576,1024]{1,0:T(8,128)(2,1)} %collective-permute-done.1.rx.x2), channel_id=1, source_target_pairs={{0,4},{1,5},{2,6},{3,7},{4,0},{5,1},{6,2},{7,3}} | collective-permute-start | bytes 3538952 | tf_op jit(solution)/shard_map/ppermute | solution.py:535
  141.2 52.4 %collective-permute-start.10 = (bf16[576,1024]{1,0:T(8,128)(2,1)}, bf16[576,1024]{1,0:T(8,128)(2,1)}, u32[]{:S(2)}, u32[]{:S(2)}) collective-permute-start(bf16[576,1024]{1,0:T(8,128)(2,1)} %collective-permute-done.8.rx.x2), channel_id=1, source_target_pairs={{0,4},{1,5},{2,6},{3,7},{4,0},{5,1},{6,2},{7,3}} | collective-permute-start | bytes 3538952 | tf_op jit(solution)/shard_map/ppermute | solution.py:535
  142.6 51.1 %collective-permute-start.22 = (bf16[4,576,256]{2,1,0:T(8,128)(2,1)}, bf16[4,576,256]{2,1,0:T(8,128)(2,1)}, u32[]{:S(2)}, u32[]{:S(2)}) collective-permute-start(bf16[4,576,256]{2,1,0:T(8,128)(2,1)} %collective-permute-done.21.b1), channel_id=1, source_target_pairs={{0,1},{1,0},{2,3},{3,2},{4,5},{5,4},{6,7},{7,6}} | collective-permute-start | bytes 3538952 | tf_op jit(solution)/shard_map/ppermute | solution.py:535
  168.4 95.0 %collective-permute-start.30 = (bf16[576,2304]{1,0:T(8,128)(2,1)}, bf16[576,2304]{1,0:T(8,128)(2,1)}, u32[]{:S(2)}, u32[]{:S(2)}) collective-permute-start(bf16[576,2304]{1,0:T(8,128)(2,1)} %pad_maximum_fusion.refs_1_.refs_5_), channel_id=1, source_target_pairs={{0,1},{1,0},{2,3},{3,2},{4,5},{5,4},{6,7},{7,6}} | collective-permute-start | bytes 7962632 | tf_op jit(solution)/shard_map/ppermute | solution.py:535
  168.4 50.1 %collective-permute-start.25 = (bf16[4,576,256]{2,1,0:T(8,128)(2,1)}, bf16[4,576,256]{2,1,0:T(8,128)(2,1)}, u32[]{:S(2)}, u32[]{:S(2)}) collective-permute-start(bf16[4,576,256]{2,1,0:T(8,128)(2,1)} %collective-permute-done.21.b1), channel_id=1, source_target_pairs={{0,4},{1,5},{2,6},{3,7},{4,0},{5,1},{6,2},{7,3}} | collective-permute-start | bytes 3538952 | tf_op jit(solution)/shard_map/ppermute | solution.py:535
  193.7 39.9 %collective-permute-start.11 = (bf16[576,1024]{1,0:T(8,128)(2,1)}, bf16[576,1024]{1,0:T(8,128)(2,1)}, u32[]{:S(2)}, u32[]{:S(2)}) collective-permute-start(bf16[576,1024]{1,0:T(8,128)(2,1)} %collective-permute-done.10.ry), channel_id=1, source_target_pairs={{0,1},{1,0},{2,3},{3,2},{4,5},{5,4},{6,7},{7,6}} | collective-permute-start | bytes 3538952 | tf_op jit(solution)/shard_map/ppermute | solution.py:535
  218.5 115.4 %collective-permute-start.31 = (bf16[576,2304]{1,0:T(8,128)(2,1)}, bf16[576,2304]{1,0:T(8,128)(2,1)}, u32[]{:S(2)}, u32[]{:S(2)}) collective-permute-start(bf16[576,2304]{1,0:T(8,128)(2,1)} %pad_maximum_fusion.1), channel_id=1, source_target_pairs={{0,2},{1,3},{2,0},{3,1},{4,6},{5,7},{6,4},{7,5}} | collective-permute-start | bytes 7962632 | tf_op jit(solution)/shard_map/ppermute | solution.py:535
  220.2 114.6 %collective-permute-start.34 = (bf16[576,2304]{1,0:T(8,128)(2,1)}, bf16[576,2304]{1,0:T(8,128)(2,1)}, u32[]{:S(2)}, u32[]{:S(2)}) collective-permute-start(bf16[576,2304]{1,0:T(8,128)(2,1)} %pad_maximum_fusion.3), channel_id=1, source_target_pairs={{0,2},{1,3},{2,0},{3,1},{4,6},{5,7},{6,4},{7,5}} | collective-permute-start | bytes 7962632 | tf_op jit(solution)/shard_map/ppermute | solution.py:535
  233.6 29.7 %collective-permute-start.24 = (bf16[4,576,256]{2,1,0:T(8,128)(2,1)}, bf16[4,576,256]{2,1,0:T(8,128)(2,1)}, u32[]{:S(2)}, u32[]{:S(2)}) collective-permute-start(bf16[4,576,256]{2,1,0:T(8,128)(2,1)} %copy-done.7), channel_id=1, source_target_pairs={{0,1},{1,0},{2,3},{3,2},{4,5},{5,4},{6,7},{7,6}} | collective-permute-start | bytes 3538952 | tf_op jit(solution)/shard_map/ppermute | solution.py:535
  237.9 98.6 %collective-permute-start.26 = (bf16[4,576,256]{2,1,0:T(8,128)(2,1)}, bf16[4,576,256]{2,1,0:T(8,128)(2,1)}, u32[]{:S(2)}, u32[]{:S(2)}) collective-permute-start(bf16[4,576,256]{2,1,0:T(8,128)(2,1)} %collective-permute-done.25.b3), channel_id=1, source_target_pairs={{0,1},{1,0},{2,3},{3,2},{4,5},{5,4},{6,7},{7,6}} | collective-permute-start | bytes 3538952 | tf_op jit(solution)/shard_map/ppermute | solution.py:535
  263.3 154.0 %collective-permute-start.38 = (bf16[576,2304]{1,0:T(8,128)(2,1)}, bf16[576,2304]{1,0:T(8,128)(2,1)}, u32[]{:S(2)}, u32[]{:S(2)}) collective-permute-start(bf16[576,2304]{1,0:T(8,128)(2,1)} %copy-done.2), channel_id=1, source_target_pairs={{0,1},{1,0},{2,3},{3,2},{4,5},{5,4},{6,7},{7,6}} | collective-permute-start | bytes 7962632 | tf_op jit(solution)/shard_map/ppermute | solution.py:535
  263.3 151.3 %collective-permute-start.33 = (bf16[576,2304]{1,0:T(8,128)(2,1)}, bf16[576,2304]{1,0:T(8,128)(2,1)}, u32[]{:S(2)}, u32[]{:S(2)}) collective-permute-start(bf16[576,2304]{1,0:T(8,128)(2,1)} %pad_maximum_fusion.2.refs_9_.refs_13_), channel_id=1, source_target_pairs={{0,1},{1,0},{2,3},{3,2},{4,5},{5,4},{6,7},{7,6}} | collective-permute-start | bytes 7962632 | tf_op jit(solution)/shard_map/ppermute | solution.py:535
  361.0 61.6 %collective-permute-start.39 = (bf16[576,2304]{1,0:T(8,128)(2,1)}, bf16[576,2304]{1,0:T(8,128)(2,1)}, u32[]{:S(2)}, u32[]{:S(2)}) collective-permute-start(bf16[576,2304]{1,0:T(8,128)(2,1)} %get-tuple-element.45), channel_id=1, source_target_pairs={{0,2},{1,3},{2,0},{3,1},{4,6},{5,7},{6,4},{7,5}} | collective-permute-start | bytes 7962632 | tf_op jit(solution)/shard_map/ppermute | solution.py:535
  372.3 50.8 %collective-permute-start.32 = (bf16[576,2304]{1,0:T(8,128)(2,1)}, bf16[576,2304]{1,0:T(8,128)(2,1)}, u32[]{:S(2)}, u32[]{:S(2)}) collective-permute-start(bf16[576,2304]{1,0:T(8,128)(2,1)} %collective-permute-done.31.refs_3_.refs_7_), channel_id=1, source_target_pairs={{0,1},{1,0},{2,3},{3,2},{4,5},{5,4},{6,7},{7,6}} | collective-permute-start | bytes 7962632 | tf_op jit(solution)/shard_map/ppermute | solution.py:535
  381.8 42.9 %collective-permute-start.35 = (bf16[576,2304]{1,0:T(8,128)(2,1)}, bf16[576,2304]{1,0:T(8,128)(2,1)}, u32[]{:S(2)}, u32[]{:S(2)}) collective-permute-start(bf16[576,2304]{1,0:T(8,128)(2,1)} %collective-permute-done.34.refs_11_.refs_15_), channel_id=1, source_target_pairs={{0,1},{1,0},{2,3},{3,2},{4,5},{5,4},{6,7},{7,6}} | collective-permute-start | bytes 7962632 | tf_op jit(solution)/shard_map/ppermute | solution.py:535
  414.7 58.5 %collective-permute-start.36 = (bf16[2304,512]{1,0:T(8,128)(2,1)}, bf16[2304,512]{1,0:T(8,128)(2,1)}, u32[]{:S(2)}, u32[]{:S(2)}) collective-permute-start(bf16[2304,512]{1,0:T(8,128)(2,1)} %get-tuple-element.30.hw1), channel_id=1, source_target_pairs={{0,2},{1,3},{2,0},{3,1},{4,6},{5,7},{6,4},{7,5}} | collective-permute-start | bytes 7077896 | tf_op jit(solution)/shard_map/ppermute | solution.py:535
  417.3 105.8 %collective-permute-start.37 = (bf16[2304,512]{1,0:T(8,128)(2,1)}, bf16[2304,512]{1,0:T(8,128)(2,1)}, u32[]{:S(2)}, u32[]{:S(2)}) collective-permute-start(bf16[2304,512]{1,0:T(8,128)(2,1)} %get-tuple-element.31.hw0), channel_id=1, source_target_pairs={{0,2},{1,3},{2,0},{3,1},{4,6},{5,7},{6,4},{7,5}} | collective-permute-start | bytes 7077896 | tf_op jit(solution)/shard_map/ppermute | solution.py:535
  422.6 145.2 %collective-permute-start.41 = (bf16[576,2304]{1,0:T(8,128)(2,1)}, bf16[576,2304]{1,0:T(8,128)(2,1)}, u32[]{:S(2)}, u32[]{:S(2)}) collective-permute-start(bf16[576,2304]{1,0:T(8,128)(2,1)} %pad_maximum_fusion.refs_1_.refs_5_), channel_id=1, source_target_pairs={{0,4},{1,5},{2,6},{3,7},{4,0},{5,1},{6,2},{7,3}} | collective-permute-start | bytes 7962632 | tf_op jit(solution)/shard_map/ppermute | solution.py:535
  423.1 145.3 %collective-permute-start.45 = (bf16[576,2304]{1,0:T(8,128)(2,1)}, bf16[576,2304]{1,0:T(8,128)(2,1)}, u32[]{:S(2)}, u32[]{:S(2)}) collective-permute-start(bf16[576,2304]{1,0:T(8,128)(2,1)} %pad_maximum_fusion.2.refs_9_.refs_13_), channel_id=1, source_target_pairs={{0,4},{1,5},{2,6},{3,7},{4,0},{5,1},{6,2},{7,3}} | collective-permute-start | bytes 7962632 | tf_op jit(solution)/shard_map/ppermute | solution.py:535
  424.7 172.5 %collective-permute-start.47 = (bf16[576,2304]{1,0:T(8,128)(2,1)}, bf16[576,2304]{1,0:T(8,128)(2,1)}, u32[]{:S(2)}, u32[]{:S(2)}) collective-permute-start(bf16[576,2304]{1,0:T(8,128)(2,1)} %collective-permute-done.34.refs_11_.refs_15_), channel_id=1, source_target_pairs={{0,4},{1,5},{2,6},{3,7},{4,0},{5,1},{6,2},{7,3}} | collective-permute-start | bytes 7962632 | tf_op jit(solution)/shard_map/ppermute | solution.py:535
  473.2 180.8 %collective-permute-start.43 = (bf16[576,2304]{1,0:T(8,128)(2,1)}, bf16[576,2304]{1,0:T(8,128)(2,1)}, u32[]{:S(2)}, u32[]{:S(2)}) collective-permute-start(bf16[576,2304]{1,0:T(8,128)(2,1)} %collective-permute-done.31.refs_3_.refs_7_), channel_id=1, source_target_pairs={{0,4},{1,5},{2,6},{3,7},{4,0},{5,1},{6,2},{7,3}} | collective-permute-start | bytes 7962632 | tf_op jit(solution)/shard_map/ppermute | solution.py:535
  523.1 107.0 %collective-permute-start.40 = (bf16[576,2304]{1,0:T(8,128)(2,1)}, bf16[576,2304]{1,0:T(8,128)(2,1)}, u32[]{:S(2)}, u32[]{:S(2)}) collective-permute-start(bf16[576,2304]{1,0:T(8,128)(2,1)} %collective-permute-done.39.d2), channel_id=1, source_target_pairs={{0,1},{1,0},{2,3},{3,2},{4,5},{5,4},{6,7},{7,6}} | collective-permute-start | bytes 7962632 | tf_op jit(solution)/shard_map/ppermute | solution.py:535
  567.9 140.9 %collective-permute-start.51 = (bf16[576,2304]{1,0:T(8,128)(2,1)}, bf16[576,2304]{1,0:T(8,128)(2,1)}, u32[]{:S(2)}, u32[]{:S(2)}) collective-permute-start(bf16[576,2304]{1,0:T(8,128)(2,1)} %collective-permute-done.39.d2), channel_id=1, source_target_pairs={{0,4},{1,5},{2,6},{3,7},{4,0},{5,1},{6,2},{7,3}} | collective-permute-start | bytes 7962632 | tf_op jit(solution)/shard_map/ppermute | solution.py:535
  568.4 119.6 %collective-permute-start.46 = (bf16[576,2304]{1,0:T(8,128)(2,1)}, bf16[576,2304]{1,0:T(8,128)(2,1)}, u32[]{:S(2)}, u32[]{:S(2)}) collective-permute-start(bf16[576,2304]{1,0:T(8,128)(2,1)} %collective-permute-done.45.refs_2_.refs_6_), channel_id=1, source_target_pairs={{0,1},{1,0},{2,3},{3,2},{4,5},{5,4},{6,7},{7,6}} | collective-permute-start | bytes 7962632 | tf_op jit(solution)/shard_map/ppermute | solution.py:535
  597.2 111.6 %collective-permute-start.48 = (bf16[576,2304]{1,0:T(8,128)(2,1)}, bf16[576,2304]{1,0:T(8,128)(2,1)}, u32[]{:S(2)}, u32[]{:S(2)}) collective-permute-start(bf16[576,2304]{1,0:T(8,128)(2,1)} %collective-permute-done.47.refs_4_.refs_8_), channel_id=1, source_target_pairs={{0,1},{1,0},{2,3},{3,2},{4,5},{5,4},{6,7},{7,6}} | collective-permute-start | bytes 7962632 | tf_op jit(solution)/shard_map/ppermute | solution.py:535
  630.1 111.6 %collective-permute-start.42 = (bf16[576,2304]{1,0:T(8,128)(2,1)}, bf16[576,2304]{1,0:T(8,128)(2,1)}, u32[]{:S(2)}, u32[]{:S(2)}) collective-permute-start(bf16[576,2304]{1,0:T(8,128)(2,1)} %collective-permute-done.41.refs_1_.refs_5_), channel_id=1, source_target_pairs={{0,1},{1,0},{2,3},{3,2},{4,5},{5,4},{6,7},{7,6}} | collective-permute-start | bytes 7962632 | tf_op jit(solution)/shard_map/ppermute | solution.py:535
  654.0 88.2 %collective-permute-start.44 = (bf16[576,2304]{1,0:T(8,128)(2,1)}, bf16[576,2304]{1,0:T(8,128)(2,1)}, u32[]{:S(2)}, u32[]{:S(2)}) collective-permute-start(bf16[576,2304]{1,0:T(8,128)(2,1)} %collective-permute-done.43.refs_3_.refs_7_), channel_id=1, source_target_pairs={{0,1},{1,0},{2,3},{3,2},{4,5},{5,4},{6,7},{7,6}} | collective-permute-start | bytes 7962632 | tf_op jit(solution)/shard_map/ppermute | solution.py:535
  688.0 52.1 %collective-permute-start.54 = (bf16[576,1280]{1,0:T(8,128)(2,1)}, bf16[576,1280]{1,0:T(8,128)(2,1)}, u32[]{:S(2)}, u32[]{:S(2)}) collective-permute-start(bf16[576,1280]{1,0:T(8,128)(2,1)} %collective-permute-done.53.e0), channel_id=1, source_target_pairs={{0,1},{1,0},{2,3},{3,2},{4,5},{5,4},{6,7},{7,6}} | collective-permute-start | bytes 4423688 | tf_op jit(solution)/shard_map/ppermute | solution.py:535
  708.7 251.0 %collective-permute-start.59 = (bf16[4096,512]{1,0:T(8,128)(2,1)}, bf16[4096,512]{1,0:T(8,128)(2,1)}, u32[]{:S(2)}, u32[]{:S(2)}) collective-permute-start(bf16[4096,512]{1,0:T(8,128)(2,1)} %get-tuple-element.26.k_ref.kv0), channel_id=1, source_target_pairs={{0,1},{1,0},{2,3},{3,2},{4,5},{5,4},{6,7},{7,6}} | collective-permute-start | bytes 12582920 | tf_op jit(solution)/shard_map/ppermute | solution.py:535
  708.7 124.2 %collective-permute-start.52 = (bf16[576,2304]{1,0:T(8,128)(2,1)}, bf16[576,2304]{1,0:T(8,128)(2,1)}, u32[]{:S(2)}, u32[]{:S(2)}) collective-permute-start(bf16[576,2304]{1,0:T(8,128)(2,1)} %collective-permute-done.51.d2), channel_id=1, source_target_pairs={{0,1},{1,0},{2,3},{3,2},{4,5},{5,4},{6,7},{7,6}} | collective-permute-start | bytes 7962632 | tf_op jit(solution)/shard_map/ppermute | solution.py:535
  740.2 39.5 %collective-permute-start.15 = (bf16[1024,512]{1,0:T(8,128)(2,1)}, bf16[1024,512]{1,0:T(8,128)(2,1)}, u32[]{:S(2)}, u32[]{:S(2)}) collective-permute-start(bf16[1024,512]{1,0:T(8,128)(2,1)} %split.9), channel_id=1, source_target_pairs={{0,2},{1,3},{2,0},{3,1},{4,6},{5,7},{6,4},{7,5}} | collective-permute-start | bytes 3145736 | tf_op jit(solution)/shard_map/ppermute | solution.py:535
  741.7 58.6 %collective-permute-start.55 = (bf16[1536,512]{1,0:T(8,128)(2,1)}, bf16[1536,512]{1,0:T(8,128)(2,1)}, u32[]{:S(2)}, u32[]{:S(2)}) collective-permute-start(bf16[1536,512]{1,0:T(8,128)(2,1)} %get-tuple-element.56), channel_id=1, source_target_pairs={{0,2},{1,3},{2,0},{3,1},{4,6},{5,7},{6,4},{7,5}} | collective-permute-start | bytes 4718600 | tf_op jit(solution)/shard_map/ppermute | solution.py:535
  742.2 90.8 %collective-permute-start.57 = (bf16[1536,512]{1,0:T(8,128)(2,1)}, bf16[1536,512]{1,0:T(8,128)(2,1)}, u32[]{:S(2)}, u32[]{:S(2)}) collective-permute-start(bf16[1536,512]{1,0:T(8,128)(2,1)} %get-tuple-element.55), channel_id=1, source_target_pairs={{0,2},{1,3},{2,0},{3,1},{4,6},{5,7},{6,4},{7,5}} | collective-permute-start | bytes 4718600 | tf_op jit(solution)/shard_map/ppermute | solution.py:535
  779.7 207.3 %collective-permute-start.16 = (bf16[1024,512]{1,0:T(8,128)(2,1)}, bf16[1024,512]{1,0:T(8,128)(2,1)}, u32[]{:S(2)}, u32[]{:S(2)}) collective-permute-start(bf16[1024,512]{1,0:T(8,128)(2,1)} %collective-permute-done.15.kv0), channel_id=1, source_target_pairs={{0,1},{1,0},{2,3},{3,2},{4,5},{5,4},{6,7},{7,6}} | collective-permute-start | bytes 3145736 | tf_op jit(solution)/shard_map/ppermute | solution.py:535
  800.2 180.2 %collective-permute-start.56 = (bf16[1536,512]{1,0:T(8,128)(2,1)}, bf16[1536,512]{1,0:T(8,128)(2,1)}, u32[]{:S(2)}, u32[]{:S(2)}) collective-permute-start(bf16[1536,512]{1,0:T(8,128)(2,1)} %collective-permute-done.55.kv0), channel_id=1, source_target_pairs={{0,1},{1,0},{2,3},{3,2},{4,5},{5,4},{6,7},{7,6}} | collective-permute-start | bytes 4718600 | tf_op jit(solution)/shard_map/ppermute | solution.py:535
  833.0 141.0 %collective-permute-start.58 = (bf16[1536,512]{1,0:T(8,128)(2,1)}, bf16[1536,512]{1,0:T(8,128)(2,1)}, u32[]{:S(2)}, u32[]{:S(2)}) collective-permute-start(bf16[1536,512]{1,0:T(8,128)(2,1)} %collective-permute-done.57.kv0), channel_id=1, source_target_pairs={{0,1},{1,0},{2,3},{3,2},{4,5},{5,4},{6,7},{7,6}} | collective-permute-start | bytes 4718600 | tf_op jit(solution)/shard_map/ppermute | solution.py:535
  (27 other events, 644.0 us)

commit v6 on v5

--- a/solution.py
+++ b/solution.py
@@ -20,7 +20,7 @@
 BIG = 2.0 ** 40
 SHRINK = 2.0 ** -88
 MT = 256
-KT = 256
+KT = 384
 KA = 768
 ANY = pl.BlockSpec(memory_space=pl.ANY)
 
@@ -300,19 +300,25 @@
         z_ref[r:r + MT, :] = (jax.nn.gelu(g, approximate=True) * u).astype(BF)
 
 
-def down_y_kernel(s_ref, zw, zf, d0, d1, d2, d3, acc_ref, d_ref):
+def down_y_kernel(s_ref, zw, zf, d0, d1, d2, d3, acc_ref, d_ref, d_sem):
     w4 = d0.shape[0]
     n = zw.shape[0]
-
-    @pl.when(pl.program_id(0) == 0)
+    at_start = pl.program_id(0) == 0
+
+    @pl.when(at_start)
     def _():
         for j, dd in enumerate((d0, d1, d2, d3)):
-            part_of(d_ref, j, w4)[...] = dd[...]
+            pltpu.make_async_copy(dd, part_of(d_ref, j, w4), d_sem.at[j]).start()
 
     z = vcat([zw[...], zf[...]])
 
     def rows(j, _):
         at = block_of(j, w4)
+
+        @pl.when(at_start)
+        def _():
+            pltpu.make_async_copy(d0, d_ref.at[at, :], d_sem.at[j]).wait()
+
         t = dot_nt(d_ref[at, :], z)
         for q in range(n // CH):
             acc_ref[q, at, :CH] = t[:, q * CH:(q + 1) * CH]
@@ -616,7 +622,7 @@
         per_half = nt // 2
         nb = S // tile
         cos_t, sin_t = call(
-            rope_kernel, (nb,), [pl.BlockSpec((1, tile), by_col), whole(hd // 2, 1)], [pl.BlockSpec((hd // 2, tile), by_col)] * 2,
+            rope_kernel, (S // MT,), [pl.BlockSpec((1, MT), by_col), whole(hd // 2, 1)], [pl.BlockSpec((hd // 2, MT), by_col)] * 2,
             [f32(hd // 2, S)] * 2, flops=hd * S * nb)(scal, pos_row, inv_freq.reshape(hd // 2, 1))
         a_all = []
         for k in sets:
@@ -703,9 +709,9 @@
         chunks = oh // CH
         yt = 2 * CH
         part = call(
-            down_y_kernel, (oh // yt,), [pl.BlockSpec((yt, F4), by_row)] * 2 + [whole(w4, F4)] * 4,
+            down_y_kernel, (oh // yt,), [pl.BlockSpec((yt, F4), by_row)] * 2 + [ANY] * 4,
             pl.BlockSpec((2, D, yt), lambda i, s: (i, 0, 0)), f32(chunks, D, yt),
-            [vmem(D, F4)], flops=D * F4 * half)(scal, zy_own, zy_for, *dn_y)
+            [vmem(D, F4), dma((4,))], flops=D * F4 * half)(scal, zy_own, zy_for, *dn_y)
         out = pl.pallas_call(
             functools.partial(tail_kernel, width=D, chunks=chunks),
             out_shape=bf(w4, rows),
@@ -724,13 +730,14 @@
         kv_sets = jnp.split(kv, [most * tile // 2, most * tile])
         kv_x = [send(t, PX) for t in kv_sets]
         kv_xc = [send(t, PC) for t in kv_x]
-        kt = tile // 2
         kv_outs = []
         for i, (t, tc, base, last) in enumerate(zip([kv] + kv_x, [kv_c] + kv_xc, (0, 0, most // 2, most), (nb, most // 2, most, nb))):
             extra = i == 3
-            n = 2 * (last - base)
+            cut = 2 if i == 0 else 1
+            kt = tile // cut
+            n = cut * (last - base)
             kv_spec = pl.BlockSpec((kt, gw), by_row)
-            at = lambda j, s, i=i, base=base: (((1 - s[0] if i else s[0]) * nb + base) * 2 + j, 0, 0)
+            at = lambda j, s, i=i, base=base, cut=cut: (((1 - s[0] if i else s[0]) * nb + base) * cut + j, 0, 0)
             cspec = [cols(w4, rows // n, lambda i, s: i)] * extra
             kv_outs = call(
                 functools.partial(kv_out_kernel, extra=int(extra)), (n,), [kv_spec] * 2 + cspec + [ANY] * len(kv_outs),

time: 998 us -> 997 us (level)
  no operation moved by 1% of the time
where the time goes in v6:
time: 997 us; the launch traced here: 996 us
  Pallas kernels  499 us (50%)
  waiting for transfers between devices  399 us (40%)
  starting transfers between devices  45.5 us (5%)
  local copies, waits for them, and re-layouts  39.2 us (4%)
  other arithmetic  12.5 us (1%)
    ppermute x60, waiting for transfers between devices, send(): return lax.ppermute(a, ('tp', 'dm'), perm)  399 us
    pallas_call x5, Pallas kernels, gated(): call(functools.partial(gate_up_kernel, groups=groups, sets=sets, steps=nf...  133 us
    pallas_call x1, Pallas kernels, layer(): pl.pallas_call(functools.partial(tail_kernel, width=D, chunks=chunks), ou...  127 us
    pallas_call x2, Pallas kernels, layer(): call(functools.partial(attn_kernel, bq=bq, bk=bk, q_block0=q0, scale=scal...  54.8 us
    ppermute x60, starting transfers between devices, send(): return lax.ppermute(a, ('tp', 'dm'), perm)  45.5 us
    pallas_call x4, Pallas kernels, layer(): call(functools.partial(kv_out_kernel, extra=int(extra)), (n,), [kv_spec]...  34 us
    pallas_call x1, Pallas kernels, layer(): call(down_y_kernel, (oh // yt,), [pl.BlockSpec((yt, F4), by_row)] * 2 + [...  32 us
    pallas_call x2, Pallas kernels, layer(): call(functools.partial(proj_kernel, width=D), (1,), [cols(gw, quarter, mi...  31.9 us
  transfers between devices with their start and end apart: 60, of which 18 were waited for; matrix products, arithmetic and copies ran while one was open for 5% of the time, Pallas kernels for 49%

profile of v6, /device:TPU:0, one launch (start us, length us, event | category | flops | bytes accessed | tf_op | source)
XLA Modules:
  0.0 995.8 jit_solution(1482885719855608779)
XLA Ops:
  0.7 3.2 dynamic-slice_bitcast_fusion.3
  3.9 3.3 collective-permute-start.1
  7.3 4.4 dynamic-slice_bitcast_fusion.1
  18.5 7.3 shard_map.150
  25.8 33.1 %collective-permute-done.6 = bf16[4,576]{1,0:T(4,128)(2,1)S(1)} collective-permute-done((bf16[4,576]{1,0:T(4,128)(2,1)S(1)}, bf16[4,576]{1,0:T(4,128)(2,1)S(1)}, u32[]{:S(2)}, u32[]{:S(2)}) %collective-permute-start.6) | collective-permute-done | bytes 4640 | tf_op jit(solution)/shard_map/ppermute | solution.py:541
  66.8 21.2 %collective-permute-done.13.w2 = bf16[576,1024]{1,0:T(8,128)(2,1)} collective-permute-done((bf16[576,1024]{1,0:T(8,128)(2,1)}, bf16[576,1024]{1,0:T(8,128)(2,1)}, u32[]{:S(2)}, u32[]{:S(2)}) %collective-permute-start.13) | collective-permute-done | bytes 1179680 | tf_op jit(solution)/shard_map/ppermute | solution.py:541
  89.8 5.1 dynamic-slice_bitcast_fusion
  94.9 17.7 %collective-permute-done.14.w3 = bf16[576,1024]{1,0:T(8,128)(2,1)} collective-permute-done((bf16[576,1024]{1,0:T(8,128)(2,1)}, bf16[576,1024]{1,0:T(8,128)(2,1)}, u32[]{:S(2)}, u32[]{:S(2)}) %collective-permute-start.14) | collective-permute-done | bytes 1179680 | tf_op jit(solution)/shard_map/ppermute | solution.py:541
  113.5 24.7 %collective-permute-done.21.b1 = bf16[4,576,256]{2,1,0:T(8,128)(2,1)} collective-permute-done((bf16[4,576,256]{2,1,0:T(8,128)(2,1)}, bf16[4,576,256]{2,1,0:T(8,128)(2,1)}, u32[]{:S(2)}, u32[]{:S(2)}) %collective-permute-start.21) | collective-permute-done | bytes 1179680 | tf_op jit(solution)/shard_map/ppermute | solution.py:541
  142.6 7.4 constant_dynamic-slice_fusion
  150.0 3.7 pad_maximum_fusion.refs_1_.refs_5_
  153.7 14.6 %collective-permute-done.3.ry = bf16[576,1024]{1,0:T(8,128)(2,1)} collective-permute-done((bf16[576,1024]{1,0:T(8,128)(2,1)}, bf16[576,1024]{1,0:T(8,128)(2,1)}, u32[]{:S(2)}, u32[]{:S(2)}) %collective-permute-start.3) | collective-permute-done | bytes 1179680 | tf_op jit(solution)/shard_map/ppermute | solution.py:541
  170.1 23.5 %collective-permute-done.10.ry = bf16[576,1024]{1,0:T(8,128)(2,1)} collective-permute-done((bf16[576,1024]{1,0:T(8,128)(2,1)}, bf16[576,1024]{1,0:T(8,128)(2,1)}, u32[]{:S(2)}, u32[]{:S(2)}) %collective-permute-start.10) | collective-permute-done | bytes 1179680 | tf_op jit(solution)/shard_map/ppermute | solution.py:541
  197.8 20.7 %collective-permute-done.25.b3 = bf16[4,576,256]{2,1,0:T(8,128)(2,1)} collective-permute-done((bf16[4,576,256]{2,1,0:T(8,128)(2,1)}, bf16[4,576,256]{2,1,0:T(8,128)(2,1)}, u32[]{:S(2)}, u32[]{:S(2)}) %collective-permute-start.25) | collective-permute-done | bytes 1179680 | tf_op jit(solution)/shard_map/ppermute | solution.py:541
  223.1 12.3 %shard_map.151 = (f32[128,4096]{1,0:T(8,128)}, f32[128,4096]{1,0:T(8,128)}) custom-call(s32[3]{0:T(128)} %pad_add_fusion.s_ref, s32[1,4096]{1,0:T(1,128)} %copy-done.9, f32[128,1]{1,0:T(8,128)} %multiply_power_fusion.freq_ref), custom_call_target="tpu_custom_call" | custom-call | flops 8388608 | tf_op jit(solution)/shard_map/pallas_call | solution.py:624
  236.3 3.4 pad_maximum_fusion.2.refs_9_.refs_13_
  241.8 11.7 %shard_map.148.rest_0_ = bf16[2304,4096]{1,0:T(8,128)(2,1)} custom-call(s32[3]{0:T(128)} %pad_add_fusion.s_ref, bf16[576,8192]{1,0:T(8,128)(2,1)} %bitcast.20, bf16[576,4096]{1,0:T(8,128)(2,1)} %collective-permute-done.own_c.x1, bf16[576,1024]{1,0:T(8,128)(2,1)} %collective-permute-done.8.rx.x2, bf16[576,1024]{1,0:T(8,128)(2,1)} %collective-permute-done.9.rxc.x3, ...), custom_call_target="tpu_custom_call" | custom-call | flops 9437184 | tf_op jit(solution)/shard_map/pallas_call | solution.py:629
  253.4 11.7 %shard_map.149.a_ref = bf16[2304,4096]{1,0:T(8,128)(2,1)} custom-call(s32[3]{0:T(128)} %pad_add_fusion.s_ref, bf16[576,8192]{1,0:T(8,128)(2,1)} %bitcast.21, bf16[576,4096]{1,0:T(8,128)(2,1)} %collective-permute-done.own_c.x1, bf16[576,1024]{1,0:T(8,128)(2,1)} %collective-permute-done.1.rx.x2, ...), custom_call_target="tpu_custom_call", output_to_operand_aliasing={{}: (8, {})} | custom-call | flops 9437184 | tf_op jit(solution)/shard_map/pallas_call | solution.py:629
  265.7 31.7 %shard_map.152 = (bf16[768,4096]{1,0:T(8,128)(2,1)}, bf16[4096,512]{1,0:T(8,128)(2,1)}) custom-call(s32[3]{0:T(128)} %pad_add_fusion.s_ref, bf16[2304,4096]{1,0:T(8,128)(2,1)} %shard_map.149.a_ref, bf16[576,1024]{1,0:T(8,128)(2,1)} %get-tuple-element.22.w0, bf16[576,1024]{1,0:T(8,128)(2,1)} %collective-permute-done.12.w1, ...), custom_call_target="tpu_custom_call" | custom-call | flops 4831838208 | tf_op jit(solution)/shard_map/pallas_call | solution.py:634
  297.4 35.9 %shard_map.153.o_own = bf16[512,2048]{1,0:T(8,128)(2,1)} custom-call(s32[8]{0:T(128)} %get-tuple-element.42.lo_ref, s32[8]{0:T(128)} %get-tuple-element.41.full_ref, bf16[768,4096]{1,0:T(8,128)(2,1)} %get-tuple-element.27.q_ref.v_ref, bf16[4096,512]{1,0:T(8,128)(2,1)} %get-tuple-element.26.k_ref.kv0, bf16[768,4096]{1,0:T(8,128)(2,1)} %get-tuple-element.27.q_ref.v_ref, ...), custom_call_target="tpu_custom_call" | custom-call | flops 4294967296 | tf_op jit(solution)/shard_map/pallas_call | solution.py:655
  337.7 18.9 %shard_map.154.o_own = bf16[512,2048]{1,0:T(8,128)(2,1)} custom-call(s32[8]{0:T(128)} %get-tuple-element.42.lo_ref, s32[8]{0:T(128)} %get-tuple-element.41.full_ref, bf16[768,4096]{1,0:T(8,128)(2,1)} %get-tuple-element.27.q_ref.v_ref, bf16[4096,512]{1,0:T(8,128)(2,1)} %get-tuple-element.26.k_ref.kv0, bf16[768,4096]{1,0:T(8,128)(2,1)} %get-tuple-element.27.q_ref.v_ref, ...), custom_call_target="tpu_custom_call" | custom-call | flops 2147483648 | tf_op jit(solution)/shard_map/pallas_call | solution.py:655
  365.8 7.6 collective-permute-done.28.o_y
  373.3 10.4 %collective-permute-done.29.o_yc = bf16[512,512]{1,0:T(8,128)(2,1)} collective-permute-done((bf16[512,512]{1,0:T(8,128)(2,1)S(1)}, bf16[512,512]{1,0:T(8,128)(2,1)}, u32[]{:S(2)}, u32[]{:S(2)}) %collective-permute-start.29) | collective-permute-done | bytes 524320 | tf_op jit(solution)/shard_map/ppermute | solution.py:541
  384.3 15.9 %shard_map.155 = (bf16[2304,512]{1,0:T(8,128)(2,1)}, bf16[1024,2304]{1,0:T(8,128)(2,1)}) custom-call(s32[3]{0:T(128)} %pad_add_fusion.s_ref, bf16[512,2048]{1,0:T(8,128)(2,1)} %shard_map.154.o_own, bf16[512,512]{1,0:T(8,128)(2,1)} %collective-permute-done.27.o_c, bf16[512,512]{1,0:T(8,128)(2,1)} %collective-permute-done.28.o_y, ...), custom_call_target="tpu_custom_call" | custom-call | flops 2415919104 | tf_op jit(solution)/shard_map/pallas_call | solution.py:670
  400.2 15.9 %shard_map.156 = (bf16[2304,512]{1,0:T(8,128)(2,1)}, bf16[1024,2304]{1,0:T(8,128)(2,1)}) custom-call(s32[3]{0:T(128)} %pad_add_fusion.s_ref, bf16[512,2048]{1,0:T(8,128)(2,1)} %shard_map.153.o_own, bf16[512,512]{1,0:T(8,128)(2,1)} %copy-done.8, bf16[512,512]{1,0:T(8,128)(2,1)} %collective-permute-done.18.o_y, ...), custom_call_target="tpu_custom_call", output_to_operand_aliasing={{1}: (18, {})} | custom-call | flops 2415919104 | tf_op jit(solution)/shard_map/pallas_call | solution.py:670
  416.2 3.0 collective-permute-start.36
  419.2 5.3 collective-permute-done.39.d2
  429.3 3.8 fusion
  433.1 41.9 %collective-permute-done.36.h_ref.hf1 = bf16[2304,512]{1,0:T(8,128)(2,1)} collective-permute-done((bf16[2304,512]{1,0:T(8,128)(2,1)}, bf16[2304,512]{1,0:T(8,128)(2,1)}, u32[]{:S(2)}, u32[]{:S(2)}) %collective-permute-start.36) | collective-permute-done | bytes 2359328 | tf_op jit(solution)/shard_map/ppermute | solution.py:541
  475.6 49.4 %collective-permute-done.37.h_ref.hf0 = bf16[2304,512]{1,0:T(8,128)(2,1)} collective-permute-done((bf16[2304,512]{1,0:T(8,128)(2,1)}, bf16[2304,512]{1,0:T(8,128)(2,1)}, u32[]{:S(2)}, u32[]{:S(2)}) %collective-permute-start.37) | collective-permute-done | bytes 2359328 | tf_op jit(solution)/shard_map/ppermute | solution.py:541
  524.9 32.9 %shard_map.157.zw = bf16[1024,2304]{1,0:T(8,128)(2,1)} custom-call(s32[3]{0:T(128)} %pad_add_fusion.s_ref, bf16[1024,2304]{1,0:T(8,128)(2,1)} %get-tuple-element.29.refs_0_, bf16[576,2304]{1,0:T(8,128)(2,1)} %pad_maximum_fusion.refs_1_.refs_5_, bf16[576,2304]{1,0:T(8,128)(2,1)} %collective-permute-done.30.refs_2_.refs_6_, ...), custom_call_target="tpu_custom_call" | custom-call | flops 21743271936 | tf_op jit(solution)/shard_map/pallas_call | solution.py:696
  557.8 6.0 shard_map.158.rest_0_
  563.8 6.0 shard_map.159.refs_0_.refs_1_
  570.5 28.5 %collective-permute-done.47.refs_4_.refs_8_ = bf16[576,2304]{1,0:T(8,128)(2,1)} collective-permute-done((bf16[576,2304]{1,0:T(8,128)(2,1)}, bf16[576,2304]{1,0:T(8,128)(2,1)}, u32[]{:S(2)}, u32[]{:S(2)}) %collective-permute-start.47) | collective-permute-done | bytes 2654240 | tf_op jit(solution)/shard_map/ppermute | solution.py:541
  599.0 32.9 %shard_map.160.zf = bf16[1024,2304]{1,0:T(8,128)(2,1)} custom-call(s32[3]{0:T(128)} %pad_add_fusion.s_ref, bf16[1024,2304]{1,0:T(8,128)(2,1)} %shard_map.159.refs_0_.refs_1_, bf16[576,2304]{1,0:T(8,128)(2,1)} %pad_maximum_fusion.refs_1_.refs_5_, bf16[576,2304]{1,0:T(8,128)(2,1)} %collective-permute-done.30.refs_2_.refs_6_, ...), custom_call_target="tpu_custom_call" | custom-call | flops 21743271936 | tf_op jit(solution)/shard_map/pallas_call | solution.py:696
  632.5 23.4 %collective-permute-done.43.refs_3_.refs_7_ = bf16[576,2304]{1,0:T(8,128)(2,1)} collective-permute-done((bf16[576,2304]{1,0:T(8,128)(2,1)}, bf16[576,2304]{1,0:T(8,128)(2,1)}, u32[]{:S(2)}, u32[]{:S(2)}) %collective-permute-start.43) | collective-permute-done | bytes 2654240 | tf_op jit(solution)/shard_map/ppermute | solution.py:541
  655.9 32.0 %shard_map.161.part = f32[8,2304,256]{2,1,0:T(8,128)} custom-call(s32[3]{0:T(128)} %pad_add_fusion.s_ref, bf16[1024,2304]{1,0:T(8,128)(2,1)} %shard_map.157.zw, bf16[1024,2304]{1,0:T(8,128)(2,1)} %shard_map.160.zf, bf16[576,2304]{1,0:T(8,128)(2,1)} %copy-done.2, bf16[576,2304]{1,0:T(8,128)(2,1)} %collective-permute-done.38.d1, ...), custom_call_target="tpu_custom_call" | custom-call | flops 10871635968 | tf_op jit(solution)/shard_map/pallas_call | solution.py:711
  688.5 22.1 %collective-permute-done.51.d2 = bf16[576,2304]{1,0:T(8,128)(2,1)} collective-permute-done((bf16[576,2304]{1,0:T(8,128)(2,1)}, bf16[576,2304]{1,0:T(8,128)(2,1)}, u32[]{:S(2)}, u32[]{:S(2)}) %collective-permute-start.51) | collective-permute-done | bytes 2654240 | tf_op jit(solution)/shard_map/ppermute | solution.py:541
  711.1 30.9 %shard_map.164.zb = bf16[2048,1152]{1,0:T(8,128)(2,1)} custom-call(s32[3]{0:T(128)} %pad_add_fusion.s_ref, bf16[1024,2304]{1,0:T(8,128)(2,1)} %get-tuple-element.29.refs_0_, bf16[1024,2304]{1,0:T(8,128)(2,1)} %shard_map.159.refs_0_.refs_1_, bf16[576,2304]{1,0:T(8,128)(2,1)} %collective-permute-done.45.refs_2_.refs_6_, ...), custom_call_target="tpu_custom_call" | custom-call | flops 21743271936 | tf_op jit(solution)/shard_map/pallas_call | solution.py:696
  745.5 18.1 %shard_map.162.zwa = bf16[1024,1152]{1,0:T(8,128)(2,1)} custom-call(s32[3]{0:T(128)} %pad_add_fusion.s_ref, bf16[1024,2304]{1,0:T(8,128)(2,1)} %get-tuple-element.29.refs_0_, bf16[576,2304]{1,0:T(8,128)(2,1)} %collective-permute-done.41.refs_1_.refs_5_, bf16[576,2304]{1,0:T(8,128)(2,1)} %collective-permute-done.42.refs_2_.refs_6_, ...), custom_call_target="tpu_custom_call" | custom-call | flops 10871635968 | tf_op jit(solution)/shard_map/pallas_call | solution.py:696
  763.6 17.9 %shard_map.163.zfa = bf16[1024,1152]{1,0:T(8,128)(2,1)} custom-call(s32[3]{0:T(128)} %pad_add_fusion.s_ref, bf16[1024,2304]{1,0:T(8,128)(2,1)} %shard_map.159.refs_0_.refs_1_, bf16[576,2304]{1,0:T(8,128)(2,1)} %collective-permute-done.41.refs_1_.refs_5_, bf16[576,2304]{1,0:T(8,128)(2,1)} %collective-permute-done.42.refs_2_.refs_6_, ...), custom_call_target="tpu_custom_call" | custom-call | flops 10871635968 | tf_op jit(solution)/shard_map/pallas_call | solution.py:696
  781.5 20.5 %collective-permute-done.55.kv0 = bf16[1536,512]{1,0:T(8,128)(2,1)} collective-permute-done((bf16[1536,512]{1,0:T(8,128)(2,1)}, bf16[1536,512]{1,0:T(8,128)(2,1)}, u32[]{:S(2)}, u32[]{:S(2)}) %collective-permute-start.55) | collective-permute-done | bytes 1572896 | tf_op jit(solution)/shard_map/ppermute | solution.py:541
  802.1 32.7 %collective-permute-done.57.kv0 = bf16[1536,512]{1,0:T(8,128)(2,1)} collective-permute-done((bf16[1536,512]{1,0:T(8,128)(2,1)}, bf16[1536,512]{1,0:T(8,128)(2,1)}, u32[]{:S(2)}, u32[]{:S(2)}) %collective-permute-start.57) | collective-permute-done | bytes 1572896 | tf_op jit(solution)/shard_map/ppermute | solution.py:541
  834.8 126.8 %tail.1.rest_0_ = bf16[576,8192]{1,0:T(8,128)(2,1)} custom-call(f32[8,2304,256]{2,1,0:T(8,128)} %shard_map.161.part, bf16[1024,1152]{1,0:T(8,128)(2,1)} %shard_map.162.zwa, bf16[1024,1152]{1,0:T(8,128)(2,1)} %shard_map.163.zfa, bf16[2048,1152]{1,0:T(8,128)(2,1)} %shard_map.164.zb, bf16[576,768]{1,0:T(8,128)(2,1)} %collective-permute-done.49.d0, ...), custom_call_target="tpu_custom_call" | custom-call | flops 21743271936 | bytes 18874368 | tf_op jit(solution)/shard_map/tail/pallas_call | solution.py:715
  961.6 14.2 %shard_map.165 = (bf16[8192,2,256]{2,1,0:T(2,128)(2,1)}, bf16[8192,2,256]{2,1,0:T(2,128)(2,1)}) custom-call(s32[3]{0:T(128)} %pad_add_fusion.s_ref, bf16[4096,512]{1,0:T(8,128)(2,1)} %get-tuple-element.26.k_ref.kv0, bf16[4096,512]{1,0:T(8,128)(2,1)} %collective-permute-done.59.kv1), custom_call_target="tpu_custom_call" | custom-call | flops 4194304 | tf_op jit(solution)/shard_map/pallas_call | solution.py:742
  975.8 5.7 shard_map.166
  981.5 5.7 shard_map.167
  987.2 8.4 shard_map.168
  (154 shorter events, 61.1 us)
Async XLA Ops:
  3.9 56.9 %collective-permute-start.1 = (bf16[576,1024]{1,0:T(8,128)(2,1)}, bf16[576,1024]{1,0:T(8,128)(2,1)}, u32[]{:S(2)}, u32[]{:S(2)}) collective-permute-start(bf16[576,1024]{1,0:T(8,128)(2,1)} %get-tuple-element.44), channel_id=1, source_target_pairs={{0,2},{1,3},{2,0},{3,1},{4,6},{5,7},{6,4},{7,5}} | collective-permute-start | bytes 3538952 | tf_op jit(solution)/shard_map/ppermute | solution.py:541
  7.2 53.8 %collective-permute-start.8 = (bf16[576,1024]{1,0:T(8,128)(2,1)}, bf16[576,1024]{1,0:T(8,128)(2,1)}, u32[]{:S(2)}, u32[]{:S(2)}) collective-permute-start(bf16[576,1024]{1,0:T(8,128)(2,1)} %get-tuple-element.43), channel_id=1, source_target_pairs={{0,2},{1,3},{2,0},{3,1},{4,6},{5,7},{6,4},{7,5}} | collective-permute-start | bytes 3538952 | tf_op jit(solution)/shard_map/ppermute | solution.py:541
  13.3 47.4 %collective-permute-start.49 = (bf16[576,768]{1,0:T(8,128)(2,1)S(1)}, bf16[576,768]{1,0:T(8,128)(2,1)}, u32[]{:S(2)}, u32[]{:S(2)}) collective-permute-start(bf16[576,768]{1,0:T(8,128)(2,1)S(1)} %slice.18), channel_id=1, source_target_pairs={{0,4},{1,5},{2,6},{3,7},{4,0},{5,1},{6,2},{7,3}} | collective-permute-start | bytes 2654216 | tf_op jit(solution)/shard_map/ppermute | solution.py:541
  15.4 43.5 %collective-permute-start.6 = (bf16[4,576]{1,0:T(4,128)(2,1)S(1)}, bf16[4,576]{1,0:T(4,128)(2,1)S(1)}, u32[]{:S(2)}, u32[]{:S(2)}) collective-permute-start(bf16[4,576]{1,0:T(4,128)(2,1)S(1)} %pad_maximum_fusion.4), channel_id=1, source_target_pairs={{0,2},{1,3},{2,0},{3,1},{4,6},{5,7},{6,4},{7,5}} | collective-permute-start | bytes 13832 | tf_op jit(solution)/shard_map/ppermute | solution.py:541
  17.0 41.9 %collective-permute-start.7 = (bf16[4,576]{1,0:T(4,128)(2,1)S(1)}, bf16[4,576]{1,0:T(4,128)(2,1)S(1)}, u32[]{:S(2)}, u32[]{:S(2)}) collective-permute-start(bf16[4,576]{1,0:T(4,128)(2,1)S(1)} %pad_maximum_fusion.4), channel_id=1, source_target_pairs={{0,3},{1,2},{2,1},{3,0},{4,7},{5,6},{6,5},{7,4}} | collective-permute-start | bytes 13832 | tf_op jit(solution)/shard_map/ppermute | solution.py:541
  58.9 29.2 %collective-permute-start.13 = (bf16[576,1024]{1,0:T(8,128)(2,1)}, bf16[576,1024]{1,0:T(8,128)(2,1)}, u32[]{:S(2)}, u32[]{:S(2)}) collective-permute-start(bf16[576,1024]{1,0:T(8,128)(2,1)} %get-tuple-element.22.w0), channel_id=1, source_target_pairs={{0,2},{1,3},{2,0},{3,1},{4,6},{5,7},{6,4},{7,5}} | collective-permute-start | bytes 3538952 | tf_op jit(solution)/shard_map/ppermute | solution.py:541
  60.6 52.0 %collective-permute-start.14 = (bf16[576,1024]{1,0:T(8,128)(2,1)}, bf16[576,1024]{1,0:T(8,128)(2,1)}, u32[]{:S(2)}, u32[]{:S(2)}) collective-permute-start(bf16[576,1024]{1,0:T(8,128)(2,1)} %get-tuple-element.23), channel_id=1, source_target_pairs={{0,3},{1,2},{2,1},{3,0},{4,7},{5,6},{6,5},{7,4}} | collective-permute-start | bytes 3538952 | tf_op jit(solution)/shard_map/ppermute | solution.py:541
  60.8 52.7 %collective-permute-start.20 = (bf16[4,576,256]{2,1,0:T(8,128)(2,1)}, bf16[4,576,256]{2,1,0:T(8,128)(2,1)S(1)}, u32[]{:S(2)}, u32[]{:S(2)}) collective-permute-start(bf16[4,576,256]{2,1,0:T(8,128)(2,1)} %bitcast.31), channel_id=1, source_target_pairs={{0,1},{1,0},{2,3},{3,2},{4,5},{5,4},{6,7},{7,6}} | collective-permute-start | bytes 3538952 | tf_op jit(solution)/shard_map/ppermute | solution.py:541
  61.1 77.1 %collective-permute-start.21 = (bf16[4,576,256]{2,1,0:T(8,128)(2,1)}, bf16[4,576,256]{2,1,0:T(8,128)(2,1)}, u32[]{:S(2)}, u32[]{:S(2)}) collective-permute-start(bf16[4,576,256]{2,1,0:T(8,128)(2,1)} %bitcast.32), channel_id=1, source_target_pairs={{0,2},{1,3},{2,0},{3,1},{4,6},{5,7},{6,4},{7,5}} | collective-permute-start | bytes 3538952 | tf_op jit(solution)/shard_map/ppermute | solution.py:541
  65.3 72.9 %collective-permute-start.23 = (bf16[4,576,256]{2,1,0:T(8,128)(2,1)S(1)}, bf16[4,576,256]{2,1,0:T(8,128)(2,1)S(1)}, u32[]{:S(2)}, u32[]{:S(2)}) collective-permute-start(bf16[4,576,256]{2,1,0:T(8,128)(2,1)S(1)} %bitcast.35), channel_id=1, source_target_pairs={{0,4},{1,5},{2,6},{3,7},{4,0},{5,1},{6,2},{7,3}} | collective-permute-start | bytes 3538952 | tf_op jit(solution)/shard_map/ppermute | solution.py:541
  88.1 52.9 %collective-permute-start.53 = (bf16[576,1152]{1,0:T(8,128)(2,1)}, bf16[576,1152]{1,0:T(8,128)(2,1)}, u32[]{:S(2)}, u32[]{:S(2)}) collective-permute-start(bf16[576,1152]{1,0:T(8,128)(2,1)} %slice.19), channel_id=1, source_target_pairs={{0,4},{1,5},{2,6},{3,7},{4,0},{5,1},{6,2},{7,3}} | collective-permute-start | bytes 3981320 | tf_op jit(solution)/shard_map/ppermute | solution.py:541
  112.6 127.2 %collective-permute-start = (bf16[576,4096]{1,0:T(8,128)(2,1)}, bf16[576,4096]{1,0:T(8,128)(2,1)}, u32[]{:S(2)}, u32[]{:S(2)}) collective-permute-start(bf16[576,4096]{1,0:T(8,128)(2,1)} %dynamic-slice_bitcast_fusion), channel_id=1, source_target_pairs={{0,1},{1,0},{2,3},{3,2},{4,5},{5,4},{6,7},{7,6}} | collective-permute-start | bytes 14155784 | tf_op jit(solution)/shard_map/ppermute | solution.py:541
  139.2 29.2 %collective-permute-start.3 = (bf16[576,1024]{1,0:T(8,128)(2,1)}, bf16[576,1024]{1,0:T(8,128)(2,1)}, u32[]{:S(2)}, u32[]{:S(2)}) collective-permute-start(bf16[576,1024]{1,0:T(8,128)(2,1)} %collective-permute-done.1.rx.x2), channel_id=1, source_target_pairs={{0,4},{1,5},{2,6},{3,7},{4,0},{5,1},{6,2},{7,3}} | collective-permute-start | bytes 3538952 | tf_op jit(solution)/shard_map/ppermute | solution.py:541
  141.2 52.4 %collective-permute-start.10 = (bf16[576,1024]{1,0:T(8,128)(2,1)}, bf16[576,1024]{1,0:T(8,128)(2,1)}, u32[]{:S(2)}, u32[]{:S(2)}) collective-permute-start(bf16[576,1024]{1,0:T(8,128)(2,1)} %collective-permute-done.8.rx.x2), channel_id=1, source_target_pairs={{0,4},{1,5},{2,6},{3,7},{4,0},{5,1},{6,2},{7,3}} | collective-permute-start | bytes 3538952 | tf_op jit(solution)/shard_map/ppermute | solution.py:541
  142.6 51.1 %collective-permute-start.22 = (bf16[4,576,256]{2,1,0:T(8,128)(2,1)}, bf16[4,576,256]{2,1,0:T(8,128)(2,1)}, u32[]{:S(2)}, u32[]{:S(2)}) collective-permute-start(bf16[4,576,256]{2,1,0:T(8,128)(2,1)} %collective-permute-done.21.b1), channel_id=1, source_target_pairs={{0,1},{1,0},{2,3},{3,2},{4,5},{5,4},{6,7},{7,6}} | collective-permute-start | bytes 3538952 | tf_op jit(solution)/shard_map/ppermute | solution.py:541
  168.4 96.8 %collective-permute-start.30 = (bf16[576,2304]{1,0:T(8,128)(2,1)}, bf16[576,2304]{1,0:T(8,128)(2,1)}, u32[]{:S(2)}, u32[]{:S(2)}) collective-permute-start(bf16[576,2304]{1,0:T(8,128)(2,1)} %pad_maximum_fusion.refs_1_.refs_5_), channel_id=1, source_target_pairs={{0,1},{1,0},{2,3},{3,2},{4,5},{5,4},{6,7},{7,6}} | collective-permute-start | bytes 7962632 | tf_op jit(solution)/shard_map/ppermute | solution.py:541
  168.4 50.1 %collective-permute-start.25 = (bf16[4,576,256]{2,1,0:T(8,128)(2,1)}, bf16[4,576,256]{2,1,0:T(8,128)(2,1)}, u32[]{:S(2)}, u32[]{:S(2)}) collective-permute-start(bf16[4,576,256]{2,1,0:T(8,128)(2,1)} %collective-permute-done.21.b1), channel_id=1, source_target_pairs={{0,4},{1,5},{2,6},{3,7},{4,0},{5,1},{6,2},{7,3}} | collective-permute-start | bytes 3538952 | tf_op jit(solution)/shard_map/ppermute | solution.py:541
  193.7 41.8 %collective-permute-start.11 = (bf16[576,1024]{1,0:T(8,128)(2,1)}, bf16[576,1024]{1,0:T(8,128)(2,1)}, u32[]{:S(2)}, u32[]{:S(2)}) collective-permute-start(bf16[576,1024]{1,0:T(8,128)(2,1)} %collective-permute-done.10.ry), channel_id=1, source_target_pairs={{0,1},{1,0},{2,3},{3,2},{4,5},{5,4},{6,7},{7,6}} | collective-permute-start | bytes 3538952 | tf_op jit(solution)/shard_map/ppermute | solution.py:541
  218.5 117.3 %collective-permute-start.31 = (bf16[576,2304]{1,0:T(8,128)(2,1)}, bf16[576,2304]{1,0:T(8,128)(2,1)}, u32[]{:S(2)}, u32[]{:S(2)}) collective-permute-start(bf16[576,2304]{1,0:T(8,128)(2,1)} %pad_maximum_fusion.1), channel_id=1, source_target_pairs={{0,2},{1,3},{2,0},{3,1},{4,6},{5,7},{6,4},{7,5}} | collective-permute-start | bytes 7962632 | tf_op jit(solution)/shard_map/ppermute | solution.py:541
  220.2 115.6 %collective-permute-start.34 = (bf16[576,2304]{1,0:T(8,128)(2,1)}, bf16[576,2304]{1,0:T(8,128)(2,1)}, u32[]{:S(2)}, u32[]{:S(2)}) collective-permute-start(bf16[576,2304]{1,0:T(8,128)(2,1)} %pad_maximum_fusion.3), channel_id=1, source_target_pairs={{0,2},{1,3},{2,0},{3,1},{4,6},{5,7},{6,4},{7,5}} | collective-permute-start | bytes 7962632 | tf_op jit(solution)/shard_map/ppermute | solution.py:541
  235.5 29.7 %collective-permute-start.24 = (bf16[4,576,256]{2,1,0:T(8,128)(2,1)}, bf16[4,576,256]{2,1,0:T(8,128)(2,1)}, u32[]{:S(2)}, u32[]{:S(2)}) collective-permute-start(bf16[4,576,256]{2,1,0:T(8,128)(2,1)} %copy-done.7), channel_id=1, source_target_pairs={{0,1},{1,0},{2,3},{3,2},{4,5},{5,4},{6,7},{7,6}} | collective-permute-start | bytes 3538952 | tf_op jit(solution)/shard_map/ppermute | solution.py:541
  239.8 97.8 %collective-permute-start.26 = (bf16[4,576,256]{2,1,0:T(8,128)(2,1)}, bf16[4,576,256]{2,1,0:T(8,128)(2,1)}, u32[]{:S(2)}, u32[]{:S(2)}) collective-permute-start(bf16[4,576,256]{2,1,0:T(8,128)(2,1)} %collective-permute-done.25.b3), channel_id=1, source_target_pairs={{0,1},{1,0},{2,3},{3,2},{4,5},{5,4},{6,7},{7,6}} | collective-permute-start | bytes 3538952 | tf_op jit(solution)/shard_map/ppermute | solution.py:541
  265.2 154.0 %collective-permute-start.38 = (bf16[576,2304]{1,0:T(8,128)(2,1)}, bf16[576,2304]{1,0:T(8,128)(2,1)}, u32[]{:S(2)}, u32[]{:S(2)}) collective-permute-start(bf16[576,2304]{1,0:T(8,128)(2,1)} %copy-done.2), channel_id=1, source_target_pairs={{0,1},{1,0},{2,3},{3,2},{4,5},{5,4},{6,7},{7,6}} | collective-permute-start | bytes 7962632 | tf_op jit(solution)/shard_map/ppermute | solution.py:541
  265.2 151.0 %collective-permute-start.33 = (bf16[576,2304]{1,0:T(8,128)(2,1)}, bf16[576,2304]{1,0:T(8,128)(2,1)}, u32[]{:S(2)}, u32[]{:S(2)}) collective-permute-start(bf16[576,2304]{1,0:T(8,128)(2,1)} %pad_maximum_fusion.2.refs_9_.refs_13_), channel_id=1, source_target_pairs={{0,1},{1,0},{2,3},{3,2},{4,5},{5,4},{6,7},{7,6}} | collective-permute-start | bytes 7962632 | tf_op jit(solution)/shard_map/ppermute | solution.py:541
  363.2 61.3 %collective-permute-start.39 = (bf16[576,2304]{1,0:T(8,128)(2,1)}, bf16[576,2304]{1,0:T(8,128)(2,1)}, u32[]{:S(2)}, u32[]{:S(2)}) collective-permute-start(bf16[576,2304]{1,0:T(8,128)(2,1)} %get-tuple-element.45), channel_id=1, source_target_pairs={{0,2},{1,3},{2,0},{3,1},{4,6},{5,7},{6,4},{7,5}} | collective-permute-start | bytes 7962632 | tf_op jit(solution)/shard_map/ppermute | solution.py:541
  373.3 51.7 %collective-permute-start.32 = (bf16[576,2304]{1,0:T(8,128)(2,1)}, bf16[576,2304]{1,0:T(8,128)(2,1)}, u32[]{:S(2)}, u32[]{:S(2)}) collective-permute-start(bf16[576,2304]{1,0:T(8,128)(2,1)} %collective-permute-done.31.refs_3_.refs_7_), channel_id=1, source_target_pairs={{0,1},{1,0},{2,3},{3,2},{4,5},{5,4},{6,7},{7,6}} | collective-permute-start | bytes 7962632 | tf_op jit(solution)/shard_map/ppermute | solution.py:541
  383.7 42.8 %collective-permute-start.35 = (bf16[576,2304]{1,0:T(8,128)(2,1)}, bf16[576,2304]{1,0:T(8,128)(2,1)}, u32[]{:S(2)}, u32[]{:S(2)}) collective-permute-start(bf16[576,2304]{1,0:T(8,128)(2,1)} %collective-permute-done.34.refs_11_.refs_15_), channel_id=1, source_target_pairs={{0,1},{1,0},{2,3},{3,2},{4,5},{5,4},{6,7},{7,6}} | collective-permute-start | bytes 7962632 | tf_op jit(solution)/shard_map/ppermute | solution.py:541
  416.2 58.9 %collective-permute-start.36 = (bf16[2304,512]{1,0:T(8,128)(2,1)}, bf16[2304,512]{1,0:T(8,128)(2,1)}, u32[]{:S(2)}, u32[]{:S(2)}) collective-permute-start(bf16[2304,512]{1,0:T(8,128)(2,1)} %get-tuple-element.30.hw1), channel_id=1, source_target_pairs={{0,2},{1,3},{2,0},{3,1},{4,6},{5,7},{6,4},{7,5}} | collective-permute-start | bytes 7077896 | tf_op jit(solution)/shard_map/ppermute | solution.py:541
  419.2 105.8 %collective-permute-start.37 = (bf16[2304,512]{1,0:T(8,128)(2,1)}, bf16[2304,512]{1,0:T(8,128)(2,1)}, u32[]{:S(2)}, u32[]{:S(2)}) collective-permute-start(bf16[2304,512]{1,0:T(8,128)(2,1)} %get-tuple-element.31.hw0), channel_id=1, source_target_pairs={{0,2},{1,3},{2,0},{3,1},{4,6},{5,7},{6,4},{7,5}} | collective-permute-start | bytes 7077896 | tf_op jit(solution)/shard_map/ppermute | solution.py:541
  424.5 145.2 %collective-permute-start.41 = (bf16[576,2304]{1,0:T(8,128)(2,1)}, bf16[576,2304]{1,0:T(8,128)(2,1)}, u32[]{:S(2)}, u32[]{:S(2)}) collective-permute-start(bf16[576,2304]{1,0:T(8,128)(2,1)} %pad_maximum_fusion.refs_1_.refs_5_), channel_id=1, source_target_pairs={{0,4},{1,5},{2,6},{3,7},{4,0},{5,1},{6,2},{7,3}} | collective-permute-start | bytes 7962632 | tf_op jit(solution)/shard_map/ppermute | solution.py:541
  425.0 145.3 %collective-permute-start.45 = (bf16[576,2304]{1,0:T(8,128)(2,1)}, bf16[576,2304]{1,0:T(8,128)(2,1)}, u32[]{:S(2)}, u32[]{:S(2)}) collective-permute-start(bf16[576,2304]{1,0:T(8,128)(2,1)} %pad_maximum_fusion.2.refs_9_.refs_13_), channel_id=1, source_target_pairs={{0,4},{1,5},{2,6},{3,7},{4,0},{5,1},{6,2},{7,3}} | collective-permute-start | bytes 7962632 | tf_op jit(solution)/shard_map/ppermute | solution.py:541
  426.5 172.5 %collective-permute-start.47 = (bf16[576,2304]{1,0:T(8,128)(2,1)}, bf16[576,2304]{1,0:T(8,128)(2,1)}, u32[]{:S(2)}, u32[]{:S(2)}) collective-permute-start(bf16[576,2304]{1,0:T(8,128)(2,1)} %collective-permute-done.34.refs_11_.refs_15_), channel_id=1, source_target_pairs={{0,4},{1,5},{2,6},{3,7},{4,0},{5,1},{6,2},{7,3}} | collective-permute-start | bytes 7962632 | tf_op jit(solution)/shard_map/ppermute | solution.py:541
  475.1 180.8 %collective-permute-start.43 = (bf16[576,2304]{1,0:T(8,128)(2,1)}, bf16[576,2304]{1,0:T(8,128)(2,1)}, u32[]{:S(2)}, u32[]{:S(2)}) collective-permute-start(bf16[576,2304]{1,0:T(8,128)(2,1)} %collective-permute-done.31.refs_3_.refs_7_), channel_id=1, source_target_pairs={{0,4},{1,5},{2,6},{3,7},{4,0},{5,1},{6,2},{7,3}} | collective-permute-start | bytes 7962632 | tf_op jit(solution)/shard_map/ppermute | solution.py:541
  524.9 107.0 %collective-permute-start.40 = (bf16[576,2304]{1,0:T(8,128)(2,1)}, bf16[576,2304]{1,0:T(8,128)(2,1)}, u32[]{:S(2)}, u32[]{:S(2)}) collective-permute-start(bf16[576,2304]{1,0:T(8,128)(2,1)} %collective-permute-done.39.d2), channel_id=1, source_target_pairs={{0,1},{1,0},{2,3},{3,2},{4,5},{5,4},{6,7},{7,6}} | collective-permute-start | bytes 7962632 | tf_op jit(solution)/shard_map/ppermute | solution.py:541
  569.7 140.8 %collective-permute-start.51 = (bf16[576,2304]{1,0:T(8,128)(2,1)}, bf16[576,2304]{1,0:T(8,128)(2,1)}, u32[]{:S(2)}, u32[]{:S(2)}) collective-permute-start(bf16[576,2304]{1,0:T(8,128)(2,1)} %collective-permute-done.39.d2), channel_id=1, source_target_pairs={{0,4},{1,5},{2,6},{3,7},{4,0},{5,1},{6,2},{7,3}} | collective-permute-start | bytes 7962632 | tf_op jit(solution)/shard_map/ppermute | solution.py:541
  570.3 117.7 %collective-permute-start.46 = (bf16[576,2304]{1,0:T(8,128)(2,1)}, bf16[576,2304]{1,0:T(8,128)(2,1)}, u32[]{:S(2)}, u32[]{:S(2)}) collective-permute-start(bf16[576,2304]{1,0:T(8,128)(2,1)} %collective-permute-done.45.refs_2_.refs_6_), channel_id=1, source_target_pairs={{0,1},{1,0},{2,3},{3,2},{4,5},{5,4},{6,7},{7,6}} | collective-permute-start | bytes 7962632 | tf_op jit(solution)/shard_map/ppermute | solution.py:541
  599.0 111.6 %collective-permute-start.48 = (bf16[576,2304]{1,0:T(8,128)(2,1)}, bf16[576,2304]{1,0:T(8,128)(2,1)}, u32[]{:S(2)}, u32[]{:S(2)}) collective-permute-start(bf16[576,2304]{1,0:T(8,128)(2,1)} %collective-permute-done.47.refs_4_.refs_8_), channel_id=1, source_target_pairs={{0,1},{1,0},{2,3},{3,2},{4,5},{5,4},{6,7},{7,6}} | collective-permute-start | bytes 7962632 | tf_op jit(solution)/shard_map/ppermute | solution.py:541
  632.0 111.5 %collective-permute-start.42 = (bf16[576,2304]{1,0:T(8,128)(2,1)}, bf16[576,2304]{1,0:T(8,128)(2,1)}, u32[]{:S(2)}, u32[]{:S(2)}) collective-permute-start(bf16[576,2304]{1,0:T(8,128)(2,1)} %collective-permute-done.41.refs_1_.refs_5_), channel_id=1, source_target_pairs={{0,1},{1,0},{2,3},{3,2},{4,5},{5,4},{6,7},{7,6}} | collective-permute-start | bytes 7962632 | tf_op jit(solution)/shard_map/ppermute | solution.py:541
  655.9 88.2 %collective-permute-start.44 = (bf16[576,2304]{1,0:T(8,128)(2,1)}, bf16[576,2304]{1,0:T(8,128)(2,1)}, u32[]{:S(2)}, u32[]{:S(2)}) collective-permute-start(bf16[576,2304]{1,0:T(8,128)(2,1)} %collective-permute-done.43.refs_3_.refs_7_), channel_id=1, source_target_pairs={{0,1},{1,0},{2,3},{3,2},{4,5},{5,4},{6,7},{7,6}} | collective-permute-start | bytes 7962632 | tf_op jit(solution)/shard_map/ppermute | solution.py:541
  688.0 54.0 %collective-permute-start.54 = (bf16[576,1152]{1,0:T(8,128)(2,1)}, bf16[576,1152]{1,0:T(8,128)(2,1)}, u32[]{:S(2)}, u32[]{:S(2)}) collective-permute-start(bf16[576,1152]{1,0:T(8,128)(2,1)} %collective-permute-done.53.e0), channel_id=1, source_target_pairs={{0,1},{1,0},{2,3},{3,2},{4,5},{5,4},{6,7},{7,6}} | collective-permute-start | bytes 3981320 | tf_op jit(solution)/shard_map/ppermute | solution.py:541
  710.6 251.0 %collective-permute-start.59 = (bf16[4096,512]{1,0:T(8,128)(2,1)}, bf16[4096,512]{1,0:T(8,128)(2,1)}, u32[]{:S(2)}, u32[]{:S(2)}) collective-permute-start(bf16[4096,512]{1,0:T(8,128)(2,1)} %get-tuple-element.26.k_ref.kv0), channel_id=1, source_target_pairs={{0,1},{1,0},{2,3},{3,2},{4,5},{5,4},{6,7},{7,6}} | collective-permute-start | bytes 12582920 | tf_op jit(solution)/shard_map/ppermute | solution.py:541
  710.6 124.2 %collective-permute-start.52 = (bf16[576,2304]{1,0:T(8,128)(2,1)}, bf16[576,2304]{1,0:T(8,128)(2,1)}, u32[]{:S(2)}, u32[]{:S(2)}) collective-permute-start(bf16[576,2304]{1,0:T(8,128)(2,1)} %collective-permute-done.51.d2), channel_id=1, source_target_pairs={{0,1},{1,0},{2,3},{3,2},{4,5},{5,4},{6,7},{7,6}} | collective-permute-start | bytes 7962632 | tf_op jit(solution)/shard_map/ppermute | solution.py:541
  742.0 39.5 %collective-permute-start.15 = (bf16[1024,512]{1,0:T(8,128)(2,1)}, bf16[1024,512]{1,0:T(8,128)(2,1)}, u32[]{:S(2)}, u32[]{:S(2)}) collective-permute-start(bf16[1024,512]{1,0:T(8,128)(2,1)} %split.9), channel_id=1, source_target_pairs={{0,2},{1,3},{2,0},{3,1},{4,6},{5,7},{6,4},{7,5}} | collective-permute-start | bytes 3145736 | tf_op jit(solution)/shard_map/ppermute | solution.py:541
  743.5 58.6 %collective-permute-start.55 = (bf16[1536,512]{1,0:T(8,128)(2,1)}, bf16[1536,512]{1,0:T(8,128)(2,1)}, u32[]{:S(2)}, u32[]{:S(2)}) collective-permute-start(bf16[1536,512]{1,0:T(8,128)(2,1)} %get-tuple-element.56), channel_id=1, source_target_pairs={{0,2},{1,3},{2,0},{3,1},{4,6},{5,7},{6,4},{7,5}} | collective-permute-start | bytes 4718600 | tf_op jit(solution)/shard_map/ppermute | solution.py:541
  744.1 90.8 %collective-permute-start.57 = (bf16[1536,512]{1,0:T(8,128)(2,1)}, bf16[1536,512]{1,0:T(8,128)(2,1)}, u32[]{:S(2)}, u32[]{:S(2)}) collective-permute-start(bf16[1536,512]{1,0:T(8,128)(2,1)} %get-tuple-element.55), channel_id=1, source_target_pairs={{0,2},{1,3},{2,0},{3,1},{4,6},{5,7},{6,4},{7,5}} | collective-permute-start | bytes 4718600 | tf_op jit(solution)/shard_map/ppermute | solution.py:541
  781.5 205.7 %collective-permute-start.16 = (bf16[1024,512]{1,0:T(8,128)(2,1)}, bf16[1024,512]{1,0:T(8,128)(2,1)}, u32[]{:S(2)}, u32[]{:S(2)}) collective-permute-start(bf16[1024,512]{1,0:T(8,128)(2,1)} %collective-permute-done.15.kv0), channel_id=1, source_target_pairs={{0,1},{1,0},{2,3},{3,2},{4,5},{5,4},{6,7},{7,6}} | collective-permute-start | bytes 3145736 | tf_op jit(solution)/shard_map/ppermute | solution.py:541
  802.1 179.5 %collective-permute-start.56 = (bf16[1536,512]{1,0:T(8,128)(2,1)}, bf16[1536,512]{1,0:T(8,128)(2,1)}, u32[]{:S(2)}, u32[]{:S(2)}) collective-permute-start(bf16[1536,512]{1,0:T(8,128)(2,1)} %collective-permute-done.55.kv0), channel_id=1, source_target_pairs={{0,1},{1,0},{2,3},{3,2},{4,5},{5,4},{6,7},{7,6}} | collective-permute-start | bytes 4718600 | tf_op jit(solution)/shard_map/ppermute | solution.py:541
  834.8 141.0 %collective-permute-start.58 = (bf16[1536,512]{1,0:T(8,128)(2,1)}, bf16[1536,512]{1,0:T(8,128)(2,1)}, u32[]{:S(2)}, u32[]{:S(2)}) collective-permute-start(bf16[1536,512]{1,0:T(8,128)(2,1)} %collective-permute-done.57.kv0), channel_id=1, source_target_pairs={{0,1},{1,0},{2,3},{3,2},{4,5},{5,4},{6,7},{7,6}} | collective-permute-start | bytes 4718600 | tf_op jit(solution)/shard_map/ppermute | solution.py:541
  (27 other events, 644.1 us)

commit v7 on v6

--- a/solution.py
+++ b/solution.py
@@ -20,7 +20,7 @@
 BIG = 2.0 ** 40
 SHRINK = 2.0 ** -88
 MT = 256
-KT = 384
+KT = 512
 KA = 768
 ANY = pl.BlockSpec(memory_space=pl.ANY)
 
@@ -185,7 +185,7 @@
             acc_ref[:, cols] += dot(vs_ref[:, rows], p.astype(BF))
             return 0
 
-        lax.fori_loop(0, groups * bq // MT, part, 0, unroll=2)
+        lax.fori_loop(0, groups * bq // MT, part, 0, unroll=2 if masked else 4)
 
     mid = jnp.maximum(jnp.minimum(full, diag), lo)
     edge = jnp.maximum(diag, mid)
@@ -466,17 +466,25 @@
     start(d_cp[:2] + e_cp + [g_cp] + h_cp)
     for q in range(2, chunks):
         start(z_cp(q))
+    for cp in d_cp[:2] + e_cp:
+        cp.wait()
+
+    def early(i, _):
+        p, at = i // 2, block_of(lax.rem(i, 2), w4)
+        lo_ref[p, at, :] = dot_nt(d_ref[at, :last], z_ref[p, :, :last]) + p_ref[p, at, :]
+        return 0
+
+    loop(4, early)
     dt_y.wait_recv()
     dt_c.start()
-    for cp in d_cp[:2] + e_cp:
-        cp.wait()
     dt_c.wait_recv()
 
-    def first_lower(p, _):
-        lower(p)
-        return 0
-
-    loop(2, first_lower)
+    def rest(i, _):
+        p, at = i // 2, block_of(lax.rem(i, 2), w4)
+        lo_ref[p, at, :] += dot_nt(d_ref[at, late], z_ref[p, :, late])
+        return 0
+
+    loop(4, rest)
     for cp in [g_cp] + h_cp:
         cp.wait()
 
@@ -627,9 +635,9 @@
         a_all = []
         for k in sets:
             a_all = [call(
-                functools.partial(norm_kernel, width=D, per_half=per_half), (nt,),
-                [cols(w4, tile, lambda i, s, k=k: s[0] * nb + k * nt + i), cols(w4, tile, lambda i, s, k=k: k * nt + i)] + [cols(w4, tile, lambda i, s: i % per_half)] * 4 + [whole(D, 4)] + [ANY] * k,
-                cols(D, tile, lambda i, s, k=k: k * nt + i), bf(D, S),
+                functools.partial(norm_kernel, width=D, per_half=half // 2 // MT), (half // MT,),
+                [cols(w4, MT, lambda i, s, k=k: (s[0] * nb + k * nt) * per_half + i), cols(w4, MT, lambda i, s, k=k: k * nt * per_half + i)] + [cols(w4, MT, lambda i, s: i % nt)] * 4 + [whole(D, 4)] + [ANY] * k,
+                cols(D, MT, lambda i, s, k=k: k * nt * per_half + i), bf(D, S),
                 flops=D * S, aliases={8: 0} if k else None)(scal, xt, own_c, rx[k], rxc[k], ry[k], ryc[k], gcol, *a_all)]
         qv, kv = call(
             functools.partial(qkv_kernel, hd=hd), (nb,),

time: 997 us -> 996 us (level)
  transfers between devices with their start and end apart: 60 -> 60, of which waited for: 18 -> 19; matrix products, arithmetic and copies ran while one was open for 5% -> 5% of each run, Pallas kernels for 49% -> 49%
where the time goes in v7:
time: 996 us; the launch traced here: 994 us
  Pallas kernels  496 us (50%)
  waiting for transfers between devices  399 us (40%)
  starting transfers between devices  45.7 us (5%)
  local copies, waits for them, and re-layouts  39 us (4%)
  other arithmetic  12.5 us (1%)
    ppermute x60, waiting for transfers between devices, send(): return lax.ppermute(a, ('tp', 'dm'), perm)  399 us
    pallas_call x5, Pallas kernels, gated(): call(functools.partial(gate_up_kernel, groups=groups, sets=sets, steps=nf...  133 us
    pallas_call x1, Pallas kernels, layer(): pl.pallas_call(functools.partial(tail_kernel, width=D, chunks=chunks), ou...  127 us
    pallas_call x2, Pallas kernels, layer(): call(functools.partial(attn_kernel, bq=bq, bk=bk, q_block0=q0, scale=scal...  49.6 us
    ppermute x60, starting transfers between devices, send(): return lax.ppermute(a, ('tp', 'dm'), perm)  45.7 us
    pallas_call x4, Pallas kernels, layer(): call(functools.partial(kv_out_kernel, extra=int(extra)), (n,), [kv_spec]...  34 us
    pallas_call x1, Pallas kernels, layer(): call(down_y_kernel, (oh // yt,), [pl.BlockSpec((yt, F4), by_row)] * 2 + [...  32.1 us
    pallas_call x2, Pallas kernels, layer(): call(functools.partial(proj_kernel, width=D), (1,), [cols(gw, quarter, mi...  31.9 us
  transfers between devices with their start and end apart: 60, of which 19 were waited for; matrix products, arithmetic and copies ran while one was open for 5% of the time, Pallas kernels for 49%

profile of v7, /device:TPU:0, one launch (start us, length us, event | category | flops | bytes accessed | tf_op | source)
XLA Modules:
  0.0 993.9 jit_solution(5820693159022872691)
XLA Ops:
  0.7 3.2 dynamic-slice_bitcast_fusion.3
  3.9 3.3 collective-permute-start.1
  7.3 4.4 dynamic-slice_bitcast_fusion.1
  18.5 7.3 shard_map.150
  25.8 33.1 %collective-permute-done.6 = bf16[4,576]{1,0:T(4,128)(2,1)S(1)} collective-permute-done((bf16[4,576]{1,0:T(4,128)(2,1)S(1)}, bf16[4,576]{1,0:T(4,128)(2,1)S(1)}, u32[]{:S(2)}, u32[]{:S(2)}) %collective-permute-start.6) | collective-permute-done | bytes 4640 | tf_op jit(solution)/shard_map/ppermute | solution.py:549
  66.7 21.4 %collective-permute-done.13.w2 = bf16[576,1024]{1,0:T(8,128)(2,1)} collective-permute-done((bf16[576,1024]{1,0:T(8,128)(2,1)}, bf16[576,1024]{1,0:T(8,128)(2,1)}, u32[]{:S(2)}, u32[]{:S(2)}) %collective-permute-start.13) | collective-permute-done | bytes 1179680 | tf_op jit(solution)/shard_map/ppermute | solution.py:549
  89.8 5.1 dynamic-slice_bitcast_fusion
  94.9 17.7 %collective-permute-done.14.w3 = bf16[576,1024]{1,0:T(8,128)(2,1)} collective-permute-done((bf16[576,1024]{1,0:T(8,128)(2,1)}, bf16[576,1024]{1,0:T(8,128)(2,1)}, u32[]{:S(2)}, u32[]{:S(2)}) %collective-permute-start.14) | collective-permute-done | bytes 1179680 | tf_op jit(solution)/shard_map/ppermute | solution.py:549
  113.5 24.7 %collective-permute-done.21.b1 = bf16[4,576,256]{2,1,0:T(8,128)(2,1)} collective-permute-done((bf16[4,576,256]{2,1,0:T(8,128)(2,1)}, bf16[4,576,256]{2,1,0:T(8,128)(2,1)}, u32[]{:S(2)}, u32[]{:S(2)}) %collective-permute-start.21) | collective-permute-done | bytes 1179680 | tf_op jit(solution)/shard_map/ppermute | solution.py:549
  143.6 7.4 constant_dynamic-slice_fusion
  151.0 3.7 pad_maximum_fusion.refs_1_.refs_5_
  154.7 12.6 %collective-permute-done.3.ry = bf16[576,1024]{1,0:T(8,128)(2,1)} collective-permute-done((bf16[576,1024]{1,0:T(8,128)(2,1)}, bf16[576,1024]{1,0:T(8,128)(2,1)}, u32[]{:S(2)}, u32[]{:S(2)}) %collective-permute-start.3) | collective-permute-done | bytes 1179680 | tf_op jit(solution)/shard_map/ppermute | solution.py:549
  169.1 23.5 %collective-permute-done.10.ry = bf16[576,1024]{1,0:T(8,128)(2,1)} collective-permute-done((bf16[576,1024]{1,0:T(8,128)(2,1)}, bf16[576,1024]{1,0:T(8,128)(2,1)}, u32[]{:S(2)}, u32[]{:S(2)}) %collective-permute-start.10) | collective-permute-done | bytes 1179680 | tf_op jit(solution)/shard_map/ppermute | solution.py:549
  196.7 20.7 %collective-permute-done.25.b3 = bf16[4,576,256]{2,1,0:T(8,128)(2,1)} collective-permute-done((bf16[4,576,256]{2,1,0:T(8,128)(2,1)}, bf16[4,576,256]{2,1,0:T(8,128)(2,1)}, u32[]{:S(2)}, u32[]{:S(2)}) %collective-permute-start.25) | collective-permute-done | bytes 1179680 | tf_op jit(solution)/shard_map/ppermute | solution.py:549
  222.1 12.3 %shard_map.151 = (f32[128,4096]{1,0:T(8,128)}, f32[128,4096]{1,0:T(8,128)}) custom-call(s32[3]{0:T(128)} %pad_add_fusion.s_ref, s32[1,4096]{1,0:T(1,128)} %copy-done.9, f32[128,1]{1,0:T(8,128)} %multiply_power_fusion.freq_ref), custom_call_target="tpu_custom_call" | custom-call | flops 8388608 | tf_op jit(solution)/shard_map/pallas_call | solution.py:632
  235.2 3.4 pad_maximum_fusion.2.refs_9_.refs_13_
  240.7 13.0 %shard_map.148.rest_0_ = bf16[2304,4096]{1,0:T(8,128)(2,1)} custom-call(s32[3]{0:T(128)} %pad_add_fusion.s_ref, bf16[576,8192]{1,0:T(8,128)(2,1)} %bitcast.20, bf16[576,4096]{1,0:T(8,128)(2,1)} %collective-permute-done.own_c.x1, bf16[576,1024]{1,0:T(8,128)(2,1)} %collective-permute-done.8.rx.x2, bf16[576,1024]{1,0:T(8,128)(2,1)} %collective-permute-done.9.rxc.x3, ...), custom_call_target="tpu_custom_call" | custom-call | flops 9437184 | tf_op jit(solution)/shard_map/pallas_call | solution.py:637
  253.8 13.1 %shard_map.149.a_ref = bf16[2304,4096]{1,0:T(8,128)(2,1)} custom-call(s32[3]{0:T(128)} %pad_add_fusion.s_ref, bf16[576,8192]{1,0:T(8,128)(2,1)} %bitcast.21, bf16[576,4096]{1,0:T(8,128)(2,1)} %collective-permute-done.own_c.x1, bf16[576,1024]{1,0:T(8,128)(2,1)} %collective-permute-done.1.rx.x2, ...), custom_call_target="tpu_custom_call", output_to_operand_aliasing={{}: (8, {})} | custom-call | flops 9437184 | tf_op jit(solution)/shard_map/pallas_call | solution.py:637
  267.4 31.7 %shard_map.152 = (bf16[768,4096]{1,0:T(8,128)(2,1)}, bf16[4096,512]{1,0:T(8,128)(2,1)}) custom-call(s32[3]{0:T(128)} %pad_add_fusion.s_ref, bf16[2304,4096]{1,0:T(8,128)(2,1)} %shard_map.149.a_ref, bf16[576,1024]{1,0:T(8,128)(2,1)} %get-tuple-element.22.w0, bf16[576,1024]{1,0:T(8,128)(2,1)} %copy-done.7, bf16[576,1024]{1,0:T(8,128)(2,1)} %collective-permute-done.13.w2, ...), custom_call_target="tpu_custom_call" | custom-call | flops 4831838208 | tf_op jit(solution)/shard_map/pallas_call | solution.py:642
  299.1 32.7 %shard_map.153.o_own = bf16[512,2048]{1,0:T(8,128)(2,1)} custom-call(s32[8]{0:T(128)} %get-tuple-element.42.lo_ref, s32[8]{0:T(128)} %get-tuple-element.41.full_ref, bf16[768,4096]{1,0:T(8,128)(2,1)} %get-tuple-element.27.q_ref.v_ref, bf16[4096,512]{1,0:T(8,128)(2,1)} %get-tuple-element.26.k_ref.kv0, bf16[768,4096]{1,0:T(8,128)(2,1)} %get-tuple-element.27.q_ref.v_ref, ...), custom_call_target="tpu_custom_call" | custom-call | flops 4294967296 | tf_op jit(solution)/shard_map/pallas_call | solution.py:663
  336.3 16.9 %shard_map.154.o_own = bf16[512,2048]{1,0:T(8,128)(2,1)} custom-call(s32[8]{0:T(128)} %get-tuple-element.42.lo_ref, s32[8]{0:T(128)} %get-tuple-element.41.full_ref, bf16[768,4096]{1,0:T(8,128)(2,1)} %get-tuple-element.27.q_ref.v_ref, bf16[4096,512]{1,0:T(8,128)(2,1)} %get-tuple-element.26.k_ref.kv0, bf16[768,4096]{1,0:T(8,128)(2,1)} %get-tuple-element.27.q_ref.v_ref, ...), custom_call_target="tpu_custom_call" | custom-call | flops 2147483648 | tf_op jit(solution)/shard_map/pallas_call | solution.py:663
  356.7 3.3 collective-permute-done.19.o_yc
  364.3 7.7 collective-permute-done.28.o_y
  372.0 10.2 %collective-permute-done.29.o_yc = bf16[512,512]{1,0:T(8,128)(2,1)} collective-permute-done((bf16[512,512]{1,0:T(8,128)(2,1)S(1)}, bf16[512,512]{1,0:T(8,128)(2,1)}, u32[]{:S(2)}, u32[]{:S(2)}) %collective-permute-start.29) | collective-permute-done | bytes 524320 | tf_op jit(solution)/shard_map/ppermute | solution.py:549
  382.9 15.9 %shard_map.155 = (bf16[2304,512]{1,0:T(8,128)(2,1)}, bf16[1024,2304]{1,0:T(8,128)(2,1)}) custom-call(s32[3]{0:T(128)} %pad_add_fusion.s_ref, bf16[512,2048]{1,0:T(8,128)(2,1)} %shard_map.154.o_own, bf16[512,512]{1,0:T(8,128)(2,1)} %collective-permute-done.27.o_c, bf16[512,512]{1,0:T(8,128)(2,1)} %collective-permute-done.28.o_y, ...), custom_call_target="tpu_custom_call" | custom-call | flops 2415919104 | tf_op jit(solution)/shard_map/pallas_call | solution.py:678
  398.8 15.9 %shard_map.156 = (bf16[2304,512]{1,0:T(8,128)(2,1)}, bf16[1024,2304]{1,0:T(8,128)(2,1)}) custom-call(s32[3]{0:T(128)} %pad_add_fusion.s_ref, bf16[512,2048]{1,0:T(8,128)(2,1)} %shard_map.153.o_own, bf16[512,512]{1,0:T(8,128)(2,1)} %copy-done.8, bf16[512,512]{1,0:T(8,128)(2,1)} %collective-permute-done.18.o_y, ...), custom_call_target="tpu_custom_call", output_to_operand_aliasing={{1}: (18, {})} | custom-call | flops 2415919104 | tf_op jit(solution)/shard_map/pallas_call | solution.py:678
  417.4 5.6 collective-permute-done.39.d2
  427.9 3.8 fusion
  431.7 41.9 %collective-permute-done.36.h_ref.hf1 = bf16[2304,512]{1,0:T(8,128)(2,1)} collective-permute-done((bf16[2304,512]{1,0:T(8,128)(2,1)}, bf16[2304,512]{1,0:T(8,128)(2,1)}, u32[]{:S(2)}, u32[]{:S(2)}) %collective-permute-start.36) | collective-permute-done | bytes 2359328 | tf_op jit(solution)/shard_map/ppermute | solution.py:549
  474.1 49.1 %collective-permute-done.37.h_ref.hf0 = bf16[2304,512]{1,0:T(8,128)(2,1)} collective-permute-done((bf16[2304,512]{1,0:T(8,128)(2,1)}, bf16[2304,512]{1,0:T(8,128)(2,1)}, u32[]{:S(2)}, u32[]{:S(2)}) %collective-permute-start.37) | collective-permute-done | bytes 2359328 | tf_op jit(solution)/shard_map/ppermute | solution.py:549
  523.2 32.9 %shard_map.157.zw = bf16[1024,2304]{1,0:T(8,128)(2,1)} custom-call(s32[3]{0:T(128)} %pad_add_fusion.s_ref, bf16[1024,2304]{1,0:T(8,128)(2,1)} %get-tuple-element.29.refs_0_, bf16[576,2304]{1,0:T(8,128)(2,1)} %pad_maximum_fusion.refs_1_.refs_5_, bf16[576,2304]{1,0:T(8,128)(2,1)} %collective-permute-done.30.refs_2_.refs_6_, ...), custom_call_target="tpu_custom_call" | custom-call | flops 21743271936 | tf_op jit(solution)/shard_map/pallas_call | solution.py:704
  556.1 6.0 shard_map.158.rest_0_
  562.0 6.0 shard_map.159.refs_0_.refs_1_
  568.9 28.7 %collective-permute-done.47.refs_4_.refs_8_ = bf16[576,2304]{1,0:T(8,128)(2,1)} collective-permute-done((bf16[576,2304]{1,0:T(8,128)(2,1)}, bf16[576,2304]{1,0:T(8,128)(2,1)}, u32[]{:S(2)}, u32[]{:S(2)}) %collective-permute-start.47) | collective-permute-done | bytes 2654240 | tf_op jit(solution)/shard_map/ppermute | solution.py:549
  597.6 32.9 %shard_map.160.zf = bf16[1024,2304]{1,0:T(8,128)(2,1)} custom-call(s32[3]{0:T(128)} %pad_add_fusion.s_ref, bf16[1024,2304]{1,0:T(8,128)(2,1)} %shard_map.159.refs_0_.refs_1_, bf16[576,2304]{1,0:T(8,128)(2,1)} %pad_maximum_fusion.refs_1_.refs_5_, bf16[576,2304]{1,0:T(8,128)(2,1)} %collective-permute-done.30.refs_2_.refs_6_, ...), custom_call_target="tpu_custom_call" | custom-call | flops 21743271936 | tf_op jit(solution)/shard_map/pallas_call | solution.py:704
  631.0 23.5 %collective-permute-done.43.refs_3_.refs_7_ = bf16[576,2304]{1,0:T(8,128)(2,1)} collective-permute-done((bf16[576,2304]{1,0:T(8,128)(2,1)}, bf16[576,2304]{1,0:T(8,128)(2,1)}, u32[]{:S(2)}, u32[]{:S(2)}) %collective-permute-start.43) | collective-permute-done | bytes 2654240 | tf_op jit(solution)/shard_map/ppermute | solution.py:549
  654.5 32.1 %shard_map.161.part = f32[8,2304,256]{2,1,0:T(8,128)} custom-call(s32[3]{0:T(128)} %pad_add_fusion.s_ref, bf16[1024,2304]{1,0:T(8,128)(2,1)} %shard_map.157.zw, bf16[1024,2304]{1,0:T(8,128)(2,1)} %shard_map.160.zf, bf16[576,2304]{1,0:T(8,128)(2,1)} %copy-done.2, bf16[576,2304]{1,0:T(8,128)(2,1)} %collective-permute-done.38.d1, ...), custom_call_target="tpu_custom_call" | custom-call | flops 10871635968 | tf_op jit(solution)/shard_map/pallas_call | solution.py:719
  687.1 21.4 %collective-permute-done.51.d2 = bf16[576,2304]{1,0:T(8,128)(2,1)} collective-permute-done((bf16[576,2304]{1,0:T(8,128)(2,1)}, bf16[576,2304]{1,0:T(8,128)(2,1)}, u32[]{:S(2)}, u32[]{:S(2)}) %collective-permute-start.51) | collective-permute-done | bytes 2654240 | tf_op jit(solution)/shard_map/ppermute | solution.py:549
  709.0 30.9 %shard_map.164.zb = bf16[2048,1152]{1,0:T(8,128)(2,1)} custom-call(s32[3]{0:T(128)} %pad_add_fusion.s_ref, bf16[1024,2304]{1,0:T(8,128)(2,1)} %get-tuple-element.29.refs_0_, bf16[1024,2304]{1,0:T(8,128)(2,1)} %shard_map.159.refs_0_.refs_1_, bf16[576,2304]{1,0:T(8,128)(2,1)} %collective-permute-done.45.refs_2_.refs_6_, ...), custom_call_target="tpu_custom_call" | custom-call | flops 21743271936 | tf_op jit(solution)/shard_map/pallas_call | solution.py:704
  743.4 18.1 %shard_map.162.zwa = bf16[1024,1152]{1,0:T(8,128)(2,1)} custom-call(s32[3]{0:T(128)} %pad_add_fusion.s_ref, bf16[1024,2304]{1,0:T(8,128)(2,1)} %get-tuple-element.29.refs_0_, bf16[576,2304]{1,0:T(8,128)(2,1)} %collective-permute-done.41.refs_1_.refs_5_, bf16[576,2304]{1,0:T(8,128)(2,1)} %collective-permute-done.42.refs_2_.refs_6_, ...), custom_call_target="tpu_custom_call" | custom-call | flops 10871635968 | tf_op jit(solution)/shard_map/pallas_call | solution.py:704
  761.5 17.9 %shard_map.163.zfa = bf16[1024,1152]{1,0:T(8,128)(2,1)} custom-call(s32[3]{0:T(128)} %pad_add_fusion.s_ref, bf16[1024,2304]{1,0:T(8,128)(2,1)} %shard_map.159.refs_0_.refs_1_, bf16[576,2304]{1,0:T(8,128)(2,1)} %collective-permute-done.41.refs_1_.refs_5_, bf16[576,2304]{1,0:T(8,128)(2,1)} %collective-permute-done.42.refs_2_.refs_6_, ...), custom_call_target="tpu_custom_call" | custom-call | flops 10871635968 | tf_op jit(solution)/shard_map/pallas_call | solution.py:704
  779.5 20.5 %collective-permute-done.55.kv0 = bf16[1536,512]{1,0:T(8,128)(2,1)} collective-permute-done((bf16[1536,512]{1,0:T(8,128)(2,1)}, bf16[1536,512]{1,0:T(8,128)(2,1)}, u32[]{:S(2)}, u32[]{:S(2)}) %collective-permute-start.55) | collective-permute-done | bytes 1572896 | tf_op jit(solution)/shard_map/ppermute | solution.py:549
  800.0 32.7 %collective-permute-done.57.kv0 = bf16[1536,512]{1,0:T(8,128)(2,1)} collective-permute-done((bf16[1536,512]{1,0:T(8,128)(2,1)}, bf16[1536,512]{1,0:T(8,128)(2,1)}, u32[]{:S(2)}, u32[]{:S(2)}) %collective-permute-start.57) | collective-permute-done | bytes 1572896 | tf_op jit(solution)/shard_map/ppermute | solution.py:549
  832.8 126.9 %tail.1.rest_0_ = bf16[576,8192]{1,0:T(8,128)(2,1)} custom-call(f32[8,2304,256]{2,1,0:T(8,128)} %shard_map.161.part, bf16[1024,1152]{1,0:T(8,128)(2,1)} %shard_map.162.zwa, bf16[1024,1152]{1,0:T(8,128)(2,1)} %shard_map.163.zfa, bf16[2048,1152]{1,0:T(8,128)(2,1)} %shard_map.164.zb, bf16[576,768]{1,0:T(8,128)(2,1)} %collective-permute-done.49.d0, ...), custom_call_target="tpu_custom_call" | custom-call | flops 21743271936 | bytes 18874368 | tf_op jit(solution)/shard_map/tail/pallas_call | solution.py:723
  959.7 14.2 %shard_map.165 = (bf16[8192,2,256]{2,1,0:T(2,128)(2,1)}, bf16[8192,2,256]{2,1,0:T(2,128)(2,1)}) custom-call(s32[3]{0:T(128)} %pad_add_fusion.s_ref, bf16[4096,512]{1,0:T(8,128)(2,1)} %get-tuple-element.26.k_ref.kv0, bf16[4096,512]{1,0:T(8,128)(2,1)} %collective-permute-done.59.kv1), custom_call_target="tpu_custom_call" | custom-call | flops 4194304 | tf_op jit(solution)/shard_map/pallas_call | solution.py:750
  973.9 5.7 shard_map.166
  979.6 5.7 shard_map.167
  985.3 8.4 shard_map.168
  (154 shorter events, 63.6 us)
Async XLA Ops:
  3.9 56.9 %collective-permute-start.1 = (bf16[576,1024]{1,0:T(8,128)(2,1)}, bf16[576,1024]{1,0:T(8,128)(2,1)}, u32[]{:S(2)}, u32[]{:S(2)}) collective-permute-start(bf16[576,1024]{1,0:T(8,128)(2,1)} %get-tuple-element.44), channel_id=1, source_target_pairs={{0,2},{1,3},{2,0},{3,1},{4,6},{5,7},{6,4},{7,5}} | collective-permute-start | bytes 3538952 | tf_op jit(solution)/shard_map/ppermute | solution.py:549
  7.2 53.8 %collective-permute-start.8 = (bf16[576,1024]{1,0:T(8,128)(2,1)}, bf16[576,1024]{1,0:T(8,128)(2,1)}, u32[]{:S(2)}, u32[]{:S(2)}) collective-permute-start(bf16[576,1024]{1,0:T(8,128)(2,1)} %get-tuple-element.43), channel_id=1, source_target_pairs={{0,2},{1,3},{2,0},{3,1},{4,6},{5,7},{6,4},{7,5}} | collective-permute-start | bytes 3538952 | tf_op jit(solution)/shard_map/ppermute | solution.py:549
  13.3 47.4 %collective-permute-start.49 = (bf16[576,768]{1,0:T(8,128)(2,1)S(1)}, bf16[576,768]{1,0:T(8,128)(2,1)}, u32[]{:S(2)}, u32[]{:S(2)}) collective-permute-start(bf16[576,768]{1,0:T(8,128)(2,1)S(1)} %slice.18), channel_id=1, source_target_pairs={{0,4},{1,5},{2,6},{3,7},{4,0},{5,1},{6,2},{7,3}} | collective-permute-start | bytes 2654216 | tf_op jit(solution)/shard_map/ppermute | solution.py:549
  15.4 43.5 %collective-permute-start.6 = (bf16[4,576]{1,0:T(4,128)(2,1)S(1)}, bf16[4,576]{1,0:T(4,128)(2,1)S(1)}, u32[]{:S(2)}, u32[]{:S(2)}) collective-permute-start(bf16[4,576]{1,0:T(4,128)(2,1)S(1)} %pad_maximum_fusion.4), channel_id=1, source_target_pairs={{0,2},{1,3},{2,0},{3,1},{4,6},{5,7},{6,4},{7,5}} | collective-permute-start | bytes 13832 | tf_op jit(solution)/shard_map/ppermute | solution.py:549
  17.0 41.9 %collective-permute-start.7 = (bf16[4,576]{1,0:T(4,128)(2,1)S(1)}, bf16[4,576]{1,0:T(4,128)(2,1)S(1)}, u32[]{:S(2)}, u32[]{:S(2)}) collective-permute-start(bf16[4,576]{1,0:T(4,128)(2,1)S(1)} %pad_maximum_fusion.4), channel_id=1, source_target_pairs={{0,3},{1,2},{2,1},{3,0},{4,7},{5,6},{6,5},{7,4}} | collective-permute-start | bytes 13832 | tf_op jit(solution)/shard_map/ppermute | solution.py:549
  58.9 29.2 %collective-permute-start.13 = (bf16[576,1024]{1,0:T(8,128)(2,1)}, bf16[576,1024]{1,0:T(8,128)(2,1)}, u32[]{:S(2)}, u32[]{:S(2)}) collective-permute-start(bf16[576,1024]{1,0:T(8,128)(2,1)} %get-tuple-element.22.w0), channel_id=1, source_target_pairs={{0,2},{1,3},{2,0},{3,1},{4,6},{5,7},{6,4},{7,5}} | collective-permute-start | bytes 3538952 | tf_op jit(solution)/shard_map/ppermute | solution.py:549
  60.6 52.0 %collective-permute-start.14 = (bf16[576,1024]{1,0:T(8,128)(2,1)}, bf16[576,1024]{1,0:T(8,128)(2,1)}, u32[]{:S(2)}, u32[]{:S(2)}) collective-permute-start(bf16[576,1024]{1,0:T(8,128)(2,1)} %get-tuple-element.23), channel_id=1, source_target_pairs={{0,3},{1,2},{2,1},{3,0},{4,7},{5,6},{6,5},{7,4}} | collective-permute-start | bytes 3538952 | tf_op jit(solution)/shard_map/ppermute | solution.py:549
  60.8 52.7 %collective-permute-start.20 = (bf16[4,576,256]{2,1,0:T(8,128)(2,1)}, bf16[4,576,256]{2,1,0:T(8,128)(2,1)S(1)}, u32[]{:S(2)}, u32[]{:S(2)}) collective-permute-start(bf16[4,576,256]{2,1,0:T(8,128)(2,1)} %bitcast.31), channel_id=1, source_target_pairs={{0,1},{1,0},{2,3},{3,2},{4,5},{5,4},{6,7},{7,6}} | collective-permute-start | bytes 3538952 | tf_op jit(solution)/shard_map/ppermute | solution.py:549
  61.1 77.1 %collective-permute-start.21 = (bf16[4,576,256]{2,1,0:T(8,128)(2,1)}, bf16[4,576,256]{2,1,0:T(8,128)(2,1)}, u32[]{:S(2)}, u32[]{:S(2)}) collective-permute-start(bf16[4,576,256]{2,1,0:T(8,128)(2,1)} %bitcast.32), channel_id=1, source_target_pairs={{0,2},{1,3},{2,0},{3,1},{4,6},{5,7},{6,4},{7,5}} | collective-permute-start | bytes 3538952 | tf_op jit(solution)/shard_map/ppermute | solution.py:549
  65.2 73.0 %collective-permute-start.23 = (bf16[4,576,256]{2,1,0:T(8,128)(2,1)}, bf16[4,576,256]{2,1,0:T(8,128)(2,1)}, u32[]{:S(2)}, u32[]{:S(2)}) collective-permute-start(bf16[4,576,256]{2,1,0:T(8,128)(2,1)} %bitcast.33), channel_id=1, source_target_pairs={{0,4},{1,5},{2,6},{3,7},{4,0},{5,1},{6,2},{7,3}} | collective-permute-start | bytes 3538952 | tf_op jit(solution)/shard_map/ppermute | solution.py:549
  88.1 51.9 %collective-permute-start.53 = (bf16[576,1024]{1,0:T(8,128)(2,1)}, bf16[576,1024]{1,0:T(8,128)(2,1)}, u32[]{:S(2)}, u32[]{:S(2)}) collective-permute-start(bf16[576,1024]{1,0:T(8,128)(2,1)} %slice.19), channel_id=1, source_target_pairs={{0,4},{1,5},{2,6},{3,7},{4,0},{5,1},{6,2},{7,3}} | collective-permute-start | bytes 3538952 | tf_op jit(solution)/shard_map/ppermute | solution.py:549
  112.6 126.2 %collective-permute-start = (bf16[576,4096]{1,0:T(8,128)(2,1)}, bf16[576,4096]{1,0:T(8,128)(2,1)}, u32[]{:S(2)}, u32[]{:S(2)}) collective-permute-start(bf16[576,4096]{1,0:T(8,128)(2,1)} %dynamic-slice_bitcast_fusion), channel_id=1, source_target_pairs={{0,1},{1,0},{2,3},{3,2},{4,5},{5,4},{6,7},{7,6}} | collective-permute-start | bytes 14155784 | tf_op jit(solution)/shard_map/ppermute | solution.py:549
  138.2 29.2 %collective-permute-start.3 = (bf16[576,1024]{1,0:T(8,128)(2,1)}, bf16[576,1024]{1,0:T(8,128)(2,1)}, u32[]{:S(2)}, u32[]{:S(2)}) collective-permute-start(bf16[576,1024]{1,0:T(8,128)(2,1)} %collective-permute-done.1.rx.x2), channel_id=1, source_target_pairs={{0,4},{1,5},{2,6},{3,7},{4,0},{5,1},{6,2},{7,3}} | collective-permute-start | bytes 3538952 | tf_op jit(solution)/shard_map/ppermute | solution.py:549
  140.8 51.8 %collective-permute-start.10 = (bf16[576,1024]{1,0:T(8,128)(2,1)}, bf16[576,1024]{1,0:T(8,128)(2,1)}, u32[]{:S(2)}, u32[]{:S(2)}) collective-permute-start(bf16[576,1024]{1,0:T(8,128)(2,1)} %collective-permute-done.8.rx.x2), channel_id=1, source_target_pairs={{0,4},{1,5},{2,6},{3,7},{4,0},{5,1},{6,2},{7,3}} | collective-permute-start | bytes 3538952 | tf_op jit(solution)/shard_map/ppermute | solution.py:549
  143.6 49.0 %collective-permute-start.22 = (bf16[4,576,256]{2,1,0:T(8,128)(2,1)}, bf16[4,576,256]{2,1,0:T(8,128)(2,1)}, u32[]{:S(2)}, u32[]{:S(2)}) collective-permute-start(bf16[4,576,256]{2,1,0:T(8,128)(2,1)} %collective-permute-done.21.b1), channel_id=1, source_target_pairs={{0,1},{1,0},{2,3},{3,2},{4,5},{5,4},{6,7},{7,6}} | collective-permute-start | bytes 3538952 | tf_op jit(solution)/shard_map/ppermute | solution.py:549
  167.3 99.6 %collective-permute-start.30 = (bf16[576,2304]{1,0:T(8,128)(2,1)}, bf16[576,2304]{1,0:T(8,128)(2,1)}, u32[]{:S(2)}, u32[]{:S(2)}) collective-permute-start(bf16[576,2304]{1,0:T(8,128)(2,1)} %pad_maximum_fusion.refs_1_.refs_5_), channel_id=1, source_target_pairs={{0,1},{1,0},{2,3},{3,2},{4,5},{5,4},{6,7},{7,6}} | collective-permute-start | bytes 7962632 | tf_op jit(solution)/shard_map/ppermute | solution.py:549
  167.3 50.1 %collective-permute-start.25 = (bf16[4,576,256]{2,1,0:T(8,128)(2,1)}, bf16[4,576,256]{2,1,0:T(8,128)(2,1)}, u32[]{:S(2)}, u32[]{:S(2)}) collective-permute-start(bf16[4,576,256]{2,1,0:T(8,128)(2,1)} %collective-permute-done.21.b1), channel_id=1, source_target_pairs={{0,4},{1,5},{2,6},{3,7},{4,0},{5,1},{6,2},{7,3}} | collective-permute-start | bytes 3538952 | tf_op jit(solution)/shard_map/ppermute | solution.py:549
  192.7 41.8 %collective-permute-start.11 = (bf16[576,1024]{1,0:T(8,128)(2,1)}, bf16[576,1024]{1,0:T(8,128)(2,1)}, u32[]{:S(2)}, u32[]{:S(2)}) collective-permute-start(bf16[576,1024]{1,0:T(8,128)(2,1)} %collective-permute-done.10.ry), channel_id=1, source_target_pairs={{0,1},{1,0},{2,3},{3,2},{4,5},{5,4},{6,7},{7,6}} | collective-permute-start | bytes 3538952 | tf_op jit(solution)/shard_map/ppermute | solution.py:549
  217.4 116.9 %collective-permute-start.31 = (bf16[576,2304]{1,0:T(8,128)(2,1)}, bf16[576,2304]{1,0:T(8,128)(2,1)}, u32[]{:S(2)}, u32[]{:S(2)}) collective-permute-start(bf16[576,2304]{1,0:T(8,128)(2,1)} %pad_maximum_fusion.1), channel_id=1, source_target_pairs={{0,2},{1,3},{2,0},{3,1},{4,6},{5,7},{6,4},{7,5}} | collective-permute-start | bytes 7962632 | tf_op jit(solution)/shard_map/ppermute | solution.py:549
  219.2 115.2 %collective-permute-start.34 = (bf16[576,2304]{1,0:T(8,128)(2,1)}, bf16[576,2304]{1,0:T(8,128)(2,1)}, u32[]{:S(2)}, u32[]{:S(2)}) collective-permute-start(bf16[576,2304]{1,0:T(8,128)(2,1)} %pad_maximum_fusion.3), channel_id=1, source_target_pairs={{0,2},{1,3},{2,0},{3,1},{4,6},{5,7},{6,4},{7,5}} | collective-permute-start | bytes 7962632 | tf_op jit(solution)/shard_map/ppermute | solution.py:549
  234.4 32.4 %collective-permute-start.24 = (bf16[4,576,256]{2,1,0:T(8,128)(2,1)}, bf16[4,576,256]{2,1,0:T(8,128)(2,1)}, u32[]{:S(2)}, u32[]{:S(2)}) collective-permute-start(bf16[4,576,256]{2,1,0:T(8,128)(2,1)} %collective-permute-done.23.b2), channel_id=1, source_target_pairs={{0,1},{1,0},{2,3},{3,2},{4,5},{5,4},{6,7},{7,6}} | collective-permute-start | bytes 3538952 | tf_op jit(solution)/shard_map/ppermute | solution.py:549
  238.8 97.4 %collective-permute-start.26 = (bf16[4,576,256]{2,1,0:T(8,128)(2,1)}, bf16[4,576,256]{2,1,0:T(8,128)(2,1)}, u32[]{:S(2)}, u32[]{:S(2)}) collective-permute-start(bf16[4,576,256]{2,1,0:T(8,128)(2,1)} %collective-permute-done.25.b3), channel_id=1, source_target_pairs={{0,1},{1,0},{2,3},{3,2},{4,5},{5,4},{6,7},{7,6}} | collective-permute-start | bytes 3538952 | tf_op jit(solution)/shard_map/ppermute | solution.py:549
  266.9 150.5 %collective-permute-start.38 = (bf16[576,2304]{1,0:T(8,128)(2,1)}, bf16[576,2304]{1,0:T(8,128)(2,1)}, u32[]{:S(2)}, u32[]{:S(2)}) collective-permute-start(bf16[576,2304]{1,0:T(8,128)(2,1)} %copy-done.2), channel_id=1, source_target_pairs={{0,1},{1,0},{2,3},{3,2},{4,5},{5,4},{6,7},{7,6}} | collective-permute-start | bytes 7962632 | tf_op jit(solution)/shard_map/ppermute | solution.py:549
  266.9 147.8 %collective-permute-start.33 = (bf16[576,2304]{1,0:T(8,128)(2,1)}, bf16[576,2304]{1,0:T(8,128)(2,1)}, u32[]{:S(2)}, u32[]{:S(2)}) collective-permute-start(bf16[576,2304]{1,0:T(8,128)(2,1)} %pad_maximum_fusion.2.refs_9_.refs_13_), channel_id=1, source_target_pairs={{0,1},{1,0},{2,3},{3,2},{4,5},{5,4},{6,7},{7,6}} | collective-permute-start | bytes 7962632 | tf_op jit(solution)/shard_map/ppermute | solution.py:549
  361.9 61.1 %collective-permute-start.39 = (bf16[576,2304]{1,0:T(8,128)(2,1)}, bf16[576,2304]{1,0:T(8,128)(2,1)}, u32[]{:S(2)}, u32[]{:S(2)}) collective-permute-start(bf16[576,2304]{1,0:T(8,128)(2,1)} %get-tuple-element.45), channel_id=1, source_target_pairs={{0,2},{1,3},{2,0},{3,1},{4,6},{5,7},{6,4},{7,5}} | collective-permute-start | bytes 7962632 | tf_op jit(solution)/shard_map/ppermute | solution.py:549
  372.0 51.6 %collective-permute-start.32 = (bf16[576,2304]{1,0:T(8,128)(2,1)}, bf16[576,2304]{1,0:T(8,128)(2,1)}, u32[]{:S(2)}, u32[]{:S(2)}) collective-permute-start(bf16[576,2304]{1,0:T(8,128)(2,1)} %collective-permute-done.31.refs_3_.refs_7_), channel_id=1, source_target_pairs={{0,1},{1,0},{2,3},{3,2},{4,5},{5,4},{6,7},{7,6}} | collective-permute-start | bytes 7962632 | tf_op jit(solution)/shard_map/ppermute | solution.py:549
  382.2 42.9 %collective-permute-start.35 = (bf16[576,2304]{1,0:T(8,128)(2,1)}, bf16[576,2304]{1,0:T(8,128)(2,1)}, u32[]{:S(2)}, u32[]{:S(2)}) collective-permute-start(bf16[576,2304]{1,0:T(8,128)(2,1)} %collective-permute-done.34.refs_11_.refs_15_), channel_id=1, source_target_pairs={{0,1},{1,0},{2,3},{3,2},{4,5},{5,4},{6,7},{7,6}} | collective-permute-start | bytes 7962632 | tf_op jit(solution)/shard_map/ppermute | solution.py:549
  414.7 58.9 %collective-permute-start.36 = (bf16[2304,512]{1,0:T(8,128)(2,1)}, bf16[2304,512]{1,0:T(8,128)(2,1)}, u32[]{:S(2)}, u32[]{:S(2)}) collective-permute-start(bf16[2304,512]{1,0:T(8,128)(2,1)} %get-tuple-element.30.hw1), channel_id=1, source_target_pairs={{0,2},{1,3},{2,0},{3,1},{4,6},{5,7},{6,4},{7,5}} | collective-permute-start | bytes 7077896 | tf_op jit(solution)/shard_map/ppermute | solution.py:549
  417.4 105.8 %collective-permute-start.37 = (bf16[2304,512]{1,0:T(8,128)(2,1)}, bf16[2304,512]{1,0:T(8,128)(2,1)}, u32[]{:S(2)}, u32[]{:S(2)}) collective-permute-start(bf16[2304,512]{1,0:T(8,128)(2,1)} %get-tuple-element.31.hw0), channel_id=1, source_target_pairs={{0,2},{1,3},{2,0},{3,1},{4,6},{5,7},{6,4},{7,5}} | collective-permute-start | bytes 7077896 | tf_op jit(solution)/shard_map/ppermute | solution.py:549
  423.1 144.9 %collective-permute-start.41 = (bf16[576,2304]{1,0:T(8,128)(2,1)}, bf16[576,2304]{1,0:T(8,128)(2,1)}, u32[]{:S(2)}, u32[]{:S(2)}) collective-permute-start(bf16[576,2304]{1,0:T(8,128)(2,1)} %pad_maximum_fusion.refs_1_.refs_5_), channel_id=1, source_target_pairs={{0,4},{1,5},{2,6},{3,7},{4,0},{5,1},{6,2},{7,3}} | collective-permute-start | bytes 7962632 | tf_op jit(solution)/shard_map/ppermute | solution.py:549
  423.6 145.1 %collective-permute-start.45 = (bf16[576,2304]{1,0:T(8,128)(2,1)}, bf16[576,2304]{1,0:T(8,128)(2,1)}, u32[]{:S(2)}, u32[]{:S(2)}) collective-permute-start(bf16[576,2304]{1,0:T(8,128)(2,1)} %pad_maximum_fusion.2.refs_9_.refs_13_), channel_id=1, source_target_pairs={{0,4},{1,5},{2,6},{3,7},{4,0},{5,1},{6,2},{7,3}} | collective-permute-start | bytes 7962632 | tf_op jit(solution)/shard_map/ppermute | solution.py:549
  425.1 172.5 %collective-permute-start.47 = (bf16[576,2304]{1,0:T(8,128)(2,1)}, bf16[576,2304]{1,0:T(8,128)(2,1)}, u32[]{:S(2)}, u32[]{:S(2)}) collective-permute-start(bf16[576,2304]{1,0:T(8,128)(2,1)} %collective-permute-done.34.refs_11_.refs_15_), channel_id=1, source_target_pairs={{0,4},{1,5},{2,6},{3,7},{4,0},{5,1},{6,2},{7,3}} | collective-permute-start | bytes 7962632 | tf_op jit(solution)/shard_map/ppermute | solution.py:549
  473.6 180.8 %collective-permute-start.43 = (bf16[576,2304]{1,0:T(8,128)(2,1)}, bf16[576,2304]{1,0:T(8,128)(2,1)}, u32[]{:S(2)}, u32[]{:S(2)}) collective-permute-start(bf16[576,2304]{1,0:T(8,128)(2,1)} %collective-permute-done.31.refs_3_.refs_7_), channel_id=1, source_target_pairs={{0,4},{1,5},{2,6},{3,7},{4,0},{5,1},{6,2},{7,3}} | collective-permute-start | bytes 7962632 | tf_op jit(solution)/shard_map/ppermute | solution.py:549
  523.2 107.3 %collective-permute-start.40 = (bf16[576,2304]{1,0:T(8,128)(2,1)}, bf16[576,2304]{1,0:T(8,128)(2,1)}, u32[]{:S(2)}, u32[]{:S(2)}) collective-permute-start(bf16[576,2304]{1,0:T(8,128)(2,1)} %collective-permute-done.39.d2), channel_id=1, source_target_pairs={{0,1},{1,0},{2,3},{3,2},{4,5},{5,4},{6,7},{7,6}} | collective-permute-start | bytes 7962632 | tf_op jit(solution)/shard_map/ppermute | solution.py:549
  568.0 140.5 %collective-permute-start.51 = (bf16[576,2304]{1,0:T(8,128)(2,1)}, bf16[576,2304]{1,0:T(8,128)(2,1)}, u32[]{:S(2)}, u32[]{:S(2)}) collective-permute-start(bf16[576,2304]{1,0:T(8,128)(2,1)} %collective-permute-done.39.d2), channel_id=1, source_target_pairs={{0,4},{1,5},{2,6},{3,7},{4,0},{5,1},{6,2},{7,3}} | collective-permute-start | bytes 7962632 | tf_op jit(solution)/shard_map/ppermute | solution.py:549
  568.7 117.9 %collective-permute-start.46 = (bf16[576,2304]{1,0:T(8,128)(2,1)}, bf16[576,2304]{1,0:T(8,128)(2,1)}, u32[]{:S(2)}, u32[]{:S(2)}) collective-permute-start(bf16[576,2304]{1,0:T(8,128)(2,1)} %collective-permute-done.45.refs_2_.refs_6_), channel_id=1, source_target_pairs={{0,1},{1,0},{2,3},{3,2},{4,5},{5,4},{6,7},{7,6}} | collective-permute-start | bytes 7962632 | tf_op jit(solution)/shard_map/ppermute | solution.py:549
  597.6 110.9 %collective-permute-start.48 = (bf16[576,2304]{1,0:T(8,128)(2,1)}, bf16[576,2304]{1,0:T(8,128)(2,1)}, u32[]{:S(2)}, u32[]{:S(2)}) collective-permute-start(bf16[576,2304]{1,0:T(8,128)(2,1)} %collective-permute-done.47.refs_4_.refs_8_), channel_id=1, source_target_pairs={{0,1},{1,0},{2,3},{3,2},{4,5},{5,4},{6,7},{7,6}} | collective-permute-start | bytes 7962632 | tf_op jit(solution)/shard_map/ppermute | solution.py:549
  630.5 110.9 %collective-permute-start.42 = (bf16[576,2304]{1,0:T(8,128)(2,1)}, bf16[576,2304]{1,0:T(8,128)(2,1)}, u32[]{:S(2)}, u32[]{:S(2)}) collective-permute-start(bf16[576,2304]{1,0:T(8,128)(2,1)} %collective-permute-done.41.refs_1_.refs_5_), channel_id=1, source_target_pairs={{0,1},{1,0},{2,3},{3,2},{4,5},{5,4},{6,7},{7,6}} | collective-permute-start | bytes 7962632 | tf_op jit(solution)/shard_map/ppermute | solution.py:549
  654.5 87.5 %collective-permute-start.44 = (bf16[576,2304]{1,0:T(8,128)(2,1)}, bf16[576,2304]{1,0:T(8,128)(2,1)}, u32[]{:S(2)}, u32[]{:S(2)}) collective-permute-start(bf16[576,2304]{1,0:T(8,128)(2,1)} %collective-permute-done.43.refs_3_.refs_7_), channel_id=1, source_target_pairs={{0,1},{1,0},{2,3},{3,2},{4,5},{5,4},{6,7},{7,6}} | collective-permute-start | bytes 7962632 | tf_op jit(solution)/shard_map/ppermute | solution.py:549
  686.5 53.4 %collective-permute-start.54 = (bf16[576,1024]{1,0:T(8,128)(2,1)}, bf16[576,1024]{1,0:T(8,128)(2,1)}, u32[]{:S(2)}, u32[]{:S(2)}) collective-permute-start(bf16[576,1024]{1,0:T(8,128)(2,1)} %collective-permute-done.53.e0), channel_id=1, source_target_pairs={{0,1},{1,0},{2,3},{3,2},{4,5},{5,4},{6,7},{7,6}} | collective-permute-start | bytes 3538952 | tf_op jit(solution)/shard_map/ppermute | solution.py:549
  708.5 251.2 %collective-permute-start.59 = (bf16[4096,512]{1,0:T(8,128)(2,1)}, bf16[4096,512]{1,0:T(8,128)(2,1)}, u32[]{:S(2)}, u32[]{:S(2)}) collective-permute-start(bf16[4096,512]{1,0:T(8,128)(2,1)} %get-tuple-element.26.k_ref.kv0), channel_id=1, source_target_pairs={{0,1},{1,0},{2,3},{3,2},{4,5},{5,4},{6,7},{7,6}} | collective-permute-start | bytes 12582920 | tf_op jit(solution)/shard_map/ppermute | solution.py:549
  708.5 124.2 %collective-permute-start.52 = (bf16[576,2304]{1,0:T(8,128)(2,1)}, bf16[576,2304]{1,0:T(8,128)(2,1)}, u32[]{:S(2)}, u32[]{:S(2)}) collective-permute-start(bf16[576,2304]{1,0:T(8,128)(2,1)} %collective-permute-done.51.d2), channel_id=1, source_target_pairs={{0,1},{1,0},{2,3},{3,2},{4,5},{5,4},{6,7},{7,6}} | collective-permute-start | bytes 7962632 | tf_op jit(solution)/shard_map/ppermute | solution.py:549
  739.9 39.5 %collective-permute-start.15 = (bf16[1024,512]{1,0:T(8,128)(2,1)}, bf16[1024,512]{1,0:T(8,128)(2,1)}, u32[]{:S(2)}, u32[]{:S(2)}) collective-permute-start(bf16[1024,512]{1,0:T(8,128)(2,1)} %split.9), channel_id=1, source_target_pairs={{0,2},{1,3},{2,0},{3,1},{4,6},{5,7},{6,4},{7,5}} | collective-permute-start | bytes 3145736 | tf_op jit(solution)/shard_map/ppermute | solution.py:549
  741.4 58.6 %collective-permute-start.55 = (bf16[1536,512]{1,0:T(8,128)(2,1)}, bf16[1536,512]{1,0:T(8,128)(2,1)}, u32[]{:S(2)}, u32[]{:S(2)}) collective-permute-start(bf16[1536,512]{1,0:T(8,128)(2,1)} %get-tuple-element.56), channel_id=1, source_target_pairs={{0,2},{1,3},{2,0},{3,1},{4,6},{5,7},{6,4},{7,5}} | collective-permute-start | bytes 4718600 | tf_op jit(solution)/shard_map/ppermute | solution.py:549
  742.0 90.8 %collective-permute-start.57 = (bf16[1536,512]{1,0:T(8,128)(2,1)}, bf16[1536,512]{1,0:T(8,128)(2,1)}, u32[]{:S(2)}, u32[]{:S(2)}) collective-permute-start(bf16[1536,512]{1,0:T(8,128)(2,1)} %get-tuple-element.55), channel_id=1, source_target_pairs={{0,2},{1,3},{2,0},{3,1},{4,6},{5,7},{6,4},{7,5}} | collective-permute-start | bytes 4718600 | tf_op jit(solution)/shard_map/ppermute | solution.py:549
  779.4 205.9 %collective-permute-start.16 = (bf16[1024,512]{1,0:T(8,128)(2,1)}, bf16[1024,512]{1,0:T(8,128)(2,1)}, u32[]{:S(2)}, u32[]{:S(2)}) collective-permute-start(bf16[1024,512]{1,0:T(8,128)(2,1)} %collective-permute-done.15.kv0), channel_id=1, source_target_pairs={{0,1},{1,0},{2,3},{3,2},{4,5},{5,4},{6,7},{7,6}} | collective-permute-start | bytes 3145736 | tf_op jit(solution)/shard_map/ppermute | solution.py:549
  800.0 179.6 %collective-permute-start.56 = (bf16[1536,512]{1,0:T(8,128)(2,1)}, bf16[1536,512]{1,0:T(8,128)(2,1)}, u32[]{:S(2)}, u32[]{:S(2)}) collective-permute-start(bf16[1536,512]{1,0:T(8,128)(2,1)} %collective-permute-done.55.kv0), channel_id=1, source_target_pairs={{0,1},{1,0},{2,3},{3,2},{4,5},{5,4},{6,7},{7,6}} | collective-permute-start | bytes 4718600 | tf_op jit(solution)/shard_map/ppermute | solution.py:549
  832.7 141.2 %collective-permute-start.58 = (bf16[1536,512]{1,0:T(8,128)(2,1)}, bf16[1536,512]{1,0:T(8,128)(2,1)}, u32[]{:S(2)}, u32[]{:S(2)}) collective-permute-start(bf16[1536,512]{1,0:T(8,128)(2,1)} %collective-permute-done.57.kv0), channel_id=1, source_target_pairs={{0,1},{1,0},{2,3},{3,2},{4,5},{5,4},{6,7},{7,6}} | collective-permute-start | bytes 4718600 | tf_op jit(solution)/shard_map/ppermute | solution.py:549
  (27 other events, 631.4 us)

commit v8 on v7

--- a/solution.py
+++ b/solution.py
@@ -15,7 +15,7 @@
 LOG2E = 1.4426950408889634
 BF = jnp.bfloat16
 F32 = jnp.float32
-VM = 63 * 1024 * 1024
+VM = 67043328
 CH = 128
 BIG = 2.0 ** 40
 SHRINK = 2.0 ** -88
@@ -375,13 +375,14 @@
         for cp in cps:
             cp.start()
 
-    start(z_cp(0) + [d_cp[2], p_cp(0), d_cp[3]] + z_cp(1))
+    start(z_cp(0) + [d_cp[2], p_cp(0), d_cp[3]])
 
     bar = pltpu.get_barrier_semaphore()
     for dev in (px, pc, py, pyc):
         pl.semaphore_signal(bar, inc=1, device_id=dev, device_id_type=pl.DeviceIdType.MESH)
     pl.semaphore_wait(bar, 4)
     dt_y.start()
+    start(z_cp(1))
 
     def lanes(q):
         return pl.ds(pl.multiple_of(CH * (x + q - 2 * x * q), CH), CH)

time: 996 us -> 998 us (level)
  no operation moved by 1% of the time
where the time goes in v8:
time: 998 us; the launch traced here: 996 us
  Pallas kernels  497 us (50%)
  waiting for transfers between devices  396 us (40%)
  starting transfers between devices  46.1 us (5%)
  local copies, waits for them, and re-layouts  41.7 us (4%)
  other arithmetic  13.9 us (1%)
    ppermute x60, waiting for transfers between devices, send(): return lax.ppermute(a, ('tp', 'dm'), perm)  396 us
    pallas_call x5, Pallas kernels, gated(): call(functools.partial(gate_up_kernel, groups=groups, sets=sets, steps=nf...  133 us
    pallas_call x1, Pallas kernels, layer(): pl.pallas_call(functools.partial(tail_kernel, width=D, chunks=chunks), ou...  128 us
    pallas_call x2, Pallas kernels, layer(): call(functools.partial(attn_kernel, bq=bq, bk=bk, q_block0=q0, scale=scal...  49.6 us
    ppermute x60, starting transfers between devices, send(): return lax.ppermute(a, ('tp', 'dm'), perm)  46.1 us
    pallas_call x4, Pallas kernels, layer(): call(functools.partial(kv_out_kernel, extra=int(extra)), (n,), [kv_spec]...  33.9 us
    pallas_call x1, Pallas kernels, layer(): call(down_y_kernel, (oh // yt,), [pl.BlockSpec((yt, F4), by_row)] * 2 + [...  32 us
    pallas_call x2, Pallas kernels, layer(): call(functools.partial(proj_kernel, width=D), (1,), [cols(gw, quarter, mi...  31.9 us
  transfers between devices with their start and end apart: 60, of which 19 were waited for; matrix products, arithmetic and copies ran while one was open for 5% of the time, Pallas kernels for 49%

profile of v8, /device:TPU:0, one launch (start us, length us, event | category | flops | bytes accessed | tf_op | source)
XLA Modules:
  0.0 995.6 jit_solution(16138322324967286068)
XLA Ops:
  0.7 3.2 dynamic-slice_bitcast_fusion.3
  3.9 3.3 collective-permute-start.1
  7.2 4.4 dynamic-slice_bitcast_fusion.1
  20.3 7.3 shard_map.150
  27.6 31.3 %collective-permute-done.6 = bf16[4,576]{1,0:T(4,128)(2,1)} collective-permute-done((bf16[4,576]{1,0:T(4,128)(2,1)}, bf16[4,576]{1,0:T(4,128)(2,1)}, u32[]{:S(2)}, u32[]{:S(2)}) %collective-permute-start.6) | collective-permute-done | bytes 4640 | tf_op jit(solution)/shard_map/ppermute | solution.py:550
  66.7 21.3 %collective-permute-done.13.w2 = bf16[576,1024]{1,0:T(8,128)(2,1)S(1)} collective-permute-done((bf16[576,1024]{1,0:T(8,128)(2,1)}, bf16[576,1024]{1,0:T(8,128)(2,1)S(1)}, u32[]{:S(2)}, u32[]{:S(2)}) %collective-permute-start.13) | collective-permute-done | bytes 1179680 | tf_op jit(solution)/shard_map/ppermute | solution.py:550
  89.8 5.1 dynamic-slice_bitcast_fusion
  94.9 17.8 %collective-permute-done.14.w3 = bf16[576,1024]{1,0:T(8,128)(2,1)} collective-permute-done((bf16[576,1024]{1,0:T(8,128)(2,1)}, bf16[576,1024]{1,0:T(8,128)(2,1)}, u32[]{:S(2)}, u32[]{:S(2)}) %collective-permute-start.14) | collective-permute-done | bytes 1179680 | tf_op jit(solution)/shard_map/ppermute | solution.py:550
  113.5 24.7 %collective-permute-done.21.b1 = bf16[4,576,256]{2,1,0:T(8,128)(2,1)} collective-permute-done((bf16[4,576,256]{2,1,0:T(8,128)(2,1)}, bf16[4,576,256]{2,1,0:T(8,128)(2,1)}, u32[]{:S(2)}, u32[]{:S(2)}) %collective-permute-start.21) | collective-permute-done | bytes 1179680 | tf_op jit(solution)/shard_map/ppermute | solution.py:550
  143.8 7.4 constant_dynamic-slice_fusion
  151.2 3.7 pad_maximum_fusion.refs_1_.refs_5_
  154.8 12.5 %collective-permute-done.3.ry = bf16[576,1024]{1,0:T(8,128)(2,1)} collective-permute-done((bf16[576,1024]{1,0:T(8,128)(2,1)}, bf16[576,1024]{1,0:T(8,128)(2,1)}, u32[]{:S(2)}, u32[]{:S(2)}) %collective-permute-start.3) | collective-permute-done | bytes 1179680 | tf_op jit(solution)/shard_map/ppermute | solution.py:550
  169.1 23.5 %collective-permute-done.10.ry = bf16[576,1024]{1,0:T(8,128)(2,1)} collective-permute-done((bf16[576,1024]{1,0:T(8,128)(2,1)}, bf16[576,1024]{1,0:T(8,128)(2,1)}, u32[]{:S(2)}, u32[]{:S(2)}) %collective-permute-start.10) | collective-permute-done | bytes 1179680 | tf_op jit(solution)/shard_map/ppermute | solution.py:550
  197.9 19.6 %collective-permute-done.25.b3 = bf16[4,576,256]{2,1,0:T(8,128)(2,1)} collective-permute-done((bf16[4,576,256]{2,1,0:T(8,128)(2,1)}, bf16[4,576,256]{2,1,0:T(8,128)(2,1)}, u32[]{:S(2)}, u32[]{:S(2)}) %collective-permute-start.25) | collective-permute-done | bytes 1179680 | tf_op jit(solution)/shard_map/ppermute | solution.py:550
  222.1 12.3 %shard_map.151 = (f32[128,4096]{1,0:T(8,128)}, f32[128,4096]{1,0:T(8,128)}) custom-call(s32[3]{0:T(128)} %pad_add_fusion.s_ref, s32[1,4096]{1,0:T(1,128)} %copy-done.7, f32[128,1]{1,0:T(8,128)} %multiply_power_fusion.freq_ref), custom_call_target="tpu_custom_call" | custom-call | flops 8388608 | tf_op jit(solution)/shard_map/pallas_call | solution.py:633
  236.0 3.4 pad_maximum_fusion.2.refs_9_.refs_13_
  242.2 13.1 %shard_map.148.rest_0_ = bf16[2304,4096]{1,0:T(8,128)(2,1)} custom-call(s32[3]{0:T(128)} %pad_add_fusion.s_ref, bf16[576,8192]{1,0:T(8,128)(2,1)} %bitcast.20, bf16[576,4096]{1,0:T(8,128)(2,1)} %collective-permute-done.own_c.x1, bf16[576,1024]{1,0:T(8,128)(2,1)} %collective-permute-done.8.rx.x2, bf16[576,1024]{1,0:T(8,128)(2,1)} %collective-permute-done.9.rxc.x3, ...), custom_call_target="tpu_custom_call" | custom-call | flops 9437184 | tf_op jit(solution)/shard_map/pallas_call | solution.py:638
  255.3 13.0 %shard_map.149.a_ref = bf16[2304,4096]{1,0:T(8,128)(2,1)} custom-call(s32[3]{0:T(128)} %pad_add_fusion.s_ref, bf16[576,8192]{1,0:T(8,128)(2,1)} %bitcast.21, bf16[576,4096]{1,0:T(8,128)(2,1)} %collective-permute-done.own_c.x1, bf16[576,1024]{1,0:T(8,128)(2,1)} %collective-permute-done.1.rx.x2, ...), custom_call_target="tpu_custom_call", output_to_operand_aliasing={{}: (8, {})} | custom-call | flops 9437184 | tf_op jit(solution)/shard_map/pallas_call | solution.py:638
  268.9 31.7 %shard_map.152 = (bf16[768,4096]{1,0:T(8,128)(2,1)}, bf16[4096,512]{1,0:T(8,128)(2,1)}) custom-call(s32[3]{0:T(128)} %pad_add_fusion.s_ref, bf16[2304,4096]{1,0:T(8,128)(2,1)} %shard_map.149.a_ref, bf16[576,1024]{1,0:T(8,128)(2,1)} %get-tuple-element.22.w0, bf16[576,1024]{1,0:T(8,128)(2,1)} %copy-done.5, bf16[576,1024]{1,0:T(8,128)(2,1)} %copy-done.6, ...), custom_call_target="tpu_custom_call" | custom-call | flops 4831838208 | tf_op jit(solution)/shard_map/pallas_call | solution.py:643
  300.6 32.7 %shard_map.153.o_own = bf16[512,2048]{1,0:T(8,128)(2,1)} custom-call(s32[8]{0:T(128)} %get-tuple-element.42.lo_ref, s32[8]{0:T(128)} %get-tuple-element.41.full_ref, bf16[768,4096]{1,0:T(8,128)(2,1)} %get-tuple-element.27.q_ref.v_ref, bf16[4096,512]{1,0:T(8,128)(2,1)} %get-tuple-element.26.k_ref.kv0, bf16[768,4096]{1,0:T(8,128)(2,1)} %get-tuple-element.27.q_ref.v_ref, ...), custom_call_target="tpu_custom_call" | custom-call | flops 4294967296 | tf_op jit(solution)/shard_map/pallas_call | solution.py:664
  337.8 16.9 %shard_map.154.o_own = bf16[512,2048]{1,0:T(8,128)(2,1)} custom-call(s32[8]{0:T(128)} %get-tuple-element.42.lo_ref, s32[8]{0:T(128)} %get-tuple-element.41.full_ref, bf16[768,4096]{1,0:T(8,128)(2,1)} %get-tuple-element.27.q_ref.v_ref, bf16[4096,512]{1,0:T(8,128)(2,1)} %get-tuple-element.26.k_ref.kv0, bf16[768,4096]{1,0:T(8,128)(2,1)} %get-tuple-element.27.q_ref.v_ref, ...), custom_call_target="tpu_custom_call" | custom-call | flops 2147483648 | tf_op jit(solution)/shard_map/pallas_call | solution.py:664
  358.2 3.4 collective-permute-done.19.o_yc
  365.9 7.7 collective-permute-done.28.o_y
  373.5 10.2 %collective-permute-done.29.o_yc = bf16[512,512]{1,0:T(8,128)(2,1)} collective-permute-done((bf16[512,512]{1,0:T(8,128)(2,1)S(1)}, bf16[512,512]{1,0:T(8,128)(2,1)}, u32[]{:S(2)}, u32[]{:S(2)}) %collective-permute-start.29) | collective-permute-done | bytes 524320 | tf_op jit(solution)/shard_map/ppermute | solution.py:550
  384.4 15.9 %shard_map.155 = (bf16[2304,512]{1,0:T(8,128)(2,1)}, bf16[1024,2304]{1,0:T(8,128)(2,1)}) custom-call(s32[3]{0:T(128)} %pad_add_fusion.s_ref, bf16[512,2048]{1,0:T(8,128)(2,1)} %shard_map.154.o_own, bf16[512,512]{1,0:T(8,128)(2,1)} %collective-permute-done.27.o_c, bf16[512,512]{1,0:T(8,128)(2,1)} %collective-permute-done.28.o_y, ...), custom_call_target="tpu_custom_call" | custom-call | flops 2415919104 | tf_op jit(solution)/shard_map/pallas_call | solution.py:679
  400.3 15.9 %shard_map.156 = (bf16[2304,512]{1,0:T(8,128)(2,1)}, bf16[1024,2304]{1,0:T(8,128)(2,1)}) custom-call(s32[3]{0:T(128)} %pad_add_fusion.s_ref, bf16[512,2048]{1,0:T(8,128)(2,1)} %shard_map.153.o_own, bf16[512,512]{1,0:T(8,128)(2,1)} %collective-permute-done.17.o_c, bf16[512,512]{1,0:T(8,128)(2,1)} %collective-permute-done.18.o_y, ...), custom_call_target="tpu_custom_call", output_to_operand_aliasing={{1}: (18, {})} | custom-call | flops 2415919104 | tf_op jit(solution)/shard_map/pallas_call | solution.py:679
  418.9 5.6 collective-permute-done.39.d2
  429.4 3.8 fusion
  433.2 42.0 %collective-permute-done.36.h_ref.hf1 = bf16[2304,512]{1,0:T(8,128)(2,1)} collective-permute-done((bf16[2304,512]{1,0:T(8,128)(2,1)}, bf16[2304,512]{1,0:T(8,128)(2,1)}, u32[]{:S(2)}, u32[]{:S(2)}) %collective-permute-start.36) | collective-permute-done | bytes 2359328 | tf_op jit(solution)/shard_map/ppermute | solution.py:550
  475.7 49.0 %collective-permute-done.37.h_ref.hf0 = bf16[2304,512]{1,0:T(8,128)(2,1)} collective-permute-done((bf16[2304,512]{1,0:T(8,128)(2,1)}, bf16[2304,512]{1,0:T(8,128)(2,1)}, u32[]{:S(2)}, u32[]{:S(2)}) %collective-permute-start.37) | collective-permute-done | bytes 2359328 | tf_op jit(solution)/shard_map/ppermute | solution.py:550
  524.7 32.9 %shard_map.157.zw = bf16[1024,2304]{1,0:T(8,128)(2,1)} custom-call(s32[3]{0:T(128)} %pad_add_fusion.s_ref, bf16[1024,2304]{1,0:T(8,128)(2,1)} %get-tuple-element.29.refs_0_, bf16[576,2304]{1,0:T(8,128)(2,1)} %pad_maximum_fusion.refs_1_.refs_5_, bf16[576,2304]{1,0:T(8,128)(2,1)} %collective-permute-done.30.refs_2_.refs_6_, ...), custom_call_target="tpu_custom_call" | custom-call | flops 21743271936 | tf_op jit(solution)/shard_map/pallas_call | solution.py:705
  557.5 6.0 shard_map.158.rest_0_
  563.5 6.0 shard_map.159.refs_0_.refs_1_
  570.5 28.6 %collective-permute-done.47.refs_4_.refs_8_ = bf16[576,2304]{1,0:T(8,128)(2,1)} collective-permute-done((bf16[576,2304]{1,0:T(8,128)(2,1)}, bf16[576,2304]{1,0:T(8,128)(2,1)}, u32[]{:S(2)}, u32[]{:S(2)}) %collective-permute-start.47) | collective-permute-done | bytes 2654240 | tf_op jit(solution)/shard_map/ppermute | solution.py:550
  599.1 32.9 %shard_map.160.zf = bf16[1024,2304]{1,0:T(8,128)(2,1)} custom-call(s32[3]{0:T(128)} %pad_add_fusion.s_ref, bf16[1024,2304]{1,0:T(8,128)(2,1)} %shard_map.159.refs_0_.refs_1_, bf16[576,2304]{1,0:T(8,128)(2,1)} %pad_maximum_fusion.refs_1_.refs_5_, bf16[576,2304]{1,0:T(8,128)(2,1)} %collective-permute-done.30.refs_2_.refs_6_, ...), custom_call_target="tpu_custom_call" | custom-call | flops 21743271936 | tf_op jit(solution)/shard_map/pallas_call | solution.py:705
  632.6 23.4 %collective-permute-done.43.refs_3_.refs_7_ = bf16[576,2304]{1,0:T(8,128)(2,1)} collective-permute-done((bf16[576,2304]{1,0:T(8,128)(2,1)}, bf16[576,2304]{1,0:T(8,128)(2,1)}, u32[]{:S(2)}, u32[]{:S(2)}) %collective-permute-start.43) | collective-permute-done | bytes 2654240 | tf_op jit(solution)/shard_map/ppermute | solution.py:550
  656.0 32.0 %shard_map.161.part = f32[8,2304,256]{2,1,0:T(8,128)} custom-call(s32[3]{0:T(128)} %pad_add_fusion.s_ref, bf16[1024,2304]{1,0:T(8,128)(2,1)} %shard_map.157.zw, bf16[1024,2304]{1,0:T(8,128)(2,1)} %shard_map.160.zf, bf16[576,2304]{1,0:T(8,128)(2,1)} %copy-done, bf16[576,2304]{1,0:T(8,128)(2,1)} %collective-permute-done.38.d1, ...), custom_call_target="tpu_custom_call" | custom-call | flops 10871635968 | tf_op jit(solution)/shard_map/pallas_call | solution.py:720
  688.6 21.4 %collective-permute-done.51.d2 = bf16[576,2304]{1,0:T(8,128)(2,1)} collective-permute-done((bf16[576,2304]{1,0:T(8,128)(2,1)}, bf16[576,2304]{1,0:T(8,128)(2,1)}, u32[]{:S(2)}, u32[]{:S(2)}) %collective-permute-start.51) | collective-permute-done | bytes 2654240 | tf_op jit(solution)/shard_map/ppermute | solution.py:550
  710.5 30.9 %shard_map.164.zb = bf16[2048,1152]{1,0:T(8,128)(2,1)} custom-call(s32[3]{0:T(128)} %pad_add_fusion.s_ref, bf16[1024,2304]{1,0:T(8,128)(2,1)} %get-tuple-element.29.refs_0_, bf16[1024,2304]{1,0:T(8,128)(2,1)} %shard_map.159.refs_0_.refs_1_, bf16[576,2304]{1,0:T(8,128)(2,1)} %collective-permute-done.45.refs_2_.refs_6_, ...), custom_call_target="tpu_custom_call" | custom-call | flops 21743271936 | tf_op jit(solution)/shard_map/pallas_call | solution.py:705
  744.9 17.9 %shard_map.162.zwa = bf16[1024,1152]{1,0:T(8,128)(2,1)} custom-call(s32[3]{0:T(128)} %pad_add_fusion.s_ref, bf16[1024,2304]{1,0:T(8,128)(2,1)} %get-tuple-element.29.refs_0_, bf16[576,2304]{1,0:T(8,128)(2,1)} %collective-permute-done.41.refs_1_.refs_5_, bf16[576,2304]{1,0:T(8,128)(2,1)} %collective-permute-done.42.refs_2_.refs_6_, ...), custom_call_target="tpu_custom_call" | custom-call | flops 10871635968 | tf_op jit(solution)/shard_map/pallas_call | solution.py:705
  762.8 17.9 %shard_map.163.zfa = bf16[1024,1152]{1,0:T(8,128)(2,1)} custom-call(s32[3]{0:T(128)} %pad_add_fusion.s_ref, bf16[1024,2304]{1,0:T(8,128)(2,1)} %shard_map.159.refs_0_.refs_1_, bf16[576,2304]{1,0:T(8,128)(2,1)} %collective-permute-done.41.refs_1_.refs_5_, bf16[576,2304]{1,0:T(8,128)(2,1)} %collective-permute-done.42.refs_2_.refs_6_, ...), custom_call_target="tpu_custom_call" | custom-call | flops 10871635968 | tf_op jit(solution)/shard_map/pallas_call | solution.py:705
  780.8 20.7 %collective-permute-done.55.kv0 = bf16[1536,512]{1,0:T(8,128)(2,1)} collective-permute-done((bf16[1536,512]{1,0:T(8,128)(2,1)}, bf16[1536,512]{1,0:T(8,128)(2,1)}, u32[]{:S(2)}, u32[]{:S(2)}) %collective-permute-start.55) | collective-permute-done | bytes 1572896 | tf_op jit(solution)/shard_map/ppermute | solution.py:550
  801.5 32.7 %collective-permute-done.57.kv0 = bf16[1536,512]{1,0:T(8,128)(2,1)} collective-permute-done((bf16[1536,512]{1,0:T(8,128)(2,1)}, bf16[1536,512]{1,0:T(8,128)(2,1)}, u32[]{:S(2)}, u32[]{:S(2)}) %collective-permute-start.57) | collective-permute-done | bytes 1572896 | tf_op jit(solution)/shard_map/ppermute | solution.py:550
  834.2 127.5 %tail.1.rest_0_ = bf16[576,8192]{1,0:T(8,128)(2,1)} custom-call(f32[8,2304,256]{2,1,0:T(8,128)} %shard_map.161.part, bf16[1024,1152]{1,0:T(8,128)(2,1)} %shard_map.162.zwa, bf16[1024,1152]{1,0:T(8,128)(2,1)} %shard_map.163.zfa, bf16[2048,1152]{1,0:T(8,128)(2,1)} %shard_map.164.zb, bf16[576,768]{1,0:T(8,128)(2,1)} %collective-permute-done.49.d0, ...), custom_call_target="tpu_custom_call" | custom-call | flops 21743271936 | bytes 18874368 | tf_op jit(solution)/shard_map/tail/pallas_call | solution.py:724
  961.7 14.2 %shard_map.165 = (bf16[8192,2,256]{2,1,0:T(2,128)(2,1)}, bf16[8192,2,256]{2,1,0:T(2,128)(2,1)}) custom-call(s32[3]{0:T(128)} %pad_add_fusion.s_ref, bf16[4096,512]{1,0:T(8,128)(2,1)} %get-tuple-element.26.k_ref.kv0, bf16[4096,512]{1,0:T(8,128)(2,1)} %collective-permute-done.59.kv1), custom_call_target="tpu_custom_call" | custom-call | flops 4194304 | tf_op jit(solution)/shard_map/pallas_call | solution.py:751
  976.0 5.7 shard_map.166
  981.7 5.7 shard_map.167
  987.4 8.2 shard_map.168
  (150 shorter events, 68.3 us)
Async XLA Ops:
  3.9 56.9 %collective-permute-start.1 = (bf16[576,1024]{1,0:T(8,128)(2,1)}, bf16[576,1024]{1,0:T(8,128)(2,1)}, u32[]{:S(2)}, u32[]{:S(2)}) collective-permute-start(bf16[576,1024]{1,0:T(8,128)(2,1)} %get-tuple-element.44), channel_id=1, source_target_pairs={{0,2},{1,3},{2,0},{3,1},{4,6},{5,7},{6,4},{7,5}} | collective-permute-start | bytes 3538952 | tf_op jit(solution)/shard_map/ppermute | solution.py:550
  7.2 53.9 %collective-permute-start.8 = (bf16[576,1024]{1,0:T(8,128)(2,1)}, bf16[576,1024]{1,0:T(8,128)(2,1)}, u32[]{:S(2)}, u32[]{:S(2)}) collective-permute-start(bf16[576,1024]{1,0:T(8,128)(2,1)} %get-tuple-element.43), channel_id=1, source_target_pairs={{0,2},{1,3},{2,0},{3,1},{4,6},{5,7},{6,4},{7,5}} | collective-permute-start | bytes 3538952 | tf_op jit(solution)/shard_map/ppermute | solution.py:550
  14.2 46.5 %collective-permute-start.49 = (bf16[576,768]{1,0:T(8,128)(2,1)}, bf16[576,768]{1,0:T(8,128)(2,1)}, u32[]{:S(2)}, u32[]{:S(2)}) collective-permute-start(bf16[576,768]{1,0:T(8,128)(2,1)} %slice.18), channel_id=1, source_target_pairs={{0,4},{1,5},{2,6},{3,7},{4,0},{5,1},{6,2},{7,3}} | collective-permute-start | bytes 2654216 | tf_op jit(solution)/shard_map/ppermute | solution.py:550
  16.9 42.0 %collective-permute-start.6 = (bf16[4,576]{1,0:T(4,128)(2,1)}, bf16[4,576]{1,0:T(4,128)(2,1)}, u32[]{:S(2)}, u32[]{:S(2)}) collective-permute-start(bf16[4,576]{1,0:T(4,128)(2,1)} %pad_maximum_fusion.4), channel_id=1, source_target_pairs={{0,2},{1,3},{2,0},{3,1},{4,6},{5,7},{6,4},{7,5}} | collective-permute-start | bytes 13832 | tf_op jit(solution)/shard_map/ppermute | solution.py:550
  18.4 40.5 %collective-permute-start.7 = (bf16[4,576]{1,0:T(4,128)(2,1)}, bf16[4,576]{1,0:T(4,128)(2,1)}, u32[]{:S(2)}, u32[]{:S(2)}) collective-permute-start(bf16[4,576]{1,0:T(4,128)(2,1)} %pad_maximum_fusion.4), channel_id=1, source_target_pairs={{0,3},{1,2},{2,1},{3,0},{4,7},{5,6},{6,5},{7,4}} | collective-permute-start | bytes 13832 | tf_op jit(solution)/shard_map/ppermute | solution.py:550
  60.7 52.0 %collective-permute-start.14 = (bf16[576,1024]{1,0:T(8,128)(2,1)}, bf16[576,1024]{1,0:T(8,128)(2,1)}, u32[]{:S(2)}, u32[]{:S(2)}) collective-permute-start(bf16[576,1024]{1,0:T(8,128)(2,1)} %get-tuple-element.23), channel_id=1, source_target_pairs={{0,3},{1,2},{2,1},{3,0},{4,7},{5,6},{6,5},{7,4}} | collective-permute-start | bytes 3538952 | tf_op jit(solution)/shard_map/ppermute | solution.py:550
  60.8 52.7 %collective-permute-start.20 = (bf16[4,576,256]{2,1,0:T(8,128)(2,1)}, bf16[4,576,256]{2,1,0:T(8,128)(2,1)S(1)}, u32[]{:S(2)}, u32[]{:S(2)}) collective-permute-start(bf16[4,576,256]{2,1,0:T(8,128)(2,1)} %bitcast.31), channel_id=1, source_target_pairs={{0,1},{1,0},{2,3},{3,2},{4,5},{5,4},{6,7},{7,6}} | collective-permute-start | bytes 3538952 | tf_op jit(solution)/shard_map/ppermute | solution.py:550
  61.1 77.1 %collective-permute-start.21 = (bf16[4,576,256]{2,1,0:T(8,128)(2,1)}, bf16[4,576,256]{2,1,0:T(8,128)(2,1)}, u32[]{:S(2)}, u32[]{:S(2)}) collective-permute-start(bf16[4,576,256]{2,1,0:T(8,128)(2,1)} %bitcast.32), channel_id=1, source_target_pairs={{0,2},{1,3},{2,0},{3,1},{4,6},{5,7},{6,4},{7,5}} | collective-permute-start | bytes 3538952 | tf_op jit(solution)/shard_map/ppermute | solution.py:550
  65.2 73.0 %collective-permute-start.23 = (bf16[4,576,256]{2,1,0:T(8,128)(2,1)}, bf16[4,576,256]{2,1,0:T(8,128)(2,1)}, u32[]{:S(2)}, u32[]{:S(2)}) collective-permute-start(bf16[4,576,256]{2,1,0:T(8,128)(2,1)} %bitcast.33), channel_id=1, source_target_pairs={{0,4},{1,5},{2,6},{3,7},{4,0},{5,1},{6,2},{7,3}} | collective-permute-start | bytes 3538952 | tf_op jit(solution)/shard_map/ppermute | solution.py:550
  88.0 52.0 %collective-permute-start.53 = (bf16[576,1024]{1,0:T(8,128)(2,1)}, bf16[576,1024]{1,0:T(8,128)(2,1)}, u32[]{:S(2)}, u32[]{:S(2)}) collective-permute-start(bf16[576,1024]{1,0:T(8,128)(2,1)} %slice.19), channel_id=1, source_target_pairs={{0,4},{1,5},{2,6},{3,7},{4,0},{5,1},{6,2},{7,3}} | collective-permute-start | bytes 3538952 | tf_op jit(solution)/shard_map/ppermute | solution.py:550
  112.6 127.6 %collective-permute-start = (bf16[576,4096]{1,0:T(8,128)(2,1)}, bf16[576,4096]{1,0:T(8,128)(2,1)}, u32[]{:S(2)}, u32[]{:S(2)}) collective-permute-start(bf16[576,4096]{1,0:T(8,128)(2,1)} %dynamic-slice_bitcast_fusion), channel_id=1, source_target_pairs={{0,1},{1,0},{2,3},{3,2},{4,5},{5,4},{6,7},{7,6}} | collective-permute-start | bytes 14155784 | tf_op jit(solution)/shard_map/ppermute | solution.py:550
  113.5 29.2 %collective-permute-start.2 = (bf16[576,1024]{1,0:T(8,128)(2,1)}, bf16[576,1024]{1,0:T(8,128)(2,1)S(1)}, u32[]{:S(2)}, u32[]{:S(2)}) collective-permute-start(bf16[576,1024]{1,0:T(8,128)(2,1)} %collective-permute-done.1.rx.x2), channel_id=1, source_target_pairs={{0,1},{1,0},{2,3},{3,2},{4,5},{5,4},{6,7},{7,6}} | collective-permute-start | bytes 3538952 | tf_op jit(solution)/shard_map/ppermute | solution.py:550
  138.2 29.2 %collective-permute-start.3 = (bf16[576,1024]{1,0:T(8,128)(2,1)}, bf16[576,1024]{1,0:T(8,128)(2,1)}, u32[]{:S(2)}, u32[]{:S(2)}) collective-permute-start(bf16[576,1024]{1,0:T(8,128)(2,1)} %collective-permute-done.1.rx.x2), channel_id=1, source_target_pairs={{0,4},{1,5},{2,6},{3,7},{4,0},{5,1},{6,2},{7,3}} | collective-permute-start | bytes 3538952 | tf_op jit(solution)/shard_map/ppermute | solution.py:550
  141.0 51.7 %collective-permute-start.10 = (bf16[576,1024]{1,0:T(8,128)(2,1)}, bf16[576,1024]{1,0:T(8,128)(2,1)}, u32[]{:S(2)}, u32[]{:S(2)}) collective-permute-start(bf16[576,1024]{1,0:T(8,128)(2,1)} %collective-permute-done.8.rx.x2), channel_id=1, source_target_pairs={{0,4},{1,5},{2,6},{3,7},{4,0},{5,1},{6,2},{7,3}} | collective-permute-start | bytes 3538952 | tf_op jit(solution)/shard_map/ppermute | solution.py:550
  143.8 48.9 %collective-permute-start.22 = (bf16[4,576,256]{2,1,0:T(8,128)(2,1)}, bf16[4,576,256]{2,1,0:T(8,128)(2,1)}, u32[]{:S(2)}, u32[]{:S(2)}) collective-permute-start(bf16[4,576,256]{2,1,0:T(8,128)(2,1)} %collective-permute-done.21.b1), channel_id=1, source_target_pairs={{0,1},{1,0},{2,3},{3,2},{4,5},{5,4},{6,7},{7,6}} | collective-permute-start | bytes 3538952 | tf_op jit(solution)/shard_map/ppermute | solution.py:550
  167.4 101.0 %collective-permute-start.30 = (bf16[576,2304]{1,0:T(8,128)(2,1)}, bf16[576,2304]{1,0:T(8,128)(2,1)}, u32[]{:S(2)}, u32[]{:S(2)}) collective-permute-start(bf16[576,2304]{1,0:T(8,128)(2,1)} %pad_maximum_fusion.refs_1_.refs_5_), channel_id=1, source_target_pairs={{0,1},{1,0},{2,3},{3,2},{4,5},{5,4},{6,7},{7,6}} | collective-permute-start | bytes 7962632 | tf_op jit(solution)/shard_map/ppermute | solution.py:550
  167.4 50.1 %collective-permute-start.25 = (bf16[4,576,256]{2,1,0:T(8,128)(2,1)}, bf16[4,576,256]{2,1,0:T(8,128)(2,1)}, u32[]{:S(2)}, u32[]{:S(2)}) collective-permute-start(bf16[4,576,256]{2,1,0:T(8,128)(2,1)} %collective-permute-done.21.b1), channel_id=1, source_target_pairs={{0,4},{1,5},{2,6},{3,7},{4,0},{5,1},{6,2},{7,3}} | collective-permute-start | bytes 3538952 | tf_op jit(solution)/shard_map/ppermute | solution.py:550
  192.7 41.8 %collective-permute-start.11 = (bf16[576,1024]{1,0:T(8,128)(2,1)}, bf16[576,1024]{1,0:T(8,128)(2,1)}, u32[]{:S(2)}, u32[]{:S(2)}) collective-permute-start(bf16[576,1024]{1,0:T(8,128)(2,1)} %collective-permute-done.10.ry), channel_id=1, source_target_pairs={{0,1},{1,0},{2,3},{3,2},{4,5},{5,4},{6,7},{7,6}} | collective-permute-start | bytes 3538952 | tf_op jit(solution)/shard_map/ppermute | solution.py:550
  217.5 118.4 %collective-permute-start.31 = (bf16[576,2304]{1,0:T(8,128)(2,1)}, bf16[576,2304]{1,0:T(8,128)(2,1)}, u32[]{:S(2)}, u32[]{:S(2)}) collective-permute-start(bf16[576,2304]{1,0:T(8,128)(2,1)} %pad_maximum_fusion.1), channel_id=1, source_target_pairs={{0,2},{1,3},{2,0},{3,1},{4,6},{5,7},{6,4},{7,5}} | collective-permute-start | bytes 7962632 | tf_op jit(solution)/shard_map/ppermute | solution.py:550
  219.2 116.7 %collective-permute-start.34 = (bf16[576,2304]{1,0:T(8,128)(2,1)}, bf16[576,2304]{1,0:T(8,128)(2,1)}, u32[]{:S(2)}, u32[]{:S(2)}) collective-permute-start(bf16[576,2304]{1,0:T(8,128)(2,1)} %pad_maximum_fusion.3), channel_id=1, source_target_pairs={{0,2},{1,3},{2,0},{3,1},{4,6},{5,7},{6,4},{7,5}} | collective-permute-start | bytes 7962632 | tf_op jit(solution)/shard_map/ppermute | solution.py:550
  234.4 33.9 %collective-permute-start.24 = (bf16[4,576,256]{2,1,0:T(8,128)(2,1)}, bf16[4,576,256]{2,1,0:T(8,128)(2,1)}, u32[]{:S(2)}, u32[]{:S(2)}) collective-permute-start(bf16[4,576,256]{2,1,0:T(8,128)(2,1)} %collective-permute-done.23.b2), channel_id=1, source_target_pairs={{0,1},{1,0},{2,3},{3,2},{4,5},{5,4},{6,7},{7,6}} | collective-permute-start | bytes 3538952 | tf_op jit(solution)/shard_map/ppermute | solution.py:550
  240.3 97.4 %collective-permute-start.26 = (bf16[4,576,256]{2,1,0:T(8,128)(2,1)}, bf16[4,576,256]{2,1,0:T(8,128)(2,1)}, u32[]{:S(2)}, u32[]{:S(2)}) collective-permute-start(bf16[4,576,256]{2,1,0:T(8,128)(2,1)} %collective-permute-done.25.b3), channel_id=1, source_target_pairs={{0,1},{1,0},{2,3},{3,2},{4,5},{5,4},{6,7},{7,6}} | collective-permute-start | bytes 3538952 | tf_op jit(solution)/shard_map/ppermute | solution.py:550
  268.4 150.5 %collective-permute-start.38 = (bf16[576,2304]{1,0:T(8,128)(2,1)}, bf16[576,2304]{1,0:T(8,128)(2,1)}, u32[]{:S(2)}, u32[]{:S(2)}) collective-permute-start(bf16[576,2304]{1,0:T(8,128)(2,1)} %copy-done), channel_id=1, source_target_pairs={{0,1},{1,0},{2,3},{3,2},{4,5},{5,4},{6,7},{7,6}} | collective-permute-start | bytes 7962632 | tf_op jit(solution)/shard_map/ppermute | solution.py:550
  268.4 147.8 %collective-permute-start.33 = (bf16[576,2304]{1,0:T(8,128)(2,1)}, bf16[576,2304]{1,0:T(8,128)(2,1)}, u32[]{:S(2)}, u32[]{:S(2)}) collective-permute-start(bf16[576,2304]{1,0:T(8,128)(2,1)} %pad_maximum_fusion.2.refs_9_.refs_13_), channel_id=1, source_target_pairs={{0,1},{1,0},{2,3},{3,2},{4,5},{5,4},{6,7},{7,6}} | collective-permute-start | bytes 7962632 | tf_op jit(solution)/shard_map/ppermute | solution.py:550
  363.4 61.1 %collective-permute-start.39 = (bf16[576,2304]{1,0:T(8,128)(2,1)}, bf16[576,2304]{1,0:T(8,128)(2,1)}, u32[]{:S(2)}, u32[]{:S(2)}) collective-permute-start(bf16[576,2304]{1,0:T(8,128)(2,1)} %get-tuple-element.45), channel_id=1, source_target_pairs={{0,2},{1,3},{2,0},{3,1},{4,6},{5,7},{6,4},{7,5}} | collective-permute-start | bytes 7962632 | tf_op jit(solution)/shard_map/ppermute | solution.py:550
  373.5 51.6 %collective-permute-start.32 = (bf16[576,2304]{1,0:T(8,128)(2,1)}, bf16[576,2304]{1,0:T(8,128)(2,1)}, u32[]{:S(2)}, u32[]{:S(2)}) collective-permute-start(bf16[576,2304]{1,0:T(8,128)(2,1)} %collective-permute-done.31.refs_3_.refs_7_), channel_id=1, source_target_pairs={{0,1},{1,0},{2,3},{3,2},{4,5},{5,4},{6,7},{7,6}} | collective-permute-start | bytes 7962632 | tf_op jit(solution)/shard_map/ppermute | solution.py:550
  383.7 42.9 %collective-permute-start.35 = (bf16[576,2304]{1,0:T(8,128)(2,1)}, bf16[576,2304]{1,0:T(8,128)(2,1)}, u32[]{:S(2)}, u32[]{:S(2)}) collective-permute-start(bf16[576,2304]{1,0:T(8,128)(2,1)} %collective-permute-done.34.refs_11_.refs_15_), channel_id=1, source_target_pairs={{0,1},{1,0},{2,3},{3,2},{4,5},{5,4},{6,7},{7,6}} | collective-permute-start | bytes 7962632 | tf_op jit(solution)/shard_map/ppermute | solution.py:550
  416.3 58.9 %collective-permute-start.36 = (bf16[2304,512]{1,0:T(8,128)(2,1)}, bf16[2304,512]{1,0:T(8,128)(2,1)}, u32[]{:S(2)}, u32[]{:S(2)}) collective-permute-start(bf16[2304,512]{1,0:T(8,128)(2,1)} %get-tuple-element.30.hw1), channel_id=1, source_target_pairs={{0,2},{1,3},{2,0},{3,1},{4,6},{5,7},{6,4},{7,5}} | collective-permute-start | bytes 7077896 | tf_op jit(solution)/shard_map/ppermute | solution.py:550
  418.9 105.8 %collective-permute-start.37 = (bf16[2304,512]{1,0:T(8,128)(2,1)}, bf16[2304,512]{1,0:T(8,128)(2,1)}, u32[]{:S(2)}, u32[]{:S(2)}) collective-permute-start(bf16[2304,512]{1,0:T(8,128)(2,1)} %get-tuple-element.31.hw0), channel_id=1, source_target_pairs={{0,2},{1,3},{2,0},{3,1},{4,6},{5,7},{6,4},{7,5}} | collective-permute-start | bytes 7077896 | tf_op jit(solution)/shard_map/ppermute | solution.py:550
  424.6 144.9 %collective-permute-start.41 = (bf16[576,2304]{1,0:T(8,128)(2,1)}, bf16[576,2304]{1,0:T(8,128)(2,1)}, u32[]{:S(2)}, u32[]{:S(2)}) collective-permute-start(bf16[576,2304]{1,0:T(8,128)(2,1)} %pad_maximum_fusion.refs_1_.refs_5_), channel_id=1, source_target_pairs={{0,4},{1,5},{2,6},{3,7},{4,0},{5,1},{6,2},{7,3}} | collective-permute-start | bytes 7962632 | tf_op jit(solution)/shard_map/ppermute | solution.py:550
  425.1 145.1 %collective-permute-start.45 = (bf16[576,2304]{1,0:T(8,128)(2,1)}, bf16[576,2304]{1,0:T(8,128)(2,1)}, u32[]{:S(2)}, u32[]{:S(2)}) collective-permute-start(bf16[576,2304]{1,0:T(8,128)(2,1)} %pad_maximum_fusion.2.refs_9_.refs_13_), channel_id=1, source_target_pairs={{0,4},{1,5},{2,6},{3,7},{4,0},{5,1},{6,2},{7,3}} | collective-permute-start | bytes 7962632 | tf_op jit(solution)/shard_map/ppermute | solution.py:550
  426.6 172.5 %collective-permute-start.47 = (bf16[576,2304]{1,0:T(8,128)(2,1)}, bf16[576,2304]{1,0:T(8,128)(2,1)}, u32[]{:S(2)}, u32[]{:S(2)}) collective-permute-start(bf16[576,2304]{1,0:T(8,128)(2,1)} %collective-permute-done.34.refs_11_.refs_15_), channel_id=1, source_target_pairs={{0,4},{1,5},{2,6},{3,7},{4,0},{5,1},{6,2},{7,3}} | collective-permute-start | bytes 7962632 | tf_op jit(solution)/shard_map/ppermute | solution.py:550
  475.1 180.8 %collective-permute-start.43 = (bf16[576,2304]{1,0:T(8,128)(2,1)}, bf16[576,2304]{1,0:T(8,128)(2,1)}, u32[]{:S(2)}, u32[]{:S(2)}) collective-permute-start(bf16[576,2304]{1,0:T(8,128)(2,1)} %collective-permute-done.31.refs_3_.refs_7_), channel_id=1, source_target_pairs={{0,4},{1,5},{2,6},{3,7},{4,0},{5,1},{6,2},{7,3}} | collective-permute-start | bytes 7962632 | tf_op jit(solution)/shard_map/ppermute | solution.py:550
  524.7 107.4 %collective-permute-start.40 = (bf16[576,2304]{1,0:T(8,128)(2,1)}, bf16[576,2304]{1,0:T(8,128)(2,1)}, u32[]{:S(2)}, u32[]{:S(2)}) collective-permute-start(bf16[576,2304]{1,0:T(8,128)(2,1)} %collective-permute-done.39.d2), channel_id=1, source_target_pairs={{0,1},{1,0},{2,3},{3,2},{4,5},{5,4},{6,7},{7,6}} | collective-permute-start | bytes 7962632 | tf_op jit(solution)/shard_map/ppermute | solution.py:550
  569.5 140.5 %collective-permute-start.51 = (bf16[576,2304]{1,0:T(8,128)(2,1)}, bf16[576,2304]{1,0:T(8,128)(2,1)}, u32[]{:S(2)}, u32[]{:S(2)}) collective-permute-start(bf16[576,2304]{1,0:T(8,128)(2,1)} %collective-permute-done.39.d2), channel_id=1, source_target_pairs={{0,4},{1,5},{2,6},{3,7},{4,0},{5,1},{6,2},{7,3}} | collective-permute-start | bytes 7962632 | tf_op jit(solution)/shard_map/ppermute | solution.py:550
  570.2 117.8 %collective-permute-start.46 = (bf16[576,2304]{1,0:T(8,128)(2,1)}, bf16[576,2304]{1,0:T(8,128)(2,1)}, u32[]{:S(2)}, u32[]{:S(2)}) collective-permute-start(bf16[576,2304]{1,0:T(8,128)(2,1)} %collective-permute-done.45.refs_2_.refs_6_), channel_id=1, source_target_pairs={{0,1},{1,0},{2,3},{3,2},{4,5},{5,4},{6,7},{7,6}} | collective-permute-start | bytes 7962632 | tf_op jit(solution)/shard_map/ppermute | solution.py:550
  599.1 110.9 %collective-permute-start.48 = (bf16[576,2304]{1,0:T(8,128)(2,1)}, bf16[576,2304]{1,0:T(8,128)(2,1)}, u32[]{:S(2)}, u32[]{:S(2)}) collective-permute-start(bf16[576,2304]{1,0:T(8,128)(2,1)} %collective-permute-done.47.refs_4_.refs_8_), channel_id=1, source_target_pairs={{0,1},{1,0},{2,3},{3,2},{4,5},{5,4},{6,7},{7,6}} | collective-permute-start | bytes 7962632 | tf_op jit(solution)/shard_map/ppermute | solution.py:550
  632.1 110.8 %collective-permute-start.42 = (bf16[576,2304]{1,0:T(8,128)(2,1)}, bf16[576,2304]{1,0:T(8,128)(2,1)}, u32[]{:S(2)}, u32[]{:S(2)}) collective-permute-start(bf16[576,2304]{1,0:T(8,128)(2,1)} %collective-permute-done.41.refs_1_.refs_5_), channel_id=1, source_target_pairs={{0,1},{1,0},{2,3},{3,2},{4,5},{5,4},{6,7},{7,6}} | collective-permute-start | bytes 7962632 | tf_op jit(solution)/shard_map/ppermute | solution.py:550
  656.0 87.5 %collective-permute-start.44 = (bf16[576,2304]{1,0:T(8,128)(2,1)}, bf16[576,2304]{1,0:T(8,128)(2,1)}, u32[]{:S(2)}, u32[]{:S(2)}) collective-permute-start(bf16[576,2304]{1,0:T(8,128)(2,1)} %collective-permute-done.43.refs_3_.refs_7_), channel_id=1, source_target_pairs={{0,1},{1,0},{2,3},{3,2},{4,5},{5,4},{6,7},{7,6}} | collective-permute-start | bytes 7962632 | tf_op jit(solution)/shard_map/ppermute | solution.py:550
  688.0 53.3 %collective-permute-start.54 = (bf16[576,1024]{1,0:T(8,128)(2,1)}, bf16[576,1024]{1,0:T(8,128)(2,1)}, u32[]{:S(2)}, u32[]{:S(2)}) collective-permute-start(bf16[576,1024]{1,0:T(8,128)(2,1)} %collective-permute-done.53.e0), channel_id=1, source_target_pairs={{0,1},{1,0},{2,3},{3,2},{4,5},{5,4},{6,7},{7,6}} | collective-permute-start | bytes 3538952 | tf_op jit(solution)/shard_map/ppermute | solution.py:550
  710.0 251.8 %collective-permute-start.59 = (bf16[4096,512]{1,0:T(8,128)(2,1)}, bf16[4096,512]{1,0:T(8,128)(2,1)}, u32[]{:S(2)}, u32[]{:S(2)}) collective-permute-start(bf16[4096,512]{1,0:T(8,128)(2,1)} %get-tuple-element.26.k_ref.kv0), channel_id=1, source_target_pairs={{0,1},{1,0},{2,3},{3,2},{4,5},{5,4},{6,7},{7,6}} | collective-permute-start | bytes 12582920 | tf_op jit(solution)/shard_map/ppermute | solution.py:550
  710.0 124.2 %collective-permute-start.52 = (bf16[576,2304]{1,0:T(8,128)(2,1)}, bf16[576,2304]{1,0:T(8,128)(2,1)}, u32[]{:S(2)}, u32[]{:S(2)}) collective-permute-start(bf16[576,2304]{1,0:T(8,128)(2,1)} %collective-permute-done.51.d2), channel_id=1, source_target_pairs={{0,1},{1,0},{2,3},{3,2},{4,5},{5,4},{6,7},{7,6}} | collective-permute-start | bytes 7962632 | tf_op jit(solution)/shard_map/ppermute | solution.py:550
  741.4 39.4 %collective-permute-start.15 = (bf16[1024,512]{1,0:T(8,128)(2,1)}, bf16[1024,512]{1,0:T(8,128)(2,1)}, u32[]{:S(2)}, u32[]{:S(2)}) collective-permute-start(bf16[1024,512]{1,0:T(8,128)(2,1)} %split.9), channel_id=1, source_target_pairs={{0,2},{1,3},{2,0},{3,1},{4,6},{5,7},{6,4},{7,5}} | collective-permute-start | bytes 3145736 | tf_op jit(solution)/shard_map/ppermute | solution.py:550
  742.9 58.6 %collective-permute-start.55 = (bf16[1536,512]{1,0:T(8,128)(2,1)}, bf16[1536,512]{1,0:T(8,128)(2,1)}, u32[]{:S(2)}, u32[]{:S(2)}) collective-permute-start(bf16[1536,512]{1,0:T(8,128)(2,1)} %get-tuple-element.56), channel_id=1, source_target_pairs={{0,2},{1,3},{2,0},{3,1},{4,6},{5,7},{6,4},{7,5}} | collective-permute-start | bytes 4718600 | tf_op jit(solution)/shard_map/ppermute | solution.py:550
  743.4 90.8 %collective-permute-start.57 = (bf16[1536,512]{1,0:T(8,128)(2,1)}, bf16[1536,512]{1,0:T(8,128)(2,1)}, u32[]{:S(2)}, u32[]{:S(2)}) collective-permute-start(bf16[1536,512]{1,0:T(8,128)(2,1)} %get-tuple-element.55), channel_id=1, source_target_pairs={{0,2},{1,3},{2,0},{3,1},{4,6},{5,7},{6,4},{7,5}} | collective-permute-start | bytes 4718600 | tf_op jit(solution)/shard_map/ppermute | solution.py:550
  780.8 206.6 %collective-permute-start.16 = (bf16[1024,512]{1,0:T(8,128)(2,1)}, bf16[1024,512]{1,0:T(8,128)(2,1)}, u32[]{:S(2)}, u32[]{:S(2)}) collective-permute-start(bf16[1024,512]{1,0:T(8,128)(2,1)} %collective-permute-done.15.kv0), channel_id=1, source_target_pairs={{0,1},{1,0},{2,3},{3,2},{4,5},{5,4},{6,7},{7,6}} | collective-permute-start | bytes 3145736 | tf_op jit(solution)/shard_map/ppermute | solution.py:550
  801.5 180.2 %collective-permute-start.56 = (bf16[1536,512]{1,0:T(8,128)(2,1)}, bf16[1536,512]{1,0:T(8,128)(2,1)}, u32[]{:S(2)}, u32[]{:S(2)}) collective-permute-start(bf16[1536,512]{1,0:T(8,128)(2,1)} %collective-permute-done.55.kv0), channel_id=1, source_target_pairs={{0,1},{1,0},{2,3},{3,2},{4,5},{5,4},{6,7},{7,6}} | collective-permute-start | bytes 4718600 | tf_op jit(solution)/shard_map/ppermute | solution.py:550
  834.2 141.8 %collective-permute-start.58 = (bf16[1536,512]{1,0:T(8,128)(2,1)}, bf16[1536,512]{1,0:T(8,128)(2,1)}, u32[]{:S(2)}, u32[]{:S(2)}) collective-permute-start(bf16[1536,512]{1,0:T(8,128)(2,1)} %collective-permute-done.57.kv0), channel_id=1, source_target_pairs={{0,1},{1,0},{2,3},{3,2},{4,5},{5,4},{6,7},{7,6}} | collective-permute-start | bytes 4718600 | tf_op jit(solution)/shard_map/ppermute | solution.py:550
  (25 other events, 437.5 us)
